TPU v7x, 512 devices: a whole 4x8x8 slice. The times are simulated.
512 devices in a mesh: req: 16 (over x, z_lo), patch: 32 (over y, z_hi, core).
Axes of the slice: x: 4, y: 8, z: 8 (z_hi: 2, z_lo: 4; z = z_hi * 4 + z_lo), core: 2. Of those that a mesh axis runs over, the one named last changes fastest.
Arguments:
- field: float32 [1024, 16, 640], P(('req', 'patch')), parts along dimension 0
- stale_conv_in: bfloat16 [1024, 16, 640], P(('req', 'patch')), parts along dimension 0, may hold values from -6 to 6
- stale_keys: bfloat16 [16384, 320], P(('req', 'patch')), parts along dimension 0, may hold values from -6 to 6
- stale_values: bfloat16 [16384, 320], P(('req', 'patch')), parts along dimension 0, may hold values from -6 to 6
- norm1_gain: float32 [640], replicated, may hold values from 0.25 to 1.75
- norm1_bias: float32 [640], replicated, may hold values from -3 to 3
- conv_weight: bfloat16 [3, 3, 640, 640], P(None, None, None, 'patch'), may hold values from -0.078125 to 0.078125
- conv_bias: float32 [640], replicated, may hold values from -3 to 3
- time_embed: float32 [32, 640], P('req'), parts along dimension 0, may hold values from -5 to 5
- norm2_gain: float32 [640], replicated, may hold values from 0.25 to 1.75
- norm2_bias: float32 [640], replicated, may hold values from -3 to 3
- w_query: bfloat16 [640, 320], replicated
- w_keyvalue: bfloat16 [640, 640], replicated, may hold values from -0.25 to 0.25
- w_out: bfloat16 [320, 640], replicated, may hold values from -0.3125 to 0.3125
Outputs:
- outputs: float32 [2, 1024, 16, 640], P(None, ('req', 'patch')), parts along dimension 1
There are 16 independent parts, one for each index of `req`. A program takes and returns all parts, laid end to end along the dimension named above; an argument that names none is the same for every part. Nothing has to cross between parts.
All inputs are finite; a program needn't handle non-finite values.
Results may differ from a plain program's by a relative error of at most 0.0047.
Values may be sent and summed in bfloat16 or wider, within the bound.
No kernel may reach another device: no remote copies, remote signals or barrier semaphores. Data moves between devices by JAX's collectives and lax.ppermute only.
A program may use at most 64 MiB of HBM per device.

v0:
```python
import jax
import jax.numpy as jnp
from jax import lax
from jax.sharding import Mesh
from jax.sharding import PartitionSpec as P

GROUPS = 32
HEADS = 5
HEAD_DIM = 64
PATCH = ("patch_0", "patch_1", "patch_2")
REQ_PATCH = ("req", "patch_0", "patch_1", "patch_2")


epsilon = 1e-05


def sent_to_all(value, axis):
    length = lax.axis_size(axis)
    return lax.all_to_all(
        jnp.broadcast_to(value[None], (length, *value.shape)), axis, 0, 0, tiled=True
    )


def of_everyone(value, axis):
    return sent_to_all(value, axis).sum(axis=0)


def together(arrays, axis):
    line, at, outs = (jnp.concatenate([a.reshape(-1) for a in arrays]), 0, [])
    total = of_everyone(line, axis)
    for a in arrays:
        outs.append(total[at : at + a.size].reshape(a.shape))
        at += a.size
    return tuple(outs)


def side_by_side(arrays, axis, dim, along):
    both = jnp.concatenate(arrays, axis=along)
    whole, at, outs = (lax.all_gather(both, axis, axis=dim, tiled=True), 0, [])
    for a in arrays:
        outs.append(lax.slice_in_dim(whole, at, at + a.shape[along], axis=along))
        at += a.shape[along]
    return tuple(outs)


def joined_along(blocks, dim):
    lengths = list(blocks.shape[1:])
    lengths[dim] *= blocks.shape[0]
    return jnp.moveaxis(blocks, 0, dim).reshape(lengths)


def all_blocks(value, axes, sequence):
    blocks = value[None]
    for k in sequence:
        blocks = lax.all_gather(blocks, axes[k], axis=0, tiled=True)
    held = [lax.axis_size(axes[k]) for k in reversed(sequence)]
    blocks = blocks.reshape(*held, *value.shape)
    turned = sorted(range(len(sequence)), key=lambda place: sequence[len(sequence) - 1 - place])
    return blocks.transpose(*turned, *range(len(sequence), blocks.ndim)).reshape(-1, *value.shape)


def gathered_by_axis(value, axes, sequence, dim):
    return joined_along(all_blocks(value, axes, sequence), dim)


def extended(block, sides, width):
    for axis, dim in sides:
        count = lax.axis_size(axis)
        forward = [(i, i + 1) for i in range(count - 1)]
        backward = [(target, source) for source, target in forward]
        low = lax.ppermute(
            lax.slice_in_dim(block, block.shape[dim] - width, None, axis=dim), axis, forward
        )
        high = lax.ppermute(lax.slice_in_dim(block, 0, width, axis=dim), axis, backward)
        block = jnp.concatenate([low, block, high], axis=dim)
    return block


def group_norm(values_in, gain, bias):
    members = values_in.shape[2] // GROUPS
    grouped = values_in.reshape(-1, GROUPS, members)
    totals, squares = together(
        (jnp.sum(grouped, axis=(0, 2)), jnp.sum(grouped * grouped, axis=(0, 2))), PATCH
    )
    number = grouped.shape[0] * lax.axis_size(PATCH) * members
    average = totals / number
    variance = squares / number - average * average
    scaled = (grouped - average[None, :, None]) * lax.rsqrt(variance + epsilon)[None, :, None]
    return scaled.reshape(values_in.shape) * gain + bias


def conv_rows(padded, kernel):
    inner = padded.shape[1] - 2
    across = padded.shape[2] - 2
    result = None
    for offset_row in range(3):
        for offset_col in range(3):
            window = padded[:, offset_row : offset_row + inner, offset_col : offset_col + across, :]
            window = window.reshape(-1, padded.shape[3])
            term = jnp.dot(
                window, kernel[offset_row, offset_col], preferred_element_type=jnp.float32
            )
            result = term if result is None else result + term
    return result


def attend(normed, w_query, w_keyvalue, w_out, prior_keys, prior_values):
    key_width = w_query.shape[1]
    own_rows = normed.shape[0]
    query = jnp.dot(normed, w_query, preferred_element_type=jnp.float32).astype(jnp.bfloat16)
    keyvalue = jnp.dot(normed, w_keyvalue, preferred_element_type=jnp.float32).astype(jnp.bfloat16)
    keys = keyvalue[:, :key_width]
    values = keyvalue[:, key_width:]
    all_keys, all_values = side_by_side((prior_keys, prior_values), PATCH, 0, 1)
    start = lax.axis_index(PATCH) * own_rows
    all_keys = lax.dynamic_update_slice_in_dim(all_keys, keys, start, 0)
    all_values = lax.dynamic_update_slice_in_dim(all_values, values, start, 0)
    query_heads = query.reshape(own_rows, HEADS, HEAD_DIM)
    key_heads = all_keys.reshape(-1, HEADS, HEAD_DIM)
    value_heads = all_values.reshape(-1, HEADS, HEAD_DIM)
    scores = jnp.einsum(
        "qhd,khd->hqk", query_heads, key_heads, preferred_element_type=jnp.float32
    ) * HEAD_DIM ** (-0.5)
    peak = jnp.max(scores, axis=-1, keepdims=True)
    expo = jnp.exp(scores - peak)
    totals = jnp.sum(expo, axis=-1, keepdims=True)
    weights = expo.astype(jnp.bfloat16)
    summed = (
        jnp.einsum("hqk,khd->hqd", weights, value_heads, preferred_element_type=jnp.float32)
        / totals
    )
    attended = summed.transpose(1, 0, 2).reshape(own_rows, key_width).astype(jnp.bfloat16)
    mixed = jnp.dot(attended, w_out, preferred_element_type=jnp.float32)
    return (mixed, keys, values)


def per_device(
    field,
    stale_conv_in,
    stale_keys,
    stale_values,
    norm1_gain,
    norm1_bias,
    conv_weight,
    conv_bias,
    time_embed,
    norm2_gain,
    norm2_bias,
    w_query,
    w_keyvalue,
    w_out,
):
    channels = field.shape[2]
    state = field
    prior_conv = stale_conv_in
    prior_keys = stale_keys
    prior_values = stale_values
    full_kernel = gathered_by_axis(conv_weight, PATCH, (1, 0, 2), 3)
    results = []
    for which_step in range(2):
        activated = jax.nn.silu(group_norm(state, norm1_gain, norm1_bias)).astype(jnp.bfloat16)
        rimmed = extended(prior_conv, ((PATCH, 0),), 1)
        stacked = jnp.concatenate([rimmed[:1], activated, rimmed[-1:]], axis=0)[None]
        padded = jnp.pad(stacked, ((0, 0), (0, 0), (1, 1), (0, 0)))
        conv_out = conv_rows(padded, full_kernel).reshape(state.shape)
        hidden = state + (conv_out + conv_bias + time_embed[which_step])
        normed = (
            group_norm(hidden, norm2_gain, norm2_bias).astype(jnp.bfloat16).reshape(-1, channels)
        )
        mixed, prior_keys, prior_values = attend(
            normed, w_query, w_keyvalue, w_out, prior_keys, prior_values
        )
        result = hidden + mixed.reshape(hidden.shape)
        results.append(result)
        state = result
        prior_conv = activated
    return jnp.stack(results)


def solution(mesh):
    torus = Mesh(
        mesh.devices.reshape(mesh.shape["req"], 8, 2, 2), ("req", "patch_0", "patch_1", "patch_2")
    )
    placed = (
        P(REQ_PATCH, None, None),
        P(REQ_PATCH, None, None),
        P(REQ_PATCH, None),
        P(REQ_PATCH, None),
        P(),
        P(),
        P(None, None, None, PATCH),
        P(),
        P("req", None),
        P(),
        P(),
        P(),
        P(),
        P(),
    )
    return jax.shard_map(
        per_device,
        mesh=torus,
        in_specs=placed,
        out_specs=P(None, REQ_PATCH, None, None),
        check_vma=False,
    )
```

profile of v0, /device:TPU:1, one launch (start us, length us, event | category | flops | bytes accessed | tf_op | source)
XLA Modules:
  0.0 354.1 jit_solution(6826312504156795108)
XLA Ops:
  6.6 20.1 %all-gather = bf16[6,3,640,20]{2,3,1,0:T(8,128)(2,1)} all-gather(bf16[3,3,640,20]{2,3,1,0:T(8,128)(2,1)} %param.20), channel_id=2, replica_groups=mesh['req'=16,'patch_0'=8,'patch_1'=2,'patch_2'=2] {'patch_1'}, dimensions={0}, use_global_device_ids=true | all-gather | bytes 691200 | tf_op jit(solution)/shard_map/all_gather | solution.py:55
  26.8 64.5 %all-gather.6.cloned.1.call-done = bf16[16,3,3,640,20]{3,4,2,1,0:T(8,128)(2,1)} async-done(((bf16[2,3,3,640,20]{3,4,2,1,0:T(8,128)(2,1)}), bf16[16,3,3,640,20]{3,4,2,1,0:T(8,128)(2,1)}) %all-gather.6.cloned.1.call-update) | async-done | bytes 3686416 | tf_op jit(solution)/shard_map/all_gather | solution.py:55
  91.3 4.7 %copy.85 = bf16[16,3,3,640,20]{3,0,4,2,1:T(8,128)(2,1)} copy(bf16[16,3,3,640,20]{3,4,2,1,0:T(8,128)(2,1)} %all-gather.6.cloned.1.call-done) | data formatting | bytes 7372800 | tf_op jit(solution)/shard_map/all_gather | solution.py:55
  97.2 11.0 %all-to-all-start = ((f32[32,1,64]{2,1,0:T(1,128)}), f32[32,1,64]{2,1,0:T(1,128)S(1)}, u32[]{:S(2)}, u32[]{:S(2)}) async-start(f32[32,1,64]{2,1,0:T(1,128)} %broadcast_in_dim.14), calls=%async_computation | async-start | bytes 32768 | tf_op jit(solution)/shard_map/all_to_all | solution.py:19
  108.3 7.4 %collective-permute-start = (bf16[1,16,640]{2,1,0:T(8,128)(2,1)S(1)}, bf16[1,16,640]{2,1,0:T(8,128)(2,1)S(1)}, u32[]{:S(2)}, u32[]{:S(2)}) collective-permute-start(bf16[1,16,640]{2,1,0:T(8,128)(2,1)S(1)} %get-tuple-element.45), channel_id=1, source_target_pairs={{0,1},{1,2},{2,3},{3,4},{4,5},{5,6},{6,7},{7,8},{8,9},{9,10},{10,1... | collective-permute-start | bytes 61448 | tf_op jit(solution)/shard_map/ppermute | solution.py:71
  115.7 1.9 collective-permute-start.1
  120.5 4.3 %collective-permute-done.1 = bf16[1,16,640]{2,1,0:T(8,128)(2,1)S(1)} collective-permute-done((bf16[1,16,640]{2,1,0:T(8,128)(2,1)S(1)}, bf16[1,16,640]{2,1,0:T(8,128)(2,1)S(1)}, u32[]{:S(2)}, u32[]{:S(2)}) %collective-permute-start.1) | collective-permute-done | bytes 20512 | tf_op jit(solution)/shard_map/ppermute | solution.py:74
  124.8 15.2 %reshape.171 = bf16[2,8,2,3,3,640,20]{5,2,1,0,6,4,3:T(2,128)(2,1)} reshape(bf16[32,3,3,640,20]{3,0,4,2,1:T(8,128)(2,1)} %all-gather.8.cloned.1.call-done) | data formatting | bytes 14745600 | tf_op jit(solution)/shard_map/reshape | solution.py:57
  140.1 13.0 %copy.86 = bf16[8,2,2,3,3,640,20]{5,2,1,0,6,4,3:T(2,128)(2,1)} copy(bf16[8,2,2,3,3,640,20]{5,1,0,2,6,4,3:T(2,128)(2,1)} %bitcast.139) | data formatting | bytes 14745600 | tf_op jit(solution)/shard_map/transpose | solution.py:59
  153.1 15.8 %reshape.172 = bf16[32,3,3,640,20]{3,0,4,2,1:T(8,128)(2,1)} reshape(bf16[8,2,2,3,3,640,20]{5,2,1,0,6,4,3:T(2,128)(2,1)} %copy.86) | data formatting | bytes 14745600 | tf_op jit(solution)/shard_map/reshape | solution.py:59
  168.9 9.6 %copy.87 = bf16[3,3,640,32,20]{2,4,3,1,0:T(8,128)(2,1)} copy(bf16[3,3,640,32,20]{2,3,4,1,0:T(8,128)(2,1)} %bitcast.140) | data formatting | bytes 14745600 | tf_op jit(solution)/shard_map/transpose | solution.py:49
  178.5 11.8 %reshape.173 = bf16[3,3,640,640]{2,3,1,0:T(8,128)(2,1)} reshape(bf16[3,3,640,32,20]{2,4,3,1,0:T(8,128)(2,1)} %copy.87) | data formatting | bytes 14745600 | tf_op jit(solution)/shard_map/reshape | solution.py:49
  205.3 10.1 %all-to-all-start.1 = ((f32[32,1,64]{2,1,0:T(1,128)}), f32[32,1,64]{2,1,0:T(1,128)S(1)}, u32[]{:S(2)}, u32[]{:S(2)}) async-start(f32[32,1,64]{2,1,0:T(1,128)} %broadcast_in_dim.17), calls=%async_computation.1 | async-start | bytes 32768 | tf_op jit(solution)/shard_map/all_to_all | solution.py:19
  215.4 1.6 all-gather.10.cloned.1.call-done
  217.1 1.8 fusion.24
  219.4 7.8 %all-to-all-done.1 = f32[32,1,64]{2,1,0:T(1,128)S(1)} async-done(((f32[32,1,64]{2,1,0:T(1,128)}), f32[32,1,64]{2,1,0:T(1,128)S(1)}, u32[]{:S(2)}, u32[]{:S(2)}) %all-to-all-start.1) | async-done | bytes 8224 | tf_op jit(solution)/shard_map/all_to_all | solution.py:19
  236.5 3.6 %all-to-all-start.2 = ((f32[32,1,64]{2,1,0:T(1,128)}), f32[32,1,64]{2,1,0:T(1,128)S(1)}, u32[]{:S(2)}, u32[]{:S(2)}) async-start(f32[32,1,64]{2,1,0:T(1,128)} %broadcast_in_dim.18), calls=%async_computation.2 | async-start | bytes 32768 | tf_op jit(solution)/shard_map/all_to_all | solution.py:19
  241.0 7.2 %collective-permute-start.2 = (bf16[1,16,640]{2,1,0:T(8,128)(2,1)S(1)}, bf16[1,16,640]{2,1,0:T(8,128)(2,1)S(1)}, u32[]{:S(2)}, u32[]{:S(2)}) collective-permute-start(bf16[1,16,640]{2,1,0:T(8,128)(2,1)S(1)} %get-tuple-element.41), channel_id=1, source_target_pairs={{0,1},{1,2},{2,3},{3,4},{4,5},{5,6},{6,7},{7,8},{8,9},{9,10},{10,1... | collective-permute-start | bytes 61448 | tf_op jit(solution)/shard_map/ppermute | solution.py:71
  248.2 1.9 collective-permute-start.3
  250.1 1.6 all-to-all-done.2
  253.0 4.2 %collective-permute-done.3 = bf16[1,16,640]{2,1,0:T(8,128)(2,1)S(1)} collective-permute-done((bf16[1,16,640]{2,1,0:T(8,128)(2,1)S(1)}, bf16[1,16,640]{2,1,0:T(8,128)(2,1)S(1)}, u32[]{:S(2)}, u32[]{:S(2)}) %collective-permute-start.3) | collective-permute-done | bytes 20512 | tf_op jit(solution)/shard_map/ppermute | solution.py:74
  271.5 20.7 %all_to_all.24 = f32[32,1,64]{2,1,0:T(1,128)S(1)} all-to-all(f32[32,1,64]{2,1,0:T(1,128)S(1)} %broadcast_in_dim.20), channel_id=1, replica_groups=mesh['req'=16,'patch_0'=8,'patch_1'=2,'patch_2'=2] {'patch_0','patch_1',..., dimensions={0} | all-to-all | bytes 16384 | tf_op jit(solution)/shard_map/all_to_all | solution.py:19
  293.9 47.5 %all-gather.12.cloned.1.call-done = bf16[1024,640]{1,0:T(8,128)(2,1)} async-done(((bf16[32,640]{1,0:T(8,128)(2,1)}), bf16[1024,640]{1,0:T(8,128)(2,1)}) %all-gather.12.cloned.1.call-update) | async-done | bytes 1310736 | tf_op jit(solution)/shard_map/all_gather | solution.py:39
  341.5 1.8 fusion.23
  (160 shorter events, 50.9 us)
Async XLA Ops:
  6.5 221.8 %copy-start = (bf16[640,640]{1,0:T(8,128)(2,1)S(1)}, bf16[640,640]{1,0:T(8,128)(2,1)}, u32[]{:S(2)}) copy-start(bf16[640,640]{1,0:T(8,128)(2,1)} %param.26) | copy-start | bytes 2457604
  6.5 89.5 %copy-start.5 = (f32[2,16,640]{2,1,0:T(8,128)S(1)}, f32[2,16,640]{2,1,0:T(8,128)}, u32[]{:S(2)}) copy-start(f32[2,16,640]{2,1,0:T(8,128)} %param.14) | copy-start | bytes 245764
  6.5 101.7 %copy-start.8 = (bf16[2,16,640]{2,1,0:T(8,128)(2,1)S(1)}, bf16[2,16,640]{2,1,0:T(8,128)(2,1)}, u32[]{:S(2)}) copy-start(bf16[2,16,640]{2,1,0:T(8,128)(2,1)} %param.15) | copy-start | bytes 122884
  6.5 111.1 %copy-start.10 = (bf16[32,320]{1,0:T(8,128)(2,1)S(1)}, bf16[32,320]{1,0:T(8,128)(2,1)}, u32[]{:S(2)}) copy-start(bf16[32,320]{1,0:T(8,128)(2,1)} %param.16) | copy-start | bytes 61444
  6.5 111.1 %copy-start.9 = (bf16[32,320]{1,0:T(8,128)(2,1)S(1)}, bf16[32,320]{1,0:T(8,128)(2,1)}, u32[]{:S(2)}) copy-start(bf16[32,320]{1,0:T(8,128)(2,1)} %param.17) | copy-start | bytes 61444
  6.5 111.9 %copy-start.18 = (f32[2,640]{1,0:T(2,128)S(1)}, f32[2,640]{1,0:T(2,128)}, u32[]{:S(2)}) copy-start(f32[2,640]{1,0:T(2,128)} %param.22) | copy-start | bytes 15364
  6.6 113.8 %copy-start.15 = (f32[640]{0:T(1024)S(1)}, f32[640]{0:T(1024)}, u32[]{:S(2)}) copy-start(f32[640]{0:T(1024)} %param.18) | copy-start | bytes 7684
  6.6 113.8 %copy-start.14 = (f32[640]{0:T(1024)S(1)}, f32[640]{0:T(1024)}, u32[]{:S(2)}) copy-start(f32[640]{0:T(1024)} %param.19) | copy-start | bytes 7684
  6.6 84.7 %all-gather.6.cloned.1.call-start = ((), (), s32[]{:S(2)}) async-start(), calls=%async_computation.4 | async-start | bytes 4976640 | tf_op jit(solution)/shard_map/all_gather | solution.py:55
  26.8 98.1 %all-gather.8.cloned.1.call-start = ((), (), s32[]{:S(2)}) async-start(), calls=%async_computation.5 | async-start | bytes 11059200 | tf_op jit(solution)/shard_map/all_gather | solution.py:55
  97.2 22.7 %all-to-all-start = ((f32[32,1,64]{2,1,0:T(1,128)}), f32[32,1,64]{2,1,0:T(1,128)S(1)}, u32[]{:S(2)}, u32[]{:S(2)}) async-start(f32[32,1,64]{2,1,0:T(1,128)} %broadcast_in_dim.14), calls=%async_computation | async-start | bytes 32768 | tf_op jit(solution)/shard_map/all_to_all | solution.py:19
  108.2 108.9 %all-gather.10.cloned.1.call-start = ((), (), s32[]{:S(2)}) async-start(), calls=%async_computation.6 | async-start | bytes 1351680 | tf_op jit(solution)/shard_map/all_gather | solution.py:39
  108.3 12.2 %collective-permute-start = (bf16[1,16,640]{2,1,0:T(8,128)(2,1)S(1)}, bf16[1,16,640]{2,1,0:T(8,128)(2,1)S(1)}, u32[]{:S(2)}, u32[]{:S(2)}) collective-permute-start(bf16[1,16,640]{2,1,0:T(8,128)(2,1)S(1)} %get-tuple-element.45), channel_id=1, source_target_pairs={{0,1},{1,2},{2,3},{3,4},{4,5},{5,6},{6,7},{7,8},{8,9},{9,10},{10,1... | collective-permute-start | bytes 61448 | tf_op jit(solution)/shard_map/ppermute | solution.py:71
  115.7 9.0 %collective-permute-start.1 = (bf16[1,16,640]{2,1,0:T(8,128)(2,1)S(1)}, bf16[1,16,640]{2,1,0:T(8,128)(2,1)S(1)}, u32[]{:S(2)}, u32[]{:S(2)}) collective-permute-start(bf16[1,16,640]{2,1,0:T(8,128)(2,1)S(1)} %get-tuple-element.46), channel_id=1, source_target_pairs={{1,0},{2,1},{3,2},{4,3},{5,4},{6,5},{7,6},{8,7},{9,8},{10,9},{11,1... | collective-permute-start | bytes 61448 | tf_op jit(solution)/shard_map/ppermute | solution.py:74
  205.3 21.9 %all-to-all-start.1 = ((f32[32,1,64]{2,1,0:T(1,128)}), f32[32,1,64]{2,1,0:T(1,128)S(1)}, u32[]{:S(2)}, u32[]{:S(2)}) async-start(f32[32,1,64]{2,1,0:T(1,128)} %broadcast_in_dim.17), calls=%async_computation.1 | async-start | bytes 32768 | tf_op jit(solution)/shard_map/all_to_all | solution.py:19
  231.7 39.2 %copy-start.13 = (f32[640]{0:T(1024)S(1)}, f32[640]{0:T(1024)}, u32[]{:S(2)}) copy-start(f32[640]{0:T(1024)} %get-tuple-element.13) | copy-start | bytes 7684
  231.7 61.0 %copy-start.16 = (f32[640]{0:T(1024)S(1)}, f32[640]{0:T(1024)}, u32[]{:S(2)}) copy-start(f32[640]{0:T(1024)} %param.24) | copy-start | bytes 7684
  231.7 61.0 %copy-start.17 = (f32[640]{0:T(1024)S(1)}, f32[640]{0:T(1024)}, u32[]{:S(2)}) copy-start(f32[640]{0:T(1024)} %param.23) | copy-start | bytes 7684
  232.8 59.9 %copy-start.2 = (bf16[640,320]{0,1:T(8,128)(2,1)S(1)}, bf16[640,320]{0,1:T(8,128)(2,1)}, u32[]{:S(2)}) copy-start(bf16[640,320]{0,1:T(8,128)(2,1)} %param.25) | copy-start | bytes 1228804
  236.5 15.2 %all-to-all-start.2 = ((f32[32,1,64]{2,1,0:T(1,128)}), f32[32,1,64]{2,1,0:T(1,128)S(1)}, u32[]{:S(2)}, u32[]{:S(2)}) async-start(f32[32,1,64]{2,1,0:T(1,128)} %broadcast_in_dim.18), calls=%async_computation.2 | async-start | bytes 32768 | tf_op jit(solution)/shard_map/all_to_all | solution.py:19
  240.2 101.3 %all-gather.12.cloned.1.call-start = ((), (), s32[]{:S(2)}) async-start(), calls=%async_computation.7 | async-start | bytes 1351680 | tf_op jit(solution)/shard_map/all_gather | solution.py:39
  241.0 12.0 %collective-permute-start.2 = (bf16[1,16,640]{2,1,0:T(8,128)(2,1)S(1)}, bf16[1,16,640]{2,1,0:T(8,128)(2,1)S(1)}, u32[]{:S(2)}, u32[]{:S(2)}) collective-permute-start(bf16[1,16,640]{2,1,0:T(8,128)(2,1)S(1)} %get-tuple-element.41), channel_id=1, source_target_pairs={{0,1},{1,2},{2,3},{3,4},{4,5},{5,6},{6,7},{7,8},{8,9},{9,10},{10,1... | collective-permute-start | bytes 61448 | tf_op jit(solution)/shard_map/ppermute | solution.py:71
  248.2 9.0 %collective-permute-start.3 = (bf16[1,16,640]{2,1,0:T(8,128)(2,1)S(1)}, bf16[1,16,640]{2,1,0:T(8,128)(2,1)S(1)}, u32[]{:S(2)}, u32[]{:S(2)}) collective-permute-start(bf16[1,16,640]{2,1,0:T(8,128)(2,1)S(1)} %get-tuple-element.42), channel_id=1, source_target_pairs={{1,0},{2,1},{3,2},{4,3},{5,4},{6,5},{7,6},{8,7},{9,8},{10,9},{11,1... | collective-permute-start | bytes 61448 | tf_op jit(solution)/shard_map/ppermute | solution.py:74
  270.9 72.4 %copy-start.4 = (f32[2,16,640]{2,1,0:T(8,128)}, f32[2,16,640]{2,1,0:T(8,128)S(1)}, u32[]{:S(2)}) copy-start(f32[2,16,640]{2,1,0:T(8,128)S(1)} %get-tuple-element.15) | copy-start | bytes 245764
  (6 other events, 142.1 us)
Sparse Core Ops, SparseCore 0:
  26.9 64.3 all-gather.5
  96.1 27.1 all-gather.7
  126.6 90.4 all-gather.9
  250.2 91.1 all-gather.11
where the time goes:
time: 357 us; the launch traced here: 354 us
  waiting for transfers between devices  133 us (37%)
  local copies, waits for them, and re-layouts  84 us (24%)
  starting transfers between devices  43.4 us (12%)
  blocking collectives  40.8 us (11%)
  matrix products  34.3 us (10%)
  between operations  13.9 us (4%)
  other arithmetic  5.16 us (1%)
    all_gather x2, waiting for transfers between devices, all_blocks(): blocks = lax.all_gather(blocks, axes[k], axis=0, tiled=True)  64.5 us
    all_gather x2, waiting for transfers between devices, side_by_side(): whole, at, outs = (lax.all_gather(both, axis, axis=dim, tiled=True), 0, [])  49.2 us
    dot_general x18, matrix products, conv_rows(): jnp.dot(window, kernel[offset_row, offset_col], preferred_element_type=jn...  27.2 us
    all_to_all x3, starting transfers between devices, sent_to_all(): lax.all_to_all(jnp.broadcast_to(value[None], (length, *value.shape)), axi...  24.8 us
    all_to_all x1, blocking collectives, sent_to_all(): lax.all_to_all(jnp.broadcast_to(value[None], (length, *value.shape)), axi...  20.7 us
    all_gather x1, blocking collectives, all_blocks(): blocks = lax.all_gather(blocks, axes[k], axis=0, tiled=True)  20.1 us
    reshape x1, local copies, waits for them, and re-layouts, all_blocks(): blocks.transpose(*turned, *range(len(sequence), blocks.ndim))  15.8 us
    reshape x1, local copies, waits for them, and re-layouts, all_blocks(): blocks = blocks.reshape(*held, *value.shape)  15.2 us
  transfers between devices with their start and end apart: 11, of which 8 were waited for; matrix products, arithmetic and copies ran while one was open for 29% of the time, Pallas kernels for 0%

commit v1 on v0

v1 whole, which is shorter than its diff:
```python
import functools

import jax
import jax.numpy as jnp
from jax import lax
from jax.experimental import pallas as pl
from jax.experimental.pallas import tpu as pltpu
from jax.sharding import Mesh
from jax.sharding import PartitionSpec as P

GROUPS = 32
HEADS = 5
HEAD_DIM = 64
WIDTH = HEADS * HEAD_DIM
CHANNELS = 640
MEMBERS = CHANNELS // GROUPS
COLS = 16
ROWS = 32
LANES = 128
POSITIONS = 1024
EPS = 1e-05

PATCH = ("y", "zh", "core")
QUAD = ("zh", "core")
REQ_PATCH = ("req", "y", "zh", "core")

F32 = jnp.float32
BF16 = jnp.bfloat16

NN = (((1,), (0,)), ((), ()))
NT = (((1,), (1,)), ((), ()))


def dot(a, b, dims=NN):
    return lax.dot_general(a, b, dims, preferred_element_type=F32)


def thirds(x):
    high = x.astype(BF16)
    rest = x - high.astype(F32)
    middle = rest.astype(BF16)
    low = (rest - middle.astype(F32)).astype(BF16)
    return high, middle, low


def picked(x, zero_one, dims=NN):
    rows = x.shape[0]
    stacked = jnp.concatenate([t.astype(F32) for t in thirds(x)], axis=0).astype(BF16)
    out = dot(stacked, zero_one, dims)
    return out[:rows] + out[rows : 2 * rows] + out[2 * rows :]


def group_matrix():
    channel = lax.broadcasted_iota(jnp.int32, (CHANNELS, LANES), 0)
    first = lax.broadcasted_iota(jnp.int32, (CHANNELS, LANES), 1) * MEMBERS
    return jnp.where((channel >= first) & (channel < first + MEMBERS), 1.0, 0.0).astype(BF16)


def eight(rows, lanes):
    have = sum(r.shape[0] for r in rows)
    return jnp.concatenate([*rows, jnp.zeros((8 - have, lanes), F32)], axis=0)


def local_sums(x, groups):
    sums = eight(
        [jnp.sum(x, axis=0, keepdims=True), jnp.sum(x * x, axis=0, keepdims=True)], CHANNELS
    )
    return picked(sums, groups)


def tell_state(x, groups, stats_ref, diff_ref):
    sums = local_sums(x, groups)
    own_mean = (sums[0:1] * (1.0 / (ROWS * MEMBERS))).astype(BF16)
    spread = dot(eight([own_mean.astype(F32)], LANES).astype(BF16), groups, NT)
    diff_ref[...] = (x - spread[0:1]).astype(BF16)
    told = jnp.concatenate(
        [sums[0:2], own_mean.astype(F32), jnp.zeros((1, LANES), F32)], axis=0
    )
    stats_ref[...] = jnp.broadcast_to(told[None], stats_ref.shape)


def mean_and_scale(total, squares):
    number = POSITIONS * MEMBERS
    mean = total * (1.0 / number)
    variance = squares * (1.0 / number) - mean * mean
    return mean, lax.rsqrt(variance + EPS)


def first_kernel(field_ref, keys_ref, values_ref, stats_ref, diff_ref, kv_ref, select_ref):
    tell_state(field_ref[...], group_matrix(), stats_ref, diff_ref)
    both = jnp.concatenate(
        [keys_ref[...].astype(F32), values_ref[...].astype(F32)], axis=1
    ).astype(BF16)
    kv_ref[...] = jnp.broadcast_to(both[None], kv_ref.shape)
    channel = lax.broadcasted_iota(jnp.int32, (CHANNELS, 256), 0)
    lane = lax.broadcasted_iota(jnp.int32, (CHANNELS, 256), 1)
    within = lane & 31
    for turn in range(4):
        meant = (lane >> 5) * (4 * MEMBERS) + turn * MEMBERS + within
        chosen = (channel == meant) & (within < MEMBERS)
        select_ref[turn] = jnp.where(chosen, 1.0, 0.0).astype(BF16)


def rows_kernel(place_ref, own_ref, one_ref, two_ref, three_ref, four_ref, first_ref, last_ref):
    a = place_ref[1]
    for k, ref in enumerate((own_ref, one_ref, two_ref, three_ref)):
        four_ref[a ^ k] = ref[...]
    first_ref[...] = four_ref[0, :COLS]
    last_ref[...] = four_ref[3, COLS:]


def conv_kernel(
    place_ref,
    stats_ref,
    d0_ref,
    d1_ref,
    d2_ref,
    d3_ref,
    prior_ref,
    above_ref,
    below_ref,
    weight_ref,
    gain_ref,
    bias_ref,
    shift_ref,
    select_ref,
    told_ref,
    o0_ref,
    o1_ref,
    o2_ref,
    o3_ref,
    act_ref,
    first_ref,
    last_ref,
    diff,
    rows,
    wide,
    outs,
):
    y = place_ref[0]
    a = place_ref[1]
    groups = group_matrix()
    for k, ref in enumerate((d0_ref, d1_ref, d2_ref, d3_ref)):
        diff[a ^ k] = ref[...]

    sums = jnp.sum(stats_ref[...], axis=0)
    mean, scale = mean_and_scale(sums[0:1], sums[1:2])
    own_means = [stats_ref[4 * y + t][2:3] for t in range(4)]
    spread = picked(eight([(m - mean) * scale for m in own_means] + [scale], LANES), groups, NT)
    gain = gain_ref[...]
    bias = bias_ref[...]
    factor = spread[4:5] * gain
    for t in range(4):
        offset = spread[t : t + 1] * gain + bias
        value = diff[t].astype(F32) * factor + offset
        act_ref[t] = (value * (1.0 / (1.0 + jnp.exp(-value)))).astype(BF16)
    first_ref[...] = act_ref[0, :COLS]
    last_ref[...] = act_ref[3, COLS:]
    for t in range(4):
        rows[t, 0:COLS] = above_ref[...] if t == 0 else prior_ref[t - 1, COLS:]
        rows[t, COLS : 3 * COLS] = act_ref[t]
        rows[t, 3 * COLS :] = below_ref[...] if t == 3 else prior_ref[t + 1, :COLS]
    window = rows[...].reshape(4 * 64, CHANNELS)

    wide[...] = jnp.zeros(wide.shape, F32)
    col = lax.broadcasted_iota(jnp.int32, (LANES, LANES), 0) & (COLS - 1)
    lane = lax.broadcasted_iota(jnp.int32, (LANES, LANES), 1)
    within = lane & 31
    halves = [jnp.zeros((LANES, LANES), F32), jnp.zeros((LANES, LANES), F32)]
    for part in range(8):
        wide[:, 0 : 9 * MEMBERS] = dot(window, weight_ref[part], NT)
        whole = wide[...].reshape(4, 64, 256)
        lines = [
            whole[:, COLS * r : COLS * r + 2 * COLS].reshape(LANES, 256) for r in range(3)
        ]
        total = (
            lines[0][:, :LANES]
            + pltpu.roll(lines[1][:, :LANES], LANES - 3 * MEMBERS, 1)
            + pltpu.roll(lines[2], 256 - 6 * MEMBERS, 1)[:, :LANES]
        )
        left = jnp.where(col > 0, pltpu.roll(total, 1, 0), 0.0)
        centre = pltpu.roll(total, LANES - MEMBERS, 1)
        right = pltpu.roll(total, LANES - 2 * MEMBERS, 1)
        right = jnp.where(col < COLS - 1, pltpu.roll(right, LANES - 1, 0), 0.0)
        made = left + centre + right
        at = 32 * (part % 4)
        if at:
            made = pltpu.roll(made, at, 1)
        kept = (lane >= at) & (lane < at + MEMBERS)
        halves[part // 4] = jnp.where(kept, made, halves[part // 4])
    made = jnp.concatenate(halves, axis=1)
    outs[...] = made.reshape(4, ROWS, 256)
    for k, ref in enumerate((o0_ref, o1_ref, o2_ref, o3_ref)):
        ref[...] = outs[a ^ k]

    select = select_ref[a]
    group = lax.broadcasted_iota(jnp.int32, (LANES, 256), 0)
    wide_lane = lax.broadcasted_iota(jnp.int32, (LANES, 256), 1)
    holds = (group == (wide_lane >> 5) * 4 + a) & ((wide_lane & 31) < MEMBERS)
    holds = jnp.where(holds, 1.0, 0.0).astype(BF16)
    state = dot(diff[...].reshape(LANES, CHANNELS), select).reshape(4, ROWS, 256)
    means = dot(eight(own_means, LANES).astype(BF16), holds)
    added = picked(eight([shift_ref[...]], CHANNELS), select)[0:1]
    total = jnp.zeros((1, 256), F32)
    squares = jnp.zeros((1, 256), F32)
    for t in range(4):
        hidden = state[t] + means[t : t + 1] + added + outs[t]
        total += jnp.sum(hidden, axis=0, keepdims=True)
        squares += jnp.sum(hidden * hidden, axis=0, keepdims=True)
    sums = picked(eight([total, squares], 256), holds, NT)
    told_ref[...] = jnp.broadcast_to(sums[None, 0:4], told_ref.shape)


def attend_kernel(
    last_step,
    n_kv,
    place_ref,
    own_ref,
    stats_ref,
    state_ref,
    c0_ref,
    c1_ref,
    c2_ref,
    c3_ref,
    select_ref,
    gain_ref,
    bias_ref,
    shift_ref,
    query_ref,
    keyvalue_ref,
    out_ref,
    *refs,
):
    kv_refs, result_ref, more = refs[:n_kv], refs[n_kv], refs[n_kv + 1 :]
    a = place_ref[1]
    own_start = own_ref[0]
    groups = group_matrix()
    conv = jnp.zeros((ROWS, CHANNELS), F32)
    for k, ref in enumerate((c0_ref, c1_ref, c2_ref, c3_ref)):
        conv += picked(ref[...], select_ref[a ^ k], NT)
    hidden = state_ref[...] + (conv + shift_ref[...])
    sums = jnp.sum(stats_ref[...], axis=0)
    mean, scale = mean_and_scale(sums[0:1], sums[1:2])
    spread = picked(eight([mean, scale], LANES), groups, NT)
    normed = (hidden - spread[0:1]) * spread[1:2] * gain_ref[...] + bias_ref[...]
    normed = normed.astype(BF16)
    query = dot(normed, query_ref[...])
    fresh = dot(normed, keyvalue_ref[...]).astype(BF16)

    lane = lax.broadcasted_iota(jnp.int32, (ROWS, CHANNELS), 1)
    padded = jnp.concatenate([query, jnp.zeros((ROWS, CHANNELS - WIDTH), F32)], axis=1)
    heads = jnp.concatenate(
        [
            jnp.where((lane >= h * HEAD_DIM) & (lane < (h + 1) * HEAD_DIM), padded, 0.0)
            for h in range(HEADS)
        ],
        axis=0,
    ).astype(BF16)
    blocks = [ref[...].reshape(-1, CHANNELS) for ref in kv_refs] + [fresh]
    scores = [dot(heads, b, NT) * HEAD_DIM ** (-0.5) for b in blocks]
    column = lax.broadcasted_iota(jnp.int32, scores[0].shape, 1)
    outside = (column < own_start) | (column >= own_start + ROWS)
    scores[0] = jnp.where(outside, scores[0], -jnp.inf)
    peak = functools.reduce(
        jnp.maximum, [jnp.max(s, axis=1, keepdims=True) for s in scores]
    )
    expo = [jnp.exp(s - peak) for s in scores]
    total = sum(jnp.sum(e, axis=1, keepdims=True) for e in expo)
    summed = sum(dot(e.astype(BF16), b) for e, b in zip(expo, blocks)) / total
    attended = jnp.zeros((ROWS, CHANNELS), F32)
    for h in range(HEADS):
        start = WIDTH + h * HEAD_DIM
        kept = (lane >= start) & (lane < start + HEAD_DIM)
        attended = jnp.where(kept, summed[h * ROWS : (h + 1) * ROWS], attended)
    attended = attended[:, WIDTH:].astype(BF16)
    result = hidden + dot(attended, out_ref[...])
    if last_step:
        result_ref[0] = state_ref[...]
        result_ref[1] = result
    else:
        stats_out, diff_out, kv_out = more
        result_ref[...] = result
        kv_out[...] = fresh
        tell_state(result, groups, stats_out, diff_out)


VMEM = pl.BlockSpec(memory_space=pltpu.VMEM)
SMEM = pl.BlockSpec(memory_space=pltpu.SMEM)


def call(kernel, name, out_shapes, args, scalars=0, scratch=(), flops=0):
    return pl.pallas_call(
        kernel,
        name=name,
        out_shape=[jax.ShapeDtypeStruct(s, t) for s, t in out_shapes],
        in_specs=[SMEM] * scalars + [VMEM] * (len(args) - scalars),
        out_specs=[VMEM] * len(out_shapes),
        scratch_shapes=list(scratch),
        cost_estimate=pl.CostEstimate(flops=flops, bytes_accessed=1 << 20, transcendentals=0),
        compiler_params=pltpu.CompilerParams(vmem_limit_bytes=48 << 20),
    )(*args)


def flipped(value, k):
    return lax.ppermute(value, QUAD, [(i, i ^ k) for i in range(4)])


def to_all(value, axes):
    return lax.all_to_all(value, axes, 0, 0, tiled=True)


def per_device(
    field,
    stale_conv_in,
    stale_keys,
    stale_values,
    norm1_gain,
    norm1_bias,
    conv_weight,
    conv_bias,
    time_embed,
    norm2_gain,
    norm2_bias,
    w_query,
    w_keyvalue,
    w_out,
):
    y = lax.axis_index("y")
    zh = lax.axis_index("zh")
    a = 2 * zh + lax.axis_index("core")
    place = jnp.stack([y, a]).astype(jnp.int32)
    owns = (((2 * y + zh) * ROWS).reshape(1).astype(jnp.int32), (y * 4 * ROWS).reshape(1).astype(jnp.int32))
    up = [(i, i + 1) for i in range(7)]
    down = [(i + 1, i) for i in range(7)]

    slices = conv_weight.transpose(0, 1, 3, 2).reshape(9 * MEMBERS, CHANNELS)
    weights = lax.all_gather(slices, "y", axis=0, tiled=False)

    state = field.reshape(ROWS, CHANNELS)
    stats, diff, kv, select = call(
        first_kernel,
        "first",
        [
            ((32, 4, LANES), F32),
            ((ROWS, CHANNELS), BF16),
            ((16, ROWS, CHANNELS), BF16),
            ((4, CHANNELS, 256), BF16),
        ],
        (state, stale_keys, stale_values),
    )
    stats = to_all(stats, PATCH)
    diffs = (diff, *(flipped(diff, k) for k in (1, 2, 3)))
    kv_same = to_all(kv, ("y", "zh"))
    kvs = (kv_same, flipped(kv_same, 1))

    stale = stale_conv_in.reshape(ROWS, CHANNELS)
    prior, first, last = call(
        rows_kernel,
        "rows",
        [((4, ROWS, CHANNELS), BF16), ((COLS, CHANNELS), BF16), ((COLS, CHANNELS), BF16)],
        (place, stale, *(flipped(stale, k) for k in (1, 2, 3))),
        scalars=1,
    )
    row = lambda v: v.reshape(1, CHANNELS)
    for step in range(2):
        above = lax.ppermute(last, "y", up)
        below = lax.ppermute(first, "y", down)
        shift = row(conv_bias + time_embed[step])
        told, o0, o1, o2, o3, prior, first, last = call(
            conv_kernel,
            f"conv{step}",
            [((32, 4, LANES), F32)]
            + [((ROWS, 256), F32)] * 4
            + [((4, ROWS, CHANNELS), BF16), ((COLS, CHANNELS), BF16), ((COLS, CHANNELS), BF16)],
            (
                place,
                stats,
                *diffs,
                prior,
                above,
                below,
                weights,
                row(norm1_gain),
                row(norm1_bias),
                shift,
                select,
            ),
            scalars=1,
            scratch=[
                pltpu.VMEM((4, ROWS, CHANNELS), BF16),
                pltpu.VMEM((4, 64, CHANNELS), BF16),
                pltpu.VMEM((256, 256), F32),
                pltpu.VMEM((4, ROWS, 256), F32),
            ],
            flops=1 << 30,
        )
        told = to_all(told, PATCH)
        parts = (o0, flipped(o1, 1), flipped(o2, 2), flipped(o3, 3))
        final = step == 1
        shapes = (
            [((2, ROWS, CHANNELS), F32)]
            if final
            else [
                ((ROWS, CHANNELS), F32),
                ((32, 4, LANES), F32),
                ((ROWS, CHANNELS), BF16),
                ((ROWS, CHANNELS), BF16),
            ]
        )
        made = call(
            functools.partial(attend_kernel, final, len(kvs)),
            f"attend{step}",
            shapes,
            (
                place,
                owns[step],
                told,
                state,
                *parts,
                select,
                row(norm2_gain),
                row(norm2_bias),
                shift,
                w_query,
                w_keyvalue,
                w_out,
                *kvs,
            ),
            scalars=2,
            flops=1 << 30,
        )
        if final:
            return made[0].reshape(2, 2, COLS, CHANNELS)
        state, stats, diff, kv = made
        stats = to_all(stats, PATCH)
        diffs = (diff, *(flipped(diff, k) for k in (1, 2, 3)))
        four = jnp.concatenate([kv, *(flipped(kv, k) for k in (1, 2, 3))], axis=0)
        kvs = (lax.all_gather(four, "y", axis=0, tiled=False),)


def solution(mesh):
    torus = Mesh(
        mesh.devices.reshape(mesh.shape["req"], 8, 2, 2), ("req", "y", "zh", "core")
    )
    placed = (
        P(REQ_PATCH, None, None),
        P(REQ_PATCH, None, None),
        P(REQ_PATCH, None),
        P(REQ_PATCH, None),
        P(),
        P(),
        P(None, None, None, PATCH),
        P(),
        P("req", None),
        P(),
        P(),
        P(),
        P(),
        P(),
    )
    return jax.shard_map(
        per_device,
        mesh=torus,
        in_specs=placed,
        out_specs=P(None, REQ_PATCH, None, None),
        check_vma=False,
    )
```

time: 357 us -> 226 us (0.63)
  waiting for transfers between devices: 133 us -> 27.5 us
  starting transfers between devices: 43.4 us -> 145 us
  local copies, waits for them, and re-layouts: 84 us -> 21.5 us
  blocking collectives: 40.8 us -> 0 us
  matrix products: 34.3 us -> 0 us
  Pallas kernels: 0 us -> 14.6 us
  other arithmetic: 5.16 us -> 1.35 us
    all_gather x4 -> x2, waiting for transfers between devices: 114 us -> 0.01 us  [the longest x1 0.01 us: per_device(): weights = lax.all_gather(slices, 'y', axis=0, tiled=False)]
    ppermute x4 -> x23, starting transfers between devices: 18.5 us -> 87.6 us  [the longest x19 78.6 us: flipped(): return lax.ppermute(value, QUAD, [(i, i ^ k) for i in range(4)])]
    reshape x5 -> x6, local copies, waits for them, and re-layouts: 44.3 us -> 0.7 us  [per_device(): row = lambda v: v.reshape(1, CHANNELS)]
    dot_general x28 -> x0, matrix products: 34.3 us -> none  [the longest x18 27.2 us: conv_rows(): jnp.dot(window, kernel[offset_row, offset_col], preferred_element_type=jn...]
    all_to_all x3 -> x5, starting transfers between devices: 24.8 us -> 57.8 us  [to_all(): return lax.all_to_all(value, axes, 0, 0, tiled=True)]
    transpose x2 -> x0, local copies, waits for them, and re-layouts: 22.6 us -> none  [the longest x1 13 us: all_blocks(): blocks.transpose(*turned, *range(len(sequence), blocks.ndim))]
    all_to_all x1 -> x0, blocking collectives: 20.7 us -> none  [sent_to_all(): lax.all_to_all(jnp.broadcast_to(value[None], (length, *value.shape)), axi...]
    all_gather x1 -> x0, blocking collectives: 20.1 us -> none  [all_blocks(): blocks = lax.all_gather(blocks, axes[k], axis=0, tiled=True)]
  transfers between devices with their start and end apart: 11 -> 30, of which waited for: 8 -> 6; matrix products, arithmetic and copies ran while one was open for 29% -> 1% of each run, Pallas kernels for 0% -> 4%
where the time goes in v1:
time: 226 us; the launch traced here: 224 us
  starting transfers between devices  145 us (64%)
  waiting for transfers between devices  27.5 us (12%)
  local copies, waits for them, and re-layouts  21.5 us (10%)
  Pallas kernels  14.6 us (6%)
  between operations  14 us (6%)
    ppermute x19, starting transfers between devices, flipped(): return lax.ppermute(value, QUAD, [(i, i ^ k) for i in range(4)])  78.6 us
    all_to_all x5, starting transfers between devices, to_all(): return lax.all_to_all(value, axes, 0, 0, tiled=True)  57.8 us
    unnamed x69, local copies, waits for them, and re-layouts  19.1 us
    pallas_call x6, Pallas kernels, call(): pl.pallas_call(kernel, name=name, out_shape=[jax.ShapeDtypeStruct(s, t) f...  14.6 us
    ppermute x19, waiting for transfers between devices, flipped(): return lax.ppermute(value, QUAD, [(i, i ^ k) for i in range(4)])  12.4 us
    all_to_all x5, waiting for transfers between devices, to_all(): return lax.all_to_all(value, axes, 0, 0, tiled=True)  9.01 us
    ppermute x2, starting transfers between devices, per_device(): above = lax.ppermute(last, 'y', up)  6.35 us
    ppermute x2, waiting for transfers between devices, per_device(): below = lax.ppermute(first, 'y', down)  6.09 us
  transfers between devices with their start and end apart: 30, of which 6 were waited for; matrix products, arithmetic and copies ran while one was open for 1% of the time, Pallas kernels for 4%

profile of v1, /device:TPU:1, one launch (start us, length us, event | category | flops | bytes accessed | tf_op | source)
XLA Modules:
  0.0 224.4 jit_solution(6022126989134058054)
XLA Ops:
  12.1 16.2 %all-to-all-start.2 = ((bf16[16,32,640]{2,1,0:T(8,128)(2,1)}), bf16[16,32,640]{2,1,0:T(8,128)(2,1)S(1)}, u32[]{:S(2)}, u32[]{:S(2)}) async-start(bf16[16,32,640]{2,1,0:T(8,128)(2,1)} %get-tuple-element.40), calls=%async_computation.2 | async-start | bytes 1310720 | tf_op jit(solution)/shard_map/all_to_all | solution.py:309
  28.3 8.3 %collective-permute-start.5 = (bf16[32,640]{1,0:T(8,128)(2,1)S(1)}, bf16[32,640]{1,0:T(8,128)(2,1)S(1)}, u32[]{:S(2)}, u32[]{:S(2)}) collective-permute-start(bf16[32,640]{1,0:T(8,128)(2,1)S(1)} %bitcast.12), channel_id=1, source_target_pairs={{0,3},{1,2},{2,1},{3,0},{4,7},{5,6},{6,5},{7,4},{8,11},{9,10},{10,... | collective-permute-start | bytes 122888 | tf_op jit(solution)/shard_map/ppermute | solution.py:305
  40.8 7.3 %collective-permute-start.2 = (bf16[32,640]{1,0:T(8,128)(2,1)S(1)}, bf16[32,640]{1,0:T(8,128)(2,1)S(1)}, u32[]{:S(2)}, u32[]{:S(2)}) collective-permute-start(bf16[32,640]{1,0:T(8,128)(2,1)S(1)} %get-tuple-element.30.d0_ref), channel_id=1, source_target_pairs={{0,3},{1,2},{2,1},{3,0},{4,7},{5,6},{6,5},{7,4},{8,11},{9,10},{10,... | collective-permute-start | bytes 122888 | tf_op jit(solution)/shard_map/ppermute | solution.py:305
  48.1 9.0 %all-to-all-done.2.refs_0_ = bf16[16,32,640]{2,1,0:T(8,128)(2,1)S(1)} async-done(((bf16[16,32,640]{2,1,0:T(8,128)(2,1)}), bf16[16,32,640]{2,1,0:T(8,128)(2,1)S(1)}, u32[]{:S(2)}, u32[]{:S(2)}) %all-to-all-start.2) | async-done | bytes 655392 | tf_op jit(solution)/shard_map/all_to_all | solution.py:309
  57.1 8.4 %all-to-all-start = ((f32[32,4,128]{2,1,0:T(4,128)}), f32[32,4,128]{2,1,0:T(4,128)S(1)}, u32[]{:S(2)}, u32[]{:S(2)}) async-start(f32[32,4,128]{2,1,0:T(4,128)} %get-tuple-element.29), calls=%async_computation | async-start | bytes 131072 | tf_op jit(solution)/shard_map/all_to_all | solution.py:309
  67.8 7.3 %collective-permute-start.1 = (bf16[32,640]{1,0:T(8,128)(2,1)S(1)}, bf16[32,640]{1,0:T(8,128)(2,1)S(1)}, u32[]{:S(2)}, u32[]{:S(2)}) collective-permute-start(bf16[32,640]{1,0:T(8,128)(2,1)S(1)} %get-tuple-element.30.d0_ref), channel_id=1, source_target_pairs={{0,2},{1,3},{2,0},{3,1},{4,6},{5,7},{6,4},{7,5},{8,10},{9,11},{10,... | collective-permute-start | bytes 122888 | tf_op jit(solution)/shard_map/ppermute | solution.py:305
  78.0 3.1 %collective-permute-start.6 = (bf16[16,640]{1,0:T(8,128)(2,1)S(1)}, bf16[16,640]{1,0:T(8,128)(2,1)S(1)}, u32[]{:S(2)}, u32[]{:S(2)}) collective-permute-start(bf16[16,640]{1,0:T(8,128)(2,1)S(1)} %get-tuple-element.32), channel_id=1, source_target_pairs={{0,4},{4,8},{8,12},{12,16},{16,20},{20,24},{24,28},{1,5},{5,9},{9,... | collective-permute-start | bytes 61448 | tf_op jit(solution)/shard_map/ppermute | solution.py:366
  83.1 2.5 %collective-permute-done.7.below_ref = bf16[16,640]{1,0:T(8,128)(2,1)S(1)} collective-permute-done((bf16[16,640]{1,0:T(8,128)(2,1)S(1)}, bf16[16,640]{1,0:T(8,128)(2,1)S(1)}, u32[]{:S(2)}, u32[]{:S(2)}) %collective-permute-start.7) | collective-permute-done | bytes 20512 | tf_op jit(solution)/shard_map/ppermute | solution.py:367
  87.2 3.0 %conv0.1 = (f32[32,4,128]{2,1,0:T(4,128)}, f32[32,256]{1,0:T(8,128)S(1)}, f32[32,256]{1,0:T(8,128)}, f32[32,256]{1,0:T(8,128)}, f32[32,256]{1,0:T(8,128)}, /*ind...) custom-call(s32[2]{0:T(128)S(1)} %pad_add_fusion.place_ref, ...), custom_call_target="tpu_custom_call" | custom-call | flops 1073741824 | bytes 1048576 | tf_op jit(solution)/shard_map/conv0/pallas_call | solution.py:292
  92.0 8.8 %all-to-all-start.1 = ((f32[32,4,128]{2,1,0:T(4,128)}), f32[32,4,128]{2,1,0:T(4,128)S(1)}, u32[]{:S(2)}, u32[]{:S(2)}) async-start(f32[32,4,128]{2,1,0:T(4,128)} %get-tuple-element.35), calls=%async_computation.1 | async-start | bytes 131072 | tf_op jit(solution)/shard_map/all_to_all | solution.py:309
  103.0 7.3 %collective-permute-start.9 = (f32[32,256]{1,0:T(8,128)}, f32[32,256]{1,0:T(8,128)S(1)}, u32[]{:S(2)}, u32[]{:S(2)}) collective-permute-start(f32[32,256]{1,0:T(8,128)} %get-tuple-element.38), channel_id=1, source_target_pairs={{0,2},{1,3},{2,0},{3,1},{4,6},{5,7},{6,4},{7,5},{8,10},{9,11},{10,... | collective-permute-start | bytes 98312 | tf_op jit(solution)/shard_map/ppermute | solution.py:305
  115.2 4.6 %collective-permute-done.10.c3_ref = f32[32,256]{1,0:T(8,128)} collective-permute-done((f32[32,256]{1,0:T(8,128)}, f32[32,256]{1,0:T(8,128)}, u32[]{:S(2)}, u32[]{:S(2)}) %collective-permute-start.10) | collective-permute-done | bytes 32800 | tf_op jit(solution)/shard_map/ppermute | solution.py:305
  122.4 3.4 %attend0.1 = (f32[32,640]{1,0:T(8,128)S(1)}, f32[32,4,128]{2,1,0:T(4,128)S(1)}, bf16[32,640]{1,0:T(8,128)(2,1)S(1)}, bf16[32,640]{1,0:T(8,128)(2,1)S(1)}) custom-call(s32[2]{0:T(128)S(1)} %pad_add_fusion.place_ref, s32[1]{0:T(128)} %bitcast.3.own_ref, f32[32,4,128]{2,1,0:T(4,128)S(1)} %all-to-all-done.1.stats_ref, f32[32,640]{1,0:T(8,128)S(1)} %bitcast.11, ...), custom_call_target="tpu_custom_call" | custom-call | flops 1073741824 | bytes 1048576 | tf_op jit(solution)/shard_map/attend0/pallas_call | solution.py:292
  127.1 2.5 %collective-permute-start.22 = (bf16[32,640]{1,0:T(8,128)(2,1)S(1)}, bf16[32,640]{1,0:T(8,128)(2,1)S(1)}, u32[]{:S(2)}, u32[]{:S(2)}) collective-permute-start(bf16[32,640]{1,0:T(8,128)(2,1)S(1)} %get-tuple-element.52), channel_id=1, source_target_pairs={{0,3},{1,2},{2,1},{3,0},{4,7},{5,6},{6,5},{7,4},{8,11},{9,10},{10,... | collective-permute-start | bytes 122888 | tf_op jit(solution)/shard_map/ppermute | solution.py:305
  129.6 6.9 %collective-permute-start.21 = (bf16[32,640]{1,0:T(8,128)(2,1)S(1)}, bf16[32,640]{1,0:T(8,128)(2,1)S(1)}, u32[]{:S(2)}, u32[]{:S(2)}) collective-permute-start(bf16[32,640]{1,0:T(8,128)(2,1)S(1)} %get-tuple-element.52), channel_id=1, source_target_pairs={{0,2},{1,3},{2,0},{3,1},{4,6},{5,7},{6,4},{7,5},{8,10},{9,11},{10,... | collective-permute-start | bytes 122888 | tf_op jit(solution)/shard_map/ppermute | solution.py:305
  140.4 11.4 %all-to-all-start.3 = ((f32[32,4,128]{2,1,0:T(4,128)}), f32[32,4,128]{2,1,0:T(4,128)S(1)}, u32[]{:S(2)}, u32[]{:S(2)}) async-start(f32[32,4,128]{2,1,0:T(4,128)} %copy-done.6), calls=%async_computation.3 | async-start | bytes 131072 | tf_op jit(solution)/shard_map/all_to_all | solution.py:309
  151.8 7.4 %collective-permute-start.14 = (bf16[32,640]{1,0:T(8,128)(2,1)}, bf16[32,640]{1,0:T(8,128)(2,1)S(1)}, u32[]{:S(2)}, u32[]{:S(2)}) collective-permute-start(bf16[32,640]{1,0:T(8,128)(2,1)} %copy-done.20), channel_id=1, source_target_pairs={{0,3},{1,2},{2,1},{3,0},{4,7},{5,6},{6,5},{7,4},{8,11},{9,10},{10,... | collective-permute-start | bytes 122888 | tf_op jit(solution)/shard_map/ppermute | solution.py:305
  163.6 3.3 %collective-permute-start.15 = (bf16[16,640]{1,0:T(8,128)(2,1)}, bf16[16,640]{1,0:T(8,128)(2,1)S(1)}, u32[]{:S(2)}, u32[]{:S(2)}) collective-permute-start(bf16[16,640]{1,0:T(8,128)(2,1)} %copy-done.25), channel_id=1, source_target_pairs={{0,4},{4,8},{8,12},{12,16},{16,20},{20,24},{24,28},{1,5},{5,9},{9,... | collective-permute-start | bytes 61448 | tf_op jit(solution)/shard_map/ppermute | solution.py:366
  168.9 3.6 %collective-permute-done.16.below_ref = bf16[16,640]{1,0:T(8,128)(2,1)S(1)} collective-permute-done((bf16[16,640]{1,0:T(8,128)(2,1)}, bf16[16,640]{1,0:T(8,128)(2,1)S(1)}, u32[]{:S(2)}, u32[]{:S(2)}) %collective-permute-start.16) | collective-permute-done | bytes 20512 | tf_op jit(solution)/shard_map/ppermute | solution.py:367
  177.0 3.0 %conv1.1 = (f32[32,4,128]{2,1,0:T(4,128)}, f32[32,256]{1,0:T(8,128)S(1)}, f32[32,256]{1,0:T(8,128)S(1)}, f32[32,256]{1,0:T(8,128)S(1)}, f32[32,256]{1,0:T(8,128)...) custom-call(s32[2]{0:T(128)S(1)} %pad_add_fusion.place_ref, ...), custom_call_target="tpu_custom_call" | custom-call | flops 1073741824 | bytes 1048576 | tf_op jit(solution)/shard_map/conv1/pallas_call | solution.py:292
  181.2 13.0 %all-to-all-start.4 = ((f32[32,4,128]{2,1,0:T(4,128)}), f32[32,4,128]{2,1,0:T(4,128)S(1)}, u32[]{:S(2)}, u32[]{:S(2)}) async-start(f32[32,4,128]{2,1,0:T(4,128)} %get-tuple-element.46), calls=%async_computation.4 | async-start | bytes 131072 | tf_op jit(solution)/shard_map/all_to_all | solution.py:309
  196.4 7.3 %collective-permute-start.18 = (f32[32,256]{1,0:T(8,128)}, f32[32,256]{1,0:T(8,128)S(1)}, u32[]{:S(2)}, u32[]{:S(2)}) collective-permute-start(f32[32,256]{1,0:T(8,128)} %copy-done.22), channel_id=1, source_target_pairs={{0,2},{1,3},{2,0},{3,1},{4,6},{5,7},{6,4},{7,5},{8,10},{9,11},{10,... | collective-permute-start | bytes 98312 | tf_op jit(solution)/shard_map/ppermute | solution.py:305
  206.1 6.9 %collective-permute-done.19.c3_ref = f32[32,256]{1,0:T(8,128)S(1)} collective-permute-done((f32[32,256]{1,0:T(8,128)S(1)}, f32[32,256]{1,0:T(8,128)S(1)}, u32[]{:S(2)}, u32[]{:S(2)}) %collective-permute-start.19) | collective-permute-done | bytes 32800 | tf_op jit(solution)/shard_map/ppermute | solution.py:305
  214.3 3.3 %attend1.1 = f32[2,32,640]{2,1,0:T(8,128)} custom-call(s32[2]{0:T(128)S(1)} %pad_add_fusion.place_ref, s32[1]{0:T(128)} %bitcast.2.own_ref, f32[32,4,128]{2,1,0:T(4,128)S(1)} %all-to-all-done.4.stats_ref, f32[32,640]{1,0:T(8,128)S(1)} %get-tuple-element.47.state_ref, f32[32,256]{1,0:T(8,128)S(1)} %get-tuple-element.48.c0_ref, ...), custom_call_target="tpu_custom_call" | custom-call | flops 1073741824 | bytes 1048576 | tf_op jit(solution)/shard_map/attend1/pallas_call | solution.py:292
  (124 shorter events, 52.6 us)
Async XLA Ops:
  6.5 79.1 %all-gather.4.cloned.1.call-start = ((), (), s32[]{:S(2)}) async-start(), calls=%async_computation.5 | async-start | bytes 2119680 | tf_op jit(solution)/shard_map/all_gather | solution.py:337
  12.1 45.0 %all-to-all-start.2 = ((bf16[16,32,640]{2,1,0:T(8,128)(2,1)}), bf16[16,32,640]{2,1,0:T(8,128)(2,1)S(1)}, u32[]{:S(2)}, u32[]{:S(2)}) async-start(bf16[16,32,640]{2,1,0:T(8,128)(2,1)} %get-tuple-element.40), calls=%async_computation.2 | async-start | bytes 1310720 | tf_op jit(solution)/shard_map/all_to_all | solution.py:309
  28.3 39.5 %collective-permute-start.5 = (bf16[32,640]{1,0:T(8,128)(2,1)S(1)}, bf16[32,640]{1,0:T(8,128)(2,1)S(1)}, u32[]{:S(2)}, u32[]{:S(2)}) collective-permute-start(bf16[32,640]{1,0:T(8,128)(2,1)S(1)} %bitcast.12), channel_id=1, source_target_pairs={{0,3},{1,2},{2,1},{3,0},{4,7},{5,6},{6,5},{7,4},{8,11},{9,10},{10,... | collective-permute-start | bytes 122888 | tf_op jit(solution)/shard_map/ppermute | solution.py:305
  36.6 38.5 %collective-permute-start.4 = (bf16[32,640]{1,0:T(8,128)(2,1)S(1)}, bf16[32,640]{1,0:T(8,128)(2,1)S(1)}, u32[]{:S(2)}, u32[]{:S(2)}) collective-permute-start(bf16[32,640]{1,0:T(8,128)(2,1)S(1)} %bitcast.13), channel_id=1, source_target_pairs={{0,2},{1,3},{2,0},{3,1},{4,6},{5,7},{6,4},{7,5},{8,10},{9,11},{10,... | collective-permute-start | bytes 122888 | tf_op jit(solution)/shard_map/ppermute | solution.py:305
  38.5 38.9 %collective-permute-start.3 = (bf16[32,640]{1,0:T(8,128)(2,1)S(1)}, bf16[32,640]{1,0:T(8,128)(2,1)S(1)}, u32[]{:S(2)}, u32[]{:S(2)}) collective-permute-start(bf16[32,640]{1,0:T(8,128)(2,1)S(1)} %bitcast.14), channel_id=1, source_target_pairs={{0,1},{1,0},{2,3},{3,2},{4,5},{5,4},{6,7},{7,6},{8,9},{9,8},{10,11... | collective-permute-start | bytes 122888 | tf_op jit(solution)/shard_map/ppermute | solution.py:305
  40.8 40.3 %collective-permute-start.2 = (bf16[32,640]{1,0:T(8,128)(2,1)S(1)}, bf16[32,640]{1,0:T(8,128)(2,1)S(1)}, u32[]{:S(2)}, u32[]{:S(2)}) collective-permute-start(bf16[32,640]{1,0:T(8,128)(2,1)S(1)} %get-tuple-element.30.d0_ref), channel_id=1, source_target_pairs={{0,3},{1,2},{2,1},{3,0},{4,7},{5,6},{6,5},{7,4},{8,11},{9,10},{10,... | collective-permute-start | bytes 122888 | tf_op jit(solution)/shard_map/ppermute | solution.py:305
  57.1 28.6 %all-to-all-start = ((f32[32,4,128]{2,1,0:T(4,128)}), f32[32,4,128]{2,1,0:T(4,128)S(1)}, u32[]{:S(2)}, u32[]{:S(2)}) async-start(f32[32,4,128]{2,1,0:T(4,128)} %get-tuple-element.29), calls=%async_computation | async-start | bytes 131072 | tf_op jit(solution)/shard_map/all_to_all | solution.py:309
  65.5 48.5 %collective-permute-start.11 = (bf16[16,32,640]{2,1,0:T(8,128)(2,1)S(1)}, bf16[16,32,640]{2,1,0:T(8,128)(2,1)}, u32[]{:S(2)}, u32[]{:S(2)}) collective-permute-start(bf16[16,32,640]{2,1,0:T(8,128)(2,1)S(1)} %all-to-all-done.2.refs_0_), channel_id=1, source_target_pairs={{0,1},{1,0},{2,3},{3,2},{4,5},{5,4},{6,7},{7,6},{8,9},{9,8},{10,11... | collective-permute-start | bytes 1966088 | tf_op jit(solution)/shard_map/ppermute | solution.py:305
  67.8 15.3 %collective-permute-start.1 = (bf16[32,640]{1,0:T(8,128)(2,1)S(1)}, bf16[32,640]{1,0:T(8,128)(2,1)S(1)}, u32[]{:S(2)}, u32[]{:S(2)}) collective-permute-start(bf16[32,640]{1,0:T(8,128)(2,1)S(1)} %get-tuple-element.30.d0_ref), channel_id=1, source_target_pairs={{0,2},{1,3},{2,0},{3,1},{4,6},{5,7},{6,4},{7,5},{8,10},{9,11},{10,... | collective-permute-start | bytes 122888 | tf_op jit(solution)/shard_map/ppermute | solution.py:305
  92.0 27.9 %all-to-all-start.1 = ((f32[32,4,128]{2,1,0:T(4,128)}), f32[32,4,128]{2,1,0:T(4,128)S(1)}, u32[]{:S(2)}, u32[]{:S(2)}) async-start(f32[32,4,128]{2,1,0:T(4,128)} %get-tuple-element.35), calls=%async_computation.1 | async-start | bytes 131072 | tf_op jit(solution)/shard_map/all_to_all | solution.py:309
  100.8 112.1 %all-gather.6.cloned.1.call-start = ((), (), s32[]{:S(2)}) async-start(), calls=%async_computation.6 | async-start | bytes 1474560 | tf_op jit(solution)/shard_map/all_gather | solution.py:438
  100.9 13.1 %collective-permute-start.8 = (f32[32,256]{1,0:T(8,128)}, f32[32,256]{1,0:T(8,128)S(1)}, u32[]{:S(2)}, u32[]{:S(2)}) collective-permute-start(f32[32,256]{1,0:T(8,128)} %get-tuple-element.37), channel_id=1, source_target_pairs={{0,1},{1,0},{2,3},{3,2},{4,5},{5,4},{6,7},{7,6},{8,9},{9,8},{10,11... | collective-permute-start | bytes 98312 | tf_op jit(solution)/shard_map/ppermute | solution.py:305
  103.0 11.6 %collective-permute-start.9 = (f32[32,256]{1,0:T(8,128)}, f32[32,256]{1,0:T(8,128)S(1)}, u32[]{:S(2)}, u32[]{:S(2)}) collective-permute-start(f32[32,256]{1,0:T(8,128)} %get-tuple-element.38), channel_id=1, source_target_pairs={{0,2},{1,3},{2,0},{3,1},{4,6},{5,7},{6,4},{7,5},{8,10},{9,11},{10,... | collective-permute-start | bytes 98312 | tf_op jit(solution)/shard_map/ppermute | solution.py:305
  110.4 9.5 %collective-permute-start.10 = (f32[32,256]{1,0:T(8,128)}, f32[32,256]{1,0:T(8,128)}, u32[]{:S(2)}, u32[]{:S(2)}) collective-permute-start(f32[32,256]{1,0:T(8,128)} %get-tuple-element.39), channel_id=1, source_target_pairs={{0,3},{1,2},{2,1},{3,0},{4,7},{5,6},{6,5},{7,4},{8,11},{9,10},{10,... | collective-permute-start | bytes 98312 | tf_op jit(solution)/shard_map/ppermute | solution.py:305
  127.1 11.8 %collective-permute-start.22 = (bf16[32,640]{1,0:T(8,128)(2,1)S(1)}, bf16[32,640]{1,0:T(8,128)(2,1)S(1)}, u32[]{:S(2)}, u32[]{:S(2)}) collective-permute-start(bf16[32,640]{1,0:T(8,128)(2,1)S(1)} %get-tuple-element.52), channel_id=1, source_target_pairs={{0,3},{1,2},{2,1},{3,0},{4,7},{5,6},{6,5},{7,4},{8,11},{9,10},{10,... | collective-permute-start | bytes 122888 | tf_op jit(solution)/shard_map/ppermute | solution.py:305
  129.6 9.3 %collective-permute-start.21 = (bf16[32,640]{1,0:T(8,128)(2,1)S(1)}, bf16[32,640]{1,0:T(8,128)(2,1)S(1)}, u32[]{:S(2)}, u32[]{:S(2)}) collective-permute-start(bf16[32,640]{1,0:T(8,128)(2,1)S(1)} %get-tuple-element.52), channel_id=1, source_target_pairs={{0,2},{1,3},{2,0},{3,1},{4,6},{5,7},{6,4},{7,5},{8,10},{9,11},{10,... | collective-permute-start | bytes 122888 | tf_op jit(solution)/shard_map/ppermute | solution.py:305
  140.4 32.0 %all-to-all-start.3 = ((f32[32,4,128]{2,1,0:T(4,128)}), f32[32,4,128]{2,1,0:T(4,128)S(1)}, u32[]{:S(2)}, u32[]{:S(2)}) async-start(f32[32,4,128]{2,1,0:T(4,128)} %copy-done.6), calls=%async_computation.3 | async-start | bytes 131072 | tf_op jit(solution)/shard_map/all_to_all | solution.py:309
  151.8 20.6 %collective-permute-start.14 = (bf16[32,640]{1,0:T(8,128)(2,1)}, bf16[32,640]{1,0:T(8,128)(2,1)S(1)}, u32[]{:S(2)}, u32[]{:S(2)}) collective-permute-start(bf16[32,640]{1,0:T(8,128)(2,1)} %copy-done.20), channel_id=1, source_target_pairs={{0,3},{1,2},{2,1},{3,0},{4,7},{5,6},{6,5},{7,4},{8,11},{9,10},{10,... | collective-permute-start | bytes 122888 | tf_op jit(solution)/shard_map/ppermute | solution.py:305
  159.3 13.2 %collective-permute-start.13 = (bf16[32,640]{1,0:T(8,128)(2,1)}, bf16[32,640]{1,0:T(8,128)(2,1)S(1)}, u32[]{:S(2)}, u32[]{:S(2)}) collective-permute-start(bf16[32,640]{1,0:T(8,128)(2,1)} %copy-done.20), channel_id=1, source_target_pairs={{0,2},{1,3},{2,0},{3,1},{4,6},{5,7},{6,4},{7,5},{8,10},{9,11},{10,... | collective-permute-start | bytes 122888 | tf_op jit(solution)/shard_map/ppermute | solution.py:305
  161.2 11.2 %collective-permute-start.12 = (bf16[32,640]{1,0:T(8,128)(2,1)}, bf16[32,640]{1,0:T(8,128)(2,1)S(1)}, u32[]{:S(2)}, u32[]{:S(2)}) collective-permute-start(bf16[32,640]{1,0:T(8,128)(2,1)} %copy-done.20), channel_id=1, source_target_pairs={{0,1},{1,0},{2,3},{3,2},{4,5},{5,4},{6,7},{7,6},{8,9},{9,8},{10,11... | collective-permute-start | bytes 122888 | tf_op jit(solution)/shard_map/ppermute | solution.py:305
  181.2 31.7 %all-to-all-start.4 = ((f32[32,4,128]{2,1,0:T(4,128)}), f32[32,4,128]{2,1,0:T(4,128)S(1)}, u32[]{:S(2)}, u32[]{:S(2)}) async-start(f32[32,4,128]{2,1,0:T(4,128)} %get-tuple-element.46), calls=%async_computation.4 | async-start | bytes 131072 | tf_op jit(solution)/shard_map/all_to_all | solution.py:309
  194.2 11.8 %collective-permute-start.17 = (f32[32,256]{1,0:T(8,128)}, f32[32,256]{1,0:T(8,128)S(1)}, u32[]{:S(2)}, u32[]{:S(2)}) collective-permute-start(f32[32,256]{1,0:T(8,128)} %copy-done.23), channel_id=1, source_target_pairs={{0,1},{1,0},{2,3},{3,2},{4,5},{5,4},{6,7},{7,6},{8,9},{9,8},{10,11... | collective-permute-start | bytes 98312 | tf_op jit(solution)/shard_map/ppermute | solution.py:305
  196.4 9.7 %collective-permute-start.18 = (f32[32,256]{1,0:T(8,128)}, f32[32,256]{1,0:T(8,128)S(1)}, u32[]{:S(2)}, u32[]{:S(2)}) collective-permute-start(f32[32,256]{1,0:T(8,128)} %copy-done.22), channel_id=1, source_target_pairs={{0,2},{1,3},{2,0},{3,1},{4,6},{5,7},{6,4},{7,5},{8,10},{9,11},{10,... | collective-permute-start | bytes 98312 | tf_op jit(solution)/shard_map/ppermute | solution.py:305
  203.7 9.2 %collective-permute-start.19 = (f32[32,256]{1,0:T(8,128)S(1)}, f32[32,256]{1,0:T(8,128)S(1)}, u32[]{:S(2)}, u32[]{:S(2)}) collective-permute-start(f32[32,256]{1,0:T(8,128)S(1)} %get-tuple-element.51), channel_id=1, source_target_pairs={{0,3},{1,2},{2,1},{3,0},{4,7},{5,6},{6,5},{7,4},{8,11},{9,10},{10,... | collective-permute-start | bytes 98312 | tf_op jit(solution)/shard_map/ppermute | solution.py:305
  (40 other events, 522.8 us)
Sparse Core Ops, SparseCore 0:
  9.4 57.1 all-gather.3
  140.6 37.1 all-gather.5

commit v2 on v1

v2 whole, which is shorter than its diff:
```python
import functools

import jax
import jax.numpy as jnp
from jax import lax
from jax.experimental import pallas as pl
from jax.experimental.pallas import tpu as pltpu
from jax.sharding import Mesh
from jax.sharding import PartitionSpec as P

GROUPS = 32
HEADS = 5
HEAD_DIM = 64
WIDTH = HEADS * HEAD_DIM
CHANNELS = 640
MEMBERS = CHANNELS // GROUPS
COLS = 16
ROWS = 32
LANES = 128
QUAD_ROWS = 4 * ROWS
POSITIONS = 1024
EPS = 1e-05

PATCH = ("y", "zh", "core")
QUAD = ("zh", "core")
REQ_PATCH = ("req", "y", "zh", "core")

F32 = jnp.float32
BF16 = jnp.bfloat16

NN = (((1,), (0,)), ((), ()))
NT = (((1,), (1,)), ((), ()))


def dot(a, b, dims=NN):
    return lax.dot_general(a, b, dims, preferred_element_type=F32)


def thirds(x):
    high = x.astype(BF16)
    rest = x - high.astype(F32)
    middle = rest.astype(BF16)
    low = (rest - middle.astype(F32)).astype(BF16)
    return high, middle, low


def picked(x, zero_one, dims=NN):
    rows = x.shape[0]
    stacked = jnp.concatenate([t.astype(F32) for t in thirds(x)], axis=0).astype(BF16)
    out = dot(stacked, zero_one, dims)
    return out[:rows] + out[rows : 2 * rows] + out[2 * rows :]


def group_matrix():
    channel = lax.broadcasted_iota(jnp.int32, (CHANNELS, LANES), 0)
    first = lax.broadcasted_iota(jnp.int32, (CHANNELS, LANES), 1) * MEMBERS
    return jnp.where((channel >= first) & (channel < first + MEMBERS), 1.0, 0.0).astype(BF16)


def eight(rows, lanes):
    have = sum(r.shape[0] for r in rows)
    return jnp.concatenate([*rows, jnp.zeros((8 - have, lanes), F32)], axis=0)


def tell_sums(x, groups, stats_ref):
    sums = eight(
        [jnp.sum(x, axis=0, keepdims=True), jnp.sum(x * x, axis=0, keepdims=True)], CHANNELS
    )
    told = picked(sums, groups)[0:4]
    stats_ref[...] = jnp.broadcast_to(told[None], stats_ref.shape)


def mean_and_scale(stats_ref, groups):
    sums = jnp.sum(stats_ref[...], axis=0)
    number = POSITIONS * MEMBERS
    mean = sums[0:1] * (1.0 / number)
    variance = sums[1:2] * (1.0 / number) - mean * mean
    spread = picked(eight([mean, lax.rsqrt(variance + EPS)], LANES), groups, NT)
    return spread[0:1], spread[1:2]


def pack_kernel(field_ref, stale_ref, keys_ref, values_ref, packed_ref):
    high, middle, _ = thirds(field_ref[...])
    both = jnp.concatenate(
        [keys_ref[...].astype(F32), values_ref[...].astype(F32)], axis=1
    ).astype(BF16)
    for to in range(4):
        packed_ref[to, 0:ROWS] = high
        packed_ref[to, ROWS : 2 * ROWS] = middle
        packed_ref[to, 2 * ROWS : 3 * ROWS] = stale_ref[...]
        packed_ref[to, 3 * ROWS :] = both


def unpack_kernel(
    place_ref,
    packed_ref,
    field_ref,
    state_ref,
    stats_ref,
    kv_ref,
    prior_ref,
    first_ref,
    last_ref,
):
    a = place_ref[1]
    for t in range(4):
        state_ref[t] = packed_ref[t, 0:ROWS].astype(F32) + packed_ref[t, ROWS : 2 * ROWS].astype(F32)
        prior_ref[t] = packed_ref[t, 2 * ROWS : 3 * ROWS]
        kv_ref[t] = packed_ref[t, 3 * ROWS :]
    state_ref[a] = field_ref[...]
    first_ref[...] = prior_ref[0, :COLS]
    last_ref[...] = prior_ref[3, COLS:]
    tell_sums(state_ref[...].reshape(QUAD_ROWS, CHANNELS), group_matrix(), stats_ref)


def conv_kernel(
    stats_ref,
    state_ref,
    prior_ref,
    above_ref,
    below_ref,
    weight_ref,
    gain_ref,
    bias_ref,
    out_ref,
    act_ref,
    first_ref,
    last_ref,
    rows,
    wide,
):
    mean, scale = mean_and_scale(stats_ref, group_matrix())
    for t in range(4):
        value = (state_ref[t] - mean) * scale * gain_ref[...] + bias_ref[...]
        act_ref[t] = (value * (1.0 / (1.0 + jnp.exp(-value)))).astype(BF16)
    first_ref[...] = act_ref[0, :COLS]
    last_ref[...] = act_ref[3, COLS:]
    for t in range(4):
        rows[t, 0:COLS] = above_ref[...] if t == 0 else prior_ref[t - 1, COLS:]
        rows[t, COLS : 3 * COLS] = act_ref[t]
        rows[t, 3 * COLS :] = below_ref[...] if t == 3 else prior_ref[t + 1, :COLS]
    window = rows[...].reshape(4 * 64, CHANNELS)

    wide[...] = jnp.zeros(wide.shape, F32)
    col = lax.broadcasted_iota(jnp.int32, (LANES, LANES), 0) & (COLS - 1)
    lane = lax.broadcasted_iota(jnp.int32, (LANES, LANES), 1)
    tiles = [jnp.zeros((LANES, LANES), F32), jnp.zeros((LANES, LANES), F32)]
    for part in range(8):
        wide[:, 0 : 9 * MEMBERS] = dot(window, weight_ref[part], NT)
        whole = wide[...].reshape(4, 64, 256)
        lines = [
            whole[:, COLS * r : COLS * r + 2 * COLS].reshape(LANES, 256) for r in range(3)
        ]
        total = (
            lines[0][:, :LANES]
            + pltpu.roll(lines[1][:, :LANES], LANES - 3 * MEMBERS, 1)
            + pltpu.roll(lines[2], 256 - 6 * MEMBERS, 1)[:, :LANES]
        )
        left = jnp.where(col > 0, pltpu.roll(total, 1, 0), 0.0)
        centre = pltpu.roll(total, LANES - MEMBERS, 1)
        right = pltpu.roll(total, LANES - 2 * MEMBERS, 1)
        right = jnp.where(col < COLS - 1, pltpu.roll(right, LANES - 1, 0), 0.0)
        made = left + centre + right
        tile, at = divmod(part, 6)
        at *= MEMBERS
        if at:
            made = pltpu.roll(made, at, 1)
        kept = (lane >= at) & (lane < at + MEMBERS)
        tiles[tile] = jnp.where(kept, made, tiles[tile])
    rest = jnp.where(
        lane[:64] < 64, tiles[1][:64], pltpu.roll(tiles[1][64:], 64, 1)
    )
    for to in range(4):
        out_ref[to, 0:LANES] = tiles[0]
        out_ref[to, LANES:] = rest


def hidden_kernel(conv_ref, state_ref, shift_ref, hidden_ref, stats_ref):
    lane = lax.broadcasted_iota(jnp.int32, (LANES, LANES), 1)
    tiles = [jnp.zeros((LANES, LANES), F32) for _ in range(5)]
    for t in range(4):
        rest = conv_ref[t, LANES:]
        sources = (
            conv_ref[t, 0:LANES],
            jnp.concatenate([rest, pltpu.roll(rest, 64, 1)], axis=0),
        )
        for part in range(8):
            source, at = divmod(part, 6)
            at *= MEMBERS
            tile, to = divmod(4 * MEMBERS * part + MEMBERS * t, LANES)
            turn = (to - at) % LANES
            block = sources[source]
            if turn:
                block = pltpu.roll(block, turn, 1)
            kept = (lane >= to) & (lane < to + MEMBERS)
            tiles[tile] = jnp.where(kept, block, tiles[tile])
            if to + MEMBERS > LANES:
                kept = lane < to + MEMBERS - LANES
                tiles[tile + 1] = jnp.where(kept, block, tiles[tile + 1])
    state = state_ref[...].reshape(QUAD_ROWS, CHANNELS)
    hidden = state + (jnp.concatenate(tiles, axis=1) + shift_ref[...])
    hidden_ref[...] = hidden.reshape(hidden_ref.shape)
    tell_sums(hidden, group_matrix(), stats_ref)


def attend(hidden, patch, y, mean, scale, gain, bias, w_query, w_keyvalue, w_out, kv_ref):
    count = hidden.shape[0]
    normed = ((hidden - mean) * scale * gain + bias).astype(BF16)
    query = dot(normed, w_query)
    fresh = dot(normed, w_keyvalue).astype(BF16)
    query = jnp.concatenate([query, jnp.zeros((count, 3 * LANES - WIDTH), F32)], axis=1)
    lane = lax.broadcasted_iota(jnp.int32, (count, LANES), 1)
    low = lane < HEAD_DIM

    column = lax.broadcasted_iota(jnp.int32, (count, POSITIONS), 1) >> 5
    replaced = column == 4 * y + patch
    if count == ROWS:
        theirs = None
    else:
        theirs = (lax.broadcasted_iota(jnp.int32, (count, count), 1) >> 5) == patch
    tiles = [jnp.zeros((count, LANES), F32) for _ in range(3)]
    for h in range(HEADS):
        at = LANES * (h // 2)
        own = low if h % 2 == 0 else ~low
        asked = jnp.where(own, query[:, at : at + LANES], 0.0).astype(BF16)
        old = dot(asked, kv_ref[:, at : at + LANES], NT) * HEAD_DIM ** (-0.5)
        old = jnp.where(replaced, -jnp.inf, old)
        new = dot(asked, fresh[:, at : at + LANES], NT) * HEAD_DIM ** (-0.5)
        if theirs is not None:
            new = jnp.where(theirs, new, -jnp.inf)
        peak = jnp.maximum(
            jnp.max(old, axis=1, keepdims=True), jnp.max(new, axis=1, keepdims=True)
        )
        old = jnp.exp(old - peak)
        new = jnp.exp(new - peak)
        total = jnp.sum(old, axis=1, keepdims=True) + jnp.sum(new, axis=1, keepdims=True)
        at = LANES * ((HEADS + h) // 2)
        summed = dot(old.astype(BF16), kv_ref[:, at : at + LANES])
        summed += dot(new.astype(BF16), fresh[:, at : at + LANES])
        summed = pltpu.roll(summed / total, HEAD_DIM, 1)
        tiles[h // 2] = jnp.where(own, summed, tiles[h // 2])
    attended = jnp.concatenate(tiles, axis=1)[:, :WIDTH].astype(BF16)
    return hidden + dot(attended, w_out), fresh


def attend_quad_kernel(
    place_ref,
    stats_ref,
    hidden_ref,
    gain_ref,
    bias_ref,
    query_ref,
    keyvalue_ref,
    out_ref,
    kv_ref,
    state_ref,
    result_ref,
    told_ref,
    fresh_ref,
):
    groups = group_matrix()
    mean, scale = mean_and_scale(stats_ref, groups)
    patch = lax.broadcasted_iota(jnp.int32, (QUAD_ROWS, 1), 0) >> 5
    result, fresh = attend(
        hidden_ref[...].reshape(QUAD_ROWS, CHANNELS),
        patch,
        place_ref[0],
        mean,
        scale,
        gain_ref[...],
        bias_ref[...],
        query_ref[...],
        keyvalue_ref[...],
        out_ref[...],
        kv_ref,
    )
    state_ref[...] = result.reshape(state_ref.shape)
    result_ref[...] = state_ref[place_ref[1]]
    fresh_ref[...] = fresh
    tell_sums(result, groups, told_ref)


def attend_own_kernel(
    place_ref,
    stats_ref,
    hidden_ref,
    gain_ref,
    bias_ref,
    query_ref,
    keyvalue_ref,
    out_ref,
    kv_ref,
    earlier_ref,
    result_ref,
):
    mean, scale = mean_and_scale(stats_ref, group_matrix())
    a = place_ref[1]
    result, _ = attend(
        hidden_ref[a],
        a,
        place_ref[0],
        mean,
        scale,
        gain_ref[...],
        bias_ref[...],
        query_ref[...],
        keyvalue_ref[...],
        out_ref[...],
        kv_ref,
    )
    result_ref[0] = earlier_ref[...]
    result_ref[1] = result


VMEM = pl.BlockSpec(memory_space=pltpu.VMEM)
SMEM = pl.BlockSpec(memory_space=pltpu.SMEM)


def call(kernel, name, out_shapes, args, scalars=0, scratch=(), flops=0):
    return pl.pallas_call(
        kernel,
        name=name,
        out_shape=[jax.ShapeDtypeStruct(s, t) for s, t in out_shapes],
        in_specs=[SMEM] * scalars + [VMEM] * (len(args) - scalars),
        out_specs=[VMEM] * len(out_shapes),
        scratch_shapes=list(scratch),
        cost_estimate=pl.CostEstimate(flops=flops, bytes_accessed=1 << 20, transcendentals=0),
        compiler_params=pltpu.CompilerParams(vmem_limit_bytes=48 << 20),
    )(*args)


def to_all(value, axes):
    return lax.all_to_all(value, axes, 0, 0, tiled=True)


def per_device(
    field,
    stale_conv_in,
    stale_keys,
    stale_values,
    norm1_gain,
    norm1_bias,
    conv_weight,
    conv_bias,
    time_embed,
    norm2_gain,
    norm2_bias,
    w_query,
    w_keyvalue,
    w_out,
):
    quad = (4, ROWS, CHANNELS)
    line = (COLS, CHANNELS)
    stats8 = ((8, 4, LANES), F32)
    y = lax.axis_index("y")
    a = 2 * lax.axis_index("zh") + lax.axis_index("core")
    place = jnp.stack([y, a]).astype(jnp.int32)
    up = [(i, i + 1) for i in range(7)]
    down = [(i + 1, i) for i in range(7)]
    row = lambda v: v.reshape(1, CHANNELS)

    slices = conv_weight.transpose(0, 1, 3, 2).reshape(9 * MEMBERS, CHANNELS)
    weights = lax.all_gather(slices, "y", axis=0, tiled=False)

    own = field.reshape(ROWS, CHANNELS)
    (packed,) = call(
        pack_kernel,
        "pack",
        [((4, 4 * ROWS, CHANNELS), BF16)],
        (own, stale_conv_in.reshape(ROWS, CHANNELS), stale_keys, stale_values),
    )
    state, stats, kv, prior, first, last = call(
        unpack_kernel,
        "unpack",
        [(quad, F32), stats8, (quad, BF16), (quad, BF16), (line, BF16), (line, BF16)],
        (place, to_all(packed, QUAD), own),
        scalars=1,
    )
    for step in range(2):
        stats = to_all(stats, "y")
        above = lax.ppermute(last, "y", up)
        below = lax.ppermute(first, "y", down)
        kv = lax.all_gather(kv.reshape(QUAD_ROWS, CHANNELS), "y", axis=0, tiled=True)
        conv, prior, first, last = call(
            conv_kernel,
            f"conv{step}",
            [((4, LANES + 64, LANES), F32), (quad, BF16), (line, BF16), (line, BF16)],
            (stats, state, prior, above, below, weights, row(norm1_gain), row(norm1_bias)),
            scratch=[pltpu.VMEM((4, 64, CHANNELS), BF16), pltpu.VMEM((256, 256), F32)],
            flops=1 << 30,
        )
        hidden, stats = call(
            hidden_kernel,
            f"hidden{step}",
            [(quad, F32), stats8],
            (to_all(conv, QUAD), state, row(conv_bias + time_embed[step])),
            flops=1 << 28,
        )
        common = (
            place,
            to_all(stats, "y"),
            hidden,
            row(norm2_gain),
            row(norm2_bias),
            w_query,
            w_keyvalue,
            w_out,
            kv,
        )
        if step == 1:
            (out,) = call(
                attend_own_kernel,
                "attend1",
                [((2, ROWS, CHANNELS), F32)],
                (*common, earlier),
                scalars=1,
                flops=1 << 30,
            )
            return out.reshape(2, 2, COLS, CHANNELS)
        state, earlier, stats, kv = call(
            attend_quad_kernel,
            "attend0",
            [(quad, F32), ((ROWS, CHANNELS), F32), stats8, ((QUAD_ROWS, CHANNELS), BF16)],
            common,
            scalars=1,
            flops=1 << 30,
        )


def solution(mesh):
    torus = Mesh(
        mesh.devices.reshape(mesh.shape["req"], 8, 2, 2), ("req", "y", "zh", "core")
    )
    placed = (
        P(REQ_PATCH, None, None),
        P(REQ_PATCH, None, None),
        P(REQ_PATCH, None),
        P(REQ_PATCH, None),
        P(),
        P(),
        P(None, None, None, PATCH),
        P(),
        P("req", None),
        P(),
        P(),
        P(),
        P(),
        P(),
    )
    return jax.shard_map(
        per_device,
        mesh=torus,
        in_specs=placed,
        out_specs=P(None, REQ_PATCH, None, None),
        check_vma=False,
    )
```

time: 226 us -> 174 us (0.77)
  starting transfers between devices: 145 us -> 66.2 us
  waiting for transfers between devices: 27.5 us -> 49.1 us
  blocking collectives: 0 us -> 13.7 us
  local copies, waits for them, and re-layouts: 21.5 us -> 12.1 us
  Pallas kernels: 14.6 us -> 17 us
    ppermute x19 -> x0, starting transfers between devices: 78.6 us -> none  [flipped(): return lax.ppermute(value, QUAD, [(i, i ^ k) for i in range(4)])]
    all_to_all x5 -> x6, waiting for transfers between devices: 9.01 us -> 35.6 us  [to_all(): return lax.all_to_all(value, axes, 0, 0, tiled=True)]
    all_to_all x0 -> x1, blocking collectives: none -> 13.7 us  [to_all(): return lax.all_to_all(value, axes, 0, 0, tiled=True)]
    ppermute x19 -> x0, waiting for transfers between devices: 12.4 us -> none  [flipped(): return lax.ppermute(value, QUAD, [(i, i ^ k) for i in range(4)])]
    unnamed x69 -> x47, local copies, waits for them, and re-layouts: 19.1 us -> 10.3 us
    all_gather x1 -> x2, waiting for transfers between devices: 0.01 us -> 6.52 us  [per_device(): lax.all_gather(kv.reshape(QUAD_ROWS, CHANNELS), 'y', axis=0, tiled=True)]
    pallas_call x6 -> x8, Pallas kernels: 14.6 us -> 17 us  [call(): pl.pallas_call(kernel, name=name, out_shape=[jax.ShapeDtypeStruct(s, t) f...]
    all_to_all x5 -> x6, starting transfers between devices: 57.8 us -> 56.9 us  [to_all(): return lax.all_to_all(value, axes, 0, 0, tiled=True)]
  transfers between devices with their start and end apart: 30 -> 13, of which waited for: 6 -> 6; matrix products, arithmetic and copies ran while one was open for 1% -> 0% of each run, Pallas kernels for 4% -> 5%
where the time goes in v2:
time: 174 us; the launch traced here: 171 us
  starting transfers between devices  66.2 us (38%)
  waiting for transfers between devices  49.1 us (28%)
  Pallas kernels  17 us (10%)
  blocking collectives  13.7 us (8%)
  between operations  13.3 us (8%)
  local copies, waits for them, and re-layouts  12.1 us (7%)
    all_to_all x6, starting transfers between devices, to_all(): return lax.all_to_all(value, axes, 0, 0, tiled=True)  56.9 us
    all_to_all x6, waiting for transfers between devices, to_all(): return lax.all_to_all(value, axes, 0, 0, tiled=True)  35.6 us
    pallas_call x8, Pallas kernels, call(): pl.pallas_call(kernel, name=name, out_shape=[jax.ShapeDtypeStruct(s, t) f...  17 us
    all_to_all x1, blocking collectives, to_all(): return lax.all_to_all(value, axes, 0, 0, tiled=True)  13.7 us
    unnamed x47, local copies, waits for them, and re-layouts  10.3 us
    ppermute x2, waiting for transfers between devices, per_device(): below = lax.ppermute(first, 'y', down)  6.83 us
    ppermute x2, starting transfers between devices, per_device(): above = lax.ppermute(last, 'y', up)  6.71 us
    all_gather x2, waiting for transfers between devices, per_device(): lax.all_gather(kv.reshape(QUAD_ROWS, CHANNELS), 'y', axis=0, tiled=True)  6.52 us
  transfers between devices with their start and end apart: 13, of which 6 were waited for; matrix products, arithmetic and copies ran while one was open for 0% of the time, Pallas kernels for 5%

profile of v2, /device:TPU:1, one launch (start us, length us, event | category | flops | bytes accessed | tf_op | source)
XLA Modules:
  0.0 171.4 jit_solution(17931988200696064767)
XLA Ops:
  6.5 1.7 all_gather_reshape.3
  12.4 11.9 %all-to-all-start = ((bf16[4,128,640]{2,1,0:T(8,128)(2,1)}), bf16[4,128,640]{2,1,0:T(8,128)(2,1)S(1)}, u32[]{:S(2)}, u32[]{:S(2)}) async-start(bf16[4,128,640]{2,1,0:T(8,128)(2,1)} %pack.1), calls=%async_computation | async-start | bytes 1310720 | tf_op jit(solution)/shard_map/all_to_all | solution.py:333
  24.3 13.3 %all-to-all-done.packed_ref = bf16[4,128,640]{2,1,0:T(8,128)(2,1)S(1)} async-done(((bf16[4,128,640]{2,1,0:T(8,128)(2,1)}), bf16[4,128,640]{2,1,0:T(8,128)(2,1)S(1)}, u32[]{:S(2)}, u32[]{:S(2)}) %all-to-all-start) | async-done | bytes 655392 | tf_op jit(solution)/shard_map/all_to_all | solution.py:333
  37.6 1.4 unpack.1
  39.1 6.8 %all-to-all-start.1 = ((f32[8,4,128]{2,1,0:T(4,128)}), f32[8,4,128]{2,1,0:T(4,128)S(1)}, u32[]{:S(2)}, u32[]{:S(2)}) async-start(f32[8,4,128]{2,1,0:T(4,128)} %get-tuple-element.24), calls=%async_computation.1 | async-start | bytes 32768 | tf_op jit(solution)/shard_map/all_to_all | solution.py:333
  45.9 3.4 %collective-permute-start = (bf16[16,640]{1,0:T(8,128)(2,1)S(1)}, bf16[16,640]{1,0:T(8,128)(2,1)S(1)}, u32[]{:S(2)}, u32[]{:S(2)}) collective-permute-start(bf16[16,640]{1,0:T(8,128)(2,1)S(1)} %get-tuple-element.27), channel_id=1, source_target_pairs={{0,4},{4,8},{8,12},{12,16},{16,20},{20,24},{24,28},{1,5},{5,9},{9,... | collective-permute-start | bytes 61448 | tf_op jit(solution)/shard_map/ppermute | solution.py:381
  50.6 3.6 %collective-permute-done.1.below_ref = bf16[16,640]{1,0:T(8,128)(2,1)S(1)} collective-permute-done((bf16[16,640]{1,0:T(8,128)(2,1)S(1)}, bf16[16,640]{1,0:T(8,128)(2,1)S(1)}, u32[]{:S(2)}, u32[]{:S(2)}) %collective-permute-start.1) | collective-permute-done | bytes 20512 | tf_op jit(solution)/shard_map/ppermute | solution.py:382
  54.2 1.5 copy-done.5
  55.8 2.4 %conv0.1 = (f32[4,192,128]{2,1,0:T(8,128)}, bf16[4,32,640]{2,1,0:T(8,128)(2,1)S(1)}, bf16[16,640]{1,0:T(8,128)(2,1)S(1)}, bf16[16,640]{1,0:T(8,128)(2,1)S(1)}) custom-call(f32[8,4,128]{2,1,0:T(4,128)S(1)} %all-to-all-done.1.stats_ref, f32[4,32,640]{2,1,0:T(8,128)S(1)} %get-tuple-element.25.state_ref, bf16[4,32,640]{2,1,0:T(8,128)(2,1)S(1)} %get-tuple-element.26.prior_ref, ...), custom_call_target="tpu_custom_call" | custom-call | flops 1073741824 | bytes 1048576 | tf_op jit(solution)/shard_map/conv0/pallas_call | solution.py:320
  58.2 12.9 %all-to-all-start.2 = ((f32[4,192,128]{2,1,0:T(8,128)}), f32[4,192,128]{2,1,0:T(8,128)S(1)}, u32[]{:S(2)}, u32[]{:S(2)}) async-start(f32[4,192,128]{2,1,0:T(8,128)} %get-tuple-element.29), calls=%async_computation.2 | async-start | bytes 786432 | tf_op jit(solution)/shard_map/all_to_all | solution.py:333
  71.2 10.3 %all-to-all-done.2.conv_ref = f32[4,192,128]{2,1,0:T(8,128)S(1)} async-done(((f32[4,192,128]{2,1,0:T(8,128)}), f32[4,192,128]{2,1,0:T(8,128)S(1)}, u32[]{:S(2)}, u32[]{:S(2)}) %all-to-all-start.2) | async-done | bytes 393248 | tf_op jit(solution)/shard_map/all_to_all | solution.py:333
  81.5 1.4 hidden0.1
  82.8 6.7 %all-to-all-start.3 = ((f32[8,4,128]{2,1,0:T(4,128)}), f32[8,4,128]{2,1,0:T(4,128)S(1)}, u32[]{:S(2)}, u32[]{:S(2)}) async-start(f32[8,4,128]{2,1,0:T(4,128)} %get-tuple-element.30), calls=%async_computation.3 | async-start | bytes 32768 | tf_op jit(solution)/shard_map/all_to_all | solution.py:333
  89.9 6.5 %all-gather.6.cloned.1.call-done.kv_ref = bf16[1024,640]{1,0:T(8,128)(2,1)} async-done(((bf16[128,640]{1,0:T(8,128)(2,1)}), bf16[1024,640]{1,0:T(8,128)(2,1)}) %all-gather.6.cloned.1.call-update) | async-done | bytes 1310736 | tf_op jit(solution)/shard_map/all_gather | solution.py:383
  96.4 1.3 copy-done.7
  98.9 4.2 %attend0.1 = (f32[4,32,640]{2,1,0:T(8,128)S(1)}, f32[32,640]{1,0:T(8,128)S(1)}, f32[8,4,128]{2,1,0:T(4,128)}, bf16[128,640]{1,0:T(8,128)(2,1)}) custom-call(s32[2]{0:T(128)S(1)} %pad_add_fusion.place_ref, f32[8,4,128]{2,1,0:T(4,128)S(1)} %all-to-all-done.3.stats_ref, f32[4,32,640]{2,1,0:T(8,128)S(1)} %get-tuple-element.31.hidden_ref, ...), custom_call_target="tpu_custom_call" | custom-call | flops 1073741824 | bytes 1048576 | tf_op jit(solution)/shard_map/attend0/pallas_call | solution.py:320
  103.7 3.4 %all-to-all-start.4 = ((f32[8,4,128]{2,1,0:T(4,128)}), f32[8,4,128]{2,1,0:T(4,128)S(1)}, u32[]{:S(2)}, u32[]{:S(2)}) async-start(f32[8,4,128]{2,1,0:T(4,128)} %get-tuple-element.33), calls=%async_computation.4 | async-start | bytes 32768 | tf_op jit(solution)/shard_map/all_to_all | solution.py:333
  107.2 3.4 %collective-permute-start.2 = (bf16[16,640]{1,0:T(8,128)(2,1)S(1)}, bf16[16,640]{1,0:T(8,128)(2,1)S(1)}, u32[]{:S(2)}, u32[]{:S(2)}) collective-permute-start(bf16[16,640]{1,0:T(8,128)(2,1)S(1)} %get-tuple-element.36), channel_id=1, source_target_pairs={{0,4},{4,8},{8,12},{12,16},{16,20},{20,24},{24,28},{1,5},{5,9},{9,... | collective-permute-start | bytes 61448 | tf_op jit(solution)/shard_map/ppermute | solution.py:381
  111.9 3.2 %collective-permute-done.3.below_ref = bf16[16,640]{1,0:T(8,128)(2,1)S(1)} collective-permute-done((bf16[16,640]{1,0:T(8,128)(2,1)S(1)}, bf16[16,640]{1,0:T(8,128)(2,1)S(1)}, u32[]{:S(2)}, u32[]{:S(2)}) %collective-permute-start.3) | collective-permute-done | bytes 20512 | tf_op jit(solution)/shard_map/ppermute | solution.py:382
  116.0 2.4 %conv1.1 = (f32[4,192,128]{2,1,0:T(8,128)}, bf16[4,32,640]{2,1,0:T(8,128)(2,1)}, bf16[16,640]{1,0:T(8,128)(2,1)}, bf16[16,640]{1,0:T(8,128)(2,1)}) custom-call(f32[8,4,128]{2,1,0:T(4,128)S(1)} %all-to-all-done.4.stats_ref, f32[4,32,640]{2,1,0:T(8,128)S(1)} %get-tuple-element.34.state_ref, bf16[4,32,640]{2,1,0:T(8,128)(2,1)S(1)} %copy-done.15, ...), custom_call_target="tpu_custom_call" | custom-call | flops 1073741824 | bytes 1048576 | tf_op jit(solution)/shard_map/conv1/pallas_call | solution.py:320
  118.4 15.1 %all-to-all-start.5 = ((f32[4,192,128]{2,1,0:T(8,128)}), f32[4,192,128]{2,1,0:T(8,128)S(1)}, u32[]{:S(2)}, u32[]{:S(2)}) async-start(f32[4,192,128]{2,1,0:T(8,128)} %get-tuple-element.38), calls=%async_computation.5 | async-start | bytes 786432 | tf_op jit(solution)/shard_map/all_to_all | solution.py:333
  133.5 12.1 %all-to-all-done.5.conv_ref = f32[4,192,128]{2,1,0:T(8,128)S(1)} async-done(((f32[4,192,128]{2,1,0:T(8,128)}), f32[4,192,128]{2,1,0:T(8,128)S(1)}, u32[]{:S(2)}, u32[]{:S(2)}) %all-to-all-start.5) | async-done | bytes 393248 | tf_op jit(solution)/shard_map/all_to_all | solution.py:333
  146.3 13.7 %all_to_all.35.stats_ref = f32[8,4,128]{2,1,0:T(4,128)S(1)} all-to-all(f32[8,4,128]{2,1,0:T(4,128)S(1)} %get-tuple-element.39), channel_id=1, replica_groups=mesh['req'=16,'y'=8,'zh'=2,'core'=2] {'y'}, dimensions={0} | all-to-all | bytes 32768 | tf_op jit(solution)/shard_map/all_to_all | solution.py:333
  161.4 3.5 %attend1.1 = f32[2,32,640]{2,1,0:T(8,128)} custom-call(s32[2]{0:T(128)S(1)} %pad_add_fusion.place_ref, f32[8,4,128]{2,1,0:T(4,128)S(1)} %all_to_all.35.stats_ref, f32[4,32,640]{2,1,0:T(8,128)S(1)} %get-tuple-element.40.hidden_ref, f32[1,640]{1,0:T(1,128)S(1)} %reshape.39.gain_ref, f32[1,640]{1,0:T(1,128)S(1)} %reshape.40.bias_ref, ...), custom_call_target="tpu_custom_call" | custom-call | flops 1073741824 | bytes 1048576 | tf_op jit(solution)/shard_map/attend1/pallas_call | solution.py:320
  (71 shorter events, 12.0 us)
Async XLA Ops:
  6.5 47.7 %all-gather.4.cloned.1.call-start = ((), (), s32[]{:S(2)}) async-start(), calls=%async_computation.7 | async-start | bytes 2119680 | tf_op jit(solution)/shard_map/all_gather | solution.py:363
  8.2 29.4 %copy-start.1 = (f32[2,16,640]{2,1,0:T(8,128)S(1)}, f32[2,16,640]{2,1,0:T(8,128)}, u32[]{:S(2)}) copy-start(f32[2,16,640]{2,1,0:T(8,128)} %param.14) | copy-start | bytes 245764
  12.4 38.2 %copy-start.19 = (f32[640]{0:T(1024)S(1)}, f32[640]{0:T(1024)}, u32[]{:S(2)}) copy-start(f32[640]{0:T(1024)} %param.18) | copy-start | bytes 7684
  12.4 38.2 %copy-start.20 = (f32[640]{0:T(1024)S(1)}, f32[640]{0:T(1024)}, u32[]{:S(2)}) copy-start(f32[640]{0:T(1024)} %param.19) | copy-start | bytes 7684
  12.4 25.3 %all-to-all-start = ((bf16[4,128,640]{2,1,0:T(8,128)(2,1)}), bf16[4,128,640]{2,1,0:T(8,128)(2,1)S(1)}, u32[]{:S(2)}, u32[]{:S(2)}) async-start(bf16[4,128,640]{2,1,0:T(8,128)(2,1)} %pack.1), calls=%async_computation | async-start | bytes 1310720 | tf_op jit(solution)/shard_map/all_to_all | solution.py:333
  24.3 72.1 %all-gather.6.cloned.1.call-start = ((), (), s32[]{:S(2)}) async-start(), calls=%async_computation.8 | async-start | bytes 1474560 | tf_op jit(solution)/shard_map/all_gather | solution.py:383
  39.1 15.2 %all-to-all-start.1 = ((f32[8,4,128]{2,1,0:T(4,128)}), f32[8,4,128]{2,1,0:T(4,128)S(1)}, u32[]{:S(2)}, u32[]{:S(2)}) async-start(f32[8,4,128]{2,1,0:T(4,128)} %get-tuple-element.24), calls=%async_computation.1 | async-start | bytes 32768 | tf_op jit(solution)/shard_map/all_to_all | solution.py:333
  45.9 4.7 %collective-permute-start = (bf16[16,640]{1,0:T(8,128)(2,1)S(1)}, bf16[16,640]{1,0:T(8,128)(2,1)S(1)}, u32[]{:S(2)}, u32[]{:S(2)}) collective-permute-start(bf16[16,640]{1,0:T(8,128)(2,1)S(1)} %get-tuple-element.27), channel_id=1, source_target_pairs={{0,4},{4,8},{8,12},{12,16},{16,20},{20,24},{24,28},{1,5},{5,9},{9,... | collective-permute-start | bytes 61448 | tf_op jit(solution)/shard_map/ppermute | solution.py:381
  49.3 5.0 %collective-permute-start.1 = (bf16[16,640]{1,0:T(8,128)(2,1)S(1)}, bf16[16,640]{1,0:T(8,128)(2,1)S(1)}, u32[]{:S(2)}, u32[]{:S(2)}) collective-permute-start(bf16[16,640]{1,0:T(8,128)(2,1)S(1)} %get-tuple-element.28), channel_id=1, source_target_pairs={{4,0},{8,4},{12,8},{16,12},{20,16},{24,20},{28,24},{5,1},{9,5},{13... | collective-permute-start | bytes 61448 | tf_op jit(solution)/shard_map/ppermute | solution.py:382
  55.8 15.4 %copy-start.18 = (f32[640]{0:T(1024)S(1)}, f32[640]{0:T(1024)}, u32[]{:S(2)}) copy-start(f32[640]{0:T(1024)} %param.21) | copy-start | bytes 7684
  58.2 31.4 %copy-start.16 = (bf16[640,320]{0,1:T(8,128)(2,1)S(1)}, bf16[640,320]{0,1:T(8,128)(2,1)}, u32[]{:S(2)}) copy-start(bf16[640,320]{0,1:T(8,128)(2,1)} %param.25) | copy-start | bytes 1228804
  58.2 31.7 %copy-start.21 = (f32[640]{0:T(1024)S(1)}, f32[640]{0:T(1024)}, u32[]{:S(2)}) copy-start(f32[640]{0:T(1024)} %param.23) | copy-start | bytes 7684
  58.2 31.7 %copy-start.22 = (f32[640]{0:T(1024)S(1)}, f32[640]{0:T(1024)}, u32[]{:S(2)}) copy-start(f32[640]{0:T(1024)} %param.24) | copy-start | bytes 7684
  58.2 38.2 %copy-start.11 = (bf16[320,640]{1,0:T(8,128)(2,1)S(1)}, bf16[320,640]{1,0:T(8,128)(2,1)}, u32[]{:S(2)}) copy-start(bf16[320,640]{1,0:T(8,128)(2,1)} %out_ref.3) | copy-start | bytes 1228804
  58.2 23.3 %all-to-all-start.2 = ((f32[4,192,128]{2,1,0:T(8,128)}), f32[4,192,128]{2,1,0:T(8,128)S(1)}, u32[]{:S(2)}, u32[]{:S(2)}) async-start(f32[4,192,128]{2,1,0:T(8,128)} %get-tuple-element.29), calls=%async_computation.2 | async-start | bytes 786432 | tf_op jit(solution)/shard_map/all_to_all | solution.py:333
  82.8 13.6 %all-to-all-start.3 = ((f32[8,4,128]{2,1,0:T(4,128)}), f32[8,4,128]{2,1,0:T(4,128)S(1)}, u32[]{:S(2)}, u32[]{:S(2)}) async-start(f32[8,4,128]{2,1,0:T(4,128)} %get-tuple-element.30), calls=%async_computation.3 | async-start | bytes 32768 | tf_op jit(solution)/shard_map/all_to_all | solution.py:333
  89.5 70.5 %all-gather.8.cloned.1.call-start = ((), (), s32[]{:S(2)}) async-start(), calls=%async_computation.9 | async-start | bytes 1474560 | tf_op jit(solution)/shard_map/all_gather | solution.py:383
  98.9 16.2 %copy-start.6 = (bf16[8,180,640]{2,1,0:T(8,128)(2,1)S(1)}, bf16[8,180,640]{2,1,0:T(8,128)(2,1)}, u32[]{:S(2)}) copy-start(bf16[8,180,640]{2,1,0:T(8,128)(2,1)} %all-gather.4.cloned.1.call-done.weight_ref) | copy-start | bytes 5529604
  103.7 11.3 %all-to-all-start.4 = ((f32[8,4,128]{2,1,0:T(4,128)}), f32[8,4,128]{2,1,0:T(4,128)S(1)}, u32[]{:S(2)}, u32[]{:S(2)}) async-start(f32[8,4,128]{2,1,0:T(4,128)} %get-tuple-element.33), calls=%async_computation.4 | async-start | bytes 32768 | tf_op jit(solution)/shard_map/all_to_all | solution.py:333
  107.2 4.7 %collective-permute-start.2 = (bf16[16,640]{1,0:T(8,128)(2,1)S(1)}, bf16[16,640]{1,0:T(8,128)(2,1)S(1)}, u32[]{:S(2)}, u32[]{:S(2)}) collective-permute-start(bf16[16,640]{1,0:T(8,128)(2,1)S(1)} %get-tuple-element.36), channel_id=1, source_target_pairs={{0,4},{4,8},{8,12},{12,16},{16,20},{20,24},{24,28},{1,5},{5,9},{9,... | collective-permute-start | bytes 61448 | tf_op jit(solution)/shard_map/ppermute | solution.py:381
  110.5 4.5 %collective-permute-start.3 = (bf16[16,640]{1,0:T(8,128)(2,1)S(1)}, bf16[16,640]{1,0:T(8,128)(2,1)S(1)}, u32[]{:S(2)}, u32[]{:S(2)}) collective-permute-start(bf16[16,640]{1,0:T(8,128)(2,1)S(1)} %get-tuple-element.37), channel_id=1, source_target_pairs={{4,0},{8,4},{12,8},{16,12},{20,16},{24,20},{28,24},{5,1},{9,5},{13... | collective-permute-start | bytes 61448 | tf_op jit(solution)/shard_map/ppermute | solution.py:382
  118.4 41.7 %copy-start.10 = (bf16[640,640]{1,0:T(8,128)(2,1)S(1)}, bf16[640,640]{1,0:T(8,128)(2,1)}, u32[]{:S(2)}) copy-start(bf16[640,640]{1,0:T(8,128)(2,1)} %keyvalue_ref.3) | copy-start | bytes 2457604
  118.4 41.7 %copy-start.13 = (f32[32,640]{1,0:T(8,128)S(1)}, f32[32,640]{1,0:T(8,128)}, u32[]{:S(2)}) copy-start(f32[32,640]{1,0:T(8,128)} %copy-done.12) | copy-start | bytes 245764
  118.4 27.2 %all-to-all-start.5 = ((f32[4,192,128]{2,1,0:T(8,128)}), f32[4,192,128]{2,1,0:T(8,128)S(1)}, u32[]{:S(2)}, u32[]{:S(2)}) async-start(f32[4,192,128]{2,1,0:T(8,128)} %get-tuple-element.38), calls=%async_computation.5 | async-start | bytes 786432 | tf_op jit(solution)/shard_map/all_to_all | solution.py:333
  (12 other events, 38.4 us)
Sparse Core Ops, SparseCore 0:
  9.4 44.3 all-gather.3
  55.9 40.4 all-gather.5
  103.9 39.7 all-gather.7

commit v3 on v2

--- a/solution.py
+++ b/solution.py
@@ -71,7 +71,10 @@
 
 
 def mean_and_scale(stats_ref, groups):
-    sums = jnp.sum(stats_ref[...], axis=0)
+    return spread_sums(jnp.sum(stats_ref[...], axis=0), groups)
+
+
+def spread_sums(sums, groups):
     number = POSITIONS * MEMBERS
     mean = sums[0:1] * (1.0 / number)
     variance = sums[1:2] * (1.0 / number) - mean * mean
@@ -113,34 +116,19 @@
     tell_sums(state_ref[...].reshape(QUAD_ROWS, CHANNELS), group_matrix(), stats_ref)
 
 
-def conv_kernel(
-    stats_ref,
-    state_ref,
-    prior_ref,
-    above_ref,
-    below_ref,
-    weight_ref,
-    gain_ref,
-    bias_ref,
-    out_ref,
-    act_ref,
-    first_ref,
-    last_ref,
-    rows,
-    wide,
-):
+def activate(stats_ref, state_ref, prior_ref, above_ref, below_ref, gain_ref, bias_ref, keep, rows):
     mean, scale = mean_and_scale(stats_ref, group_matrix())
     for t in range(4):
         value = (state_ref[t] - mean) * scale * gain_ref[...] + bias_ref[...]
-        act_ref[t] = (value * (1.0 / (1.0 + jnp.exp(-value)))).astype(BF16)
-    first_ref[...] = act_ref[0, :COLS]
-    last_ref[...] = act_ref[3, COLS:]
-    for t in range(4):
+        act = (value * (1.0 / (1.0 + jnp.exp(-value)))).astype(BF16)
+        rows[t, COLS : 3 * COLS] = act
+        keep(t, act)
         rows[t, 0:COLS] = above_ref[...] if t == 0 else prior_ref[t - 1, COLS:]
-        rows[t, COLS : 3 * COLS] = act_ref[t]
         rows[t, 3 * COLS :] = below_ref[...] if t == 3 else prior_ref[t + 1, :COLS]
+
+
+def convolve(rows, weight_ref, wide):
     window = rows[...].reshape(4 * 64, CHANNELS)
-
     wide[...] = jnp.zeros(wide.shape, F32)
     col = lax.broadcasted_iota(jnp.int32, (LANES, LANES), 0) & (COLS - 1)
     lane = lax.broadcasted_iota(jnp.int32, (LANES, LANES), 1)
@@ -167,21 +155,114 @@
             made = pltpu.roll(made, at, 1)
         kept = (lane >= at) & (lane < at + MEMBERS)
         tiles[tile] = jnp.where(kept, made, tiles[tile])
-    rest = jnp.where(
-        lane[:64] < 64, tiles[1][:64], pltpu.roll(tiles[1][64:], 64, 1)
-    )
+    return tiles
+
+
+def folded(tile):
+    half = tile.shape[0] // 2
+    lane = lax.broadcasted_iota(jnp.int32, (half, LANES), 1)
+    return jnp.where(lane < 64, tile[:half], pltpu.roll(tile[half:], 64, 1))
+
+
+def conv_quad_kernel(
+    stats_ref,
+    state_ref,
+    prior_ref,
+    above_ref,
+    below_ref,
+    weight_ref,
+    gain_ref,
+    bias_ref,
+    out_ref,
+    act_ref,
+    first_ref,
+    last_ref,
+    rows,
+    wide,
+):
+    def keep(t, act):
+        act_ref[t] = act
+        if t == 0:
+            first_ref[...] = act[:COLS]
+        if t == 3:
+            last_ref[...] = act[COLS:]
+
+    activate(stats_ref, state_ref, prior_ref, above_ref, below_ref, gain_ref, bias_ref, keep, rows)
+    tiles = convolve(rows, weight_ref, wide)
+    rest = folded(tiles[1])
     for to in range(4):
         out_ref[to, 0:LANES] = tiles[0]
         out_ref[to, LANES:] = rest
 
 
-def hidden_kernel(conv_ref, state_ref, shift_ref, hidden_ref, stats_ref):
-    lane = lax.broadcasted_iota(jnp.int32, (LANES, LANES), 1)
-    tiles = [jnp.zeros((LANES, LANES), F32) for _ in range(5)]
+def shard_lanes(shape, dim):
+    lane = lax.broadcasted_iota(jnp.int32, shape, dim)
+    inner = lane & (LANES - 1)
+    part = (inner * 3277) >> 16
+    within = inner - MEMBERS * part
+    second = lane >= LANES
+    used = part < jnp.where(second, 2, 6)
+    return part + jnp.where(second, 6, 0), within, used
+
+
+def conv_own_kernel(
+    place_ref,
+    stats_ref,
+    state_ref,
+    prior_ref,
+    above_ref,
+    below_ref,
+    weight_ref,
+    gain_ref,
+    bias_ref,
+    shift_ref,
+    out_ref,
+    told_ref,
+    rows,
+    wide,
+):
+    a = place_ref[1]
+    activate(
+        stats_ref, state_ref, prior_ref, above_ref, below_ref, gain_ref, bias_ref, lambda t, act: None, rows
+    )
+    tiles = convolve(rows, weight_ref, wide)
     for t in range(4):
-        rest = conv_ref[t, LANES:]
+        mine = slice(t * ROWS, (t + 1) * ROWS)
+        out_ref[t, 0:ROWS] = tiles[0][mine]
+        out_ref[t, ROWS:] = folded(tiles[1][mine])
+    part, within, used = shard_lanes((CHANNELS, 256), 1)
+    channel = lax.broadcasted_iota(jnp.int32, (CHANNELS, 256), 0)
+    select = used & (channel == 4 * MEMBERS * part + MEMBERS * a + within)
+    select = jnp.where(select, 1.0, 0.0).astype(BF16)
+    part, _, used = shard_lanes((LANES, 256), 1)
+    group = lax.broadcasted_iota(jnp.int32, (LANES, 256), 0)
+    holds = jnp.where(used & (group == 4 * part + a), 1.0, 0.0).astype(BF16)
+    state = state_ref[...].reshape(QUAD_ROWS, CHANNELS)
+    hidden = picked(state, select) + (
+        jnp.concatenate(tiles, axis=1) + picked(eight([shift_ref[...]], CHANNELS), select)[0:1]
+    )
+    sums = eight(
+        [jnp.sum(hidden, axis=0, keepdims=True), jnp.sum(hidden * hidden, axis=0, keepdims=True)],
+        256,
+    )
+    told = picked(sums, holds, NT)[0:4]
+    told_ref[...] = jnp.broadcast_to(told[None], told_ref.shape)
+
+
+def insert_kernel(conv_ref, stats_ref, out_ref):
+    sums = jnp.sum(stats_ref[...], axis=0)
+    for to in range(4):
+        out_ref[to, 0:48] = conv_ref[to]
+        out_ref[to, 48:] = eight([sums], LANES)
+
+
+def assembled(conv_ref, count):
+    lane = lax.broadcasted_iota(jnp.int32, (count, LANES), 1)
+    tiles = [jnp.zeros((count, LANES), F32) for _ in range(5)]
+    for t in range(4):
+        rest = conv_ref[t, count : count + count // 2]
         sources = (
-            conv_ref[t, 0:LANES],
+            conv_ref[t, 0:count],
             jnp.concatenate([rest, pltpu.roll(rest, 64, 1)], axis=0),
         )
         for part in range(8):
@@ -197,18 +278,37 @@
             if to + MEMBERS > LANES:
                 kept = lane < to + MEMBERS - LANES
                 tiles[tile + 1] = jnp.where(kept, block, tiles[tile + 1])
+    return jnp.concatenate(tiles, axis=1)
+
+
+def hidden_kernel(conv_ref, state_ref, shift_ref, hidden_ref, stats_ref):
     state = state_ref[...].reshape(QUAD_ROWS, CHANNELS)
-    hidden = state + (jnp.concatenate(tiles, axis=1) + shift_ref[...])
+    hidden = state + (assembled(conv_ref, QUAD_ROWS) + shift_ref[...])
     hidden_ref[...] = hidden.reshape(hidden_ref.shape)
     tell_sums(hidden, group_matrix(), stats_ref)
 
 
-def attend(hidden, patch, y, mean, scale, gain, bias, w_query, w_keyvalue, w_out, kv_ref):
-    count = hidden.shape[0]
-    normed = ((hidden - mean) * scale * gain + bias).astype(BF16)
-    query = dot(normed, w_query)
-    fresh = dot(normed, w_keyvalue).astype(BF16)
-    query = jnp.concatenate([query, jnp.zeros((count, 3 * LANES - WIDTH), F32)], axis=1)
+def project(hidden, mean, scale, gain_ref, bias_ref, query_ref, keyvalue_ref):
+    normed = ((hidden - mean) * scale * gain_ref[...] + bias_ref[...]).astype(BF16)
+    query = dot(normed, query_ref[...]).astype(BF16).astype(F32)
+    query = jnp.concatenate(
+        [query, jnp.zeros((hidden.shape[0], 3 * LANES - WIDTH), F32)], axis=1
+    )
+    return query.astype(BF16), dot(normed, keyvalue_ref[...]).astype(BF16)
+
+
+def project_kernel(
+    stats_ref, hidden_ref, gain_ref, bias_ref, query_ref, keyvalue_ref, asked_ref, fresh_ref
+):
+    mean, scale = mean_and_scale(stats_ref, group_matrix())
+    hidden = hidden_ref[...].reshape(QUAD_ROWS, CHANNELS)
+    asked, fresh = project(hidden, mean, scale, gain_ref, bias_ref, query_ref, keyvalue_ref)
+    asked_ref[...] = asked
+    fresh_ref[...] = fresh
+
+
+def attend(query, fresh, patch, y, kv_ref):
+    count = query.shape[0]
     lane = lax.broadcasted_iota(jnp.int32, (count, LANES), 1)
     low = lane < HEAD_DIM
 
@@ -222,7 +322,7 @@
     for h in range(HEADS):
         at = LANES * (h // 2)
         own = low if h % 2 == 0 else ~low
-        asked = jnp.where(own, query[:, at : at + LANES], 0.0).astype(BF16)
+        asked = jnp.where(own, query[:, at : at + LANES].astype(F32), 0.0).astype(BF16)
         old = dot(asked, kv_ref[:, at : at + LANES], NT) * HEAD_DIM ** (-0.5)
         old = jnp.where(replaced, -jnp.inf, old)
         new = dot(asked, fresh[:, at : at + LANES], NT) * HEAD_DIM ** (-0.5)
@@ -239,77 +339,43 @@
         summed += dot(new.astype(BF16), fresh[:, at : at + LANES])
         summed = pltpu.roll(summed / total, HEAD_DIM, 1)
         tiles[h // 2] = jnp.where(own, summed, tiles[h // 2])
-    attended = jnp.concatenate(tiles, axis=1)[:, :WIDTH].astype(BF16)
-    return hidden + dot(attended, w_out), fresh
+    return jnp.concatenate(tiles, axis=1)[:, :WIDTH].astype(BF16)
 
 
 def attend_quad_kernel(
+    place_ref, asked_ref, fresh_ref, hidden_ref, out_ref, kv_ref, state_ref, told_ref
+):
+    patch = lax.broadcasted_iota(jnp.int32, (QUAD_ROWS, 1), 0) >> 5
+    attended = attend(asked_ref[...], fresh_ref[...], patch, place_ref[0], kv_ref)
+    result = hidden_ref[...].reshape(QUAD_ROWS, CHANNELS) + dot(attended, out_ref[...])
+    state_ref[...] = result.reshape(state_ref.shape)
+    tell_sums(result, group_matrix(), told_ref)
+
+
+def attend_own_kernel(
     place_ref,
-    stats_ref,
-    hidden_ref,
+    conv_ref,
+    state_ref,
+    shift_ref,
     gain_ref,
     bias_ref,
     query_ref,
     keyvalue_ref,
     out_ref,
     kv_ref,
-    state_ref,
     result_ref,
-    told_ref,
-    fresh_ref,
-):
-    groups = group_matrix()
-    mean, scale = mean_and_scale(stats_ref, groups)
-    patch = lax.broadcasted_iota(jnp.int32, (QUAD_ROWS, 1), 0) >> 5
-    result, fresh = attend(
-        hidden_ref[...].reshape(QUAD_ROWS, CHANNELS),
-        patch,
-        place_ref[0],
-        mean,
-        scale,
-        gain_ref[...],
-        bias_ref[...],
-        query_ref[...],
-        keyvalue_ref[...],
-        out_ref[...],
-        kv_ref,
-    )
-    state_ref[...] = result.reshape(state_ref.shape)
-    result_ref[...] = state_ref[place_ref[1]]
-    fresh_ref[...] = fresh
-    tell_sums(result, groups, told_ref)
-
-
-def attend_own_kernel(
-    place_ref,
-    stats_ref,
-    hidden_ref,
-    gain_ref,
-    bias_ref,
-    query_ref,
-    keyvalue_ref,
-    out_ref,
-    kv_ref,
-    earlier_ref,
-    result_ref,
-):
-    mean, scale = mean_and_scale(stats_ref, group_matrix())
+):
     a = place_ref[1]
-    result, _ = attend(
-        hidden_ref[a],
-        a,
-        place_ref[0],
-        mean,
-        scale,
-        gain_ref[...],
-        bias_ref[...],
-        query_ref[...],
-        keyvalue_ref[...],
-        out_ref[...],
-        kv_ref,
-    )
-    result_ref[0] = earlier_ref[...]
-    result_ref[1] = result
+    earlier = state_ref[a]
+    hidden = earlier + (assembled(conv_ref, ROWS) + shift_ref[...])
+    sums = jnp.zeros((8, LANES), F32)
+    for t in range(4):
+        sums += conv_ref[t, 48:56]
+    mean, scale = spread_sums(sums, group_matrix())
+    query, fresh = project(hidden, mean, scale, gain_ref, bias_ref, query_ref, keyvalue_ref)
+    attended = attend(query, fresh, a, place_ref[0], kv_ref)
+    result_ref[0] = earlier
+    result_ref[1] = hidden + dot(attended, out_ref[...])
 
 
 VMEM = pl.BlockSpec(memory_space=pltpu.VMEM)
@@ -325,7 +391,7 @@
         out_specs=[VMEM] * len(out_shapes),
         scratch_shapes=list(scratch),
         cost_estimate=pl.CostEstimate(flops=flops, bytes_accessed=1 << 20, transcendentals=0),
-        compiler_params=pltpu.CompilerParams(vmem_limit_bytes=48 << 20),
+        compiler_params=pltpu.CompilerParams(vmem_limit_bytes=20 << 20),
     )(*args)
 
 
@@ -376,55 +442,76 @@
         (place, to_all(packed, QUAD), own),
         scalars=1,
     )
-    for step in range(2):
-        stats = to_all(stats, "y")
-        above = lax.ppermute(last, "y", up)
-        below = lax.ppermute(first, "y", down)
-        kv = lax.all_gather(kv.reshape(QUAD_ROWS, CHANNELS), "y", axis=0, tiled=True)
-        conv, prior, first, last = call(
-            conv_kernel,
-            f"conv{step}",
-            [((4, LANES + 64, LANES), F32), (quad, BF16), (line, BF16), (line, BF16)],
-            (stats, state, prior, above, below, weights, row(norm1_gain), row(norm1_bias)),
-            scratch=[pltpu.VMEM((4, 64, CHANNELS), BF16), pltpu.VMEM((256, 256), F32)],
-            flops=1 << 30,
-        )
-        hidden, stats = call(
-            hidden_kernel,
-            f"hidden{step}",
-            [(quad, F32), stats8],
-            (to_all(conv, QUAD), state, row(conv_bias + time_embed[step])),
-            flops=1 << 28,
-        )
-        common = (
-            place,
-            to_all(stats, "y"),
-            hidden,
-            row(norm2_gain),
-            row(norm2_bias),
-            w_query,
-            w_keyvalue,
-            w_out,
-            kv,
-        )
-        if step == 1:
-            (out,) = call(
-                attend_own_kernel,
-                "attend1",
-                [((2, ROWS, CHANNELS), F32)],
-                (*common, earlier),
-                scalars=1,
-                flops=1 << 30,
-            )
-            return out.reshape(2, 2, COLS, CHANNELS)
-        state, earlier, stats, kv = call(
-            attend_quad_kernel,
-            "attend0",
-            [(quad, F32), ((ROWS, CHANNELS), F32), stats8, ((QUAD_ROWS, CHANNELS), BF16)],
-            common,
-            scalars=1,
-            flops=1 << 30,
-        )
+    norm1 = (row(norm1_gain), row(norm1_bias))
+    norm2 = (row(norm2_gain), row(norm2_bias))
+    buffers = [pltpu.VMEM((4, 64, CHANNELS), BF16), pltpu.VMEM((256, 256), F32)]
+    gathered = lambda v: lax.all_gather(
+        v.reshape(QUAD_ROWS, CHANNELS), "y", axis=0, tiled=True
+    )
+    above = lax.ppermute(last, "y", up)
+    below = lax.ppermute(first, "y", down)
+    old = gathered(kv)
+
+    conv, prior, first, last = call(
+        conv_quad_kernel,
+        "conv0",
+        [((4, LANES + 64, LANES), F32), (quad, BF16), (line, BF16), (line, BF16)],
+        (to_all(stats, "y"), state, prior, above, below, weights, *norm1),
+        scratch=buffers,
+        flops=1 << 30,
+    )
+    conv, above, below = lax.optimization_barrier(
+        (to_all(conv, QUAD), lax.ppermute(last, "y", up), lax.ppermute(first, "y", down))
+    )
+    hidden, stats = call(
+        hidden_kernel,
+        "hidden0",
+        [(quad, F32), stats8],
+        (conv, state, row(conv_bias + time_embed[0])),
+        flops=1 << 28,
+    )
+    asked, fresh = call(
+        project_kernel,
+        "project0",
+        [((QUAD_ROWS, 3 * LANES), BF16), ((QUAD_ROWS, CHANNELS), BF16)],
+        (to_all(stats, "y"), hidden, *norm2, w_query, w_keyvalue),
+        flops=1 << 28,
+    )
+    kv = gathered(fresh)
+    state, stats = call(
+        attend_quad_kernel,
+        "attend0",
+        [(quad, F32), stats8],
+        (place, asked, fresh, hidden, w_out, old),
+        scalars=1,
+        flops=1 << 30,
+    )
+    shift = row(conv_bias + time_embed[1])
+    conv, stats = call(
+        conv_own_kernel,
+        "conv1",
+        [((4, ROWS + ROWS // 2, LANES), F32), stats8],
+        (place, to_all(stats, "y"), state, prior, above, below, weights, *norm1, shift),
+        scalars=1,
+        scratch=buffers,
+        flops=1 << 30,
+    )
+    (conv,) = call(
+        insert_kernel,
+        "insert1",
+        [((4, 56, LANES), F32)],
+        (conv, to_all(stats, "y")),
+        flops=1 << 24,
+    )
+    (out,) = call(
+        attend_own_kernel,
+        "attend1",
+        [((2, ROWS, CHANNELS), F32)],
+        (place, to_all(conv, QUAD), state, shift, *norm2, w_query, w_keyvalue, w_out, kv),
+        scalars=1,
+        flops=1 << 30,
+    )
+    return out.reshape(2, 2, COLS, CHANNELS)
 
 
 def solution(mesh):

time: 174 us -> 160 us (0.920)
  blocking collectives: 13.7 us -> 30.5 us
  starting transfers between devices: 66.2 us -> 50.7 us
  waiting for transfers between devices: 49.1 us -> 35.8 us
    all_to_all x1 -> x2, blocking collectives: 13.7 us -> 30.5 us  [to_all(): return lax.all_to_all(value, axes, 0, 0, tiled=True)]
    all_to_all x6 -> x5, starting transfers between devices: 56.9 us -> 41.6 us  [to_all(): return lax.all_to_all(value, axes, 0, 0, tiled=True)]
    all_to_all x6 -> x5, waiting for transfers between devices: 35.6 us -> 27.7 us  [to_all(): return lax.all_to_all(value, axes, 0, 0, tiled=True)]
    all_gather x2, waiting for transfers between devices: 6.52 us -> 0.02 us  [per_device(): lax.all_gather(v.reshape(QUAD_ROWS, CHANNELS), 'y', axis=0, tiled=True)]
    ppermute x0 -> x2, waiting for transfers between devices: none -> 4.42 us  [the longest x1 4.42 us: per_device(): lax.ppermute(first, 'y', down)]
    ppermute x0 -> x2, starting transfers between devices: none -> 4.38 us  [the longest x1 3.09 us: per_device(): lax.ppermute(last, 'y', up)]
    ppermute x2 -> x1, starting transfers between devices: 6.71 us -> 3.35 us  [per_device(): above = lax.ppermute(last, 'y', up)]
    ppermute x2 -> x1, waiting for transfers between devices: 6.83 us -> 3.66 us  [per_device(): below = lax.ppermute(first, 'y', down)]
  transfers between devices with their start and end apart: 13 -> 12, of which waited for: 6 -> 6; matrix products, arithmetic and copies ran while one was open for 0% -> 0% of each run, Pallas kernels for 5% -> 9%
where the time goes in v3:
time: 160 us; the launch traced here: 159 us
  starting transfers between devices  50.7 us (32%)
  waiting for transfers between devices  35.8 us (22%)
  blocking collectives  30.5 us (19%)
  Pallas kernels  17.4 us (11%)
  between operations  13.3 us (8%)
  local copies, waits for them, and re-layouts  10.9 us (7%)
    all_to_all x5, starting transfers between devices, to_all(): return lax.all_to_all(value, axes, 0, 0, tiled=True)  41.6 us
    all_to_all x2, blocking collectives, to_all(): return lax.all_to_all(value, axes, 0, 0, tiled=True)  30.5 us
    all_to_all x5, waiting for transfers between devices, to_all(): return lax.all_to_all(value, axes, 0, 0, tiled=True)  27.7 us
    pallas_call x9, Pallas kernels, call(): pl.pallas_call(kernel, name=name, out_shape=[jax.ShapeDtypeStruct(s, t) f...  17.4 us
    unnamed x37, local copies, waits for them, and re-layouts  9.15 us
    ppermute x1, waiting for transfers between devices, per_device(): lax.ppermute(first, 'y', down)  4.42 us
    ppermute x1, waiting for transfers between devices, per_device(): below = lax.ppermute(first, 'y', down)  3.66 us
    ppermute x1, starting transfers between devices, per_device(): above = lax.ppermute(last, 'y', up)  3.35 us
  transfers between devices with their start and end apart: 12, of which 6 were waited for; matrix products, arithmetic and copies ran while one was open for 0% of the time, Pallas kernels for 9%

profile of v3, /device:TPU:1, one launch (start us, length us, event | category | flops | bytes accessed | tf_op | source)
XLA Modules:
  0.0 158.7 jit_solution(10888212744681151109)
XLA Ops:
  6.5 1.7 %all_gather_reshape.3 = bf16[1,180,640]{2,1,0:T(8,128)(2,1)} reshape(bf16[3,3,20,640]{3,2,1,0:T(8,128)(2,1)} %bitcast.10) | data formatting | bytes 460800 | tf_op jit(solution)/shard_map/all_gather;reshape | solution.py:429
  12.4 11.9 %all-to-all-start = ((bf16[4,128,640]{2,1,0:T(8,128)(2,1)}), bf16[4,128,640]{2,1,0:T(8,128)(2,1)S(1)}, u32[]{:S(2)}, u32[]{:S(2)}) async-start(bf16[4,128,640]{2,1,0:T(8,128)(2,1)} %pack.1), calls=%async_computation | async-start | bytes 1310720 | tf_op jit(solution)/shard_map/all_to_all | solution.py:399
  24.4 13.3 %all-to-all-done.packed_ref = bf16[4,128,640]{2,1,0:T(8,128)(2,1)S(1)} async-done(((bf16[4,128,640]{2,1,0:T(8,128)(2,1)}), bf16[4,128,640]{2,1,0:T(8,128)(2,1)S(1)}, u32[]{:S(2)}, u32[]{:S(2)}) %all-to-all-start) | async-done | bytes 655392 | tf_op jit(solution)/shard_map/all_to_all | solution.py:399
  37.7 1.4 unpack.1
  39.1 6.8 %all-to-all-start.1 = ((f32[8,4,128]{2,1,0:T(4,128)}), f32[8,4,128]{2,1,0:T(4,128)S(1)}, u32[]{:S(2)}, u32[]{:S(2)}) async-start(f32[8,4,128]{2,1,0:T(4,128)} %get-tuple-element.26), calls=%async_computation.1 | async-start | bytes 32768 | tf_op jit(solution)/shard_map/all_to_all | solution.py:399
  45.9 3.4 %collective-permute-start = (bf16[16,640]{1,0:T(8,128)(2,1)S(1)}, bf16[16,640]{1,0:T(8,128)(2,1)S(1)}, u32[]{:S(2)}, u32[]{:S(2)}) collective-permute-start(bf16[16,640]{1,0:T(8,128)(2,1)S(1)} %get-tuple-element.29), channel_id=1, source_target_pairs={{0,4},{4,8},{8,12},{12,16},{16,20},{20,24},{24,28},{1,5},{5,9},{9,... | collective-permute-start | bytes 61448 | tf_op jit(solution)/shard_map/ppermute | solution.py:451
  50.7 3.7 %collective-permute-done.1.below_ref = bf16[16,640]{1,0:T(8,128)(2,1)S(1)} collective-permute-done((bf16[16,640]{1,0:T(8,128)(2,1)S(1)}, bf16[16,640]{1,0:T(8,128)(2,1)S(1)}, u32[]{:S(2)}, u32[]{:S(2)}) %collective-permute-start.1) | collective-permute-done | bytes 20512 | tf_op jit(solution)/shard_map/ppermute | solution.py:452
  54.3 1.5 copy-done.6
  55.8 2.4 %conv0.1 = (f32[4,192,128]{2,1,0:T(8,128)}, bf16[4,32,640]{2,1,0:T(8,128)(2,1)S(1)}, bf16[16,640]{1,0:T(8,128)(2,1)S(1)}, bf16[16,640]{1,0:T(8,128)(2,1)S(1)}) custom-call(f32[8,4,128]{2,1,0:T(4,128)S(1)} %all-to-all-done.1.stats_ref, f32[4,32,640]{2,1,0:T(8,128)S(1)} %get-tuple-element.27.state_ref, bf16[4,32,640]{2,1,0:T(8,128)(2,1)S(1)} %get-tuple-element.28.prior_ref, ...), custom_call_target="tpu_custom_call" | custom-call | flops 1073741824 | bytes 1048576 | tf_op jit(solution)/shard_map/conv0/pallas_call | solution.py:386
  58.3 12.9 %all-to-all-start.2 = ((f32[4,192,128]{2,1,0:T(8,128)}), f32[4,192,128]{2,1,0:T(8,128)S(1)}, u32[]{:S(2)}, u32[]{:S(2)}) async-start(f32[4,192,128]{2,1,0:T(8,128)} %get-tuple-element.31), calls=%async_computation.2 | async-start | bytes 786432 | tf_op jit(solution)/shard_map/all_to_all | solution.py:399
  71.2 3.1 %collective-permute-start.2 = (bf16[16,640]{1,0:T(8,128)(2,1)S(1)}, bf16[16,640]{1,0:T(8,128)(2,1)S(1)}, u32[]{:S(2)}, u32[]{:S(2)}) collective-permute-start(bf16[16,640]{1,0:T(8,128)(2,1)S(1)} %get-tuple-element.32), channel_id=1, source_target_pairs={{0,4},{4,8},{8,12},{12,16},{16,20},{20,24},{24,28},{1,5},{5,9},{9,... | collective-permute-start | bytes 61448 | tf_op jit(solution)/shard_map/ppermute | solution.py:464
  75.6 4.4 %collective-permute-done.3.below_ref = bf16[16,640]{1,0:T(8,128)(2,1)S(1)} collective-permute-done((bf16[16,640]{1,0:T(8,128)(2,1)S(1)}, bf16[16,640]{1,0:T(8,128)(2,1)S(1)}, u32[]{:S(2)}, u32[]{:S(2)}) %collective-permute-start.3) | collective-permute-done | bytes 20512 | tf_op jit(solution)/shard_map/ppermute | solution.py:464
  80.0 1.5 all-to-all-done.2.conv_ref
  81.5 1.4 hidden0.1
  82.9 6.7 %all-to-all-start.3 = ((f32[8,4,128]{2,1,0:T(4,128)}), f32[8,4,128]{2,1,0:T(4,128)S(1)}, u32[]{:S(2)}, u32[]{:S(2)}) async-start(f32[8,4,128]{2,1,0:T(4,128)} %get-tuple-element.35), calls=%async_computation.3 | async-start | bytes 32768 | tf_op jit(solution)/shard_map/all_to_all | solution.py:399
  89.9 6.4 %all-to-all-done.3.stats_ref = f32[8,4,128]{2,1,0:T(4,128)S(1)} async-done(((f32[8,4,128]{2,1,0:T(4,128)}), f32[8,4,128]{2,1,0:T(4,128)S(1)}, u32[]{:S(2)}, u32[]{:S(2)}) %all-to-all-start.3) | async-done | bytes 16416 | tf_op jit(solution)/shard_map/all_to_all | solution.py:399
  99.0 4.2 %attend0.1 = (f32[4,32,640]{2,1,0:T(8,128)S(1)}, f32[8,4,128]{2,1,0:T(4,128)}) custom-call(s32[2]{0:T(128)S(1)} %pad_add_fusion.place_ref, bf16[128,384]{1,0:T(8,128)(2,1)S(1)} %get-tuple-element.37.asked_ref, bf16[128,640]{1,0:T(8,128)(2,1)} %get-tuple-element.38.fresh_ref, f32[4,32,640]{2,1,0:T(8,128)S(1)} %get-tuple-element.36.hidden_ref, ...), custom_call_target="tpu_custom_call" | custom-call | flops 1073741824 | bytes 1048576 | tf_op jit(solution)/shard_map/attend0/pallas_call | solution.py:386
  103.1 3.3 %all-to-all-start.4 = ((f32[8,4,128]{2,1,0:T(4,128)}), f32[8,4,128]{2,1,0:T(4,128)S(1)}, u32[]{:S(2)}, u32[]{:S(2)}) async-start(f32[8,4,128]{2,1,0:T(4,128)} %get-tuple-element.40), calls=%async_computation.4 | async-start | bytes 32768 | tf_op jit(solution)/shard_map/all_to_all | solution.py:399
  106.5 6.5 %all-to-all-done.4.stats_ref = f32[8,4,128]{2,1,0:T(4,128)S(1)} async-done(((f32[8,4,128]{2,1,0:T(4,128)}), f32[8,4,128]{2,1,0:T(4,128)S(1)}, u32[]{:S(2)}, u32[]{:S(2)}) %all-to-all-start.4) | async-done | bytes 16416 | tf_op jit(solution)/shard_map/all_to_all | solution.py:399
  113.0 1.5 copy-done.7
  114.5 2.3 %conv1.1 = (f32[4,48,128]{2,1,0:T(8,128)S(1)}, f32[8,4,128]{2,1,0:T(4,128)S(1)}) custom-call(s32[2]{0:T(128)S(1)} %pad_add_fusion.place_ref, f32[8,4,128]{2,1,0:T(4,128)S(1)} %all-to-all-done.4.stats_ref, f32[4,32,640]{2,1,0:T(8,128)S(1)} %get-tuple-element.41.state_ref, bf16[4,32,640]{2,1,0:T(8,128)(2,1)S(1)} %get-tuple-element.42.prior_ref, ...), custom_call_target="tpu_custom_call" | custom-call | flops 1073741824 | bytes 1048576 | tf_op jit(solution)/shard_map/conv1/pallas_call | solution.py:386
  116.8 9.2 %all_to_all.35.stats_ref = f32[8,4,128]{2,1,0:T(4,128)S(1)} all-to-all(f32[8,4,128]{2,1,0:T(4,128)S(1)} %get-tuple-element.46), channel_id=1, replica_groups=mesh['req'=16,'y'=8,'zh'=2,'core'=2] {'y'}, dimensions={0} | all-to-all | bytes 32768 | tf_op jit(solution)/shard_map/all_to_all | solution.py:399
  126.0 21.3 %all_to_all.36.conv_ref = f32[4,56,128]{2,1,0:T(8,128)S(1)} all-to-all(f32[4,56,128]{2,1,0:T(8,128)S(1)} %insert1.1), channel_id=1, replica_groups=mesh['req'=16,'y'=8,'zh'=2,'core'=2] {'zh','core'}, dimensions={0} | all-to-all | bytes 229376 | tf_op jit(solution)/shard_map/all_to_all | solution.py:399
  148.7 3.5 %attend1.1 = f32[2,32,640]{2,1,0:T(8,128)} custom-call(s32[2]{0:T(128)S(1)} %pad_add_fusion.place_ref, f32[4,56,128]{2,1,0:T(8,128)S(1)} %all_to_all.36.conv_ref, f32[4,32,640]{2,1,0:T(8,128)S(1)} %get-tuple-element.41.state_ref, f32[1,640]{1,0:T(1,128)S(1)} %reshape.38.shift_ref, f32[1,640]{1,0:T(1,128)S(1)} %reshape.35.gain_ref, ...), custom_call_target="tpu_custom_call" | custom-call | flops 1073741824 | bytes 1048576 | tf_op jit(solution)/shard_map/attend1/pallas_call | solution.py:386
  (61 shorter events, 11.1 us)
Async XLA Ops:
  6.5 47.8 %all-gather.4.cloned.1.call-start = ((), (), s32[]{:S(2)}) async-start(), calls=%async_computation.7 | async-start | bytes 2119680 | tf_op jit(solution)/shard_map/all_gather | solution.py:429
  8.3 29.4 %copy-start.2 = (f32[2,16,640]{2,1,0:T(8,128)S(1)}, f32[2,16,640]{2,1,0:T(8,128)}, u32[]{:S(2)}) copy-start(f32[2,16,640]{2,1,0:T(8,128)} %param.14) | copy-start | bytes 245764
  12.4 38.2 %copy-start.14 = (f32[640]{0:T(1024)S(1)}, f32[640]{0:T(1024)}, u32[]{:S(2)}) copy-start(f32[640]{0:T(1024)} %param.18) | copy-start | bytes 7684
  12.4 38.2 %copy-start.15 = (f32[640]{0:T(1024)S(1)}, f32[640]{0:T(1024)}, u32[]{:S(2)}) copy-start(f32[640]{0:T(1024)} %param.19) | copy-start | bytes 7684
  12.4 25.3 %all-to-all-start = ((bf16[4,128,640]{2,1,0:T(8,128)(2,1)}), bf16[4,128,640]{2,1,0:T(8,128)(2,1)S(1)}, u32[]{:S(2)}, u32[]{:S(2)}) async-start(bf16[4,128,640]{2,1,0:T(8,128)(2,1)} %pack.1), calls=%async_computation | async-start | bytes 1310720 | tf_op jit(solution)/shard_map/all_to_all | solution.py:399
  24.3 73.3 %all-gather.6.cloned.1.call-start = ((), (), s32[]{:S(2)}) async-start(), calls=%async_computation.8 | async-start | bytes 1474560 | tf_op jit(solution)/shard_map/all_gather | solution.py:448
  39.1 15.2 %all-to-all-start.1 = ((f32[8,4,128]{2,1,0:T(4,128)}), f32[8,4,128]{2,1,0:T(4,128)S(1)}, u32[]{:S(2)}, u32[]{:S(2)}) async-start(f32[8,4,128]{2,1,0:T(4,128)} %get-tuple-element.26), calls=%async_computation.1 | async-start | bytes 32768 | tf_op jit(solution)/shard_map/all_to_all | solution.py:399
  45.9 4.7 %collective-permute-start = (bf16[16,640]{1,0:T(8,128)(2,1)S(1)}, bf16[16,640]{1,0:T(8,128)(2,1)S(1)}, u32[]{:S(2)}, u32[]{:S(2)}) collective-permute-start(bf16[16,640]{1,0:T(8,128)(2,1)S(1)} %get-tuple-element.29), channel_id=1, source_target_pairs={{0,4},{4,8},{8,12},{12,16},{16,20},{20,24},{24,28},{1,5},{5,9},{9,... | collective-permute-start | bytes 61448 | tf_op jit(solution)/shard_map/ppermute | solution.py:451
  49.3 5.0 %collective-permute-start.1 = (bf16[16,640]{1,0:T(8,128)(2,1)S(1)}, bf16[16,640]{1,0:T(8,128)(2,1)S(1)}, u32[]{:S(2)}, u32[]{:S(2)}) collective-permute-start(bf16[16,640]{1,0:T(8,128)(2,1)S(1)} %get-tuple-element.30), channel_id=1, source_target_pairs={{4,0},{8,4},{12,8},{16,12},{20,16},{24,20},{28,24},{5,1},{9,5},{13... | collective-permute-start | bytes 61448 | tf_op jit(solution)/shard_map/ppermute | solution.py:452
  54.3 1.5 copy-start.6
  55.8 15.3 %copy-start.12 = (f32[2,640]{1,0:T(2,128)S(1)}, f32[2,640]{1,0:T(2,128)}, u32[]{:S(2)}) copy-start(f32[2,640]{1,0:T(2,128)} %param.22) | copy-start | bytes 15364
  55.8 19.7 %copy-start.13 = (f32[640]{0:T(1024)S(1)}, f32[640]{0:T(1024)}, u32[]{:S(2)}) copy-start(f32[640]{0:T(1024)} %param.21) | copy-start | bytes 7684
  58.3 31.4 %copy-start.11 = (bf16[640,320]{0,1:T(8,128)(2,1)S(1)}, bf16[640,320]{0,1:T(8,128)(2,1)}, u32[]{:S(2)}) copy-start(bf16[640,320]{0,1:T(8,128)(2,1)} %param.25) | copy-start | bytes 1228804
  58.3 31.6 %copy-start.16 = (f32[640]{0:T(1024)S(1)}, f32[640]{0:T(1024)}, u32[]{:S(2)}) copy-start(f32[640]{0:T(1024)} %param.23) | copy-start | bytes 7684
  58.3 31.7 %copy-start.17 = (f32[640]{0:T(1024)S(1)}, f32[640]{0:T(1024)}, u32[]{:S(2)}) copy-start(f32[640]{0:T(1024)} %param.24) | copy-start | bytes 7684
  58.3 38.1 %copy-start = (bf16[640,640]{1,0:T(8,128)(2,1)S(1)}, bf16[640,640]{1,0:T(8,128)(2,1)}, u32[]{:S(2)}) copy-start(bf16[640,640]{1,0:T(8,128)(2,1)} %keyvalue_ref.3) | copy-start | bytes 2457604
  58.3 23.2 %all-to-all-start.2 = ((f32[4,192,128]{2,1,0:T(8,128)}), f32[4,192,128]{2,1,0:T(8,128)S(1)}, u32[]{:S(2)}, u32[]{:S(2)}) async-start(f32[4,192,128]{2,1,0:T(8,128)} %get-tuple-element.31), calls=%async_computation.2 | async-start | bytes 786432 | tf_op jit(solution)/shard_map/all_to_all | solution.py:399
  71.2 4.4 %collective-permute-start.2 = (bf16[16,640]{1,0:T(8,128)(2,1)S(1)}, bf16[16,640]{1,0:T(8,128)(2,1)S(1)}, u32[]{:S(2)}, u32[]{:S(2)}) collective-permute-start(bf16[16,640]{1,0:T(8,128)(2,1)S(1)} %get-tuple-element.32), channel_id=1, source_target_pairs={{0,4},{4,8},{8,12},{12,16},{16,20},{20,24},{24,28},{1,5},{5,9},{9,... | collective-permute-start | bytes 61448 | tf_op jit(solution)/shard_map/ppermute | solution.py:464
  74.3 5.8 %collective-permute-start.3 = (bf16[16,640]{1,0:T(8,128)(2,1)S(1)}, bf16[16,640]{1,0:T(8,128)(2,1)S(1)}, u32[]{:S(2)}, u32[]{:S(2)}) collective-permute-start(bf16[16,640]{1,0:T(8,128)(2,1)S(1)} %get-tuple-element.33), channel_id=1, source_target_pairs={{4,0},{8,4},{12,8},{16,12},{20,16},{24,20},{28,24},{5,1},{9,5},{13... | collective-permute-start | bytes 61448 | tf_op jit(solution)/shard_map/ppermute | solution.py:464
  82.9 13.4 %all-to-all-start.3 = ((f32[8,4,128]{2,1,0:T(4,128)}), f32[8,4,128]{2,1,0:T(4,128)S(1)}, u32[]{:S(2)}, u32[]{:S(2)}) async-start(f32[8,4,128]{2,1,0:T(4,128)} %get-tuple-element.35), calls=%async_computation.3 | async-start | bytes 32768 | tf_op jit(solution)/shard_map/all_to_all | solution.py:399
  89.6 8.1 %copy-start.10 = (bf16[320,640]{1,0:T(8,128)(2,1)S(1)}, bf16[320,640]{1,0:T(8,128)(2,1)}, u32[]{:S(2)}) copy-start(bf16[320,640]{1,0:T(8,128)(2,1)} %out_ref.3) | copy-start | bytes 1228804
  89.6 57.8 %all-gather.8.cloned.1.call-start = ((), (), s32[]{:S(2)}) async-start(), calls=%async_computation.9 | async-start | bytes 1474560 | tf_op jit(solution)/shard_map/all_gather | solution.py:448
  103.1 9.9 %all-to-all-start.4 = ((f32[8,4,128]{2,1,0:T(4,128)}), f32[8,4,128]{2,1,0:T(4,128)S(1)}, u32[]{:S(2)}, u32[]{:S(2)}) async-start(f32[8,4,128]{2,1,0:T(4,128)} %get-tuple-element.40), calls=%async_computation.4 | async-start | bytes 32768 | tf_op jit(solution)/shard_map/all_to_all | solution.py:399
  113.0 1.5 copy-start.7
  (6 other events, 5.8 us)
Sparse Core Ops, SparseCore 0:
  9.4 44.3 all-gather.3
  55.9 40.5 all-gather.5
  98.6 39.5 all-gather.7

commit v4 on v3

--- a/solution.py
+++ b/solution.py
@@ -127,14 +127,15 @@
         rows[t, 3 * COLS :] = below_ref[...] if t == 3 else prior_ref[t + 1, :COLS]
 
 
-def convolve(rows, weight_ref, wide):
+def convolve(rows, weight_refs, y, wide):
     window = rows[...].reshape(4 * 64, CHANNELS)
     wide[...] = jnp.zeros(wide.shape, F32)
     col = lax.broadcasted_iota(jnp.int32, (LANES, LANES), 0) & (COLS - 1)
     lane = lax.broadcasted_iota(jnp.int32, (LANES, LANES), 1)
     tiles = [jnp.zeros((LANES, LANES), F32), jnp.zeros((LANES, LANES), F32)]
-    for part in range(8):
-        wide[:, 0 : 9 * MEMBERS] = dot(window, weight_ref[part], NT)
+    for turn, weight_ref in enumerate(weight_refs):
+        part = (y - turn) & 7
+        wide[:, 0 : 9 * MEMBERS] = dot(window, weight_ref[...], NT)
         whole = wide[...].reshape(4, 64, 256)
         lines = [
             whole[:, COLS * r : COLS * r + 2 * COLS].reshape(LANES, 256) for r in range(3)
@@ -149,12 +150,11 @@
         right = pltpu.roll(total, LANES - 2 * MEMBERS, 1)
         right = jnp.where(col < COLS - 1, pltpu.roll(right, LANES - 1, 0), 0.0)
         made = left + centre + right
-        tile, at = divmod(part, 6)
-        at *= MEMBERS
-        if at:
-            made = pltpu.roll(made, at, 1)
+        at = MEMBERS * jnp.where(part < 6, part, part - 6)
+        made = pltpu.roll(made, at, 1)
         kept = (lane >= at) & (lane < at + MEMBERS)
-        tiles[tile] = jnp.where(kept, made, tiles[tile])
+        tiles[0] = jnp.where(kept & (part < 6), made, tiles[0])
+        tiles[1] = jnp.where(kept & (part >= 6), made, tiles[1])
     return tiles
 
 
@@ -165,21 +165,19 @@
 
 
 def conv_quad_kernel(
+    place_ref,
     stats_ref,
     state_ref,
     prior_ref,
     above_ref,
     below_ref,
-    weight_ref,
     gain_ref,
     bias_ref,
-    out_ref,
-    act_ref,
-    first_ref,
-    last_ref,
-    rows,
-    wide,
-):
+    *refs,
+):
+    weight_refs = refs[:8]
+    out_ref, act_ref, first_ref, last_ref, rows, wide = refs[8:]
+
     def keep(t, act):
         act_ref[t] = act
         if t == 0:
@@ -188,7 +186,7 @@
             last_ref[...] = act[COLS:]
 
     activate(stats_ref, state_ref, prior_ref, above_ref, below_ref, gain_ref, bias_ref, keep, rows)
-    tiles = convolve(rows, weight_ref, wide)
+    tiles = convolve(rows, weight_refs, place_ref[0], wide)
     rest = folded(tiles[1])
     for to in range(4):
         out_ref[to, 0:LANES] = tiles[0]
@@ -212,20 +210,18 @@
     prior_ref,
     above_ref,
     below_ref,
-    weight_ref,
     gain_ref,
     bias_ref,
     shift_ref,
-    out_ref,
-    told_ref,
-    rows,
-    wide,
-):
+    *refs,
+):
+    weight_refs = refs[:8]
+    out_ref, told_ref, rows, wide = refs[8:]
     a = place_ref[1]
     activate(
         stats_ref, state_ref, prior_ref, above_ref, below_ref, gain_ref, bias_ref, lambda t, act: None, rows
     )
-    tiles = convolve(rows, weight_ref, wide)
+    tiles = convolve(rows, weight_refs, place_ref[0], wide)
     for t in range(4):
         mine = slice(t * ROWS, (t + 1) * ROWS)
         out_ref[t, 0:ROWS] = tiles[0][mine]
@@ -426,7 +422,17 @@
     row = lambda v: v.reshape(1, CHANNELS)
 
     slices = conv_weight.transpose(0, 1, 3, 2).reshape(9 * MEMBERS, CHANNELS)
-    weights = lax.all_gather(slices, "y", axis=0, tiled=False)
+    onward = [(i, (i + 1) % 8) for i in range(8)]
+    back = [((i + 1) % 8, i) for i in range(8)]
+    weights = [slices] + [None] * 7
+
+    def pass_on(hop):
+        weights[hop] = lax.ppermute(weights[hop - 1], "y", onward)
+        if hop < 4:
+            weights[-hop] = lax.ppermute(weights[(1 - hop) % 8], "y", back)
+
+    pass_on(1)
+    pass_on(2)
 
     own = field.reshape(ROWS, CHANNELS)
     (packed,) = call(
@@ -435,13 +441,18 @@
         [((4, 4 * ROWS, CHANNELS), BF16)],
         (own, stale_conv_in.reshape(ROWS, CHANNELS), stale_keys, stale_values),
     )
+    packed, weights[1], weights[7], weights[2], weights[6] = lax.optimization_barrier(
+        (to_all(packed, QUAD), weights[1], weights[7], weights[2], weights[6])
+    )
     state, stats, kv, prior, first, last = call(
         unpack_kernel,
         "unpack",
         [(quad, F32), stats8, (quad, BF16), (quad, BF16), (line, BF16), (line, BF16)],
-        (place, to_all(packed, QUAD), own),
+        (place, packed, own),
         scalars=1,
     )
+    pass_on(3)
+    pass_on(4)
     norm1 = (row(norm1_gain), row(norm1_bias))
     norm2 = (row(norm2_gain), row(norm2_bias))
     buffers = [pltpu.VMEM((4, 64, CHANNELS), BF16), pltpu.VMEM((256, 256), F32)]
@@ -456,7 +467,8 @@
         conv_quad_kernel,
         "conv0",
         [((4, LANES + 64, LANES), F32), (quad, BF16), (line, BF16), (line, BF16)],
-        (to_all(stats, "y"), state, prior, above, below, weights, *norm1),
+        (place, to_all(stats, "y"), state, prior, above, below, *norm1, *weights),
+        scalars=1,
         scratch=buffers,
         flops=1 << 30,
     )
@@ -491,7 +503,7 @@
         conv_own_kernel,
         "conv1",
         [((4, ROWS + ROWS // 2, LANES), F32), stats8],
-        (place, to_all(stats, "y"), state, prior, above, below, weights, *norm1, shift),
+        (place, to_all(stats, "y"), state, prior, above, below, *norm1, shift, *weights),
         scalars=1,
         scratch=buffers,
         flops=1 << 30,

time: 160 us -> 179 us (1.12)
  starting transfers between devices: 50.7 us -> 71.2 us
  waiting for transfers between devices: 35.8 us -> 29.8 us
  local copies, waits for them, and re-layouts: 10.9 us -> 16.2 us
  blocking collectives: 30.5 us -> 28.3 us
    ppermute x0 -> x7, starting transfers between devices: none -> 22.6 us  [the longest x3 12.5 us: pass_on(): weights[-hop] = lax.ppermute(weights[(1 - hop) % 8], 'y', back)]
    all_to_all x5, waiting for transfers between devices: 27.7 us -> 14.7 us  [to_all(): return lax.all_to_all(value, axes, 0, 0, tiled=True)]
    ppermute x0 -> x7, waiting for transfers between devices: none -> 10.8 us  [the longest x4 9.84 us: pass_on(): weights[hop] = lax.ppermute(weights[hop - 1], 'y', onward)]
    unnamed x37 -> x51, local copies, waits for them, and re-layouts: 9.15 us -> 14.8 us
    ppermute x1, waiting for transfers between devices: 4.42 us -> 0.01 us  [per_device(): lax.ppermute(first, 'y', down)]
    all_to_all x5, starting transfers between devices: 41.6 us -> 38.6 us  [to_all(): return lax.all_to_all(value, axes, 0, 0, tiled=True)]
    all_to_all x2, blocking collectives: 30.5 us -> 28.3 us  [to_all(): return lax.all_to_all(value, axes, 0, 0, tiled=True)]
  transfers between devices with their start and end apart: 12 -> 18, of which waited for: 6 -> 9; matrix products, arithmetic and copies ran while one was open for 0% -> 2% of each run, Pallas kernels for 9% -> 7%
where the time goes in v4:
time: 179 us; the launch traced here: 177 us
  starting transfers between devices  71.2 us (40%)
  waiting for transfers between devices  29.8 us (17%)
  blocking collectives  28.3 us (16%)
  Pallas kernels  17.9 us (10%)
  local copies, waits for them, and re-layouts  16.2 us (9%)
  between operations  13.7 us (8%)
    all_to_all x5, starting transfers between devices, to_all(): return lax.all_to_all(value, axes, 0, 0, tiled=True)  38.6 us
    all_to_all x2, blocking collectives, to_all(): return lax.all_to_all(value, axes, 0, 0, tiled=True)  28.3 us
    pallas_call x9, Pallas kernels, call(): pl.pallas_call(kernel, name=name, out_shape=[jax.ShapeDtypeStruct(s, t) f...  17.9 us
    unnamed x51, local copies, waits for them, and re-layouts  14.8 us
    all_to_all x5, waiting for transfers between devices, to_all(): return lax.all_to_all(value, axes, 0, 0, tiled=True)  14.7 us
    ppermute x3, starting transfers between devices, pass_on(): weights[-hop] = lax.ppermute(weights[(1 - hop) % 8], 'y', back)  12.5 us
    ppermute x4, starting transfers between devices, pass_on(): weights[hop] = lax.ppermute(weights[hop - 1], 'y', onward)  10.2 us
    ppermute x4, waiting for transfers between devices, pass_on(): weights[hop] = lax.ppermute(weights[hop - 1], 'y', onward)  9.84 us
  transfers between devices with their start and end apart: 18, of which 9 were waited for; matrix products, arithmetic and copies ran while one was open for 2% of the time, Pallas kernels for 7%

profile of v4, /device:TPU:1, one launch (start us, length us, event | category | flops | bytes accessed | tf_op | source)
XLA Modules:
  0.0 177.3 jit_solution(2242005680778355434)
XLA Ops:
  10.6 11.9 %all-to-all-start = ((bf16[4,128,640]{2,1,0:T(8,128)(2,1)}), bf16[4,128,640]{2,1,0:T(8,128)(2,1)S(1)}, u32[]{:S(2)}, u32[]{:S(2)}) async-start(bf16[4,128,640]{2,1,0:T(8,128)(2,1)} %pack.1), calls=%async_computation | async-start | bytes 1310720 | tf_op jit(solution)/shard_map/all_to_all | solution.py:395
  22.6 3.2 %collective-permute-start = (bf16[180,640]{1,0:T(8,128)(2,1)S(1)}, bf16[180,640]{1,0:T(8,128)(2,1)S(1)}, u32[]{:S(2)}, u32[]{:S(2)}) collective-permute-start(bf16[180,640]{1,0:T(8,128)(2,1)S(1)} %reshape.35.refs_0_), channel_id=1, source_target_pairs={{0,4},{4,8},{8,12},{12,16},{16,20},{20,24},{24,28},{28,0},{1,5},{5... | collective-permute-start | bytes 691208 | tf_op jit(solution)/shard_map/ppermute | solution.py:430
  25.8 3.8 %collective-permute-start.1 = (bf16[180,640]{1,0:T(8,128)(2,1)S(1)}, bf16[180,640]{1,0:T(8,128)(2,1)S(1)}, u32[]{:S(2)}, u32[]{:S(2)}) collective-permute-start(bf16[180,640]{1,0:T(8,128)(2,1)S(1)} %reshape.35.refs_0_), channel_id=1, source_target_pairs={{4,0},{8,4},{12,8},{16,12},{20,16},{24,20},{28,24},{0,28},{5,1},{9... | collective-permute-start | bytes 691208 | tf_op jit(solution)/shard_map/ppermute | solution.py:432
  29.6 4.2 %collective-permute-done.refs_1_ = bf16[180,640]{1,0:T(8,128)(2,1)S(1)} collective-permute-done((bf16[180,640]{1,0:T(8,128)(2,1)S(1)}, bf16[180,640]{1,0:T(8,128)(2,1)S(1)}, u32[]{:S(2)}, u32[]{:S(2)}) %collective-permute-start) | collective-permute-done | bytes 230432 | tf_op jit(solution)/shard_map/ppermute | solution.py:430
  35.7 4.6 %collective-permute-start.3 = (bf16[180,640]{1,0:T(8,128)(2,1)S(1)}, bf16[180,640]{1,0:T(8,128)(2,1)S(1)}, u32[]{:S(2)}, u32[]{:S(2)}) collective-permute-start(bf16[180,640]{1,0:T(8,128)(2,1)S(1)} %collective-permute-done.1.refs_7_), channel_id=1, source_target_pairs={{4,0},{8,4},{12,8},{16,12},{20,16},{24,20},{28,24},{0,28},{5,1},{9... | collective-permute-start | bytes 691208 | tf_op jit(solution)/shard_map/ppermute | solution.py:432
  40.4 3.2 %collective-permute-done.2.refs_2_ = bf16[180,640]{1,0:T(8,128)(2,1)S(1)} collective-permute-done((bf16[180,640]{1,0:T(8,128)(2,1)S(1)}, bf16[180,640]{1,0:T(8,128)(2,1)S(1)}, u32[]{:S(2)}, u32[]{:S(2)}) %collective-permute-start.2) | collective-permute-done | bytes 230432 | tf_op jit(solution)/shard_map/ppermute | solution.py:430
  45.9 3.2 %collective-permute-start.6 = (bf16[180,640]{1,0:T(8,128)(2,1)S(1)}, bf16[180,640]{1,0:T(8,128)(2,1)S(1)}, u32[]{:S(2)}, u32[]{:S(2)}) collective-permute-start(bf16[180,640]{1,0:T(8,128)(2,1)S(1)} %collective-permute-done.2.refs_2_), channel_id=1, source_target_pairs={{0,4},{4,8},{8,12},{12,16},{16,20},{20,24},{24,28},{28,0},{1,5},{5... | collective-permute-start | bytes 691208 | tf_op jit(solution)/shard_map/ppermute | solution.py:430
  49.1 4.1 %collective-permute-start.8 = (bf16[180,640]{1,0:T(8,128)(2,1)S(1)}, bf16[180,640]{1,0:T(8,128)(2,1)S(1)}, u32[]{:S(2)}, u32[]{:S(2)}) collective-permute-start(bf16[180,640]{1,0:T(8,128)(2,1)S(1)} %collective-permute-done.3.refs_6_), channel_id=1, source_target_pairs={{4,0},{8,4},{12,8},{16,12},{20,16},{24,20},{28,24},{0,28},{5,1},{9... | collective-permute-start | bytes 691208 | tf_op jit(solution)/shard_map/ppermute | solution.py:432
  53.2 2.5 %collective-permute-done.6.refs_3_ = bf16[180,640]{1,0:T(8,128)(2,1)S(1)} collective-permute-done((bf16[180,640]{1,0:T(8,128)(2,1)S(1)}, bf16[180,640]{1,0:T(8,128)(2,1)S(1)}, u32[]{:S(2)}, u32[]{:S(2)}) %collective-permute-start.6) | collective-permute-done | bytes 230432 | tf_op jit(solution)/shard_map/ppermute | solution.py:430
  57.6 5.7 %all-to-all-start.1 = ((f32[8,4,128]{2,1,0:T(4,128)}), f32[8,4,128]{2,1,0:T(4,128)S(1)}, u32[]{:S(2)}, u32[]{:S(2)}) async-start(f32[8,4,128]{2,1,0:T(4,128)} %get-tuple-element.32), calls=%async_computation.1 | async-start | bytes 32768 | tf_op jit(solution)/shard_map/all_to_all | solution.py:395
  63.3 3.4 %collective-permute-start.4 = (bf16[16,640]{1,0:T(8,128)(2,1)S(1)}, bf16[16,640]{1,0:T(8,128)(2,1)S(1)}, u32[]{:S(2)}, u32[]{:S(2)}) collective-permute-start(bf16[16,640]{1,0:T(8,128)(2,1)S(1)} %get-tuple-element.35), channel_id=1, source_target_pairs={{0,4},{4,8},{8,12},{12,16},{16,20},{20,24},{24,28},{1,5},{5,9},{9,... | collective-permute-start | bytes 61448 | tf_op jit(solution)/shard_map/ppermute | solution.py:462
  68.0 3.5 %collective-permute-done.5.below_ref = bf16[16,640]{1,0:T(8,128)(2,1)S(1)} collective-permute-done((bf16[16,640]{1,0:T(8,128)(2,1)S(1)}, bf16[16,640]{1,0:T(8,128)(2,1)S(1)}, u32[]{:S(2)}, u32[]{:S(2)}) %collective-permute-start.5) | collective-permute-done | bytes 20512 | tf_op jit(solution)/shard_map/ppermute | solution.py:463
  71.6 3.0 %conv0.1 = (f32[4,192,128]{2,1,0:T(8,128)}, bf16[4,32,640]{2,1,0:T(8,128)(2,1)S(1)}, bf16[16,640]{1,0:T(8,128)(2,1)S(1)}, bf16[16,640]{1,0:T(8,128)(2,1)S(1)}) custom-call(s32[2]{0:T(128)S(1)} %pad_add_fusion.place_ref, f32[8,4,128]{2,1,0:T(4,128)S(1)} %all-to-all-done.1.stats_ref, f32[4,32,640]{2,1,0:T(8,128)S(1)} %get-tuple-element.33.state_ref, ...), custom_call_target="tpu_custom_call" | custom-call | flops 1073741824 | bytes 1048576 | tf_op jit(solution)/shard_map/conv0/pallas_call | solution.py:382
  75.3 10.8 %all-to-all-start.2 = ((f32[4,192,128]{2,1,0:T(8,128)}), f32[4,192,128]{2,1,0:T(8,128)S(1)}, u32[]{:S(2)}, u32[]{:S(2)}) async-start(f32[4,192,128]{2,1,0:T(8,128)} %get-tuple-element.41), calls=%async_computation.2 | async-start | bytes 786432 | tf_op jit(solution)/shard_map/all_to_all | solution.py:395
  87.4 4.0 %collective-permute-start.9 = (bf16[16,640]{1,0:T(8,128)(2,1)S(1)}, bf16[16,640]{1,0:T(8,128)(2,1)S(1)}, u32[]{:S(2)}, u32[]{:S(2)}) collective-permute-start(bf16[16,640]{1,0:T(8,128)(2,1)S(1)} %get-tuple-element.42), channel_id=1, source_target_pairs={{0,4},{4,8},{8,12},{12,16},{16,20},{20,24},{24,28},{1,5},{5,9},{9,... | collective-permute-start | bytes 61448 | tf_op jit(solution)/shard_map/ppermute | solution.py:476
  92.3 4.1 %all-to-all-done.2.conv_ref = f32[4,192,128]{2,1,0:T(8,128)S(1)} async-done(((f32[4,192,128]{2,1,0:T(8,128)}), f32[4,192,128]{2,1,0:T(8,128)S(1)}, u32[]{:S(2)}, u32[]{:S(2)}) %all-to-all-start.2) | async-done | bytes 393248 | tf_op jit(solution)/shard_map/all_to_all | solution.py:395
  97.8 6.8 %all-to-all-start.3 = ((f32[8,4,128]{2,1,0:T(4,128)}), f32[8,4,128]{2,1,0:T(4,128)S(1)}, u32[]{:S(2)}, u32[]{:S(2)}) async-start(f32[8,4,128]{2,1,0:T(4,128)} %get-tuple-element.45), calls=%async_computation.3 | async-start | bytes 32768 | tf_op jit(solution)/shard_map/all_to_all | solution.py:395
  107.4 3.9 %all-to-all-done.3.stats_ref = f32[8,4,128]{2,1,0:T(4,128)S(1)} async-done(((f32[8,4,128]{2,1,0:T(4,128)}), f32[8,4,128]{2,1,0:T(4,128)S(1)}, u32[]{:S(2)}, u32[]{:S(2)}) %all-to-all-start.3) | async-done | bytes 16416 | tf_op jit(solution)/shard_map/all_to_all | solution.py:395
  115.4 4.2 %attend0.1 = (f32[4,32,640]{2,1,0:T(8,128)S(1)}, f32[8,4,128]{2,1,0:T(4,128)}) custom-call(s32[2]{0:T(128)S(1)} %pad_add_fusion.place_ref, bf16[128,384]{1,0:T(8,128)(2,1)S(1)} %copy-done.14, bf16[128,640]{1,0:T(8,128)(2,1)} %get-tuple-element.48.fresh_ref, f32[4,32,640]{2,1,0:T(8,128)S(1)} %get-tuple-element.46.hidden_ref, bf16[320,640]{1,0:T(8,128)(2,1)S(1)} %copy-done.8, ...), custom_call_target="tpu_custom_call" | custom-call | flops 1073741824 | bytes 1048576 | tf_op jit(solution)/shard_map/attend0/pallas_call | solution.py:382
  120.3 3.3 %all-to-all-start.4 = ((f32[8,4,128]{2,1,0:T(4,128)}), f32[8,4,128]{2,1,0:T(4,128)S(1)}, u32[]{:S(2)}, u32[]{:S(2)}) async-start(f32[8,4,128]{2,1,0:T(4,128)} %get-tuple-element.50), calls=%async_computation.4 | async-start | bytes 32768 | tf_op jit(solution)/shard_map/all_to_all | solution.py:395
  123.7 6.6 %all-to-all-done.4.stats_ref = f32[8,4,128]{2,1,0:T(4,128)S(1)} async-done(((f32[8,4,128]{2,1,0:T(4,128)}), f32[8,4,128]{2,1,0:T(4,128)S(1)}, u32[]{:S(2)}, u32[]{:S(2)}) %all-to-all-start.4) | async-done | bytes 16416 | tf_op jit(solution)/shard_map/all_to_all | solution.py:395
  136.3 9.1 %all_to_all.35.stats_ref = f32[8,4,128]{2,1,0:T(4,128)S(1)} all-to-all(f32[8,4,128]{2,1,0:T(4,128)S(1)} %get-tuple-element.56), channel_id=1, replica_groups=mesh['req'=16,'y'=8,'zh'=2,'core'=2] {'y'}, dimensions={0} | all-to-all | bytes 32768 | tf_op jit(solution)/shard_map/all_to_all | solution.py:395
  145.4 19.2 %all_to_all.36.conv_ref = f32[4,56,128]{2,1,0:T(8,128)S(1)} all-to-all(f32[4,56,128]{2,1,0:T(8,128)S(1)} %insert1.1), channel_id=1, replica_groups=mesh['req'=16,'y'=8,'zh'=2,'core'=2] {'zh','core'}, dimensions={0} | all-to-all | bytes 229376 | tf_op jit(solution)/shard_map/all_to_all | solution.py:395
  166.9 3.5 %attend1.1 = f32[2,32,640]{2,1,0:T(8,128)} custom-call(s32[2]{0:T(128)S(1)} %pad_add_fusion.place_ref, f32[4,56,128]{2,1,0:T(8,128)S(1)} %all_to_all.36.conv_ref, f32[4,32,640]{2,1,0:T(8,128)S(1)} %copy-done.17, f32[1,640]{1,0:T(1,128)S(1)} %reshape.42.shift_ref, f32[1,640]{1,0:T(1,128)S(1)} %reshape.39.gain_ref, f32[1,640]{1,0:T(1,128)S(1)} %reshape.40.bias_ref, ...), custom_call_target="tpu_custom_call" | custom-call | flops 1073741824 | bytes 1048576 | tf_op jit(solution)/shard_map/attend1/pallas_call | solution.py:382
  (86 shorter events, 31.9 us)
Async XLA Ops:
  9.7 34.8 %copy-start.2 = (f32[2,16,640]{2,1,0:T(8,128)S(1)}, f32[2,16,640]{2,1,0:T(8,128)}, u32[]{:S(2)}) copy-start(f32[2,16,640]{2,1,0:T(8,128)} %param.14) | copy-start | bytes 245764
  10.6 57.4 %copy-start.23 = (f32[640]{0:T(1024)S(1)}, f32[640]{0:T(1024)}, u32[]{:S(2)}) copy-start(f32[640]{0:T(1024)} %param.18) | copy-start | bytes 7684
  10.6 57.4 %copy-start.24 = (f32[640]{0:T(1024)S(1)}, f32[640]{0:T(1024)}, u32[]{:S(2)}) copy-start(f32[640]{0:T(1024)} %param.19) | copy-start | bytes 7684
  10.6 33.9 %all-to-all-start = ((bf16[4,128,640]{2,1,0:T(8,128)(2,1)}), bf16[4,128,640]{2,1,0:T(8,128)(2,1)S(1)}, u32[]{:S(2)}, u32[]{:S(2)}) async-start(bf16[4,128,640]{2,1,0:T(8,128)(2,1)} %pack.1), calls=%async_computation | async-start | bytes 1310720 | tf_op jit(solution)/shard_map/all_to_all | solution.py:395
  22.5 90.7 %all-gather.3.cloned.1.call-start = ((), (), s32[]{:S(2)}) async-start(), calls=%async_computation.7 | async-start | bytes 1474560 | tf_op jit(solution)/shard_map/all_gather | solution.py:459
  22.6 11.2 %collective-permute-start = (bf16[180,640]{1,0:T(8,128)(2,1)S(1)}, bf16[180,640]{1,0:T(8,128)(2,1)S(1)}, u32[]{:S(2)}, u32[]{:S(2)}) collective-permute-start(bf16[180,640]{1,0:T(8,128)(2,1)S(1)} %reshape.35.refs_0_), channel_id=1, source_target_pairs={{0,4},{4,8},{8,12},{12,16},{16,20},{20,24},{24,28},{28,0},{1,5},{5... | collective-permute-start | bytes 691208 | tf_op jit(solution)/shard_map/ppermute | solution.py:430
  25.8 9.9 %collective-permute-start.1 = (bf16[180,640]{1,0:T(8,128)(2,1)S(1)}, bf16[180,640]{1,0:T(8,128)(2,1)S(1)}, u32[]{:S(2)}, u32[]{:S(2)}) collective-permute-start(bf16[180,640]{1,0:T(8,128)(2,1)S(1)} %reshape.35.refs_0_), channel_id=1, source_target_pairs={{4,0},{8,4},{12,8},{16,12},{20,16},{24,20},{28,24},{0,28},{5,1},{9... | collective-permute-start | bytes 691208 | tf_op jit(solution)/shard_map/ppermute | solution.py:432
  33.8 9.8 %collective-permute-start.2 = (bf16[180,640]{1,0:T(8,128)(2,1)S(1)}, bf16[180,640]{1,0:T(8,128)(2,1)S(1)}, u32[]{:S(2)}, u32[]{:S(2)}) collective-permute-start(bf16[180,640]{1,0:T(8,128)(2,1)S(1)} %collective-permute-done.refs_1_), channel_id=1, source_target_pairs={{0,4},{4,8},{8,12},{12,16},{16,20},{20,24},{24,28},{28,0},{1,5},{5... | collective-permute-start | bytes 691208 | tf_op jit(solution)/shard_map/ppermute | solution.py:430
  35.7 8.8 %collective-permute-start.3 = (bf16[180,640]{1,0:T(8,128)(2,1)S(1)}, bf16[180,640]{1,0:T(8,128)(2,1)S(1)}, u32[]{:S(2)}, u32[]{:S(2)}) collective-permute-start(bf16[180,640]{1,0:T(8,128)(2,1)S(1)} %collective-permute-done.1.refs_7_), channel_id=1, source_target_pairs={{4,0},{8,4},{12,8},{16,12},{20,16},{24,20},{28,24},{0,28},{5,1},{9... | collective-permute-start | bytes 691208 | tf_op jit(solution)/shard_map/ppermute | solution.py:432
  45.9 9.7 %collective-permute-start.6 = (bf16[180,640]{1,0:T(8,128)(2,1)S(1)}, bf16[180,640]{1,0:T(8,128)(2,1)S(1)}, u32[]{:S(2)}, u32[]{:S(2)}) collective-permute-start(bf16[180,640]{1,0:T(8,128)(2,1)S(1)} %collective-permute-done.2.refs_2_), channel_id=1, source_target_pairs={{0,4},{4,8},{8,12},{12,16},{16,20},{20,24},{24,28},{28,0},{1,5},{5... | collective-permute-start | bytes 691208 | tf_op jit(solution)/shard_map/ppermute | solution.py:430
  49.1 22.4 %collective-permute-start.8 = (bf16[180,640]{1,0:T(8,128)(2,1)S(1)}, bf16[180,640]{1,0:T(8,128)(2,1)S(1)}, u32[]{:S(2)}, u32[]{:S(2)}) collective-permute-start(bf16[180,640]{1,0:T(8,128)(2,1)S(1)} %collective-permute-done.3.refs_6_), channel_id=1, source_target_pairs={{4,0},{8,4},{12,8},{16,12},{20,16},{24,20},{28,24},{0,28},{5,1},{9... | collective-permute-start | bytes 691208 | tf_op jit(solution)/shard_map/ppermute | solution.py:432
  55.7 15.9 %collective-permute-start.7 = (bf16[180,640]{1,0:T(8,128)(2,1)S(1)}, bf16[180,640]{1,0:T(8,128)(2,1)S(1)}, u32[]{:S(2)}, u32[]{:S(2)}) collective-permute-start(bf16[180,640]{1,0:T(8,128)(2,1)S(1)} %collective-permute-done.6.refs_3_), channel_id=1, source_target_pairs={{0,4},{4,8},{8,12},{12,16},{16,20},{20,24},{24,28},{28,0},{1,5},{5... | collective-permute-start | bytes 691208 | tf_op jit(solution)/shard_map/ppermute | solution.py:430
  57.6 14.0 %all-to-all-start.1 = ((f32[8,4,128]{2,1,0:T(4,128)}), f32[8,4,128]{2,1,0:T(4,128)S(1)}, u32[]{:S(2)}, u32[]{:S(2)}) async-start(f32[8,4,128]{2,1,0:T(4,128)} %get-tuple-element.32), calls=%async_computation.1 | async-start | bytes 32768 | tf_op jit(solution)/shard_map/all_to_all | solution.py:395
  63.3 4.7 %collective-permute-start.4 = (bf16[16,640]{1,0:T(8,128)(2,1)S(1)}, bf16[16,640]{1,0:T(8,128)(2,1)S(1)}, u32[]{:S(2)}, u32[]{:S(2)}) collective-permute-start(bf16[16,640]{1,0:T(8,128)(2,1)S(1)} %get-tuple-element.35), channel_id=1, source_target_pairs={{0,4},{4,8},{8,12},{12,16},{16,20},{20,24},{24,28},{1,5},{5,9},{9,... | collective-permute-start | bytes 61448 | tf_op jit(solution)/shard_map/ppermute | solution.py:462
  66.7 4.9 %collective-permute-start.5 = (bf16[16,640]{1,0:T(8,128)(2,1)S(1)}, bf16[16,640]{1,0:T(8,128)(2,1)S(1)}, u32[]{:S(2)}, u32[]{:S(2)}) collective-permute-start(bf16[16,640]{1,0:T(8,128)(2,1)S(1)} %get-tuple-element.36), channel_id=1, source_target_pairs={{4,0},{8,4},{12,8},{16,12},{20,16},{24,20},{28,24},{5,1},{9,5},{13... | collective-permute-start | bytes 61448 | tf_op jit(solution)/shard_map/ppermute | solution.py:463
  71.6 14.5 %copy-start.21 = (f32[2,640]{1,0:T(2,128)S(1)}, f32[2,640]{1,0:T(2,128)}, u32[]{:S(2)}) copy-start(f32[2,640]{1,0:T(2,128)} %param.22) | copy-start | bytes 15364
  71.6 19.8 %copy-start.22 = (f32[640]{0:T(1024)S(1)}, f32[640]{0:T(1024)}, u32[]{:S(2)}) copy-start(f32[640]{0:T(1024)} %param.21) | copy-start | bytes 7684
  75.3 36.0 %copy-start = (bf16[640,640]{1,0:T(8,128)(2,1)S(1)}, bf16[640,640]{1,0:T(8,128)(2,1)}, u32[]{:S(2)}) copy-start(bf16[640,640]{1,0:T(8,128)(2,1)} %keyvalue_ref.3) | copy-start | bytes 2457604
  75.3 21.2 %all-to-all-start.2 = ((f32[4,192,128]{2,1,0:T(8,128)}), f32[4,192,128]{2,1,0:T(8,128)S(1)}, u32[]{:S(2)}, u32[]{:S(2)}) async-start(f32[4,192,128]{2,1,0:T(8,128)} %get-tuple-element.41), calls=%async_computation.2 | async-start | bytes 786432 | tf_op jit(solution)/shard_map/all_to_all | solution.py:395
  86.1 5.3 %collective-permute-start.10 = (bf16[16,640]{1,0:T(8,128)(2,1)S(1)}, bf16[16,640]{1,0:T(8,128)(2,1)S(1)}, u32[]{:S(2)}, u32[]{:S(2)}) collective-permute-start(bf16[16,640]{1,0:T(8,128)(2,1)S(1)} %get-tuple-element.43), channel_id=1, source_target_pairs={{4,0},{8,4},{12,8},{16,12},{20,16},{24,20},{28,24},{5,1},{9,5},{13... | collective-permute-start | bytes 61448 | tf_op jit(solution)/shard_map/ppermute | solution.py:476
  87.4 4.9 %collective-permute-start.9 = (bf16[16,640]{1,0:T(8,128)(2,1)S(1)}, bf16[16,640]{1,0:T(8,128)(2,1)S(1)}, u32[]{:S(2)}, u32[]{:S(2)}) collective-permute-start(bf16[16,640]{1,0:T(8,128)(2,1)S(1)} %get-tuple-element.42), channel_id=1, source_target_pairs={{0,4},{4,8},{8,12},{12,16},{16,20},{20,24},{24,28},{1,5},{5,9},{9,... | collective-permute-start | bytes 61448 | tf_op jit(solution)/shard_map/ppermute | solution.py:476
  97.8 13.4 %all-to-all-start.3 = ((f32[8,4,128]{2,1,0:T(4,128)}), f32[8,4,128]{2,1,0:T(4,128)S(1)}, u32[]{:S(2)}, u32[]{:S(2)}) async-start(f32[8,4,128]{2,1,0:T(4,128)} %get-tuple-element.45), calls=%async_computation.3 | async-start | bytes 32768 | tf_op jit(solution)/shard_map/all_to_all | solution.py:395
  104.6 60.0 %all-gather.5.cloned.1.call-start = ((), (), s32[]{:S(2)}) async-start(), calls=%async_computation.8 | async-start | bytes 1474560 | tf_op jit(solution)/shard_map/all_gather | solution.py:459
  120.3 10.0 %all-to-all-start.4 = ((f32[8,4,128]{2,1,0:T(4,128)}), f32[8,4,128]{2,1,0:T(4,128)S(1)}, u32[]{:S(2)}, u32[]{:S(2)}) async-start(f32[8,4,128]{2,1,0:T(4,128)} %get-tuple-element.50), calls=%async_computation.4 | async-start | bytes 32768 | tf_op jit(solution)/shard_map/all_to_all | solution.py:395
  (19 other events, 40.9 us)
Sparse Core Ops, SparseCore 0:
  46.1 39.6 all-gather.2
  113.3 36.2 all-gather.4

commit v5 on v3

--- a/solution.py
+++ b/solution.py
@@ -82,49 +82,74 @@
     return spread[0:1], spread[1:2]
 
 
-def pack_kernel(field_ref, stale_ref, keys_ref, values_ref, packed_ref):
+def tell_sums_and_edges(x, y, first, last, out_ref):
+    sums = eight(
+        [jnp.sum(x, axis=0, keepdims=True), jnp.sum(x * x, axis=0, keepdims=True)], CHANNELS
+    )
+    terms = [t.astype(F32)[0:2] for t in thirds(picked(sums, group_matrix()))]
+    told = jnp.concatenate([*terms, jnp.zeros((10, LANES), F32)], axis=0).astype(BF16)
+    for to in range(8):
+        out_ref[to, 0:COLS] = told
+        edge = jnp.where(y + 1 == to, last.astype(F32), first.astype(F32)).astype(BF16)
+        for k in range(5):
+            out_ref[to, COLS * (k + 1) : COLS * (k + 2)] = edge[:, LANES * k : LANES * (k + 1)]
+
+
+def heard_sums(heard_ref):
+    terms = jnp.sum(heard_ref[:, 0:COLS].astype(F32), axis=0)
+    return terms[0:2] + terms[2:4] + terms[4:6]
+
+
+def heard_edge(heard_ref, sender, exists):
+    row = jnp.concatenate(
+        [heard_ref[sender, COLS * (k + 1) : COLS * (k + 2)] for k in range(5)], axis=1
+    )
+    return jnp.where(exists, row.astype(F32), 0.0).astype(BF16)
+
+
+def heard_edges(heard_ref, y):
+    return heard_edge(heard_ref, (y - 1) & 7, y > 0), heard_edge(heard_ref, (y + 1) & 7, y < 7)
+
+
+def pack_kernel(field_ref, stale_ref, keys_ref, values_ref, packed_ref, kv_ref):
     high, middle, _ = thirds(field_ref[...])
+    packed_ref[0:ROWS] = high
+    packed_ref[ROWS : 2 * ROWS] = middle
+    packed_ref[2 * ROWS :] = stale_ref[...]
     both = jnp.concatenate(
         [keys_ref[...].astype(F32), values_ref[...].astype(F32)], axis=1
     ).astype(BF16)
-    for to in range(4):
-        packed_ref[to, 0:ROWS] = high
-        packed_ref[to, ROWS : 2 * ROWS] = middle
-        packed_ref[to, 2 * ROWS : 3 * ROWS] = stale_ref[...]
-        packed_ref[to, 3 * ROWS :] = both
+    kv_ref[...] = jnp.broadcast_to(both[None], kv_ref.shape)
 
 
 def unpack_kernel(
-    place_ref,
-    packed_ref,
-    field_ref,
-    state_ref,
-    stats_ref,
-    kv_ref,
-    prior_ref,
-    first_ref,
-    last_ref,
+    place_ref, field_ref, stale_ref, one_ref, two_ref, three_ref, state_ref, prior_ref, told_ref
 ):
     a = place_ref[1]
-    for t in range(4):
-        state_ref[t] = packed_ref[t, 0:ROWS].astype(F32) + packed_ref[t, ROWS : 2 * ROWS].astype(F32)
-        prior_ref[t] = packed_ref[t, 2 * ROWS : 3 * ROWS]
-        kv_ref[t] = packed_ref[t, 3 * ROWS :]
     state_ref[a] = field_ref[...]
-    first_ref[...] = prior_ref[0, :COLS]
-    last_ref[...] = prior_ref[3, COLS:]
-    tell_sums(state_ref[...].reshape(QUAD_ROWS, CHANNELS), group_matrix(), stats_ref)
-
-
-def activate(stats_ref, state_ref, prior_ref, above_ref, below_ref, gain_ref, bias_ref, keep, rows):
-    mean, scale = mean_and_scale(stats_ref, group_matrix())
+    prior_ref[a] = stale_ref[...]
+    for k, ref in enumerate((one_ref, two_ref, three_ref), 1):
+        state_ref[a ^ k] = ref[0:ROWS].astype(F32) + ref[ROWS : 2 * ROWS].astype(F32)
+        prior_ref[a ^ k] = ref[2 * ROWS :]
+    tell_sums_and_edges(
+        state_ref[...].reshape(QUAD_ROWS, CHANNELS),
+        place_ref[0],
+        prior_ref[0, :COLS],
+        prior_ref[3, COLS:],
+        told_ref,
+    )
+
+
+def activate(sums, edges, state_ref, prior_ref, gain_ref, bias_ref, keep, rows):
+    mean, scale = spread_sums(sums, group_matrix())
+    above, below = edges
     for t in range(4):
         value = (state_ref[t] - mean) * scale * gain_ref[...] + bias_ref[...]
         act = (value * (1.0 / (1.0 + jnp.exp(-value)))).astype(BF16)
         rows[t, COLS : 3 * COLS] = act
         keep(t, act)
-        rows[t, 0:COLS] = above_ref[...] if t == 0 else prior_ref[t - 1, COLS:]
-        rows[t, 3 * COLS :] = below_ref[...] if t == 3 else prior_ref[t + 1, :COLS]
+        rows[t, 0:COLS] = above if t == 0 else prior_ref[t - 1, COLS:]
+        rows[t, 3 * COLS :] = below if t == 3 else prior_ref[t + 1, :COLS]
 
 
 def convolve(rows, weight_ref, wide):
@@ -165,11 +190,10 @@
 
 
 def conv_quad_kernel(
-    stats_ref,
+    place_ref,
+    heard_ref,
     state_ref,
     prior_ref,
-    above_ref,
-    below_ref,
     weight_ref,
     gain_ref,
     bias_ref,
@@ -187,7 +211,8 @@
         if t == 3:
             last_ref[...] = act[COLS:]
 
-    activate(stats_ref, state_ref, prior_ref, above_ref, below_ref, gain_ref, bias_ref, keep, rows)
+    edges = heard_edges(heard_ref, place_ref[0])
+    activate(heard_sums(heard_ref), edges, state_ref, prior_ref, gain_ref, bias_ref, keep, rows)
     tiles = convolve(rows, weight_ref, wide)
     rest = folded(tiles[1])
     for to in range(4):
@@ -208,10 +233,9 @@
 def conv_own_kernel(
     place_ref,
     stats_ref,
+    heard_ref,
     state_ref,
     prior_ref,
-    above_ref,
-    below_ref,
     weight_ref,
     gain_ref,
     bias_ref,
@@ -223,7 +247,14 @@
 ):
     a = place_ref[1]
     activate(
-        stats_ref, state_ref, prior_ref, above_ref, below_ref, gain_ref, bias_ref, lambda t, act: None, rows
+        jnp.sum(stats_ref[...], axis=0),
+        heard_edges(heard_ref, place_ref[0]),
+        state_ref,
+        prior_ref,
+        gain_ref,
+        bias_ref,
+        lambda t, act: None,
+        rows,
     )
     tiles = convolve(rows, weight_ref, wide)
     for t in range(4):
@@ -281,11 +312,13 @@
     return jnp.concatenate(tiles, axis=1)
 
 
-def hidden_kernel(conv_ref, state_ref, shift_ref, hidden_ref, stats_ref):
+def hidden_kernel(
+    place_ref, conv_ref, state_ref, shift_ref, first_ref, last_ref, hidden_ref, told_ref
+):
     state = state_ref[...].reshape(QUAD_ROWS, CHANNELS)
     hidden = state + (assembled(conv_ref, QUAD_ROWS) + shift_ref[...])
     hidden_ref[...] = hidden.reshape(hidden_ref.shape)
-    tell_sums(hidden, group_matrix(), stats_ref)
+    tell_sums_and_edges(hidden, place_ref[0], first_ref[...], last_ref[...], told_ref)
 
 
 def project(hidden, mean, scale, gain_ref, bias_ref, query_ref, keyvalue_ref):
@@ -298,22 +331,24 @@
 
 
 def project_kernel(
-    stats_ref, hidden_ref, gain_ref, bias_ref, query_ref, keyvalue_ref, asked_ref, fresh_ref
-):
-    mean, scale = mean_and_scale(stats_ref, group_matrix())
+    heard_ref, hidden_ref, gain_ref, bias_ref, query_ref, keyvalue_ref, asked_ref, fresh_ref
+):
+    mean, scale = spread_sums(heard_sums(heard_ref), group_matrix())
     hidden = hidden_ref[...].reshape(QUAD_ROWS, CHANNELS)
     asked, fresh = project(hidden, mean, scale, gain_ref, bias_ref, query_ref, keyvalue_ref)
     asked_ref[...] = asked
     fresh_ref[...] = fresh
 
 
-def attend(query, fresh, patch, y, kv_ref):
+def attend(query, fresh, patch, y, kvs):
     count = query.shape[0]
     lane = lax.broadcasted_iota(jnp.int32, (count, LANES), 1)
     low = lane < HEAD_DIM
 
-    column = lax.broadcasted_iota(jnp.int32, (count, POSITIONS), 1) >> 5
-    replaced = column == 4 * y + patch
+    replaced = []
+    for kv_ref, step, first in kvs:
+        block = lax.broadcasted_iota(jnp.int32, (count, kv_ref.shape[0]), 1) >> 5
+        replaced.append(step * block + first == 4 * y + patch)
     if count == ROWS:
         theirs = None
     else:
@@ -323,19 +358,23 @@
         at = LANES * (h // 2)
         own = low if h % 2 == 0 else ~low
         asked = jnp.where(own, query[:, at : at + LANES].astype(F32), 0.0).astype(BF16)
-        old = dot(asked, kv_ref[:, at : at + LANES], NT) * HEAD_DIM ** (-0.5)
-        old = jnp.where(replaced, -jnp.inf, old)
+        olds = [
+            jnp.where(own_patch, -jnp.inf, dot(asked, ref[:, at : at + LANES], NT) * HEAD_DIM ** (-0.5))
+            for own_patch, (ref, _, _) in zip(replaced, kvs)
+        ]
         new = dot(asked, fresh[:, at : at + LANES], NT) * HEAD_DIM ** (-0.5)
         if theirs is not None:
             new = jnp.where(theirs, new, -jnp.inf)
-        peak = jnp.maximum(
-            jnp.max(old, axis=1, keepdims=True), jnp.max(new, axis=1, keepdims=True)
+        peak = functools.reduce(
+            jnp.maximum, [jnp.max(e, axis=1, keepdims=True) for e in (*olds, new)]
         )
-        old = jnp.exp(old - peak)
+        olds = [jnp.exp(old - peak) for old in olds]
         new = jnp.exp(new - peak)
-        total = jnp.sum(old, axis=1, keepdims=True) + jnp.sum(new, axis=1, keepdims=True)
+        total = sum(jnp.sum(e, axis=1, keepdims=True) for e in (*olds, new))
         at = LANES * ((HEADS + h) // 2)
-        summed = dot(old.astype(BF16), kv_ref[:, at : at + LANES])
+        summed = sum(
+            dot(old.astype(BF16), ref[:, at : at + LANES]) for old, (ref, _, _) in zip(olds, kvs)
+        )
         summed += dot(new.astype(BF16), fresh[:, at : at + LANES])
         summed = pltpu.roll(summed / total, HEAD_DIM, 1)
         tiles[h // 2] = jnp.where(own, summed, tiles[h // 2])
@@ -343,10 +382,12 @@
 
 
 def attend_quad_kernel(
-    place_ref, asked_ref, fresh_ref, hidden_ref, out_ref, kv_ref, state_ref, told_ref
-):
+    place_ref, asked_ref, fresh_ref, hidden_ref, out_ref, same_ref, other_ref, state_ref, told_ref
+):
+    core = place_ref[1] & 1
+    kvs = ((same_ref, 2, core), (other_ref, 2, 1 - core))
     patch = lax.broadcasted_iota(jnp.int32, (QUAD_ROWS, 1), 0) >> 5
-    attended = attend(asked_ref[...], fresh_ref[...], patch, place_ref[0], kv_ref)
+    attended = attend(asked_ref[...], fresh_ref[...], patch, place_ref[0], kvs)
     result = hidden_ref[...].reshape(QUAD_ROWS, CHANNELS) + dot(attended, out_ref[...])
     state_ref[...] = result.reshape(state_ref.shape)
     tell_sums(result, group_matrix(), told_ref)
@@ -373,7 +414,7 @@
         sums += conv_ref[t, 48:56]
     mean, scale = spread_sums(sums, group_matrix())
     query, fresh = project(hidden, mean, scale, gain_ref, bias_ref, query_ref, keyvalue_ref)
-    attended = attend(query, fresh, a, place_ref[0], kv_ref)
+    attended = attend(query, fresh, a, place_ref[0], ((kv_ref, 1, 0),))
     result_ref[0] = earlier
     result_ref[1] = hidden + dot(attended, out_ref[...])
 
@@ -418,71 +459,78 @@
     quad = (4, ROWS, CHANNELS)
     line = (COLS, CHANNELS)
     stats8 = ((8, 4, LANES), F32)
+    told8 = ((8, 6 * COLS, LANES), BF16)
     y = lax.axis_index("y")
     a = 2 * lax.axis_index("zh") + lax.axis_index("core")
     place = jnp.stack([y, a]).astype(jnp.int32)
-    up = [(i, i + 1) for i in range(7)]
-    down = [(i + 1, i) for i in range(7)]
     row = lambda v: v.reshape(1, CHANNELS)
+    swapped = lambda v, axis: lax.ppermute(v, axis, [(0, 1), (1, 0)])
 
     slices = conv_weight.transpose(0, 1, 3, 2).reshape(9 * MEMBERS, CHANNELS)
     weights = lax.all_gather(slices, "y", axis=0, tiled=False)
 
     own = field.reshape(ROWS, CHANNELS)
-    (packed,) = call(
+    stale = stale_conv_in.reshape(ROWS, CHANNELS)
+    packed, kv = call(
         pack_kernel,
         "pack",
-        [((4, 4 * ROWS, CHANNELS), BF16)],
-        (own, stale_conv_in.reshape(ROWS, CHANNELS), stale_keys, stale_values),
-    )
-    state, stats, kv, prior, first, last = call(
+        [((3 * ROWS, CHANNELS), BF16), ((16, ROWS, CHANNELS), BF16)],
+        (own, stale, stale_keys, stale_values),
+    )
+    across = swapped(packed, "zh")
+    kv, beside, across, corner = lax.optimization_barrier(
+        (
+            to_all(kv, ("y", "zh")),
+            swapped(packed, "core"),
+            across,
+            swapped(across, "core"),
+        )
+    )
+    kv = kv.reshape(16 * ROWS, CHANNELS)
+    state, prior, told = call(
         unpack_kernel,
         "unpack",
-        [(quad, F32), stats8, (quad, BF16), (quad, BF16), (line, BF16), (line, BF16)],
-        (place, to_all(packed, QUAD), own),
+        [(quad, F32), (quad, BF16), told8],
+        (place, own, stale, beside, across, corner),
         scalars=1,
     )
     norm1 = (row(norm1_gain), row(norm1_bias))
     norm2 = (row(norm2_gain), row(norm2_bias))
     buffers = [pltpu.VMEM((4, 64, CHANNELS), BF16), pltpu.VMEM((256, 256), F32)]
-    gathered = lambda v: lax.all_gather(
-        v.reshape(QUAD_ROWS, CHANNELS), "y", axis=0, tiled=True
-    )
-    above = lax.ppermute(last, "y", up)
-    below = lax.ppermute(first, "y", down)
-    old = gathered(kv)
-
+
+    told, other = lax.optimization_barrier((to_all(told, "y"), swapped(kv, "core")))
+    olds = (kv, other)
     conv, prior, first, last = call(
         conv_quad_kernel,
         "conv0",
         [((4, LANES + 64, LANES), F32), (quad, BF16), (line, BF16), (line, BF16)],
-        (to_all(stats, "y"), state, prior, above, below, weights, *norm1),
+        (place, told, state, prior, weights, *norm1),
+        scalars=1,
         scratch=buffers,
         flops=1 << 30,
     )
-    conv, above, below = lax.optimization_barrier(
-        (to_all(conv, QUAD), lax.ppermute(last, "y", up), lax.ppermute(first, "y", down))
-    )
-    hidden, stats = call(
+    hidden, told = call(
         hidden_kernel,
         "hidden0",
-        [(quad, F32), stats8],
-        (conv, state, row(conv_bias + time_embed[0])),
+        [(quad, F32), told8],
+        (place, to_all(conv, QUAD), state, row(conv_bias + time_embed[0]), first, last),
+        scalars=1,
         flops=1 << 28,
     )
+    heard = to_all(told, "y")
     asked, fresh = call(
         project_kernel,
         "project0",
         [((QUAD_ROWS, 3 * LANES), BF16), ((QUAD_ROWS, CHANNELS), BF16)],
-        (to_all(stats, "y"), hidden, *norm2, w_query, w_keyvalue),
+        (heard, hidden, *norm2, w_query, w_keyvalue),
         flops=1 << 28,
     )
-    kv = gathered(fresh)
+    kv = lax.all_gather(fresh, "y", axis=0, tiled=True)
     state, stats = call(
         attend_quad_kernel,
         "attend0",
         [(quad, F32), stats8],
-        (place, asked, fresh, hidden, w_out, old),
+        (place, asked, fresh, hidden, w_out, *olds),
         scalars=1,
         flops=1 << 30,
     )
@@ -491,7 +539,7 @@
         conv_own_kernel,
         "conv1",
         [((4, ROWS + ROWS // 2, LANES), F32), stats8],
-        (place, to_all(stats, "y"), state, prior, above, below, weights, *norm1, shift),
+        (place, to_all(stats, "y"), heard, state, prior, weights, *norm1, shift),
         scalars=1,
         scratch=buffers,
         flops=1 << 30,

time: 160 us -> 178 us (1.11)
  waiting for transfers between devices: 35.8 us -> 51.2 us
  blocking collectives: 30.5 us -> 23.6 us
  starting transfers between devices: 50.7 us -> 55.5 us
  local copies, waits for them, and re-layouts: 10.9 us -> 13.3 us
    all_to_all x5, waiting for transfers between devices: 27.7 us -> 50.2 us  [to_all(): return lax.all_to_all(value, axes, 0, 0, tiled=True)]
    ppermute x4, starting transfers between devices: 9.03 us -> 18.9 us  [per_device(): swapped = lambda v, axis: lax.ppermute(v, axis, [(0, 1), (1, 0)])]
    ppermute x4, waiting for transfers between devices: 8.08 us -> 0.95 us  [per_device(): swapped = lambda v, axis: lax.ppermute(v, axis, [(0, 1), (1, 0)])]
    all_to_all x2, blocking collectives: 30.5 us -> 23.6 us  [to_all(): return lax.all_to_all(value, axes, 0, 0, tiled=True)]
    all_to_all x5, starting transfers between devices: 41.6 us -> 36.6 us  [to_all(): return lax.all_to_all(value, axes, 0, 0, tiled=True)]
    unnamed x37 -> x47, local copies, waits for them, and re-layouts: 9.15 us -> 11.5 us
  transfers between devices with their start and end apart: 12 -> 11, of which waited for: 6 -> 6; matrix products, arithmetic and copies ran while one was open for 0% -> 1% of each run, Pallas kernels for 9% -> 5%
where the time goes in v5:
time: 178 us; the launch traced here: 176 us
  starting transfers between devices  55.5 us (31%)
  waiting for transfers between devices  51.2 us (29%)
  blocking collectives  23.6 us (13%)
  Pallas kernels  18.6 us (10%)
  between operations  13.6 us (8%)
  local copies, waits for them, and re-layouts  13.3 us (7%)
    all_to_all x5, waiting for transfers between devices, to_all(): return lax.all_to_all(value, axes, 0, 0, tiled=True)  50.2 us
    all_to_all x5, starting transfers between devices, to_all(): return lax.all_to_all(value, axes, 0, 0, tiled=True)  36.6 us
    all_to_all x2, blocking collectives, to_all(): return lax.all_to_all(value, axes, 0, 0, tiled=True)  23.6 us
    ppermute x4, starting transfers between devices, per_device(): swapped = lambda v, axis: lax.ppermute(v, axis, [(0, 1), (1, 0)])  18.9 us
    pallas_call x9, Pallas kernels, call(): pl.pallas_call(kernel, name=name, out_shape=[jax.ShapeDtypeStruct(s, t) f...  18.6 us
    unnamed x47, local copies, waits for them, and re-layouts  11.5 us
  transfers between devices with their start and end apart: 11, of which 6 were waited for; matrix products, arithmetic and copies ran while one was open for 1% of the time, Pallas kernels for 5%

profile of v5, /device:TPU:1, one launch (start us, length us, event | category | flops | bytes accessed | tf_op | source)
XLA Modules:
  0.0 175.9 jit_solution(4960288555579151305)
XLA Ops:
  6.6 1.7 all_gather_reshape.3
  12.4 16.2 %all-to-all-start = ((bf16[16,32,640]{2,1,0:T(8,128)(2,1)}), bf16[16,32,640]{2,1,0:T(8,128)(2,1)S(1)}, u32[]{:S(2)}, u32[]{:S(2)}) async-start(bf16[16,32,640]{2,1,0:T(8,128)(2,1)} %get-tuple-element.28), calls=%async_computation | async-start | bytes 1310720 | tf_op jit(solution)/shard_map/all_to_all | solution.py:440
  28.6 7.2 %collective-permute-start.1 = (bf16[96,640]{1,0:T(8,128)(2,1)S(1)}, bf16[96,640]{1,0:T(8,128)(2,1)S(1)}, u32[]{:S(2)}, u32[]{:S(2)}) collective-permute-start(bf16[96,640]{1,0:T(8,128)(2,1)S(1)} %get-tuple-element.29), channel_id=1, source_target_pairs={{0,2},{2,0},{1,3},{3,1},{4,6},{6,4},{5,7},{7,5},{8,10},{10,8},{9,1... | collective-permute-start | bytes 368648 | tf_op jit(solution)/shard_map/ppermute | solution.py:467
  35.8 3.4 %collective-permute-start = (bf16[96,640]{1,0:T(8,128)(2,1)S(1)}, bf16[96,640]{1,0:T(8,128)(2,1)S(1)}, u32[]{:S(2)}, u32[]{:S(2)}) collective-permute-start(bf16[96,640]{1,0:T(8,128)(2,1)S(1)} %get-tuple-element.29), channel_id=1, source_target_pairs={{0,1},{1,0},{2,3},{3,2},{4,5},{5,4},{6,7},{7,6},{8,9},{9,8},{10,11... | collective-permute-start | bytes 368648 | tf_op jit(solution)/shard_map/ppermute | solution.py:467
  39.3 3.3 %collective-permute-start.2 = (bf16[96,640]{1,0:T(8,128)(2,1)S(1)}, bf16[96,640]{1,0:T(8,128)(2,1)S(1)}, u32[]{:S(2)}, u32[]{:S(2)}) collective-permute-start(bf16[96,640]{1,0:T(8,128)(2,1)S(1)} %collective-permute-done.1.two_ref), channel_id=1, source_target_pairs={{0,1},{1,0},{2,3},{3,2},{4,5},{5,4},{6,7},{7,6},{8,9},{9,8},{10,11... | collective-permute-start | bytes 368648 | tf_op jit(solution)/shard_map/ppermute | solution.py:467
  43.5 14.0 %all-to-all-done = bf16[16,32,640]{2,1,0:T(8,128)(2,1)S(1)} async-done(((bf16[16,32,640]{2,1,0:T(8,128)(2,1)}), bf16[16,32,640]{2,1,0:T(8,128)(2,1)S(1)}, u32[]{:S(2)}, u32[]{:S(2)}) %all-to-all-start) | async-done | bytes 655392 | tf_op jit(solution)/shard_map/all_to_all | solution.py:440
  57.5 5.0 %collective-permute-start.3 = (bf16[512,640]{1,0:T(8,128)(2,1)S(1)}, bf16[512,640]{1,0:T(8,128)(2,1)S(1)}, u32[]{:S(2)}, u32[]{:S(2)}) collective-permute-start(bf16[512,640]{1,0:T(8,128)(2,1)S(1)} %bitcast.7), channel_id=1, source_target_pairs={{0,1},{1,0},{2,3},{3,2},{4,5},{5,4},{6,7},{7,6},{8,9},{9,8},{10,11... | collective-permute-start | bytes 1966088 | tf_op jit(solution)/shard_map/ppermute | solution.py:467
  64.1 4.1 %all-to-all-start.1 = ((bf16[8,96,128]{2,1,0:T(8,128)(2,1)}), bf16[8,96,128]{2,1,0:T(8,128)(2,1)S(1)}, u32[]{:S(2)}, u32[]{:S(2)}) async-start(bf16[8,96,128]{2,1,0:T(8,128)(2,1)} %get-tuple-element.33), calls=%async_computation.1 | async-start | bytes 393216 | tf_op jit(solution)/shard_map/all_to_all | solution.py:440
  68.2 9.8 %all-to-all-done.1.heard_ref = bf16[8,96,128]{2,1,0:T(8,128)(2,1)S(1)} async-done(((bf16[8,96,128]{2,1,0:T(8,128)(2,1)}), bf16[8,96,128]{2,1,0:T(8,128)(2,1)S(1)}, u32[]{:S(2)}, u32[]{:S(2)}) %all-to-all-start.1) | async-done | bytes 196640 | tf_op jit(solution)/shard_map/all_to_all | solution.py:440
  78.0 1.5 copy-done.7
  79.5 3.0 %conv0.1 = (f32[4,192,128]{2,1,0:T(8,128)}, bf16[4,32,640]{2,1,0:T(8,128)(2,1)S(1)}, bf16[16,640]{1,0:T(8,128)(2,1)S(1)}, bf16[16,640]{1,0:T(8,128)(2,1)S(1)}) custom-call(s32[2]{0:T(128)S(1)} %pad_add_fusion.place_ref, bf16[8,96,128]{2,1,0:T(8,128)(2,1)S(1)} %all-to-all-done.1.heard_ref, f32[4,32,640]{2,1,0:T(8,128)S(1)} %get-tuple-element.36.state_ref, ...), custom_call_target="tpu_custom_call" | custom-call | flops 1073741824 | bytes 1048576 | tf_op jit(solution)/shard_map/conv0/pallas_call | solution.py:427
  82.5 9.6 %all-to-all-start.2 = ((f32[4,192,128]{2,1,0:T(8,128)}), f32[4,192,128]{2,1,0:T(8,128)S(1)}, u32[]{:S(2)}, u32[]{:S(2)}) async-start(f32[4,192,128]{2,1,0:T(8,128)} %get-tuple-element.38), calls=%async_computation.2 | async-start | bytes 786432 | tf_op jit(solution)/shard_map/all_to_all | solution.py:440
  92.1 12.2 %all-to-all-done.2.conv_ref = f32[4,192,128]{2,1,0:T(8,128)S(1)} async-done(((f32[4,192,128]{2,1,0:T(8,128)}), f32[4,192,128]{2,1,0:T(8,128)S(1)}, u32[]{:S(2)}, u32[]{:S(2)}) %all-to-all-start.2) | async-done | bytes 393248 | tf_op jit(solution)/shard_map/all_to_all | solution.py:440
  104.3 2.0 %hidden0.1 = (f32[4,32,640]{2,1,0:T(8,128)S(1)}, bf16[8,96,128]{2,1,0:T(8,128)(2,1)}) custom-call(s32[2]{0:T(128)S(1)} %pad_add_fusion.place_ref, f32[4,192,128]{2,1,0:T(8,128)S(1)} %all-to-all-done.2.conv_ref, f32[4,32,640]{2,1,0:T(8,128)S(1)} %get-tuple-element.36.state_ref, f32[1,640]{1,0:T(1,128)S(1)} %reshape.35.shift_ref, ...), custom_call_target="tpu_custom_call" | custom-call | flops 268435456 | bytes 1048576 | tf_op jit(solution)/shard_map/hidden0/pallas_call | solution.py:427
  106.3 3.4 %all-to-all-start.3 = ((bf16[8,96,128]{2,1,0:T(8,128)(2,1)}), bf16[8,96,128]{2,1,0:T(8,128)(2,1)S(1)}, u32[]{:S(2)}, u32[]{:S(2)}) async-start(bf16[8,96,128]{2,1,0:T(8,128)(2,1)} %get-tuple-element.41), calls=%async_computation.3 | async-start | bytes 393216 | tf_op jit(solution)/shard_map/all_to_all | solution.py:440
  111.1 7.5 %all-to-all-done.3.heard_ref = bf16[8,96,128]{2,1,0:T(8,128)(2,1)S(1)} async-done(((bf16[8,96,128]{2,1,0:T(8,128)(2,1)}), bf16[8,96,128]{2,1,0:T(8,128)(2,1)S(1)}, u32[]{:S(2)}, u32[]{:S(2)}) %all-to-all-start.3) | async-done | bytes 196640 | tf_op jit(solution)/shard_map/all_to_all | solution.py:440
  120.9 4.1 %attend0.1 = (f32[4,32,640]{2,1,0:T(8,128)S(1)}, f32[8,4,128]{2,1,0:T(4,128)}) custom-call(s32[2]{0:T(128)S(1)} %pad_add_fusion.place_ref, bf16[128,384]{1,0:T(8,128)(2,1)S(1)} %get-tuple-element.43.asked_ref, bf16[128,640]{1,0:T(8,128)(2,1)} %get-tuple-element.44.fresh_ref, f32[4,32,640]{2,1,0:T(8,128)S(1)} %get-tuple-element.42.hidden_ref, ...), custom_call_target="tpu_custom_call" | custom-call | flops 1073741824 | bytes 1048576 | tf_op jit(solution)/shard_map/attend0/pallas_call | solution.py:427
  125.7 3.3 %all-to-all-start.4 = ((f32[8,4,128]{2,1,0:T(4,128)}), f32[8,4,128]{2,1,0:T(4,128)S(1)}, u32[]{:S(2)}, u32[]{:S(2)}) async-start(f32[8,4,128]{2,1,0:T(4,128)} %get-tuple-element.46), calls=%async_computation.4 | async-start | bytes 32768 | tf_op jit(solution)/shard_map/all_to_all | solution.py:440
  129.1 6.7 %all-to-all-done.4.stats_ref = f32[8,4,128]{2,1,0:T(4,128)S(1)} async-done(((f32[8,4,128]{2,1,0:T(4,128)}), f32[8,4,128]{2,1,0:T(4,128)S(1)}, u32[]{:S(2)}, u32[]{:S(2)}) %all-to-all-start.4) | async-done | bytes 16416 | tf_op jit(solution)/shard_map/all_to_all | solution.py:440
  135.8 1.5 copy-done.8
  138.3 2.3 %conv1.1 = (f32[4,48,128]{2,1,0:T(8,128)S(1)}, f32[8,4,128]{2,1,0:T(4,128)S(1)}) custom-call(s32[2]{0:T(128)S(1)} %pad_add_fusion.place_ref, f32[8,4,128]{2,1,0:T(4,128)S(1)} %all-to-all-done.4.stats_ref, bf16[8,96,128]{2,1,0:T(8,128)(2,1)S(1)} %all-to-all-done.3.heard_ref, f32[4,32,640]{2,1,0:T(8,128)S(1)} %copy-done.13, ...), custom_call_target="tpu_custom_call" | custom-call | flops 1073741824 | bytes 1048576 | tf_op jit(solution)/shard_map/conv1/pallas_call | solution.py:427
  140.6 9.0 %all_to_all.35.stats_ref = f32[8,4,128]{2,1,0:T(4,128)S(1)} all-to-all(f32[8,4,128]{2,1,0:T(4,128)S(1)} %get-tuple-element.50), channel_id=1, replica_groups=mesh['req'=16,'y'=8,'zh'=2,'core'=2] {'y'}, dimensions={0} | all-to-all | bytes 32768 | tf_op jit(solution)/shard_map/all_to_all | solution.py:440
  149.6 14.6 %all_to_all.36.conv_ref = f32[4,56,128]{2,1,0:T(8,128)S(1)} all-to-all(f32[4,56,128]{2,1,0:T(8,128)S(1)} %insert1.1), channel_id=1, replica_groups=mesh['req'=16,'y'=8,'zh'=2,'core'=2] {'zh','core'}, dimensions={0} | all-to-all | bytes 229376 | tf_op jit(solution)/shard_map/all_to_all | solution.py:440
  165.5 3.5 %attend1.1 = f32[2,32,640]{2,1,0:T(8,128)} custom-call(s32[2]{0:T(128)S(1)} %pad_add_fusion.place_ref, f32[4,56,128]{2,1,0:T(8,128)S(1)} %all_to_all.36.conv_ref, f32[4,32,640]{2,1,0:T(8,128)S(1)} %copy-done.14, f32[1,640]{1,0:T(1,128)S(1)} %reshape.38.shift_ref, f32[1,640]{1,0:T(1,128)S(1)} %reshape.36.gain_ref, f32[1,640]{1,0:T(1,128)S(1)} %reshape.37.bias_ref, ...), custom_call_target="tpu_custom_call" | custom-call | flops 1073741824 | bytes 1048576 | tf_op jit(solution)/shard_map/attend1/pallas_call | solution.py:427
  (68 shorter events, 13.3 us)
Async XLA Ops:
  6.5 56.1 %copy-start.2 = (f32[2,16,640]{2,1,0:T(8,128)S(1)}, f32[2,16,640]{2,1,0:T(8,128)}, u32[]{:S(2)}) copy-start(f32[2,16,640]{2,1,0:T(8,128)} %param.14) | copy-start | bytes 245764
  6.5 56.1 %copy-start.4 = (bf16[2,16,640]{2,1,0:T(8,128)(2,1)S(1)}, bf16[2,16,640]{2,1,0:T(8,128)(2,1)}, u32[]{:S(2)}) copy-start(bf16[2,16,640]{2,1,0:T(8,128)(2,1)} %param.15) | copy-start | bytes 122884
  6.5 61.6 %copy-start.19 = (f32[640]{0:T(1024)S(1)}, f32[640]{0:T(1024)}, u32[]{:S(2)}) copy-start(f32[640]{0:T(1024)} %param.18) | copy-start | bytes 7684
  6.5 61.7 %copy-start.20 = (f32[640]{0:T(1024)S(1)}, f32[640]{0:T(1024)}, u32[]{:S(2)}) copy-start(f32[640]{0:T(1024)} %param.19) | copy-start | bytes 7684
  6.5 71.5 %all-gather.3.cloned.1.call-start = ((), (), s32[]{:S(2)}) async-start(), calls=%async_computation.7 | async-start | bytes 2119680 | tf_op jit(solution)/shard_map/all_gather | solution.py:470
  12.4 45.1 %all-to-all-start = ((bf16[16,32,640]{2,1,0:T(8,128)(2,1)}), bf16[16,32,640]{2,1,0:T(8,128)(2,1)S(1)}, u32[]{:S(2)}, u32[]{:S(2)}) async-start(bf16[16,32,640]{2,1,0:T(8,128)(2,1)} %get-tuple-element.28), calls=%async_computation | async-start | bytes 1310720 | tf_op jit(solution)/shard_map/all_to_all | solution.py:440
  28.6 10.6 %collective-permute-start.1 = (bf16[96,640]{1,0:T(8,128)(2,1)S(1)}, bf16[96,640]{1,0:T(8,128)(2,1)S(1)}, u32[]{:S(2)}, u32[]{:S(2)}) collective-permute-start(bf16[96,640]{1,0:T(8,128)(2,1)S(1)} %get-tuple-element.29), channel_id=1, source_target_pairs={{0,2},{2,0},{1,3},{3,1},{4,6},{6,4},{5,7},{7,5},{8,10},{10,8},{9,1... | collective-permute-start | bytes 368648 | tf_op jit(solution)/shard_map/ppermute | solution.py:467
  35.8 6.8 %collective-permute-start = (bf16[96,640]{1,0:T(8,128)(2,1)S(1)}, bf16[96,640]{1,0:T(8,128)(2,1)S(1)}, u32[]{:S(2)}, u32[]{:S(2)}) collective-permute-start(bf16[96,640]{1,0:T(8,128)(2,1)S(1)} %get-tuple-element.29), channel_id=1, source_target_pairs={{0,1},{1,0},{2,3},{3,2},{4,5},{5,4},{6,7},{7,6},{8,9},{9,8},{10,11... | collective-permute-start | bytes 368648 | tf_op jit(solution)/shard_map/ppermute | solution.py:467
  39.3 4.3 %collective-permute-start.2 = (bf16[96,640]{1,0:T(8,128)(2,1)S(1)}, bf16[96,640]{1,0:T(8,128)(2,1)S(1)}, u32[]{:S(2)}, u32[]{:S(2)}) collective-permute-start(bf16[96,640]{1,0:T(8,128)(2,1)S(1)} %collective-permute-done.1.two_ref), channel_id=1, source_target_pairs={{0,1},{1,0},{2,3},{3,2},{4,5},{5,4},{6,7},{7,6},{8,9},{9,8},{10,11... | collective-permute-start | bytes 368648 | tf_op jit(solution)/shard_map/ppermute | solution.py:467
  57.5 20.5 %collective-permute-start.3 = (bf16[512,640]{1,0:T(8,128)(2,1)S(1)}, bf16[512,640]{1,0:T(8,128)(2,1)S(1)}, u32[]{:S(2)}, u32[]{:S(2)}) collective-permute-start(bf16[512,640]{1,0:T(8,128)(2,1)S(1)} %bitcast.7), channel_id=1, source_target_pairs={{0,1},{1,0},{2,3},{3,2},{4,5},{5,4},{6,7},{7,6},{8,9},{9,8},{10,11... | collective-permute-start | bytes 1966088 | tf_op jit(solution)/shard_map/ppermute | solution.py:467
  64.1 13.9 %all-to-all-start.1 = ((bf16[8,96,128]{2,1,0:T(8,128)(2,1)}), bf16[8,96,128]{2,1,0:T(8,128)(2,1)S(1)}, u32[]{:S(2)}, u32[]{:S(2)}) async-start(bf16[8,96,128]{2,1,0:T(8,128)(2,1)} %get-tuple-element.33), calls=%async_computation.1 | async-start | bytes 393216 | tf_op jit(solution)/shard_map/all_to_all | solution.py:440
  79.5 12.6 %copy-start.17 = (f32[2,640]{1,0:T(2,128)S(1)}, f32[2,640]{1,0:T(2,128)}, u32[]{:S(2)}) copy-start(f32[2,640]{1,0:T(2,128)} %param.22) | copy-start | bytes 15364
  79.5 12.6 %copy-start.18 = (f32[640]{0:T(1024)S(1)}, f32[640]{0:T(1024)}, u32[]{:S(2)}) copy-start(f32[640]{0:T(1024)} %param.21) | copy-start | bytes 7684
  82.5 21.9 %copy-start.15 = (bf16[4,32,640]{2,1,0:T(8,128)(2,1)}, bf16[4,32,640]{2,1,0:T(8,128)(2,1)S(1)}, u32[]{:S(2)}) copy-start(bf16[4,32,640]{2,1,0:T(8,128)(2,1)S(1)} %get-tuple-element.48.prior_ref) | copy-start | bytes 491524
  82.5 28.6 %copy-start.21 = (f32[640]{0:T(1024)S(1)}, f32[640]{0:T(1024)}, u32[]{:S(2)}) copy-start(f32[640]{0:T(1024)} %param.23) | copy-start | bytes 7684
  82.5 28.6 %copy-start.22 = (f32[640]{0:T(1024)S(1)}, f32[640]{0:T(1024)}, u32[]{:S(2)}) copy-start(f32[640]{0:T(1024)} %param.24) | copy-start | bytes 7684
  82.5 36.1 %copy-start = (bf16[640,640]{1,0:T(8,128)(2,1)S(1)}, bf16[640,640]{1,0:T(8,128)(2,1)}, u32[]{:S(2)}) copy-start(bf16[640,640]{1,0:T(8,128)(2,1)} %keyvalue_ref.3) | copy-start | bytes 2457604
  82.5 21.9 %all-to-all-start.2 = ((f32[4,192,128]{2,1,0:T(8,128)}), f32[4,192,128]{2,1,0:T(8,128)S(1)}, u32[]{:S(2)}, u32[]{:S(2)}) async-start(f32[4,192,128]{2,1,0:T(8,128)} %get-tuple-element.38), calls=%async_computation.2 | async-start | bytes 786432 | tf_op jit(solution)/shard_map/all_to_all | solution.py:440
  106.3 12.2 %all-to-all-start.3 = ((bf16[8,96,128]{2,1,0:T(8,128)(2,1)}), bf16[8,96,128]{2,1,0:T(8,128)(2,1)S(1)}, u32[]{:S(2)}, u32[]{:S(2)}) async-start(bf16[8,96,128]{2,1,0:T(8,128)(2,1)} %get-tuple-element.41), calls=%async_computation.3 | async-start | bytes 393216 | tf_op jit(solution)/shard_map/all_to_all | solution.py:440
  109.7 54.4 %all-gather.5.cloned.1.call-start = ((), (), s32[]{:S(2)}) async-start(), calls=%async_computation.8 | async-start | bytes 1474560 | tf_op jit(solution)/shard_map/all_gather | solution.py:528
  120.9 14.9 %copy-start.16 = (bf16[4,32,640]{2,1,0:T(8,128)(2,1)S(1)}, bf16[4,32,640]{2,1,0:T(8,128)(2,1)}, u32[]{:S(2)}) copy-start(bf16[4,32,640]{2,1,0:T(8,128)(2,1)} %copy-done.15) | copy-start | bytes 491524
  125.7 10.1 %all-to-all-start.4 = ((f32[8,4,128]{2,1,0:T(4,128)}), f32[8,4,128]{2,1,0:T(4,128)S(1)}, u32[]{:S(2)}, u32[]{:S(2)}) async-start(f32[8,4,128]{2,1,0:T(4,128)} %get-tuple-element.46), calls=%async_computation.4 | async-start | bytes 32768 | tf_op jit(solution)/shard_map/all_to_all | solution.py:440
  138.3 25.9 %copy-start.11 = (bf16[320,640]{1,0:T(8,128)(2,1)S(1)}, bf16[320,640]{1,0:T(8,128)(2,1)}, u32[]{:S(2)}) copy-start(bf16[320,640]{1,0:T(8,128)(2,1)} %out_ref.3) | copy-start | bytes 1228804
  138.3 25.9 %copy-start.14 = (f32[4,32,640]{2,1,0:T(8,128)S(1)}, f32[4,32,640]{2,1,0:T(8,128)}, u32[]{:S(2)}) copy-start(f32[4,32,640]{2,1,0:T(8,128)} %copy-done.12) | copy-start | bytes 983044
  (10 other events, 10.2 us)
Sparse Core Ops, SparseCore 0:
  9.4 56.9 all-gather.2
  120.0 31.0 all-gather.4

commit v6 on v5

--- a/solution.py
+++ b/solution.py
@@ -21,9 +21,10 @@
 POSITIONS = 1024
 EPS = 1e-05
 
-PATCH = ("y", "zh", "core")
+Y = ("yh", "yl")
 QUAD = ("zh", "core")
-REQ_PATCH = ("req", "y", "zh", "core")
+REQ_PATCH = ("req", "yh", "yl", "zh", "core")
+PATCH = ("yh", "yl", "zh", "core")
 
 F32 = jnp.float32
 BF16 = jnp.bfloat16
@@ -111,26 +112,24 @@
     return heard_edge(heard_ref, (y - 1) & 7, y > 0), heard_edge(heard_ref, (y + 1) & 7, y < 7)
 
 
-def pack_kernel(field_ref, stale_ref, keys_ref, values_ref, packed_ref, kv_ref):
+def pack_kernel(field_ref, stale_ref, keys_ref, values_ref, packed_ref):
     high, middle, _ = thirds(field_ref[...])
-    packed_ref[0:ROWS] = high
-    packed_ref[ROWS : 2 * ROWS] = middle
-    packed_ref[2 * ROWS :] = stale_ref[...]
     both = jnp.concatenate(
         [keys_ref[...].astype(F32), values_ref[...].astype(F32)], axis=1
     ).astype(BF16)
-    kv_ref[...] = jnp.broadcast_to(both[None], kv_ref.shape)
-
-
-def unpack_kernel(
-    place_ref, field_ref, stale_ref, one_ref, two_ref, three_ref, state_ref, prior_ref, told_ref
-):
-    a = place_ref[1]
-    state_ref[a] = field_ref[...]
-    prior_ref[a] = stale_ref[...]
-    for k, ref in enumerate((one_ref, two_ref, three_ref), 1):
-        state_ref[a ^ k] = ref[0:ROWS].astype(F32) + ref[ROWS : 2 * ROWS].astype(F32)
-        prior_ref[a ^ k] = ref[2 * ROWS :]
+    for to in range(4):
+        packed_ref[to, 0:ROWS] = high
+        packed_ref[to, ROWS : 2 * ROWS] = middle
+        packed_ref[to, 2 * ROWS : 3 * ROWS] = stale_ref[...]
+        packed_ref[to, 3 * ROWS :] = both
+
+
+def unpack_kernel(place_ref, packed_ref, field_ref, state_ref, kv_ref, prior_ref, told_ref):
+    for t in range(4):
+        state_ref[t] = packed_ref[t, 0:ROWS].astype(F32) + packed_ref[t, ROWS : 2 * ROWS].astype(F32)
+        prior_ref[t] = packed_ref[t, 2 * ROWS : 3 * ROWS]
+        kv_ref[t] = packed_ref[t, 3 * ROWS :]
+    state_ref[place_ref[1]] = field_ref[...]
     tell_sums_and_edges(
         state_ref[...].reshape(QUAD_ROWS, CHANNELS),
         place_ref[0],
@@ -140,11 +139,11 @@
     )
 
 
-def activate(sums, edges, state_ref, prior_ref, gain_ref, bias_ref, keep, rows):
+def activate(sums, edges, state_ref, prior_ref, vectors_ref, keep, rows):
     mean, scale = spread_sums(sums, group_matrix())
     above, below = edges
     for t in range(4):
-        value = (state_ref[t] - mean) * scale * gain_ref[...] + bias_ref[...]
+        value = (state_ref[t] - mean) * scale * vectors_ref[0:1] + vectors_ref[1:2]
         act = (value * (1.0 / (1.0 + jnp.exp(-value)))).astype(BF16)
         rows[t, COLS : 3 * COLS] = act
         keep(t, act)
@@ -195,8 +194,7 @@
     state_ref,
     prior_ref,
     weight_ref,
-    gain_ref,
-    bias_ref,
+    vectors_ref,
     out_ref,
     act_ref,
     first_ref,
@@ -212,7 +210,7 @@
             last_ref[...] = act[COLS:]
 
     edges = heard_edges(heard_ref, place_ref[0])
-    activate(heard_sums(heard_ref), edges, state_ref, prior_ref, gain_ref, bias_ref, keep, rows)
+    activate(heard_sums(heard_ref), edges, state_ref, prior_ref, vectors_ref, keep, rows)
     tiles = convolve(rows, weight_ref, wide)
     rest = folded(tiles[1])
     for to in range(4):
@@ -237,9 +235,7 @@
     state_ref,
     prior_ref,
     weight_ref,
-    gain_ref,
-    bias_ref,
-    shift_ref,
+    vectors_ref,
     out_ref,
     told_ref,
     rows,
@@ -251,8 +247,7 @@
         heard_edges(heard_ref, place_ref[0]),
         state_ref,
         prior_ref,
-        gain_ref,
-        bias_ref,
+        vectors_ref,
         lambda t, act: None,
         rows,
     )
@@ -270,7 +265,7 @@
     holds = jnp.where(used & (group == 4 * part + a), 1.0, 0.0).astype(BF16)
     state = state_ref[...].reshape(QUAD_ROWS, CHANNELS)
     hidden = picked(state, select) + (
-        jnp.concatenate(tiles, axis=1) + picked(eight([shift_ref[...]], CHANNELS), select)[0:1]
+        jnp.concatenate(tiles, axis=1) + picked(eight([vectors_ref[5:6]], CHANNELS), select)[0:1]
     )
     sums = eight(
         [jnp.sum(hidden, axis=0, keepdims=True), jnp.sum(hidden * hidden, axis=0, keepdims=True)],
@@ -313,42 +308,37 @@
 
 
 def hidden_kernel(
-    place_ref, conv_ref, state_ref, shift_ref, first_ref, last_ref, hidden_ref, told_ref
+    place_ref, conv_ref, state_ref, vectors_ref, first_ref, last_ref, hidden_ref, told_ref
 ):
     state = state_ref[...].reshape(QUAD_ROWS, CHANNELS)
-    hidden = state + (assembled(conv_ref, QUAD_ROWS) + shift_ref[...])
+    hidden = state + (assembled(conv_ref, QUAD_ROWS) + vectors_ref[4:5])
     hidden_ref[...] = hidden.reshape(hidden_ref.shape)
     tell_sums_and_edges(hidden, place_ref[0], first_ref[...], last_ref[...], told_ref)
 
 
-def project(hidden, mean, scale, gain_ref, bias_ref, query_ref, keyvalue_ref):
-    normed = ((hidden - mean) * scale * gain_ref[...] + bias_ref[...]).astype(BF16)
-    query = dot(normed, query_ref[...]).astype(BF16).astype(F32)
-    query = jnp.concatenate(
-        [query, jnp.zeros((hidden.shape[0], 3 * LANES - WIDTH), F32)], axis=1
-    )
-    return query.astype(BF16), dot(normed, keyvalue_ref[...]).astype(BF16)
+def project(hidden, mean, scale, vectors_ref, query_ref, keyvalue_ref):
+    normed = ((hidden - mean) * scale * vectors_ref[2:3] + vectors_ref[3:4]).astype(BF16)
+    query = dot(normed, query_ref[...]).astype(BF16)
+    return query, dot(normed, keyvalue_ref[...]).astype(BF16)
 
 
 def project_kernel(
-    heard_ref, hidden_ref, gain_ref, bias_ref, query_ref, keyvalue_ref, asked_ref, fresh_ref
+    heard_ref, hidden_ref, vectors_ref, query_ref, keyvalue_ref, asked_ref, fresh_ref
 ):
     mean, scale = spread_sums(heard_sums(heard_ref), group_matrix())
     hidden = hidden_ref[...].reshape(QUAD_ROWS, CHANNELS)
-    asked, fresh = project(hidden, mean, scale, gain_ref, bias_ref, query_ref, keyvalue_ref)
+    asked, fresh = project(hidden, mean, scale, vectors_ref, query_ref, keyvalue_ref)
     asked_ref[...] = asked
     fresh_ref[...] = fresh
 
 
-def attend(query, fresh, patch, y, kvs):
+def attend(query, fresh, patch, y, kv_ref, turned):
     count = query.shape[0]
     lane = lax.broadcasted_iota(jnp.int32, (count, LANES), 1)
     low = lane < HEAD_DIM
 
-    replaced = []
-    for kv_ref, step, first in kvs:
-        block = lax.broadcasted_iota(jnp.int32, (count, kv_ref.shape[0]), 1) >> 5
-        replaced.append(step * block + first == 4 * y + patch)
+    block = lax.broadcasted_iota(jnp.int32, (count, POSITIONS), 1) >> 5
+    replaced = (block ^ turned) == 4 * y + patch
     if count == ROWS:
         theirs = None
     else:
@@ -358,23 +348,19 @@
         at = LANES * (h // 2)
         own = low if h % 2 == 0 else ~low
         asked = jnp.where(own, query[:, at : at + LANES].astype(F32), 0.0).astype(BF16)
-        olds = [
-            jnp.where(own_patch, -jnp.inf, dot(asked, ref[:, at : at + LANES], NT) * HEAD_DIM ** (-0.5))
-            for own_patch, (ref, _, _) in zip(replaced, kvs)
-        ]
+        old = dot(asked, kv_ref[:, at : at + LANES], NT) * HEAD_DIM ** (-0.5)
+        old = jnp.where(replaced, -jnp.inf, old)
         new = dot(asked, fresh[:, at : at + LANES], NT) * HEAD_DIM ** (-0.5)
         if theirs is not None:
             new = jnp.where(theirs, new, -jnp.inf)
-        peak = functools.reduce(
-            jnp.maximum, [jnp.max(e, axis=1, keepdims=True) for e in (*olds, new)]
+        peak = jnp.maximum(
+            jnp.max(old, axis=1, keepdims=True), jnp.max(new, axis=1, keepdims=True)
         )
-        olds = [jnp.exp(old - peak) for old in olds]
+        old = jnp.exp(old - peak)
         new = jnp.exp(new - peak)
-        total = sum(jnp.sum(e, axis=1, keepdims=True) for e in (*olds, new))
+        total = jnp.sum(old, axis=1, keepdims=True) + jnp.sum(new, axis=1, keepdims=True)
         at = LANES * ((HEADS + h) // 2)
-        summed = sum(
-            dot(old.astype(BF16), ref[:, at : at + LANES]) for old, (ref, _, _) in zip(olds, kvs)
-        )
+        summed = dot(old.astype(BF16), kv_ref[:, at : at + LANES])
         summed += dot(new.astype(BF16), fresh[:, at : at + LANES])
         summed = pltpu.roll(summed / total, HEAD_DIM, 1)
         tiles[h // 2] = jnp.where(own, summed, tiles[h // 2])
@@ -382,12 +368,11 @@
 
 
 def attend_quad_kernel(
-    place_ref, asked_ref, fresh_ref, hidden_ref, out_ref, same_ref, other_ref, state_ref, told_ref
-):
-    core = place_ref[1] & 1
-    kvs = ((same_ref, 2, core), (other_ref, 2, 1 - core))
+    place_ref, asked_ref, fresh_ref, hidden_ref, out_ref, kv_ref, state_ref, told_ref
+):
+    turned = 4 * (place_ref[0] & 1)
     patch = lax.broadcasted_iota(jnp.int32, (QUAD_ROWS, 1), 0) >> 5
-    attended = attend(asked_ref[...], fresh_ref[...], patch, place_ref[0], kvs)
+    attended = attend(asked_ref[...], fresh_ref[...], patch, place_ref[0], kv_ref, turned)
     result = hidden_ref[...].reshape(QUAD_ROWS, CHANNELS) + dot(attended, out_ref[...])
     state_ref[...] = result.reshape(state_ref.shape)
     tell_sums(result, group_matrix(), told_ref)
@@ -397,9 +382,7 @@
     place_ref,
     conv_ref,
     state_ref,
-    shift_ref,
-    gain_ref,
-    bias_ref,
+    vectors_ref,
     query_ref,
     keyvalue_ref,
     out_ref,
@@ -408,13 +391,13 @@
 ):
     a = place_ref[1]
     earlier = state_ref[a]
-    hidden = earlier + (assembled(conv_ref, ROWS) + shift_ref[...])
+    hidden = earlier + (assembled(conv_ref, ROWS) + vectors_ref[5:6])
     sums = jnp.zeros((8, LANES), F32)
     for t in range(4):
         sums += conv_ref[t, 48:56]
     mean, scale = spread_sums(sums, group_matrix())
-    query, fresh = project(hidden, mean, scale, gain_ref, bias_ref, query_ref, keyvalue_ref)
-    attended = attend(query, fresh, a, place_ref[0], ((kv_ref, 1, 0),))
+    query, fresh = project(hidden, mean, scale, vectors_ref, query_ref, keyvalue_ref)
+    attended = attend(query, fresh, a, place_ref[0], kv_ref, 0)
     result_ref[0] = earlier
     result_ref[1] = hidden + dot(attended, out_ref[...])
 
@@ -460,51 +443,56 @@
     line = (COLS, CHANNELS)
     stats8 = ((8, 4, LANES), F32)
     told8 = ((8, 6 * COLS, LANES), BF16)
-    y = lax.axis_index("y")
+    y = 2 * lax.axis_index("yh") + lax.axis_index("yl")
     a = 2 * lax.axis_index("zh") + lax.axis_index("core")
     place = jnp.stack([y, a]).astype(jnp.int32)
-    row = lambda v: v.reshape(1, CHANNELS)
-    swapped = lambda v, axis: lax.ppermute(v, axis, [(0, 1), (1, 0)])
 
     slices = conv_weight.transpose(0, 1, 3, 2).reshape(9 * MEMBERS, CHANNELS)
-    weights = lax.all_gather(slices, "y", axis=0, tiled=False)
+    weights = lax.all_gather(slices, Y, axis=0, tiled=False)
 
     own = field.reshape(ROWS, CHANNELS)
-    stale = stale_conv_in.reshape(ROWS, CHANNELS)
-    packed, kv = call(
+    (packed,) = call(
         pack_kernel,
         "pack",
-        [((3 * ROWS, CHANNELS), BF16), ((16, ROWS, CHANNELS), BF16)],
-        (own, stale, stale_keys, stale_values),
-    )
-    across = swapped(packed, "zh")
-    kv, beside, across, corner = lax.optimization_barrier(
-        (
-            to_all(kv, ("y", "zh")),
-            swapped(packed, "core"),
-            across,
-            swapped(across, "core"),
-        )
-    )
-    kv = kv.reshape(16 * ROWS, CHANNELS)
-    state, prior, told = call(
+        [((4, 4 * ROWS, CHANNELS), BF16)],
+        (own, stale_conv_in.reshape(ROWS, CHANNELS), stale_keys, stale_values),
+    )
+    vectors = jnp.stack(
+        [
+            norm1_gain,
+            norm1_bias,
+            norm2_gain,
+            norm2_bias,
+            conv_bias + time_embed[0],
+            conv_bias + time_embed[1],
+            jnp.zeros_like(conv_bias),
+            jnp.zeros_like(conv_bias),
+        ]
+    )
+    w_query = jnp.pad(w_query, ((0, 0), (0, 3 * LANES - WIDTH)))
+    packed, vectors, w_query, place = lax.optimization_barrier(
+        (to_all(packed, QUAD), vectors, w_query, place)
+    )
+    state, kv, prior, told = call(
         unpack_kernel,
         "unpack",
-        [(quad, F32), (quad, BF16), told8],
-        (place, own, stale, beside, across, corner),
+        [(quad, F32), (quad, BF16), (quad, BF16), told8],
+        (place, packed, own),
         scalars=1,
     )
-    norm1 = (row(norm1_gain), row(norm1_bias))
-    norm2 = (row(norm2_gain), row(norm2_bias))
+    kv = kv.reshape(QUAD_ROWS, CHANNELS)
+    told, partner = lax.optimization_barrier(
+        (to_all(told, Y), lax.ppermute(kv, "yl", [(0, 1), (1, 0)]))
+    )
+    pair = jnp.concatenate([kv, partner], axis=0)
+    old = lax.all_gather(pair, "yh", axis=0, tiled=True)
     buffers = [pltpu.VMEM((4, 64, CHANNELS), BF16), pltpu.VMEM((256, 256), F32)]
 
-    told, other = lax.optimization_barrier((to_all(told, "y"), swapped(kv, "core")))
-    olds = (kv, other)
     conv, prior, first, last = call(
         conv_quad_kernel,
         "conv0",
         [((4, LANES + 64, LANES), F32), (quad, BF16), (line, BF16), (line, BF16)],
-        (place, told, state, prior, weights, *norm1),
+        (place, told, state, prior, weights, vectors),
         scalars=1,
         scratch=buffers,
         flops=1 << 30,
@@ -513,33 +501,32 @@
         hidden_kernel,
         "hidden0",
         [(quad, F32), told8],
-        (place, to_all(conv, QUAD), state, row(conv_bias + time_embed[0]), first, last),
+        (place, to_all(conv, QUAD), state, vectors, first, last),
         scalars=1,
         flops=1 << 28,
     )
-    heard = to_all(told, "y")
+    heard = to_all(told, Y)
     asked, fresh = call(
         project_kernel,
         "project0",
         [((QUAD_ROWS, 3 * LANES), BF16), ((QUAD_ROWS, CHANNELS), BF16)],
-        (heard, hidden, *norm2, w_query, w_keyvalue),
+        (heard, hidden, vectors, w_query, w_keyvalue),
         flops=1 << 28,
     )
-    kv = lax.all_gather(fresh, "y", axis=0, tiled=True)
+    kv = lax.all_gather(fresh, Y, axis=0, tiled=True)
     state, stats = call(
         attend_quad_kernel,
         "attend0",
         [(quad, F32), stats8],
-        (place, asked, fresh, hidden, w_out, *olds),
+        (place, asked, fresh, hidden, w_out, old),
         scalars=1,
         flops=1 << 30,
     )
-    shift = row(conv_bias + time_embed[1])
     conv, stats = call(
         conv_own_kernel,
         "conv1",
         [((4, ROWS + ROWS // 2, LANES), F32), stats8],
-        (place, to_all(stats, "y"), heard, state, prior, weights, *norm1, shift),
+        (place, to_all(stats, Y), heard, state, prior, weights, vectors),
         scalars=1,
         scratch=buffers,
         flops=1 << 30,
@@ -548,14 +535,14 @@
         insert_kernel,
         "insert1",
         [((4, 56, LANES), F32)],
-        (conv, to_all(stats, "y")),
+        (conv, to_all(stats, Y)),
         flops=1 << 24,
     )
     (out,) = call(
         attend_own_kernel,
         "attend1",
         [((2, ROWS, CHANNELS), F32)],
-        (place, to_all(conv, QUAD), state, shift, *norm2, w_query, w_keyvalue, w_out, kv),
+        (place, to_all(conv, QUAD), state, vectors, w_query, w_keyvalue, w_out, kv),
         scalars=1,
         flops=1 << 30,
     )
@@ -564,7 +551,7 @@
 
 def solution(mesh):
     torus = Mesh(
-        mesh.devices.reshape(mesh.shape["req"], 8, 2, 2), ("req", "y", "zh", "core")
+        mesh.devices.reshape(mesh.shape["req"], 4, 2, 2, 2), REQ_PATCH
     )
     placed = (
         P(REQ_PATCH, None, None),

time: 178 us -> 166 us (0.933)
  blocking collectives: 23.6 us -> 82.2 us
  starting transfers between devices: 55.5 us -> 22 us
  waiting for transfers between devices: 51.2 us -> 20.6 us
  local copies, waits for them, and re-layouts: 13.3 us -> 9.5 us
  Pallas kernels: 18.6 us -> 16.7 us
    all_to_all x2 -> x5, blocking collectives: 23.6 us -> 82.2 us  [to_all(): return lax.all_to_all(value, axes, 0, 0, tiled=True)]
    all_to_all x5 -> x2, waiting for transfers between devices: 50.2 us -> 12.8 us  [to_all(): return lax.all_to_all(value, axes, 0, 0, tiled=True)]
    all_to_all x5 -> x2, starting transfers between devices: 36.6 us -> 18.6 us  [to_all(): return lax.all_to_all(value, axes, 0, 0, tiled=True)]
    ppermute x4 -> x1, starting transfers between devices: 18.9 us -> 3.32 us  [per_device(): lax.ppermute(kv, 'yl', [(0, 1), (1, 0)])]
    ppermute x4 -> x1, waiting for transfers between devices: 0.95 us -> 6.99 us  [per_device(): lax.ppermute(kv, 'yl', [(0, 1), (1, 0)])]
    unnamed x47 -> x37, local copies, waits for them, and re-layouts: 11.5 us -> 7.62 us
    pallas_call x9, Pallas kernels: 18.6 us -> 16.7 us  [call(): pl.pallas_call(kernel, name=name, out_shape=[jax.ShapeDtypeStruct(s, t) f...]
  transfers between devices with their start and end apart: 11 -> 6, of which waited for: 6 -> 4; matrix products, arithmetic and copies ran while one was open for 1% -> 1% of each run, Pallas kernels for 5% -> 8%
where the time goes in v6:
time: 166 us; the launch traced here: 165 us
  blocking collectives  82.2 us (50%)
  starting transfers between devices  22 us (13%)
  waiting for transfers between devices  20.6 us (12%)
  Pallas kernels  16.7 us (10%)
  between operations  13.3 us (8%)
  local copies, waits for them, and re-layouts  9.5 us (6%)
    all_to_all x5, blocking collectives, to_all(): return lax.all_to_all(value, axes, 0, 0, tiled=True)  82.2 us
    all_to_all x2, starting transfers between devices, to_all(): return lax.all_to_all(value, axes, 0, 0, tiled=True)  18.6 us
    pallas_call x9, Pallas kernels, call(): pl.pallas_call(kernel, name=name, out_shape=[jax.ShapeDtypeStruct(s, t) f...  16.7 us
    all_to_all x2, waiting for transfers between devices, to_all(): return lax.all_to_all(value, axes, 0, 0, tiled=True)  12.8 us
    unnamed x37, local copies, waits for them, and re-layouts  7.62 us
    ppermute x1, waiting for transfers between devices, per_device(): lax.ppermute(kv, 'yl', [(0, 1), (1, 0)])  6.99 us
  transfers between devices with their start and end apart: 6, of which 4 were waited for; matrix products, arithmetic and copies ran while one was open for 1% of the time, Pallas kernels for 8%

profile of v6, /device:TPU:1, one launch (start us, length us, event | category | flops | bytes accessed | tf_op | source)
XLA Modules:
  0.0 165.2 jit_solution(9655323116939277530)
XLA Ops:
  6.5 1.7 %all_gather_reshape.3 = bf16[1,180,640]{2,1,0:T(8,128)(2,1)} reshape(bf16[3,3,20,640]{3,2,1,0:T(8,128)(2,1)} %bitcast.12) | data formatting | bytes 460800 | tf_op jit(solution)/shard_map/all_gather;reshape | solution.py:451
  8.3 0.9 copy-done.1
  9.3 0.8 copy-done.3
  11.5 0.9 pack.1
  12.4 11.8 %all-to-all-start = ((bf16[4,128,640]{2,1,0:T(8,128)(2,1)}), bf16[4,128,640]{2,1,0:T(8,128)(2,1)S(1)}, u32[]{:S(2)}, u32[]{:S(2)}) async-start(bf16[4,128,640]{2,1,0:T(8,128)(2,1)} %pack.1), calls=%async_computation | async-start | bytes 1310720 | tf_op jit(solution)/shard_map/all_to_all | solution.py:423
  24.9 12.7 %all-to-all-done.packed_ref = bf16[4,128,640]{2,1,0:T(8,128)(2,1)S(1)} async-done(((bf16[4,128,640]{2,1,0:T(8,128)(2,1)}), bf16[4,128,640]{2,1,0:T(8,128)(2,1)S(1)}, u32[]{:S(2)}, u32[]{:S(2)}) %all-to-all-start) | async-done | bytes 655392 | tf_op jit(solution)/shard_map/all_to_all | solution.py:423
  37.6 1.5 unpack.1
  39.1 6.8 %all-to-all-start.1 = ((bf16[8,96,128]{2,1,0:T(8,128)(2,1)}), bf16[8,96,128]{2,1,0:T(8,128)(2,1)S(1)}, u32[]{:S(2)}, u32[]{:S(2)}) async-start(bf16[8,96,128]{2,1,0:T(8,128)(2,1)} %get-tuple-element.29), calls=%async_computation.1 | async-start | bytes 393216 | tf_op jit(solution)/shard_map/all_to_all | solution.py:423
  46.0 3.3 %collective-permute-start = (bf16[128,640]{1,0:T(8,128)(2,1)S(1)}, bf16[128,640]{1,0:T(8,128)(2,1)S(1)}, u32[]{:S(2)}, u32[]{:S(2)}) collective-permute-start(bf16[128,640]{1,0:T(8,128)(2,1)S(1)} %bitcast.9), channel_id=1, source_target_pairs={{0,4},{4,0},{1,5},{5,1},{2,6},{6,2},{3,7},{7,3},{8,12},{12,8},{9,1... | collective-permute-start | bytes 491528 | tf_op jit(solution)/shard_map/ppermute | solution.py:485
  49.3 7.0 %collective-permute-done = bf16[128,640]{1,0:T(8,128)(2,1)S(1)} collective-permute-done((bf16[128,640]{1,0:T(8,128)(2,1)S(1)}, bf16[128,640]{1,0:T(8,128)(2,1)S(1)}, u32[]{:S(2)}, u32[]{:S(2)}) %collective-permute-start) | collective-permute-done | bytes 163872 | tf_op jit(solution)/shard_map/ppermute | solution.py:485
  57.2 1.5 copy-done.6
  58.7 2.2 %conv0.1 = (f32[4,192,128]{2,1,0:T(8,128)S(1)}, bf16[4,32,640]{2,1,0:T(8,128)(2,1)S(1)}, bf16[16,640]{1,0:T(8,128)(2,1)S(1)}, bf16[16,640]{1,0:T(8,128)(2,1)S(1)}) custom-call(s32[2]{0:T(128)S(1)} %pad_add_fusion.place_ref, bf16[8,96,128]{2,1,0:T(8,128)(2,1)S(1)} %all-to-all-done.1.heard_ref, f32[4,32,640]{2,1,0:T(8,128)S(1)} %get-tuple-element.32.state_ref, ...), custom_call_target="tpu_custom_call" | custom-call | flops 1073741824 | bytes 1048576 | tf_op jit(solution)/shard_map/conv0/pallas_call | solution.py:410
  61.0 25.7 %all_to_all.35.conv_ref = f32[4,192,128]{2,1,0:T(8,128)S(1)} all-to-all(f32[4,192,128]{2,1,0:T(8,128)S(1)} %get-tuple-element.35), channel_id=1, replica_groups=mesh['req'=16,'yh'=4,'yl'=2,'zh'=2,'core'=2] {'zh','core'}, dimensions={0} | all-to-all | bytes 786432 | tf_op jit(solution)/shard_map/all_to_all | solution.py:423
  86.7 1.3 hidden0.1
  88.0 19.0 %all_to_all.36.heard_ref = bf16[8,96,128]{2,1,0:T(8,128)(2,1)S(1)} all-to-all(bf16[8,96,128]{2,1,0:T(8,128)(2,1)S(1)} %get-tuple-element.38), channel_id=1, replica_groups=mesh['req'=16,'yh'=4,'yl'=2,'zh'=2,'core'=2] {'yh','yl'}, dimensions={0} | all-to-all | bytes 393216 | tf_op jit(solution)/shard_map/all_to_all | solution.py:423
  107.0 1.2 project0.1
  109.0 1.3 copy-done.8
  110.3 3.7 %attend0.1 = (f32[4,32,640]{2,1,0:T(8,128)S(1)}, f32[8,4,128]{2,1,0:T(4,128)S(1)}) custom-call(s32[2]{0:T(128)S(1)} %pad_add_fusion.place_ref, bf16[128,384]{1,0:T(8,128)(2,1)S(1)} %get-tuple-element.41.asked_ref, bf16[128,640]{1,0:T(8,128)(2,1)} %get-tuple-element.42.fresh_ref, f32[4,32,640]{2,1,0:T(8,128)S(1)} %get-tuple-element.39.hidden_ref, ...), custom_call_target="tpu_custom_call" | custom-call | flops 1073741824 | bytes 1048576 | tf_op jit(solution)/shard_map/attend0/pallas_call | solution.py:410
  114.0 9.9 %all_to_all.37.stats_ref = f32[8,4,128]{2,1,0:T(4,128)S(1)} all-to-all(f32[8,4,128]{2,1,0:T(4,128)S(1)} %get-tuple-element.44), channel_id=1, replica_groups=mesh['req'=16,'yh'=4,'yl'=2,'zh'=2,'core'=2] {'yh','yl'}, dimensions={0} | all-to-all | bytes 32768 | tf_op jit(solution)/shard_map/all_to_all | solution.py:423
  123.9 2.3 %conv1.1 = (f32[4,48,128]{2,1,0:T(8,128)S(1)}, f32[8,4,128]{2,1,0:T(4,128)S(1)}) custom-call(s32[2]{0:T(128)S(1)} %pad_add_fusion.place_ref, f32[8,4,128]{2,1,0:T(4,128)S(1)} %all_to_all.37.stats_ref, bf16[8,96,128]{2,1,0:T(8,128)(2,1)S(1)} %all_to_all.36.heard_ref, f32[4,32,640]{2,1,0:T(8,128)S(1)} %get-tuple-element.45.state_ref, ...), custom_call_target="tpu_custom_call" | custom-call | flops 1073741824 | bytes 1048576 | tf_op jit(solution)/shard_map/conv1/pallas_call | solution.py:410
  126.2 9.0 %all_to_all.38.stats_ref = f32[8,4,128]{2,1,0:T(4,128)S(1)} all-to-all(f32[8,4,128]{2,1,0:T(4,128)S(1)} %get-tuple-element.48), channel_id=1, replica_groups=mesh['req'=16,'yh'=4,'yl'=2,'zh'=2,'core'=2] {'yh','yl'}, dimensions={0} | all-to-all | bytes 32768 | tf_op jit(solution)/shard_map/all_to_all | solution.py:423
  135.3 18.6 %all_to_all.39.conv_ref = f32[4,56,128]{2,1,0:T(8,128)S(1)} all-to-all(f32[4,56,128]{2,1,0:T(8,128)S(1)} %insert1.1), channel_id=1, replica_groups=mesh['req'=16,'yh'=4,'yl'=2,'zh'=2,'core'=2] {'zh','core'}, dimensions={0} | all-to-all | bytes 229376 | tf_op jit(solution)/shard_map/all_to_all | solution.py:423
  153.8 1.3 copy-done.9
  155.1 3.5 %attend1.1 = f32[2,32,640]{2,1,0:T(8,128)} custom-call(s32[2]{0:T(128)S(1)} %pad_add_fusion.place_ref, f32[4,56,128]{2,1,0:T(8,128)S(1)} %all_to_all.39.conv_ref, f32[4,32,640]{2,1,0:T(8,128)S(1)} %get-tuple-element.45.state_ref, f32[8,640]{1,0:T(8,128)S(1)} %stack.40.vectors_ref, bf16[640,384]{1,0:T(8,128)(2,1)S(1)} %pad.4.query_ref, ...), custom_call_target="tpu_custom_call" | custom-call | flops 1073741824 | bytes 1048576 | tf_op jit(solution)/shard_map/attend1/pallas_call | solution.py:410
  (56 shorter events, 3.8 us)
Async XLA Ops:
  6.5 50.7 %all-gather.4.cloned.1.call-start = ((), (), s32[]{:S(2)}) async-start(), calls=%async_computation.7 | async-start | bytes 2119680 | tf_op jit(solution)/shard_map/all_gather | solution.py:451
  6.5 17.8 %copy-start.11 = (bf16[640,320]{0,1:T(8,128)(2,1)S(1)}, bf16[640,320]{0,1:T(8,128)(2,1)}, u32[]{:S(2)}) copy-start(bf16[640,320]{0,1:T(8,128)(2,1)} %param.25) | copy-start | bytes 1228804
  8.3 15.9 %copy-start.14 = (f32[640]{0:T(1024)S(1)}, f32[640]{0:T(1024)}, u32[]{:S(2)}) copy-start(f32[640]{0:T(1024)} %param.18) | copy-start | bytes 7684
  8.3 15.9 %copy-start.15 = (f32[640]{0:T(1024)S(1)}, f32[640]{0:T(1024)}, u32[]{:S(2)}) copy-start(f32[640]{0:T(1024)} %param.19) | copy-start | bytes 7684
  8.3 16.0 %copy-start.16 = (f32[640]{0:T(1024)S(1)}, f32[640]{0:T(1024)}, u32[]{:S(2)}) copy-start(f32[640]{0:T(1024)} %param.23) | copy-start | bytes 7684
  8.3 16.0 %copy-start.17 = (f32[640]{0:T(1024)S(1)}, f32[640]{0:T(1024)}, u32[]{:S(2)}) copy-start(f32[640]{0:T(1024)} %param.24) | copy-start | bytes 7684
  8.3 16.0 %copy-start.12 = (f32[2,640]{1,0:T(2,128)S(1)}, f32[2,640]{1,0:T(2,128)}, u32[]{:S(2)}) copy-start(f32[2,640]{1,0:T(2,128)} %param.22) | copy-start | bytes 15364
  8.3 16.0 %copy-start.13 = (f32[640]{0:T(1024)S(1)}, f32[640]{0:T(1024)}, u32[]{:S(2)}) copy-start(f32[640]{0:T(1024)} %param.21) | copy-start | bytes 7684
  8.3 0.9 copy-start.1
  9.3 0.8 copy-start.3
  10.0 0.7 copy-start.4
  10.8 0.7 copy-start.5
  12.4 25.1 %all-to-all-start = ((bf16[4,128,640]{2,1,0:T(8,128)(2,1)}), bf16[4,128,640]{2,1,0:T(8,128)(2,1)S(1)}, u32[]{:S(2)}, u32[]{:S(2)}) async-start(bf16[4,128,640]{2,1,0:T(8,128)(2,1)} %pack.1), calls=%async_computation | async-start | bytes 1310720 | tf_op jit(solution)/shard_map/all_to_all | solution.py:423
  24.2 13.4 %copy-start.2 = (f32[2,16,640]{2,1,0:T(8,128)S(1)}, f32[2,16,640]{2,1,0:T(8,128)}, u32[]{:S(2)}) copy-start(f32[2,16,640]{2,1,0:T(8,128)} %param.14) | copy-start | bytes 245764
  39.1 17.3 %all-to-all-start.1 = ((bf16[8,96,128]{2,1,0:T(8,128)(2,1)}), bf16[8,96,128]{2,1,0:T(8,128)(2,1)S(1)}, u32[]{:S(2)}, u32[]{:S(2)}) async-start(bf16[8,96,128]{2,1,0:T(8,128)(2,1)} %get-tuple-element.29), calls=%async_computation.1 | async-start | bytes 393216 | tf_op jit(solution)/shard_map/all_to_all | solution.py:423
  45.9 63.1 %all-gather.6.cloned.1.call-start = ((), (), s32[]{:S(2)}) async-start(), calls=%async_computation.8 | async-start | bytes 1638400 | tf_op jit(solution)/shard_map/all_gather | solution.py:488
  46.0 10.3 %collective-permute-start = (bf16[128,640]{1,0:T(8,128)(2,1)S(1)}, bf16[128,640]{1,0:T(8,128)(2,1)S(1)}, u32[]{:S(2)}, u32[]{:S(2)}) collective-permute-start(bf16[128,640]{1,0:T(8,128)(2,1)S(1)} %bitcast.9), channel_id=1, source_target_pairs={{0,4},{4,0},{1,5},{5,1},{2,6},{6,2},{3,7},{7,3},{8,12},{12,8},{9,1... | collective-permute-start | bytes 491528 | tf_op jit(solution)/shard_map/ppermute | solution.py:485
  57.2 96.7 %all-gather.8.cloned.1.call-start = ((), (), s32[]{:S(2)}) async-start(), calls=%async_computation.9 | async-start | bytes 1474560 | tf_op jit(solution)/shard_map/all_gather | solution.py:516
  57.2 1.5 copy-start.6
  61.0 46.0 %copy-start = (bf16[640,640]{1,0:T(8,128)(2,1)S(1)}, bf16[640,640]{1,0:T(8,128)(2,1)}, u32[]{:S(2)}) copy-start(bf16[640,640]{1,0:T(8,128)(2,1)} %keyvalue_ref.3) | copy-start | bytes 2457604
  88.0 21.0 %copy-start.10 = (bf16[320,640]{1,0:T(8,128)(2,1)S(1)}, bf16[320,640]{1,0:T(8,128)(2,1)}, u32[]{:S(2)}) copy-start(bf16[320,640]{1,0:T(8,128)(2,1)} %out_ref.3) | copy-start | bytes 1228804
  109.0 1.3 copy-start.8
  110.3 13.6 %copy-start.7 = (bf16[8,180,640]{2,1,0:T(8,128)(2,1)S(1)}, bf16[8,180,640]{2,1,0:T(8,128)(2,1)}, u32[]{:S(2)}) copy-start(bf16[8,180,640]{2,1,0:T(8,128)(2,1)} %all-gather.4.cloned.1.call-done.weight_ref) | copy-start | bytes 5529604
  153.8 1.3 copy-start.9
Sparse Core Ops, SparseCore 0:
  9.4 45.8 all-gather.3
  57.4 51.5 all-gather.5
  111.1 35.5 all-gather.7

commit v7 on v6

--- a/solution.py
+++ b/solution.py
@@ -231,7 +231,8 @@
 def conv_own_kernel(
     place_ref,
     stats_ref,
-    heard_ref,
+    above_ref,
+    below_ref,
     state_ref,
     prior_ref,
     weight_ref,
@@ -244,7 +245,7 @@
     a = place_ref[1]
     activate(
         jnp.sum(stats_ref[...], axis=0),
-        heard_edges(heard_ref, place_ref[0]),
+        (above_ref[...], below_ref[...]),
         state_ref,
         prior_ref,
         vectors_ref,
@@ -307,13 +308,11 @@
     return jnp.concatenate(tiles, axis=1)
 
 
-def hidden_kernel(
-    place_ref, conv_ref, state_ref, vectors_ref, first_ref, last_ref, hidden_ref, told_ref
-):
+def hidden_kernel(conv_ref, state_ref, vectors_ref, hidden_ref, stats_ref):
     state = state_ref[...].reshape(QUAD_ROWS, CHANNELS)
     hidden = state + (assembled(conv_ref, QUAD_ROWS) + vectors_ref[4:5])
     hidden_ref[...] = hidden.reshape(hidden_ref.shape)
-    tell_sums_and_edges(hidden, place_ref[0], first_ref[...], last_ref[...], told_ref)
+    tell_sums(hidden, group_matrix(), stats_ref)
 
 
 def project(hidden, mean, scale, vectors_ref, query_ref, keyvalue_ref):
@@ -323,22 +322,22 @@
 
 
 def project_kernel(
-    heard_ref, hidden_ref, vectors_ref, query_ref, keyvalue_ref, asked_ref, fresh_ref
+    stats_ref, hidden_ref, vectors_ref, query_ref, keyvalue_ref, asked_ref, fresh_ref
 ):
-    mean, scale = spread_sums(heard_sums(heard_ref), group_matrix())
+    mean, scale = mean_and_scale(stats_ref, group_matrix())
     hidden = hidden_ref[...].reshape(QUAD_ROWS, CHANNELS)
     asked, fresh = project(hidden, mean, scale, vectors_ref, query_ref, keyvalue_ref)
     asked_ref[...] = asked
     fresh_ref[...] = fresh
 
 
-def attend(query, fresh, patch, y, kv_ref, turned):
+def attend(query, fresh, patch, y, kv_ref):
     count = query.shape[0]
     lane = lax.broadcasted_iota(jnp.int32, (count, LANES), 1)
     low = lane < HEAD_DIM
 
     block = lax.broadcasted_iota(jnp.int32, (count, POSITIONS), 1) >> 5
-    replaced = (block ^ turned) == 4 * y + patch
+    replaced = block == 4 * y + patch
     if count == ROWS:
         theirs = None
     else:
@@ -370,9 +369,8 @@
 def attend_quad_kernel(
     place_ref, asked_ref, fresh_ref, hidden_ref, out_ref, kv_ref, state_ref, told_ref
 ):
-    turned = 4 * (place_ref[0] & 1)
     patch = lax.broadcasted_iota(jnp.int32, (QUAD_ROWS, 1), 0) >> 5
-    attended = attend(asked_ref[...], fresh_ref[...], patch, place_ref[0], kv_ref, turned)
+    attended = attend(asked_ref[...], fresh_ref[...], patch, place_ref[0], kv_ref)
     result = hidden_ref[...].reshape(QUAD_ROWS, CHANNELS) + dot(attended, out_ref[...])
     state_ref[...] = result.reshape(state_ref.shape)
     tell_sums(result, group_matrix(), told_ref)
@@ -397,7 +395,7 @@
         sums += conv_ref[t, 48:56]
     mean, scale = spread_sums(sums, group_matrix())
     query, fresh = project(hidden, mean, scale, vectors_ref, query_ref, keyvalue_ref)
-    attended = attend(query, fresh, a, place_ref[0], kv_ref, 0)
+    attended = attend(query, fresh, a, place_ref[0], kv_ref)
     result_ref[0] = earlier
     result_ref[1] = hidden + dot(attended, out_ref[...])
 
@@ -481,36 +479,36 @@
         scalars=1,
     )
     kv = kv.reshape(QUAD_ROWS, CHANNELS)
-    told, partner = lax.optimization_barrier(
-        (to_all(told, Y), lax.ppermute(kv, "yl", [(0, 1), (1, 0)]))
-    )
-    pair = jnp.concatenate([kv, partner], axis=0)
-    old = lax.all_gather(pair, "yh", axis=0, tiled=True)
+    old = lax.all_gather(kv, Y, axis=0, tiled=True)
     buffers = [pltpu.VMEM((4, 64, CHANNELS), BF16), pltpu.VMEM((256, 256), F32)]
 
     conv, prior, first, last = call(
         conv_quad_kernel,
         "conv0",
         [((4, LANES + 64, LANES), F32), (quad, BF16), (line, BF16), (line, BF16)],
-        (place, told, state, prior, weights, vectors),
+        (place, to_all(told, Y), state, prior, weights, vectors),
         scalars=1,
         scratch=buffers,
         flops=1 << 30,
     )
-    hidden, told = call(
+    hidden, stats = call(
         hidden_kernel,
         "hidden0",
-        [(quad, F32), told8],
-        (place, to_all(conv, QUAD), state, vectors, first, last),
-        scalars=1,
+        [(quad, F32), stats8],
+        (to_all(conv, QUAD), state, vectors),
         flops=1 << 28,
     )
-    heard = to_all(told, Y)
+    up = [(i, i + 1) for i in range(7)]
+    down = [(i + 1, i) for i in range(7)]
+    last, first, hidden, stats = lax.optimization_barrier((last, first, hidden, stats))
+    stats, above, below = lax.optimization_barrier(
+        (to_all(stats, Y), lax.ppermute(last, Y, up), lax.ppermute(first, Y, down))
+    )
     asked, fresh = call(
         project_kernel,
         "project0",
         [((QUAD_ROWS, 3 * LANES), BF16), ((QUAD_ROWS, CHANNELS), BF16)],
-        (heard, hidden, vectors, w_query, w_keyvalue),
+        (stats, hidden, vectors, w_query, w_keyvalue),
         flops=1 << 28,
     )
     kv = lax.all_gather(fresh, Y, axis=0, tiled=True)
@@ -526,7 +524,7 @@
         conv_own_kernel,
         "conv1",
         [((4, ROWS + ROWS // 2, LANES), F32), stats8],
-        (place, to_all(stats, Y), heard, state, prior, weights, vectors),
+        (place, to_all(stats, Y), above, below, state, prior, weights, vectors),
         scalars=1,
         scratch=buffers,
         flops=1 << 30,

time: 166 us -> 160 us (0.964)
  waiting for transfers between devices: 20.6 us -> 16.6 us
  starting transfers between devices: 22 us -> 20.1 us
    ppermute x1 -> x2, waiting for transfers between devices: 6.99 us -> 3.79 us  [the longest x1 3.78 us: per_device(): lax.ppermute(first, Y, down)]
    all_to_all x2, starting transfers between devices: 18.6 us -> 15.4 us  [to_all(): return lax.all_to_all(value, axes, 0, 0, tiled=True)]
    ppermute x1 -> x2, starting transfers between devices: 3.32 us -> 4.6 us  [the longest x1 3.31 us: per_device(): lax.ppermute(last, Y, up)]
  transfers between devices with their start and end apart: 6 -> 7, of which waited for: 4 -> 2; matrix products, arithmetic and copies ran while one was open for 1% -> 0% of each run, Pallas kernels for 8% -> 8%
where the time goes in v7:
time: 160 us
  blocking collectives  83.4 us (52%)
  starting transfers between devices  20.1 us (13%)
  Pallas kernels  16.7 us (10%)
  waiting for transfers between devices  16.6 us (10%)
  between operations  13.3 us (8%)
  local copies, waits for them, and re-layouts  9.5 us (6%)
    all_to_all x5, blocking collectives, to_all(): return lax.all_to_all(value, axes, 0, 0, tiled=True)  83.4 us
    pallas_call x9, Pallas kernels, call(): pl.pallas_call(kernel, name=name, out_shape=[jax.ShapeDtypeStruct(s, t) f...  16.7 us
    all_to_all x2, starting transfers between devices, to_all(): return lax.all_to_all(value, axes, 0, 0, tiled=True)  15.4 us
    all_to_all x2, waiting for transfers between devices, to_all(): return lax.all_to_all(value, axes, 0, 0, tiled=True)  12.7 us
    unnamed x37, local copies, waits for them, and re-layouts  7.62 us
    ppermute x1, waiting for transfers between devices, per_device(): lax.ppermute(first, Y, down)  3.78 us
    ppermute x1, starting transfers between devices, per_device(): lax.ppermute(last, Y, up)  3.31 us
  transfers between devices with their start and end apart: 7, of which 2 were waited for; matrix products, arithmetic and copies ran while one was open for 0% of the time, Pallas kernels for 8%

profile of v7, /device:TPU:1, one launch (start us, length us, event | category | flops | bytes accessed | tf_op | source)
XLA Modules:
  0.0 159.6 jit_solution(17502294672539133697)
XLA Ops:
  6.5 1.7 %all_gather_reshape.3 = bf16[1,180,640]{2,1,0:T(8,128)(2,1)} reshape(bf16[3,3,20,640]{3,2,1,0:T(8,128)(2,1)} %bitcast.10) | data formatting | bytes 460800 | tf_op jit(solution)/shard_map/all_gather;reshape | solution.py:449
  8.3 0.9 copy-done.1
  11.5 0.9 pack.1
  12.5 11.8 %all-to-all-start = ((bf16[4,128,640]{2,1,0:T(8,128)(2,1)}), bf16[4,128,640]{2,1,0:T(8,128)(2,1)S(1)}, u32[]{:S(2)}, u32[]{:S(2)}) async-start(bf16[4,128,640]{2,1,0:T(8,128)(2,1)} %pack.1), calls=%async_computation | async-start | bytes 1310720 | tf_op jit(solution)/shard_map/all_to_all | solution.py:421
  24.9 12.7 %all-to-all-done.packed_ref = bf16[4,128,640]{2,1,0:T(8,128)(2,1)S(1)} async-done(((bf16[4,128,640]{2,1,0:T(8,128)(2,1)}), bf16[4,128,640]{2,1,0:T(8,128)(2,1)S(1)}, u32[]{:S(2)}, u32[]{:S(2)}) %all-to-all-start) | async-done | bytes 655392 | tf_op jit(solution)/shard_map/all_to_all | solution.py:421
  37.6 1.4 unpack.1
  39.0 17.3 %all_to_all.35.heard_ref = bf16[8,96,128]{2,1,0:T(8,128)(2,1)S(1)} all-to-all(bf16[8,96,128]{2,1,0:T(8,128)(2,1)S(1)} %get-tuple-element.34), channel_id=1, replica_groups=mesh['req'=16,'yh'=4,'yl'=2,'zh'=2,'core'=2] {'yh','yl'}, dimensions={0} | all-to-all | bytes 393216 | tf_op jit(solution)/shard_map/all_to_all | solution.py:421
  56.3 1.5 copy-done.6
  57.8 2.2 %conv0.1 = (f32[4,192,128]{2,1,0:T(8,128)S(1)}, bf16[4,32,640]{2,1,0:T(8,128)(2,1)S(1)}, bf16[16,640]{1,0:T(8,128)(2,1)S(1)}, bf16[16,640]{1,0:T(8,128)(2,1)S(1)}) custom-call(s32[2]{0:T(128)S(1)} %pad_add_fusion.place_ref, bf16[8,96,128]{2,1,0:T(8,128)(2,1)S(1)} %all_to_all.35.heard_ref, f32[4,32,640]{2,1,0:T(8,128)S(1)} %get-tuple-element.35.state_ref, ...), custom_call_target="tpu_custom_call" | custom-call | flops 1073741824 | bytes 1048576 | tf_op jit(solution)/shard_map/conv0/pallas_call | solution.py:408
  60.0 24.9 %all_to_all.36.conv_ref = f32[4,192,128]{2,1,0:T(8,128)S(1)} all-to-all(f32[4,192,128]{2,1,0:T(8,128)S(1)} %get-tuple-element.40), channel_id=1, replica_groups=mesh['req'=16,'yh'=4,'yl'=2,'zh'=2,'core'=2] {'zh','core'}, dimensions={0} | all-to-all | bytes 786432 | tf_op jit(solution)/shard_map/all_to_all | solution.py:421
  85.0 1.4 hidden0.1
  86.3 3.6 %all-to-all-start.3 = ((f32[8,4,128]{2,1,0:T(4,128)}), f32[8,4,128]{2,1,0:T(4,128)S(1)}, u32[]{:S(2)}, u32[]{:S(2)}) async-start(f32[8,4,128]{2,1,0:T(4,128)} %get-tuple-element.43), calls=%async_computation.3 | async-start | bytes 32768 | tf_op jit(solution)/shard_map/all_to_all | solution.py:421
  90.0 3.3 %collective-permute-start = (bf16[16,640]{1,0:T(8,128)(2,1)S(1)}, bf16[16,640]{1,0:T(8,128)(2,1)S(1)}, u32[]{:S(2)}, u32[]{:S(2)}) collective-permute-start(bf16[16,640]{1,0:T(8,128)(2,1)S(1)} %get-tuple-element.44), channel_id=1, source_target_pairs={{0,4},{4,8},{8,12},{12,16},{16,20},{20,24},{24,28},{1,5},{5,9},{9,... | collective-permute-start | bytes 61448 | tf_op jit(solution)/shard_map/ppermute | solution.py:505
  93.3 1.3 collective-permute-start.1
  94.7 3.8 %collective-permute-done.1.below_ref = bf16[16,640]{1,0:T(8,128)(2,1)S(1)} collective-permute-done((bf16[16,640]{1,0:T(8,128)(2,1)S(1)}, bf16[16,640]{1,0:T(8,128)(2,1)S(1)}, u32[]{:S(2)}, u32[]{:S(2)}) %collective-permute-start.1) | collective-permute-done | bytes 20512 | tf_op jit(solution)/shard_map/ppermute | solution.py:505
  98.4 1.3 project0.1
  99.8 1.3 copy-done.8
  101.1 3.7 %attend0.1 = (f32[4,32,640]{2,1,0:T(8,128)S(1)}, f32[8,4,128]{2,1,0:T(4,128)S(1)}) custom-call(s32[2]{0:T(128)S(1)} %pad_add_fusion.place_ref, bf16[128,384]{1,0:T(8,128)(2,1)S(1)} %get-tuple-element.49.asked_ref, bf16[128,640]{1,0:T(8,128)(2,1)} %get-tuple-element.50.fresh_ref, f32[4,32,640]{2,1,0:T(8,128)S(1)} %get-tuple-element.47.hidden_ref, ...), custom_call_target="tpu_custom_call" | custom-call | flops 1073741824 | bytes 1048576 | tf_op jit(solution)/shard_map/attend0/pallas_call | solution.py:408
  104.8 13.1 %all_to_all.37.stats_ref = f32[8,4,128]{2,1,0:T(4,128)S(1)} all-to-all(f32[8,4,128]{2,1,0:T(4,128)S(1)} %get-tuple-element.52), channel_id=1, replica_groups=mesh['req'=16,'yh'=4,'yl'=2,'zh'=2,'core'=2] {'yh','yl'}, dimensions={0} | all-to-all | bytes 32768 | tf_op jit(solution)/shard_map/all_to_all | solution.py:421
  117.9 2.3 %conv1.1 = (f32[4,48,128]{2,1,0:T(8,128)S(1)}, f32[8,4,128]{2,1,0:T(4,128)S(1)}) custom-call(s32[2]{0:T(128)S(1)} %pad_add_fusion.place_ref, f32[8,4,128]{2,1,0:T(4,128)S(1)} %all_to_all.37.stats_ref, bf16[16,640]{1,0:T(8,128)(2,1)S(1)} %collective-permute-done.above_ref, bf16[16,640]{1,0:T(8,128)(2,1)S(1)} %collective-permute-done.1.below_ref, ...), custom_call_target="tpu_custom_call" | custom-call | flops 1073741824 | bytes 1048576 | tf_op jit(solution)/shard_map/conv1/pallas_call | solution.py:408
  120.2 9.1 %all_to_all.38.stats_ref = f32[8,4,128]{2,1,0:T(4,128)S(1)} all-to-all(f32[8,4,128]{2,1,0:T(4,128)S(1)} %get-tuple-element.58), channel_id=1, replica_groups=mesh['req'=16,'yh'=4,'yl'=2,'zh'=2,'core'=2] {'yh','yl'}, dimensions={0} | all-to-all | bytes 32768 | tf_op jit(solution)/shard_map/all_to_all | solution.py:421
  129.2 19.0 %all_to_all.39.conv_ref = f32[4,56,128]{2,1,0:T(8,128)S(1)} all-to-all(f32[4,56,128]{2,1,0:T(8,128)S(1)} %insert1.1), channel_id=1, replica_groups=mesh['req'=16,'yh'=4,'yl'=2,'zh'=2,'core'=2] {'zh','core'}, dimensions={0} | all-to-all | bytes 229376 | tf_op jit(solution)/shard_map/all_to_all | solution.py:421
  148.2 1.3 copy-done.9
  149.6 3.5 %attend1.1 = f32[2,32,640]{2,1,0:T(8,128)} custom-call(s32[2]{0:T(128)S(1)} %pad_add_fusion.place_ref, f32[4,56,128]{2,1,0:T(8,128)S(1)} %all_to_all.39.conv_ref, f32[4,32,640]{2,1,0:T(8,128)S(1)} %get-tuple-element.55.state_ref, f32[8,640]{1,0:T(8,128)S(1)} %stack.40.vectors_ref, bf16[640,384]{1,0:T(8,128)(2,1)S(1)} %pad.4.query_ref, ...), custom_call_target="tpu_custom_call" | custom-call | flops 1073741824 | bytes 1048576 | tf_op jit(solution)/shard_map/attend1/pallas_call | solution.py:408
  (57 shorter events, 2.9 us)
Async XLA Ops:
  6.5 49.8 %all-gather.4.cloned.1.call-start = ((), (), s32[]{:S(2)}) async-start(), calls=%async_computation.7 | async-start | bytes 2119680 | tf_op jit(solution)/shard_map/all_gather | solution.py:449
  6.5 17.9 %copy-start.11 = (bf16[640,320]{0,1:T(8,128)(2,1)S(1)}, bf16[640,320]{0,1:T(8,128)(2,1)}, u32[]{:S(2)}) copy-start(bf16[640,320]{0,1:T(8,128)(2,1)} %param.25) | copy-start | bytes 1228804
  8.3 16.0 %copy-start.12 = (f32[2,640]{1,0:T(2,128)S(1)}, f32[2,640]{1,0:T(2,128)}, u32[]{:S(2)}) copy-start(f32[2,640]{1,0:T(2,128)} %param.22) | copy-start | bytes 15364
  8.3 16.0 %copy-start.13 = (f32[640]{0:T(1024)S(1)}, f32[640]{0:T(1024)}, u32[]{:S(2)}) copy-start(f32[640]{0:T(1024)} %param.21) | copy-start | bytes 7684
  8.3 16.0 %copy-start.14 = (f32[640]{0:T(1024)S(1)}, f32[640]{0:T(1024)}, u32[]{:S(2)}) copy-start(f32[640]{0:T(1024)} %param.18) | copy-start | bytes 7684
  8.3 16.0 %copy-start.15 = (f32[640]{0:T(1024)S(1)}, f32[640]{0:T(1024)}, u32[]{:S(2)}) copy-start(f32[640]{0:T(1024)} %param.19) | copy-start | bytes 7684
  8.3 16.1 %copy-start.16 = (f32[640]{0:T(1024)S(1)}, f32[640]{0:T(1024)}, u32[]{:S(2)}) copy-start(f32[640]{0:T(1024)} %param.23) | copy-start | bytes 7684
  8.3 16.1 %copy-start.17 = (f32[640]{0:T(1024)S(1)}, f32[640]{0:T(1024)}, u32[]{:S(2)}) copy-start(f32[640]{0:T(1024)} %param.24) | copy-start | bytes 7684
  8.3 0.9 copy-start.1
  9.3 0.8 copy-start.3
  10.0 0.7 copy-start.4
  12.5 25.1 %all-to-all-start = ((bf16[4,128,640]{2,1,0:T(8,128)(2,1)}), bf16[4,128,640]{2,1,0:T(8,128)(2,1)S(1)}, u32[]{:S(2)}, u32[]{:S(2)}) async-start(bf16[4,128,640]{2,1,0:T(8,128)(2,1)} %pack.1), calls=%async_computation | async-start | bytes 1310720 | tf_op jit(solution)/shard_map/all_to_all | solution.py:421
  24.2 13.4 %copy-start.2 = (f32[2,16,640]{2,1,0:T(8,128)S(1)}, f32[2,16,640]{2,1,0:T(8,128)}, u32[]{:S(2)}) copy-start(f32[2,16,640]{2,1,0:T(8,128)} %param.14) | copy-start | bytes 245764
  24.2 75.5 %all-gather.6.cloned.1.call-start = ((), (), s32[]{:S(2)}) async-start(), calls=%async_computation.8 | async-start | bytes 1474560 | tf_op jit(solution)/shard_map/all_gather | solution.py:482
  56.3 1.5 copy-start.6
  60.0 38.4 %copy-start = (bf16[640,640]{1,0:T(8,128)(2,1)S(1)}, bf16[640,640]{1,0:T(8,128)(2,1)}, u32[]{:S(2)}) copy-start(bf16[640,640]{1,0:T(8,128)(2,1)} %keyvalue_ref.3) | copy-start | bytes 2457604
  85.0 14.8 %copy-start.10 = (bf16[320,640]{1,0:T(8,128)(2,1)S(1)}, bf16[320,640]{1,0:T(8,128)(2,1)}, u32[]{:S(2)}) copy-start(bf16[320,640]{1,0:T(8,128)(2,1)} %out_ref.3) | copy-start | bytes 1228804
  86.3 12.1 %all-to-all-start.3 = ((f32[8,4,128]{2,1,0:T(4,128)}), f32[8,4,128]{2,1,0:T(4,128)S(1)}, u32[]{:S(2)}, u32[]{:S(2)}) async-start(f32[8,4,128]{2,1,0:T(4,128)} %get-tuple-element.43), calls=%async_computation.3 | async-start | bytes 32768 | tf_op jit(solution)/shard_map/all_to_all | solution.py:421
  90.0 58.3 %all-gather.8.cloned.1.call-start = ((), (), s32[]{:S(2)}) async-start(), calls=%async_computation.9 | async-start | bytes 1474560 | tf_op jit(solution)/shard_map/all_gather | solution.py:514
  90.0 4.6 %collective-permute-start = (bf16[16,640]{1,0:T(8,128)(2,1)S(1)}, bf16[16,640]{1,0:T(8,128)(2,1)S(1)}, u32[]{:S(2)}, u32[]{:S(2)}) collective-permute-start(bf16[16,640]{1,0:T(8,128)(2,1)S(1)} %get-tuple-element.44), channel_id=1, source_target_pairs={{0,4},{4,8},{8,12},{12,16},{16,20},{20,24},{24,28},{1,5},{5,9},{9,... | collective-permute-start | bytes 61448 | tf_op jit(solution)/shard_map/ppermute | solution.py:505
  93.3 5.1 %collective-permute-start.1 = (bf16[16,640]{1,0:T(8,128)(2,1)S(1)}, bf16[16,640]{1,0:T(8,128)(2,1)S(1)}, u32[]{:S(2)}, u32[]{:S(2)}) collective-permute-start(bf16[16,640]{1,0:T(8,128)(2,1)S(1)} %get-tuple-element.45), channel_id=1, source_target_pairs={{4,0},{8,4},{12,8},{16,12},{20,16},{24,20},{28,24},{5,1},{9,5},{13... | collective-permute-start | bytes 61448 | tf_op jit(solution)/shard_map/ppermute | solution.py:505
  99.8 1.3 copy-start.8
  101.1 16.8 %copy-start.7 = (bf16[8,180,640]{2,1,0:T(8,128)(2,1)S(1)}, bf16[8,180,640]{2,1,0:T(8,128)(2,1)}, u32[]{:S(2)}) copy-start(bf16[8,180,640]{2,1,0:T(8,128)(2,1)} %all-gather.4.cloned.1.call-done.weight_ref) | copy-start | bytes 5529604
  148.2 1.3 copy-start.9
  (1 other events, 0.7 us)
Sparse Core Ops, SparseCore 0:
  9.4 44.9 all-gather.3
  56.5 42.7 all-gather.5
  101.3 39.6 all-gather.7

commit v8 on v7

--- a/solution.py
+++ b/solution.py
@@ -83,60 +83,24 @@
     return spread[0:1], spread[1:2]
 
 
-def tell_sums_and_edges(x, y, first, last, out_ref):
-    sums = eight(
-        [jnp.sum(x, axis=0, keepdims=True), jnp.sum(x * x, axis=0, keepdims=True)], CHANNELS
-    )
-    terms = [t.astype(F32)[0:2] for t in thirds(picked(sums, group_matrix()))]
-    told = jnp.concatenate([*terms, jnp.zeros((10, LANES), F32)], axis=0).astype(BF16)
-    for to in range(8):
-        out_ref[to, 0:COLS] = told
-        edge = jnp.where(y + 1 == to, last.astype(F32), first.astype(F32)).astype(BF16)
-        for k in range(5):
-            out_ref[to, COLS * (k + 1) : COLS * (k + 2)] = edge[:, LANES * k : LANES * (k + 1)]
-
-
-def heard_sums(heard_ref):
-    terms = jnp.sum(heard_ref[:, 0:COLS].astype(F32), axis=0)
-    return terms[0:2] + terms[2:4] + terms[4:6]
-
-
-def heard_edge(heard_ref, sender, exists):
-    row = jnp.concatenate(
-        [heard_ref[sender, COLS * (k + 1) : COLS * (k + 2)] for k in range(5)], axis=1
-    )
-    return jnp.where(exists, row.astype(F32), 0.0).astype(BF16)
-
-
-def heard_edges(heard_ref, y):
-    return heard_edge(heard_ref, (y - 1) & 7, y > 0), heard_edge(heard_ref, (y + 1) & 7, y < 7)
-
-
-def pack_kernel(field_ref, stale_ref, keys_ref, values_ref, packed_ref):
+def pack_kernel(field_ref, stale_ref, packed_ref):
     high, middle, _ = thirds(field_ref[...])
-    both = jnp.concatenate(
-        [keys_ref[...].astype(F32), values_ref[...].astype(F32)], axis=1
-    ).astype(BF16)
     for to in range(4):
         packed_ref[to, 0:ROWS] = high
         packed_ref[to, ROWS : 2 * ROWS] = middle
-        packed_ref[to, 2 * ROWS : 3 * ROWS] = stale_ref[...]
-        packed_ref[to, 3 * ROWS :] = both
-
-
-def unpack_kernel(place_ref, packed_ref, field_ref, state_ref, kv_ref, prior_ref, told_ref):
+        packed_ref[to, 2 * ROWS :] = stale_ref[...]
+
+
+def unpack_kernel(
+    place_ref, packed_ref, field_ref, state_ref, prior_ref, first_ref, last_ref, stats_ref
+):
     for t in range(4):
         state_ref[t] = packed_ref[t, 0:ROWS].astype(F32) + packed_ref[t, ROWS : 2 * ROWS].astype(F32)
-        prior_ref[t] = packed_ref[t, 2 * ROWS : 3 * ROWS]
-        kv_ref[t] = packed_ref[t, 3 * ROWS :]
+        prior_ref[t] = packed_ref[t, 2 * ROWS :]
     state_ref[place_ref[1]] = field_ref[...]
-    tell_sums_and_edges(
-        state_ref[...].reshape(QUAD_ROWS, CHANNELS),
-        place_ref[0],
-        prior_ref[0, :COLS],
-        prior_ref[3, COLS:],
-        told_ref,
-    )
+    first_ref[...] = prior_ref[0, :COLS]
+    last_ref[...] = prior_ref[3, COLS:]
+    tell_sums(state_ref[...].reshape(QUAD_ROWS, CHANNELS), group_matrix(), stats_ref)
 
 
 def activate(sums, edges, state_ref, prior_ref, vectors_ref, keep, rows):
@@ -158,7 +122,7 @@
     lane = lax.broadcasted_iota(jnp.int32, (LANES, LANES), 1)
     tiles = [jnp.zeros((LANES, LANES), F32), jnp.zeros((LANES, LANES), F32)]
     for part in range(8):
-        wide[:, 0 : 9 * MEMBERS] = dot(window, weight_ref[part], NT)
+        wide[:, 0 : 9 * MEMBERS] = dot(window, weight_ref[part, ROWS:], NT)
         whole = wide[...].reshape(4, 64, 256)
         lines = [
             whole[:, COLS * r : COLS * r + 2 * COLS].reshape(LANES, 256) for r in range(3)
@@ -189,8 +153,9 @@
 
 
 def conv_quad_kernel(
-    place_ref,
-    heard_ref,
+    stats_ref,
+    above_ref,
+    below_ref,
     state_ref,
     prior_ref,
     weight_ref,
@@ -209,8 +174,9 @@
         if t == 3:
             last_ref[...] = act[COLS:]
 
-    edges = heard_edges(heard_ref, place_ref[0])
-    activate(heard_sums(heard_ref), edges, state_ref, prior_ref, vectors_ref, keep, rows)
+    edges = (above_ref[...], below_ref[...])
+    sums = jnp.sum(stats_ref[...], axis=0)
+    activate(sums, edges, state_ref, prior_ref, vectors_ref, keep, rows)
     tiles = convolve(rows, weight_ref, wide)
     rest = folded(tiles[1])
     for to in range(4):
@@ -331,13 +297,15 @@
     fresh_ref[...] = fresh
 
 
-def attend(query, fresh, patch, y, kv_ref):
+def attend(query, fresh, patch, y, kvs):
     count = query.shape[0]
     lane = lax.broadcasted_iota(jnp.int32, (count, LANES), 1)
     low = lane < HEAD_DIM
 
-    block = lax.broadcasted_iota(jnp.int32, (count, POSITIONS), 1) >> 5
-    replaced = block == 4 * y + patch
+    replaced = []
+    for ref, step, first in kvs:
+        block = lax.broadcasted_iota(jnp.int32, (count, ref.shape[0]), 1) >> 5
+        replaced.append(step * block + first == 4 * y + patch)
     if count == ROWS:
         theirs = None
     else:
@@ -347,19 +315,21 @@
         at = LANES * (h // 2)
         own = low if h % 2 == 0 else ~low
         asked = jnp.where(own, query[:, at : at + LANES].astype(F32), 0.0).astype(BF16)
-        old = dot(asked, kv_ref[:, at : at + LANES], NT) * HEAD_DIM ** (-0.5)
-        old = jnp.where(replaced, -jnp.inf, old)
+        olds = [dot(asked, ref[:, at : at + LANES], NT) * HEAD_DIM ** (-0.5) for ref, _, _ in kvs]
+        olds = [jnp.where(r, -jnp.inf, old) for r, old in zip(replaced, olds)]
         new = dot(asked, fresh[:, at : at + LANES], NT) * HEAD_DIM ** (-0.5)
         if theirs is not None:
             new = jnp.where(theirs, new, -jnp.inf)
-        peak = jnp.maximum(
-            jnp.max(old, axis=1, keepdims=True), jnp.max(new, axis=1, keepdims=True)
+        peak = functools.reduce(
+            jnp.maximum, [jnp.max(e, axis=1, keepdims=True) for e in (*olds, new)]
         )
-        old = jnp.exp(old - peak)
+        olds = [jnp.exp(old - peak) for old in olds]
         new = jnp.exp(new - peak)
-        total = jnp.sum(old, axis=1, keepdims=True) + jnp.sum(new, axis=1, keepdims=True)
+        total = sum(jnp.sum(e, axis=1, keepdims=True) for e in (*olds, new))
         at = LANES * ((HEADS + h) // 2)
-        summed = dot(old.astype(BF16), kv_ref[:, at : at + LANES])
+        summed = sum(
+            dot(old.astype(BF16), ref[:, at : at + LANES]) for old, (ref, _, _) in zip(olds, kvs)
+        )
         summed += dot(new.astype(BF16), fresh[:, at : at + LANES])
         summed = pltpu.roll(summed / total, HEAD_DIM, 1)
         tiles[h // 2] = jnp.where(own, summed, tiles[h // 2])
@@ -367,10 +337,22 @@
 
 
 def attend_quad_kernel(
-    place_ref, asked_ref, fresh_ref, hidden_ref, out_ref, kv_ref, state_ref, told_ref
-):
+    place_ref,
+    asked_ref,
+    fresh_ref,
+    hidden_ref,
+    out_ref,
+    own_ref,
+    beside_ref,
+    across_ref,
+    corner_ref,
+    state_ref,
+    told_ref,
+):
+    a = place_ref[1]
+    kvs = [(r, 4, a ^ k) for k, r in enumerate((own_ref, beside_ref, across_ref, corner_ref))]
     patch = lax.broadcasted_iota(jnp.int32, (QUAD_ROWS, 1), 0) >> 5
-    attended = attend(asked_ref[...], fresh_ref[...], patch, place_ref[0], kv_ref)
+    attended = attend(asked_ref[...], fresh_ref[...], patch, place_ref[0], kvs)
     result = hidden_ref[...].reshape(QUAD_ROWS, CHANNELS) + dot(attended, out_ref[...])
     state_ref[...] = result.reshape(state_ref.shape)
     tell_sums(result, group_matrix(), told_ref)
@@ -395,7 +377,7 @@
         sums += conv_ref[t, 48:56]
     mean, scale = spread_sums(sums, group_matrix())
     query, fresh = project(hidden, mean, scale, vectors_ref, query_ref, keyvalue_ref)
-    attended = attend(query, fresh, a, place_ref[0], kv_ref)
+    attended = attend(query, fresh, a, place_ref[0], ((kv_ref, 1, 0),))
     result_ref[0] = earlier
     result_ref[1] = hidden + dot(attended, out_ref[...])
 
@@ -440,20 +422,20 @@
     quad = (4, ROWS, CHANNELS)
     line = (COLS, CHANNELS)
     stats8 = ((8, 4, LANES), F32)
-    told8 = ((8, 6 * COLS, LANES), BF16)
     y = 2 * lax.axis_index("yh") + lax.axis_index("yl")
     a = 2 * lax.axis_index("zh") + lax.axis_index("core")
     place = jnp.stack([y, a]).astype(jnp.int32)
 
     slices = conv_weight.transpose(0, 1, 3, 2).reshape(9 * MEMBERS, CHANNELS)
-    weights = lax.all_gather(slices, Y, axis=0, tiled=False)
+    stale_kv = jnp.concatenate([stale_keys, stale_values], axis=1)
+    weights = lax.all_gather(jnp.concatenate([stale_kv, slices], axis=0), Y, axis=0, tiled=False)
 
     own = field.reshape(ROWS, CHANNELS)
     (packed,) = call(
         pack_kernel,
         "pack",
-        [((4, 4 * ROWS, CHANNELS), BF16)],
-        (own, stale_conv_in.reshape(ROWS, CHANNELS), stale_keys, stale_values),
+        [((4, 3 * ROWS, CHANNELS), BF16)],
+        (own, stale_conv_in.reshape(ROWS, CHANNELS)),
     )
     vectors = jnp.stack(
         [
@@ -471,38 +453,41 @@
     packed, vectors, w_query, place = lax.optimization_barrier(
         (to_all(packed, QUAD), vectors, w_query, place)
     )
-    state, kv, prior, told = call(
+    state, prior, first, last, stats = call(
         unpack_kernel,
         "unpack",
-        [(quad, F32), (quad, BF16), (quad, BF16), told8],
+        [(quad, F32), (quad, BF16), (line, BF16), (line, BF16), stats8],
         (place, packed, own),
         scalars=1,
     )
-    kv = kv.reshape(QUAD_ROWS, CHANNELS)
-    old = lax.all_gather(kv, Y, axis=0, tiled=True)
     buffers = [pltpu.VMEM((4, 64, CHANNELS), BF16), pltpu.VMEM((256, 256), F32)]
+    up = [(i, i + 1) for i in range(7)]
+    down = [(i + 1, i) for i in range(7)]
+    swapped = lambda v, axis: lax.ppermute(v, axis, [(0, 1), (1, 0)])
+    above = lax.ppermute(last, Y, up)
+    below = lax.ppermute(first, Y, down)
 
     conv, prior, first, last = call(
         conv_quad_kernel,
         "conv0",
         [((4, LANES + 64, LANES), F32), (quad, BF16), (line, BF16), (line, BF16)],
-        (place, to_all(told, Y), state, prior, weights, vectors),
-        scalars=1,
+        (to_all(stats, Y), above, below, state, prior, weights, vectors),
         scratch=buffers,
         flops=1 << 30,
     )
+    conv, old = lax.optimization_barrier((conv, weights[:, :ROWS].reshape(8 * ROWS, CHANNELS)))
+    across = swapped(old, "zh")
+    conv, beside = lax.optimization_barrier((to_all(conv, QUAD), swapped(old, "core")))
     hidden, stats = call(
         hidden_kernel,
         "hidden0",
         [(quad, F32), stats8],
-        (to_all(conv, QUAD), state, vectors),
+        (conv, state, vectors),
         flops=1 << 28,
     )
-    up = [(i, i + 1) for i in range(7)]
-    down = [(i + 1, i) for i in range(7)]
     last, first, hidden, stats = lax.optimization_barrier((last, first, hidden, stats))
-    stats, above, below = lax.optimization_barrier(
-        (to_all(stats, Y), lax.ppermute(last, Y, up), lax.ppermute(first, Y, down))
+    stats, above, below, across = lax.optimization_barrier(
+        (to_all(stats, Y), lax.ppermute(last, Y, up), lax.ppermute(first, Y, down), across)
     )
     asked, fresh = call(
         project_kernel,
@@ -516,7 +501,7 @@
         attend_quad_kernel,
         "attend0",
         [(quad, F32), stats8],
-        (place, asked, fresh, hidden, w_out, old),
+        (place, asked, fresh, hidden, w_out, old, beside, across, swapped(across, "core")),
         scalars=1,
         flops=1 << 30,
     )

time: 160 us -> 165 us (1.031)
  blocking collectives: 83.4 us -> 35.2 us
  starting transfers between devices: 20.1 us -> 59.6 us
  waiting for transfers between devices: 16.6 us -> 25.4 us
    all_to_all x5 -> x3, blocking collectives: 83.4 us -> 35.2 us  [to_all(): return lax.all_to_all(value, axes, 0, 0, tiled=True)]
    ppermute x0 -> x5, starting transfers between devices: none -> 20.3 us  [the longest x3 15.6 us: per_device(): swapped = lambda v, axis: lax.ppermute(v, axis, [(0, 1), (1, 0)])]
    all_to_all x2 -> x4, starting transfers between devices: 15.4 us -> 34.6 us  [to_all(): return lax.all_to_all(value, axes, 0, 0, tiled=True)]
    all_gather x2 -> x1, waiting for transfers between devices: 0.02 us -> 6.74 us  [per_device(): lax.all_gather(jnp.concatenate([stale_kv, slices], axis=0), Y, axis=0, ti...]
    ppermute x0 -> x5, waiting for transfers between devices: none -> 4.72 us  [the longest x3 4.72 us: per_device(): swapped = lambda v, axis: lax.ppermute(v, axis, [(0, 1), (1, 0)])]
    ppermute x1, waiting for transfers between devices: 3.78 us -> 0.04 us  [per_device(): lax.ppermute(first, Y, down)]
    another operation x1 -> x0, local copies, waits for them, and re-layouts: 1.74 us -> none  [per_device(): weights = lax.all_gather(slices, Y, axis=0, tiled=False)]
    all_to_all x2 -> x4, waiting for transfers between devices: 12.7 us -> 13.9 us  [to_all(): return lax.all_to_all(value, axes, 0, 0, tiled=True)]
  transfers between devices with their start and end apart: 7 -> 13, of which waited for: 2 -> 5; matrix products, arithmetic and copies ran while one was open for 0% -> 1% of each run, Pallas kernels for 8% -> 6%
where the time goes in v8:
time: 165 us; the launch traced here: 163 us
  starting transfers between devices  59.6 us (36%)
  blocking collectives  35.2 us (21%)
  waiting for transfers between devices  25.4 us (15%)
  Pallas kernels  16.8 us (10%)
  between operations  13.7 us (8%)
  local copies, waits for them, and re-layouts  10.7 us (6%)
    all_to_all x3, blocking collectives, to_all(): return lax.all_to_all(value, axes, 0, 0, tiled=True)  35.2 us
    all_to_all x4, starting transfers between devices, to_all(): return lax.all_to_all(value, axes, 0, 0, tiled=True)  34.6 us
    pallas_call x9, Pallas kernels, call(): pl.pallas_call(kernel, name=name, out_shape=[jax.ShapeDtypeStruct(s, t) f...  16.8 us
    ppermute x3, starting transfers between devices, per_device(): swapped = lambda v, axis: lax.ppermute(v, axis, [(0, 1), (1, 0)])  15.6 us
    all_to_all x4, waiting for transfers between devices, to_all(): return lax.all_to_all(value, axes, 0, 0, tiled=True)  13.9 us
    unnamed x43, local copies, waits for them, and re-layouts  8.44 us
    all_gather x1, waiting for transfers between devices, per_device(): lax.all_gather(jnp.concatenate([stale_kv, slices], axis=0), Y, axis=0, ti...  6.74 us
    ppermute x3, waiting for transfers between devices, per_device(): swapped = lambda v, axis: lax.ppermute(v, axis, [(0, 1), (1, 0)])  4.72 us
  transfers between devices with their start and end apart: 13, of which 5 were waited for; matrix products, arithmetic and copies ran while one was open for 1% of the time, Pallas kernels for 6%

profile of v8, /device:TPU:1, one launch (start us, length us, event | category | flops | bytes accessed | tf_op | source)
XLA Modules:
  0.0 163.1 jit_solution(11867075943327506516)
XLA Ops:
  7.7 1.6 maximum_bitcast_fusion
  11.8 11.8 %all-to-all-start = ((bf16[4,96,640]{2,1,0:T(8,128)(2,1)}), bf16[4,96,640]{2,1,0:T(8,128)(2,1)S(1)}, u32[]{:S(2)}, u32[]{:S(2)}) async-start(bf16[4,96,640]{2,1,0:T(8,128)(2,1)} %pack.1), calls=%async_computation | async-start | bytes 983040 | tf_op jit(solution)/shard_map/all_to_all | solution.py:403
  24.2 10.9 %all-to-all-done.packed_ref = bf16[4,96,640]{2,1,0:T(8,128)(2,1)S(1)} async-done(((bf16[4,96,640]{2,1,0:T(8,128)(2,1)}), bf16[4,96,640]{2,1,0:T(8,128)(2,1)S(1)}, u32[]{:S(2)}, u32[]{:S(2)}) %all-to-all-start) | async-done | bytes 491552 | tf_op jit(solution)/shard_map/all_to_all | solution.py:403
  35.1 1.4 unpack.1
  36.6 6.8 %all-to-all-start.1 = ((f32[8,4,128]{2,1,0:T(4,128)}), f32[8,4,128]{2,1,0:T(4,128)S(1)}, u32[]{:S(2)}, u32[]{:S(2)}) async-start(f32[8,4,128]{2,1,0:T(4,128)} %get-tuple-element.40), calls=%async_computation.1 | async-start | bytes 32768 | tf_op jit(solution)/shard_map/all_to_all | solution.py:403
  43.4 3.4 %collective-permute-start = (bf16[16,640]{1,0:T(8,128)(2,1)S(1)}, bf16[16,640]{1,0:T(8,128)(2,1)S(1)}, u32[]{:S(2)}, u32[]{:S(2)}) collective-permute-start(bf16[16,640]{1,0:T(8,128)(2,1)S(1)} %get-tuple-element.41), channel_id=1, source_target_pairs={{0,4},{4,8},{8,12},{12,16},{16,20},{20,24},{24,28},{1,5},{5,9},{9,... | collective-permute-start | bytes 61448 | tf_op jit(solution)/shard_map/ppermute | solution.py:467
  48.1 6.7 %all-gather.7.cloned.1.call-done.weight_ref = bf16[8,212,640]{2,1,0:T(8,128)(2,1)} async-done(((bf16[1,212,640]{2,1,0:T(8,128)(2,1)}), bf16[8,212,640]{2,1,0:T(8,128)(2,1)}) %all-gather.7.cloned.1.call-update) | async-done | bytes 2170896 | tf_op jit(solution)/shard_map/all_gather | solution.py:431
  55.8 1.6 copy-done.3
  57.5 2.4 %conv0.1 = (f32[4,192,128]{2,1,0:T(8,128)}, bf16[4,32,640]{2,1,0:T(8,128)(2,1)S(1)}, bf16[16,640]{1,0:T(8,128)(2,1)S(1)}, bf16[16,640]{1,0:T(8,128)(2,1)S(1)}) custom-call(f32[8,4,128]{2,1,0:T(4,128)S(1)} %all-to-all-done.1.stats_ref, bf16[16,640]{1,0:T(8,128)(2,1)S(1)} %collective-permute-done.above_ref, ...), custom_call_target="tpu_custom_call" | custom-call | flops 1073741824 | bytes 1048576 | tf_op jit(solution)/shard_map/conv0/pallas_call | solution.py:390
  60.5 12.4 %all-to-all-start.2 = ((f32[4,192,128]{2,1,0:T(8,128)}), f32[4,192,128]{2,1,0:T(8,128)S(1)}, u32[]{:S(2)}, u32[]{:S(2)}) async-start(f32[4,192,128]{2,1,0:T(8,128)} %get-tuple-element.49), calls=%async_computation.2 | async-start | bytes 786432 | tf_op jit(solution)/shard_map/all_to_all | solution.py:403
  72.9 1.9 %collective-permute-start.2 = (bf16[256,640]{1,0:T(8,128)(2,1)S(1)}, bf16[256,640]{1,0:T(8,128)(2,1)S(1)}, u32[]{:S(2)}, u32[]{:S(2)}) collective-permute-start(bf16[256,640]{1,0:T(8,128)(2,1)S(1)} %bitcast.9), channel_id=1, source_target_pairs={{0,1},{1,0},{2,3},{3,2},{4,5},{5,4},{6,7},{7,6},{8,9},{9,8},{10,11... | collective-permute-start | bytes 983048 | tf_op jit(solution)/shard_map/ppermute | solution.py:466
  74.8 7.5 %collective-permute-start.5 = (bf16[256,640]{1,0:T(8,128)(2,1)S(1)}, bf16[256,640]{1,0:T(8,128)(2,1)S(1)}, u32[]{:S(2)}, u32[]{:S(2)}) collective-permute-start(bf16[256,640]{1,0:T(8,128)(2,1)S(1)} %bitcast.10), channel_id=1, source_target_pairs={{0,2},{2,0},{1,3},{3,1},{4,6},{6,4},{5,7},{7,5},{8,10},{10,8},{9,1... | collective-permute-start | bytes 983048 | tf_op jit(solution)/shard_map/ppermute | solution.py:466
  82.4 3.0 %all-to-all-done.2.conv_ref = f32[4,192,128]{2,1,0:T(8,128)S(1)} async-done(((f32[4,192,128]{2,1,0:T(8,128)}), f32[4,192,128]{2,1,0:T(8,128)S(1)}, u32[]{:S(2)}, u32[]{:S(2)}) %all-to-all-start.2) | async-done | bytes 393248 | tf_op jit(solution)/shard_map/all_to_all | solution.py:403
  86.4 1.4 hidden0.1
  87.8 3.7 %all-to-all-start.3 = ((f32[8,4,128]{2,1,0:T(4,128)}), f32[8,4,128]{2,1,0:T(4,128)S(1)}, u32[]{:S(2)}, u32[]{:S(2)}) async-start(f32[8,4,128]{2,1,0:T(4,128)} %get-tuple-element.54), calls=%async_computation.3 | async-start | bytes 32768 | tf_op jit(solution)/shard_map/all_to_all | solution.py:403
  91.5 3.3 %collective-permute-start.3 = (bf16[16,640]{1,0:T(8,128)(2,1)S(1)}, bf16[16,640]{1,0:T(8,128)(2,1)S(1)}, u32[]{:S(2)}, u32[]{:S(2)}) collective-permute-start(bf16[16,640]{1,0:T(8,128)(2,1)S(1)} %get-tuple-element.55), channel_id=1, source_target_pairs={{0,4},{4,8},{8,12},{12,16},{16,20},{20,24},{24,28},{1,5},{5,9},{9,... | collective-permute-start | bytes 61448 | tf_op jit(solution)/shard_map/ppermute | solution.py:490
  96.1 3.5 %collective-permute-done.5.across_ref = bf16[256,640]{1,0:T(8,128)(2,1)S(1)} collective-permute-done((bf16[256,640]{1,0:T(8,128)(2,1)S(1)}, bf16[256,640]{1,0:T(8,128)(2,1)S(1)}, u32[]{:S(2)}, u32[]{:S(2)}) %collective-permute-start.5) | collective-permute-done | bytes 327712 | tf_op jit(solution)/shard_map/ppermute | solution.py:466
  100.9 6.2 %collective-permute-start.6 = (bf16[256,640]{1,0:T(8,128)(2,1)S(1)}, bf16[256,640]{1,0:T(8,128)(2,1)S(1)}, u32[]{:S(2)}, u32[]{:S(2)}) collective-permute-start(bf16[256,640]{1,0:T(8,128)(2,1)S(1)} %collective-permute-done.5.across_ref), channel_id=1, source_target_pairs={{0,1},{1,0},{2,3},{3,2},{4,5},{5,4},{6,7},{7,6},{8,9},{9,8},{10,11... | collective-permute-start | bytes 983048 | tf_op jit(solution)/shard_map/ppermute | solution.py:466
  108.3 3.7 %attend0.1 = (f32[4,32,640]{2,1,0:T(8,128)S(1)}, f32[8,4,128]{2,1,0:T(4,128)S(1)}) custom-call(s32[2]{0:T(128)S(1)} %pad_add_fusion.place_ref, bf16[128,384]{1,0:T(8,128)(2,1)S(1)} %get-tuple-element.60.asked_ref, bf16[128,640]{1,0:T(8,128)(2,1)} %get-tuple-element.61.fresh_ref, f32[4,32,640]{2,1,0:T(8,128)S(1)} %get-tuple-element.58.hidden_ref, ...), custom_call_target="tpu_custom_call" | custom-call | flops 1073741824 | bytes 1048576 | tf_op jit(solution)/shard_map/attend0/pallas_call | solution.py:390
  112.0 13.2 %all_to_all.35.stats_ref = f32[8,4,128]{2,1,0:T(4,128)S(1)} all-to-all(f32[8,4,128]{2,1,0:T(4,128)S(1)} %get-tuple-element.64), channel_id=1, replica_groups=mesh['req'=16,'yh'=4,'yl'=2,'zh'=2,'core'=2] {'yh','yl'}, dimensions={0} | all-to-all | bytes 32768 | tf_op jit(solution)/shard_map/all_to_all | solution.py:403
  126.1 2.3 %conv1.1 = (f32[4,48,128]{2,1,0:T(8,128)S(1)}, f32[8,4,128]{2,1,0:T(4,128)S(1)}) custom-call(s32[2]{0:T(128)S(1)} %pad_add_fusion.place_ref, f32[8,4,128]{2,1,0:T(4,128)S(1)} %all_to_all.35.stats_ref, bf16[16,640]{1,0:T(8,128)(2,1)S(1)} %collective-permute-done.3.above_ref, bf16[16,640]{1,0:T(8,128)(2,1)S(1)} %collective-permute-done.4.below_ref, ...), custom_call_target="tpu_custom_call" | custom-call | flops 1073741824 | bytes 1048576 | tf_op jit(solution)/shard_map/conv1/pallas_call | solution.py:390
  128.4 9.1 %all_to_all.36.stats_ref = f32[8,4,128]{2,1,0:T(4,128)S(1)} all-to-all(f32[8,4,128]{2,1,0:T(4,128)S(1)} %get-tuple-element.70), channel_id=1, replica_groups=mesh['req'=16,'yh'=4,'yl'=2,'zh'=2,'core'=2] {'yh','yl'}, dimensions={0} | all-to-all | bytes 32768 | tf_op jit(solution)/shard_map/all_to_all | solution.py:403
  137.5 13.0 %all_to_all.37.conv_ref = f32[4,56,128]{2,1,0:T(8,128)S(1)} all-to-all(f32[4,56,128]{2,1,0:T(8,128)S(1)} %insert1.1), channel_id=1, replica_groups=mesh['req'=16,'yh'=4,'yl'=2,'zh'=2,'core'=2] {'zh','core'}, dimensions={0} | all-to-all | bytes 229376 | tf_op jit(solution)/shard_map/all_to_all | solution.py:403
  152.7 3.5 %attend1.1 = f32[2,32,640]{2,1,0:T(8,128)} custom-call(s32[2]{0:T(128)S(1)} %pad_add_fusion.place_ref, f32[4,56,128]{2,1,0:T(8,128)S(1)} %all_to_all.37.conv_ref, f32[4,32,640]{2,1,0:T(8,128)S(1)} %copy-done.11, f32[8,640]{1,0:T(8,128)S(1)} %stack.40.vectors_ref, bf16[640,384]{1,0:T(8,128)(2,1)S(1)} %pad.4.query_ref, bf16[640,640]{1,0:T(8,128)(2,1)S(1)} %copy-done, ...), custom_call_target="tpu_custom_call" | custom-call | flops 1073741824 | bytes 1048576 | tf_op jit(solution)/shard_map/attend1/pallas_call | solution.py:390
  (74 shorter events, 15.2 us)
Async XLA Ops:
  6.5 17.1 %copy-start.17 = (f32[640]{0:T(1024)S(1)}, f32[640]{0:T(1024)}, u32[]{:S(2)}) copy-start(f32[640]{0:T(1024)} %param.18) | copy-start | bytes 7684
  6.5 17.1 %copy-start.18 = (f32[640]{0:T(1024)S(1)}, f32[640]{0:T(1024)}, u32[]{:S(2)}) copy-start(f32[640]{0:T(1024)} %param.19) | copy-start | bytes 7684
  6.5 17.2 %copy-start.19 = (f32[640]{0:T(1024)S(1)}, f32[640]{0:T(1024)}, u32[]{:S(2)}) copy-start(f32[640]{0:T(1024)} %param.23) | copy-start | bytes 7684
  6.5 17.2 %copy-start.20 = (f32[640]{0:T(1024)S(1)}, f32[640]{0:T(1024)}, u32[]{:S(2)}) copy-start(f32[640]{0:T(1024)} %param.24) | copy-start | bytes 7684
  6.6 17.2 %copy-start.14 = (bf16[640,320]{0,1:T(8,128)(2,1)S(1)}, bf16[640,320]{0,1:T(8,128)(2,1)}, u32[]{:S(2)}) copy-start(bf16[640,320]{0,1:T(8,128)(2,1)} %param.25) | copy-start | bytes 1228804
  6.6 48.2 %all-gather.7.cloned.1.call-start = ((), (), s32[]{:S(2)}) async-start(), calls=%async_computation.8 | async-start | bytes 2488320 | tf_op jit(solution)/shard_map/all_gather | solution.py:431
  7.7 27.4 %copy-start.2 = (f32[2,16,640]{2,1,0:T(8,128)S(1)}, f32[2,16,640]{2,1,0:T(8,128)}, u32[]{:S(2)}) copy-start(f32[2,16,640]{2,1,0:T(8,128)} %param.14) | copy-start | bytes 245764
  11.8 23.3 %all-to-all-start = ((bf16[4,96,640]{2,1,0:T(8,128)(2,1)}), bf16[4,96,640]{2,1,0:T(8,128)(2,1)S(1)}, u32[]{:S(2)}, u32[]{:S(2)}) async-start(bf16[4,96,640]{2,1,0:T(8,128)(2,1)} %pack.1), calls=%async_computation | async-start | bytes 983040 | tf_op jit(solution)/shard_map/all_to_all | solution.py:403
  36.6 23.3 %copy-start.8 = (f32[4,32,640]{2,1,0:T(8,128)}, f32[4,32,640]{2,1,0:T(8,128)S(1)}, u32[]{:S(2)}) copy-start(f32[4,32,640]{2,1,0:T(8,128)S(1)} %get-tuple-element.43.state_ref) | copy-start | bytes 983044
  36.6 19.2 %all-to-all-start.1 = ((f32[8,4,128]{2,1,0:T(4,128)}), f32[8,4,128]{2,1,0:T(4,128)S(1)}, u32[]{:S(2)}, u32[]{:S(2)}) async-start(f32[8,4,128]{2,1,0:T(4,128)} %get-tuple-element.40), calls=%async_computation.1 | async-start | bytes 32768 | tf_op jit(solution)/shard_map/all_to_all | solution.py:403
  43.4 12.4 %collective-permute-start = (bf16[16,640]{1,0:T(8,128)(2,1)S(1)}, bf16[16,640]{1,0:T(8,128)(2,1)S(1)}, u32[]{:S(2)}, u32[]{:S(2)}) collective-permute-start(bf16[16,640]{1,0:T(8,128)(2,1)S(1)} %get-tuple-element.41), channel_id=1, source_target_pairs={{0,4},{4,8},{8,12},{12,16},{16,20},{20,24},{24,28},{1,5},{5,9},{9,... | collective-permute-start | bytes 61448 | tf_op jit(solution)/shard_map/ppermute | solution.py:467
  46.8 9.1 %collective-permute-start.1 = (bf16[16,640]{1,0:T(8,128)(2,1)S(1)}, bf16[16,640]{1,0:T(8,128)(2,1)S(1)}, u32[]{:S(2)}, u32[]{:S(2)}) collective-permute-start(bf16[16,640]{1,0:T(8,128)(2,1)S(1)} %get-tuple-element.42), channel_id=1, source_target_pairs={{4,0},{8,4},{12,8},{16,12},{20,16},{24,20},{28,24},{5,1},{9,5},{13... | collective-permute-start | bytes 61448 | tf_op jit(solution)/shard_map/ppermute | solution.py:468
  57.5 42.2 %copy-start = (bf16[640,640]{1,0:T(8,128)(2,1)S(1)}, bf16[640,640]{1,0:T(8,128)(2,1)}, u32[]{:S(2)}) copy-start(bf16[640,640]{1,0:T(8,128)(2,1)} %keyvalue_ref.3) | copy-start | bytes 2457604
  60.5 47.8 %copy-start.7 = (bf16[320,640]{1,0:T(8,128)(2,1)S(1)}, bf16[320,640]{1,0:T(8,128)(2,1)}, u32[]{:S(2)}) copy-start(bf16[320,640]{1,0:T(8,128)(2,1)} %out_ref.3) | copy-start | bytes 1228804
  60.5 24.9 %all-to-all-start.2 = ((f32[4,192,128]{2,1,0:T(8,128)}), f32[4,192,128]{2,1,0:T(8,128)S(1)}, u32[]{:S(2)}, u32[]{:S(2)}) async-start(f32[4,192,128]{2,1,0:T(8,128)} %get-tuple-element.49), calls=%async_computation.2 | async-start | bytes 786432 | tf_op jit(solution)/shard_map/all_to_all | solution.py:403
  72.9 9.5 %collective-permute-start.2 = (bf16[256,640]{1,0:T(8,128)(2,1)S(1)}, bf16[256,640]{1,0:T(8,128)(2,1)S(1)}, u32[]{:S(2)}, u32[]{:S(2)}) collective-permute-start(bf16[256,640]{1,0:T(8,128)(2,1)S(1)} %bitcast.9), channel_id=1, source_target_pairs={{0,1},{1,0},{2,3},{3,2},{4,5},{5,4},{6,7},{7,6},{8,9},{9,8},{10,11... | collective-permute-start | bytes 983048 | tf_op jit(solution)/shard_map/ppermute | solution.py:466
  74.8 24.7 %collective-permute-start.5 = (bf16[256,640]{1,0:T(8,128)(2,1)S(1)}, bf16[256,640]{1,0:T(8,128)(2,1)S(1)}, u32[]{:S(2)}, u32[]{:S(2)}) collective-permute-start(bf16[256,640]{1,0:T(8,128)(2,1)S(1)} %bitcast.10), channel_id=1, source_target_pairs={{0,2},{2,0},{1,3},{3,1},{4,6},{6,4},{5,7},{7,5},{8,10},{10,8},{9,1... | collective-permute-start | bytes 983048 | tf_op jit(solution)/shard_map/ppermute | solution.py:466
  87.8 11.9 %all-to-all-start.3 = ((f32[8,4,128]{2,1,0:T(4,128)}), f32[8,4,128]{2,1,0:T(4,128)S(1)}, u32[]{:S(2)}, u32[]{:S(2)}) async-start(f32[8,4,128]{2,1,0:T(4,128)} %get-tuple-element.54), calls=%async_computation.3 | async-start | bytes 32768 | tf_op jit(solution)/shard_map/all_to_all | solution.py:403
  91.4 59.0 %all-gather.5.cloned.1.call-start = ((), (), s32[]{:S(2)}) async-start(), calls=%async_computation.7 | async-start | bytes 1474560 | tf_op jit(solution)/shard_map/all_gather | solution.py:499
  91.5 8.1 %collective-permute-start.3 = (bf16[16,640]{1,0:T(8,128)(2,1)S(1)}, bf16[16,640]{1,0:T(8,128)(2,1)S(1)}, u32[]{:S(2)}, u32[]{:S(2)}) collective-permute-start(bf16[16,640]{1,0:T(8,128)(2,1)S(1)} %get-tuple-element.55), channel_id=1, source_target_pairs={{0,4},{4,8},{8,12},{12,16},{16,20},{20,24},{24,28},{1,5},{5,9},{9,... | collective-permute-start | bytes 61448 | tf_op jit(solution)/shard_map/ppermute | solution.py:490
  94.8 4.8 %collective-permute-start.4 = (bf16[16,640]{1,0:T(8,128)(2,1)S(1)}, bf16[16,640]{1,0:T(8,128)(2,1)S(1)}, u32[]{:S(2)}, u32[]{:S(2)}) collective-permute-start(bf16[16,640]{1,0:T(8,128)(2,1)S(1)} %get-tuple-element.56), channel_id=1, source_target_pairs={{4,0},{8,4},{12,8},{16,12},{20,16},{24,20},{28,24},{5,1},{9,5},{13... | collective-permute-start | bytes 61448 | tf_op jit(solution)/shard_map/ppermute | solution.py:490
  100.9 24.3 %copy-start.4 = (bf16[8,212,640]{2,1,0:T(8,128)(2,1)S(1)}, bf16[8,212,640]{2,1,0:T(8,128)(2,1)}, u32[]{:S(2)}) copy-start(bf16[8,212,640]{2,1,0:T(8,128)(2,1)} %all-gather.7.cloned.1.call-done.weight_ref) | copy-start | bytes 6512644
  100.9 7.4 %collective-permute-start.6 = (bf16[256,640]{1,0:T(8,128)(2,1)S(1)}, bf16[256,640]{1,0:T(8,128)(2,1)S(1)}, u32[]{:S(2)}, u32[]{:S(2)}) collective-permute-start(bf16[256,640]{1,0:T(8,128)(2,1)S(1)} %collective-permute-done.5.across_ref), channel_id=1, source_target_pairs={{0,1},{1,0},{2,3},{3,2},{4,5},{5,4},{6,7},{7,6},{8,9},{9,8},{10,11... | collective-permute-start | bytes 983048 | tf_op jit(solution)/shard_map/ppermute | solution.py:466
  112.0 25.5 %copy-start.10 = (f32[4,32,640]{2,1,0:T(8,128)}, f32[4,32,640]{2,1,0:T(8,128)S(1)}, u32[]{:S(2)}) copy-start(f32[4,32,640]{2,1,0:T(8,128)S(1)} %get-tuple-element.67.state_ref) | copy-start | bytes 983044
  (10 other events, 42.3 us)
Sparse Core Ops, SparseCore 0:
  9.5 45.2 all-gather.6
  101.0 39.5 all-gather.4

commit v9 on v7

--- a/solution.py
+++ b/solution.py
@@ -83,35 +83,6 @@
     return spread[0:1], spread[1:2]
 
 
-def tell_sums_and_edges(x, y, first, last, out_ref):
-    sums = eight(
-        [jnp.sum(x, axis=0, keepdims=True), jnp.sum(x * x, axis=0, keepdims=True)], CHANNELS
-    )
-    terms = [t.astype(F32)[0:2] for t in thirds(picked(sums, group_matrix()))]
-    told = jnp.concatenate([*terms, jnp.zeros((10, LANES), F32)], axis=0).astype(BF16)
-    for to in range(8):
-        out_ref[to, 0:COLS] = told
-        edge = jnp.where(y + 1 == to, last.astype(F32), first.astype(F32)).astype(BF16)
-        for k in range(5):
-            out_ref[to, COLS * (k + 1) : COLS * (k + 2)] = edge[:, LANES * k : LANES * (k + 1)]
-
-
-def heard_sums(heard_ref):
-    terms = jnp.sum(heard_ref[:, 0:COLS].astype(F32), axis=0)
-    return terms[0:2] + terms[2:4] + terms[4:6]
-
-
-def heard_edge(heard_ref, sender, exists):
-    row = jnp.concatenate(
-        [heard_ref[sender, COLS * (k + 1) : COLS * (k + 2)] for k in range(5)], axis=1
-    )
-    return jnp.where(exists, row.astype(F32), 0.0).astype(BF16)
-
-
-def heard_edges(heard_ref, y):
-    return heard_edge(heard_ref, (y - 1) & 7, y > 0), heard_edge(heard_ref, (y + 1) & 7, y < 7)
-
-
 def pack_kernel(field_ref, stale_ref, keys_ref, values_ref, packed_ref):
     high, middle, _ = thirds(field_ref[...])
     both = jnp.concatenate(
@@ -124,19 +95,25 @@
         packed_ref[to, 3 * ROWS :] = both
 
 
-def unpack_kernel(place_ref, packed_ref, field_ref, state_ref, kv_ref, prior_ref, told_ref):
+def unpack_kernel(
+    place_ref,
+    packed_ref,
+    field_ref,
+    state_ref,
+    kv_ref,
+    prior_ref,
+    first_ref,
+    last_ref,
+    stats_ref,
+):
     for t in range(4):
         state_ref[t] = packed_ref[t, 0:ROWS].astype(F32) + packed_ref[t, ROWS : 2 * ROWS].astype(F32)
         prior_ref[t] = packed_ref[t, 2 * ROWS : 3 * ROWS]
         kv_ref[t] = packed_ref[t, 3 * ROWS :]
     state_ref[place_ref[1]] = field_ref[...]
-    tell_sums_and_edges(
-        state_ref[...].reshape(QUAD_ROWS, CHANNELS),
-        place_ref[0],
-        prior_ref[0, :COLS],
-        prior_ref[3, COLS:],
-        told_ref,
-    )
+    first_ref[...] = prior_ref[0, :COLS]
+    last_ref[...] = prior_ref[3, COLS:]
+    tell_sums(state_ref[...].reshape(QUAD_ROWS, CHANNELS), group_matrix(), stats_ref)
 
 
 def activate(sums, edges, state_ref, prior_ref, vectors_ref, keep, rows):
@@ -189,8 +166,9 @@
 
 
 def conv_quad_kernel(
-    place_ref,
-    heard_ref,
+    stats_ref,
+    above_ref,
+    below_ref,
     state_ref,
     prior_ref,
     weight_ref,
@@ -209,8 +187,9 @@
         if t == 3:
             last_ref[...] = act[COLS:]
 
-    edges = heard_edges(heard_ref, place_ref[0])
-    activate(heard_sums(heard_ref), edges, state_ref, prior_ref, vectors_ref, keep, rows)
+    edges = (above_ref[...], below_ref[...])
+    sums = jnp.sum(stats_ref[...], axis=0)
+    activate(sums, edges, state_ref, prior_ref, vectors_ref, keep, rows)
     tiles = convolve(rows, weight_ref, wide)
     rest = folded(tiles[1])
     for to in range(4):
@@ -440,7 +419,6 @@
     quad = (4, ROWS, CHANNELS)
     line = (COLS, CHANNELS)
     stats8 = ((8, 4, LANES), F32)
-    told8 = ((8, 6 * COLS, LANES), BF16)
     y = 2 * lax.axis_index("yh") + lax.axis_index("yl")
     a = 2 * lax.axis_index("zh") + lax.axis_index("core")
     place = jnp.stack([y, a]).astype(jnp.int32)
@@ -471,23 +449,26 @@
     packed, vectors, w_query, place = lax.optimization_barrier(
         (to_all(packed, QUAD), vectors, w_query, place)
     )
-    state, kv, prior, told = call(
+    state, kv, prior, first, last, stats = call(
         unpack_kernel,
         "unpack",
-        [(quad, F32), (quad, BF16), (quad, BF16), told8],
+        [(quad, F32), (quad, BF16), (quad, BF16), (line, BF16), (line, BF16), stats8],
         (place, packed, own),
         scalars=1,
     )
     kv = kv.reshape(QUAD_ROWS, CHANNELS)
     old = lax.all_gather(kv, Y, axis=0, tiled=True)
+    up = [(i, i + 1) for i in range(7)]
+    down = [(i + 1, i) for i in range(7)]
+    above = lax.ppermute(last, Y, up)
+    below = lax.ppermute(first, Y, down)
     buffers = [pltpu.VMEM((4, 64, CHANNELS), BF16), pltpu.VMEM((256, 256), F32)]
 
     conv, prior, first, last = call(
         conv_quad_kernel,
         "conv0",
         [((4, LANES + 64, LANES), F32), (quad, BF16), (line, BF16), (line, BF16)],
-        (place, to_all(told, Y), state, prior, weights, vectors),
-        scalars=1,
+        (to_all(stats, Y), above, below, state, prior, weights, vectors),
         scratch=buffers,
         flops=1 << 30,
     )
@@ -498,8 +479,6 @@
         (to_all(conv, QUAD), state, vectors),
         flops=1 << 28,
     )
-    up = [(i, i + 1) for i in range(7)]
-    down = [(i + 1, i) for i in range(7)]
     last, first, hidden, stats = lax.optimization_barrier((last, first, hidden, stats))
     stats, above, below = lax.optimization_barrier(
         (to_all(stats, Y), lax.ppermute(last, Y, up), lax.ppermute(first, Y, down))

time: 160 us -> 158 us (0.988)
  blocking collectives: 83.4 us -> 63.1 us
  starting transfers between devices: 20.1 us -> 34.6 us
  waiting for transfers between devices: 16.6 us -> 20.1 us
    all_to_all x5 -> x4, blocking collectives: 83.4 us -> 63.1 us  [to_all(): return lax.all_to_all(value, axes, 0, 0, tiled=True)]
    all_to_all x2 -> x3, starting transfers between devices: 15.4 us -> 25.3 us  [to_all(): return lax.all_to_all(value, axes, 0, 0, tiled=True)]
    ppermute x0 -> x2, starting transfers between devices: none -> 4.65 us  [the longest x1 3.35 us: per_device(): above = lax.ppermute(last, Y, up)]
    ppermute x0 -> x2, waiting for transfers between devices: none -> 3.62 us  [the longest x1 3.62 us: per_device(): below = lax.ppermute(first, Y, down)]
    all_to_all x2 -> x3, waiting for transfers between devices: 12.7 us -> 12.7 us  [to_all(): return lax.all_to_all(value, axes, 0, 0, tiled=True)]
  transfers between devices with their start and end apart: 7 -> 10, of which waited for: 2 -> 3; matrix products, arithmetic and copies ran while one was open for 0% -> 0% of each run, Pallas kernels for 8% -> 8%
where the time goes in v9:
time: 158 us; the launch traced here: 157 us
  blocking collectives  63.1 us (40%)
  starting transfers between devices  34.6 us (22%)
  waiting for transfers between devices  20.1 us (13%)
  Pallas kernels  16.1 us (10%)
  between operations  13.4 us (8%)
  local copies, waits for them, and re-layouts  9.5 us (6%)
    all_to_all x4, blocking collectives, to_all(): return lax.all_to_all(value, axes, 0, 0, tiled=True)  63.1 us
    all_to_all x3, starting transfers between devices, to_all(): return lax.all_to_all(value, axes, 0, 0, tiled=True)  25.3 us
    pallas_call x9, Pallas kernels, call(): pl.pallas_call(kernel, name=name, out_shape=[jax.ShapeDtypeStruct(s, t) f...  16.1 us
    all_to_all x3, waiting for transfers between devices, to_all(): return lax.all_to_all(value, axes, 0, 0, tiled=True)  12.7 us
    unnamed x37, local copies, waits for them, and re-layouts  7.62 us
    ppermute x1, waiting for transfers between devices, per_device(): lax.ppermute(first, Y, down)  3.7 us
    ppermute x1, waiting for transfers between devices, per_device(): below = lax.ppermute(first, Y, down)  3.62 us
    ppermute x1, starting transfers between devices, per_device(): above = lax.ppermute(last, Y, up)  3.35 us
  transfers between devices with their start and end apart: 10, of which 3 were waited for; matrix products, arithmetic and copies ran while one was open for 0% of the time, Pallas kernels for 8%

profile of v9, /device:TPU:1, one launch (start us, length us, event | category | flops | bytes accessed | tf_op | source)
XLA Modules:
  0.0 156.9 jit_solution(10992113874235198193)
XLA Ops:
  6.5 1.7 %all_gather_reshape.3 = bf16[1,180,640]{2,1,0:T(8,128)(2,1)} reshape(bf16[3,3,20,640]{3,2,1,0:T(8,128)(2,1)} %bitcast.10) | data formatting | bytes 460800 | tf_op jit(solution)/shard_map/all_gather;reshape | solution.py:427
  12.4 11.8 %all-to-all-start = ((bf16[4,128,640]{2,1,0:T(8,128)(2,1)}), bf16[4,128,640]{2,1,0:T(8,128)(2,1)S(1)}, u32[]{:S(2)}, u32[]{:S(2)}) async-start(bf16[4,128,640]{2,1,0:T(8,128)(2,1)} %pack.1), calls=%async_computation | async-start | bytes 1310720 | tf_op jit(solution)/shard_map/all_to_all | solution.py:400
  24.8 12.7 %all-to-all-done.packed_ref = bf16[4,128,640]{2,1,0:T(8,128)(2,1)S(1)} async-done(((bf16[4,128,640]{2,1,0:T(8,128)(2,1)}), bf16[4,128,640]{2,1,0:T(8,128)(2,1)S(1)}, u32[]{:S(2)}, u32[]{:S(2)}) %all-to-all-start) | async-done | bytes 655392 | tf_op jit(solution)/shard_map/all_to_all | solution.py:400
  37.6 1.4 unpack.1
  39.0 6.8 %all-to-all-start.1 = ((f32[8,4,128]{2,1,0:T(4,128)}), f32[8,4,128]{2,1,0:T(4,128)S(1)}, u32[]{:S(2)}, u32[]{:S(2)}) async-start(f32[8,4,128]{2,1,0:T(4,128)} %get-tuple-element.36), calls=%async_computation.1 | async-start | bytes 32768 | tf_op jit(solution)/shard_map/all_to_all | solution.py:400
  45.8 3.4 %collective-permute-start = (bf16[16,640]{1,0:T(8,128)(2,1)S(1)}, bf16[16,640]{1,0:T(8,128)(2,1)S(1)}, u32[]{:S(2)}, u32[]{:S(2)}) collective-permute-start(bf16[16,640]{1,0:T(8,128)(2,1)S(1)} %get-tuple-element.37), channel_id=1, source_target_pairs={{0,4},{4,8},{8,12},{12,16},{16,20},{20,24},{24,28},{1,5},{5,9},{9,... | collective-permute-start | bytes 61448 | tf_op jit(solution)/shard_map/ppermute | solution.py:463
  49.2 1.3 collective-permute-start.1
  50.5 3.6 %collective-permute-done.1.below_ref = bf16[16,640]{1,0:T(8,128)(2,1)S(1)} collective-permute-done((bf16[16,640]{1,0:T(8,128)(2,1)S(1)}, bf16[16,640]{1,0:T(8,128)(2,1)S(1)}, u32[]{:S(2)}, u32[]{:S(2)}) %collective-permute-start.1) | collective-permute-done | bytes 20512 | tf_op jit(solution)/shard_map/ppermute | solution.py:464
  54.1 1.5 copy-done.6
  55.6 1.6 %conv0.1 = (f32[4,192,128]{2,1,0:T(8,128)S(1)}, bf16[4,32,640]{2,1,0:T(8,128)(2,1)S(1)}, bf16[16,640]{1,0:T(8,128)(2,1)S(1)}, bf16[16,640]{1,0:T(8,128)(2,1)S(1)}) custom-call(f32[8,4,128]{2,1,0:T(4,128)S(1)} %all-to-all-done.1.stats_ref, bf16[16,640]{1,0:T(8,128)(2,1)S(1)} %collective-permute-done.above_ref, ...), custom_call_target="tpu_custom_call" | custom-call | flops 1073741824 | bytes 1048576 | tf_op jit(solution)/shard_map/conv0/pallas_call | solution.py:387
  57.3 22.3 %all_to_all.35.conv_ref = f32[4,192,128]{2,1,0:T(8,128)S(1)} all-to-all(f32[4,192,128]{2,1,0:T(8,128)S(1)} %get-tuple-element.44), channel_id=1, replica_groups=mesh['req'=16,'yh'=4,'yl'=2,'zh'=2,'core'=2] {'zh','core'}, dimensions={0} | all-to-all | bytes 786432 | tf_op jit(solution)/shard_map/all_to_all | solution.py:400
  79.6 1.4 hidden0.1
  81.0 6.7 %all-to-all-start.3 = ((f32[8,4,128]{2,1,0:T(4,128)}), f32[8,4,128]{2,1,0:T(4,128)S(1)}, u32[]{:S(2)}, u32[]{:S(2)}) async-start(f32[8,4,128]{2,1,0:T(4,128)} %get-tuple-element.47), calls=%async_computation.3 | async-start | bytes 32768 | tf_op jit(solution)/shard_map/all_to_all | solution.py:400
  87.7 3.3 %collective-permute-start.2 = (bf16[16,640]{1,0:T(8,128)(2,1)S(1)}, bf16[16,640]{1,0:T(8,128)(2,1)S(1)}, u32[]{:S(2)}, u32[]{:S(2)}) collective-permute-start(bf16[16,640]{1,0:T(8,128)(2,1)S(1)} %get-tuple-element.48), channel_id=1, source_target_pairs={{0,4},{4,8},{8,12},{12,16},{16,20},{20,24},{24,28},{1,5},{5,9},{9,... | collective-permute-start | bytes 61448 | tf_op jit(solution)/shard_map/ppermute | solution.py:484
  91.0 1.3 collective-permute-start.3
  92.3 3.7 %collective-permute-done.3.below_ref = bf16[16,640]{1,0:T(8,128)(2,1)S(1)} collective-permute-done((bf16[16,640]{1,0:T(8,128)(2,1)S(1)}, bf16[16,640]{1,0:T(8,128)(2,1)S(1)}, u32[]{:S(2)}, u32[]{:S(2)}) %collective-permute-start.3) | collective-permute-done | bytes 20512 | tf_op jit(solution)/shard_map/ppermute | solution.py:484
  97.4 1.3 copy-done.8
  98.7 3.7 %attend0.1 = (f32[4,32,640]{2,1,0:T(8,128)S(1)}, f32[8,4,128]{2,1,0:T(4,128)S(1)}) custom-call(s32[2]{0:T(128)S(1)} %pad_add_fusion.place_ref, bf16[128,384]{1,0:T(8,128)(2,1)S(1)} %get-tuple-element.53.asked_ref, bf16[128,640]{1,0:T(8,128)(2,1)} %get-tuple-element.54.fresh_ref, f32[4,32,640]{2,1,0:T(8,128)S(1)} %get-tuple-element.51.hidden_ref, ...), custom_call_target="tpu_custom_call" | custom-call | flops 1073741824 | bytes 1048576 | tf_op jit(solution)/shard_map/attend0/pallas_call | solution.py:387
  102.4 12.6 %all_to_all.36.stats_ref = f32[8,4,128]{2,1,0:T(4,128)S(1)} all-to-all(f32[8,4,128]{2,1,0:T(4,128)S(1)} %get-tuple-element.56), channel_id=1, replica_groups=mesh['req'=16,'yh'=4,'yl'=2,'zh'=2,'core'=2] {'yh','yl'}, dimensions={0} | all-to-all | bytes 32768 | tf_op jit(solution)/shard_map/all_to_all | solution.py:400
  115.0 2.3 %conv1.1 = (f32[4,48,128]{2,1,0:T(8,128)S(1)}, f32[8,4,128]{2,1,0:T(4,128)S(1)}) custom-call(s32[2]{0:T(128)S(1)} %pad_add_fusion.place_ref, f32[8,4,128]{2,1,0:T(4,128)S(1)} %all_to_all.36.stats_ref, bf16[16,640]{1,0:T(8,128)(2,1)S(1)} %collective-permute-done.2.above_ref, bf16[16,640]{1,0:T(8,128)(2,1)S(1)} %collective-permute-done.3.below_ref, ...), custom_call_target="tpu_custom_call" | custom-call | flops 1073741824 | bytes 1048576 | tf_op jit(solution)/shard_map/conv1/pallas_call | solution.py:387
  117.3 9.1 %all_to_all.37.stats_ref = f32[8,4,128]{2,1,0:T(4,128)S(1)} all-to-all(f32[8,4,128]{2,1,0:T(4,128)S(1)} %get-tuple-element.62), channel_id=1, replica_groups=mesh['req'=16,'yh'=4,'yl'=2,'zh'=2,'core'=2] {'yh','yl'}, dimensions={0} | all-to-all | bytes 32768 | tf_op jit(solution)/shard_map/all_to_all | solution.py:400
  126.4 19.1 %all_to_all.38.conv_ref = f32[4,56,128]{2,1,0:T(8,128)S(1)} all-to-all(f32[4,56,128]{2,1,0:T(8,128)S(1)} %insert1.1), channel_id=1, replica_groups=mesh['req'=16,'yh'=4,'yl'=2,'zh'=2,'core'=2] {'zh','core'}, dimensions={0} | all-to-all | bytes 229376 | tf_op jit(solution)/shard_map/all_to_all | solution.py:400
  145.5 1.3 copy-done.9
  146.8 3.5 %attend1.1 = f32[2,32,640]{2,1,0:T(8,128)} custom-call(s32[2]{0:T(128)S(1)} %pad_add_fusion.place_ref, f32[4,56,128]{2,1,0:T(8,128)S(1)} %all_to_all.38.conv_ref, f32[4,32,640]{2,1,0:T(8,128)S(1)} %get-tuple-element.59.state_ref, f32[8,640]{1,0:T(8,128)S(1)} %stack.40.vectors_ref, bf16[640,384]{1,0:T(8,128)(2,1)S(1)} %pad.4.query_ref, ...), custom_call_target="tpu_custom_call" | custom-call | flops 1073741824 | bytes 1048576 | tf_op jit(solution)/shard_map/attend1/pallas_call | solution.py:387
  (62 shorter events, 6.0 us)
Async XLA Ops:
  6.5 47.6 %all-gather.4.cloned.1.call-start = ((), (), s32[]{:S(2)}) async-start(), calls=%async_computation.7 | async-start | bytes 2119680 | tf_op jit(solution)/shard_map/all_gather | solution.py:427
  6.5 17.8 %copy-start.11 = (bf16[640,320]{0,1:T(8,128)(2,1)S(1)}, bf16[640,320]{0,1:T(8,128)(2,1)}, u32[]{:S(2)}) copy-start(bf16[640,320]{0,1:T(8,128)(2,1)} %param.25) | copy-start | bytes 1228804
  8.3 15.9 %copy-start.12 = (f32[2,640]{1,0:T(2,128)S(1)}, f32[2,640]{1,0:T(2,128)}, u32[]{:S(2)}) copy-start(f32[2,640]{1,0:T(2,128)} %param.22) | copy-start | bytes 15364
  8.3 16.0 %copy-start.13 = (f32[640]{0:T(1024)S(1)}, f32[640]{0:T(1024)}, u32[]{:S(2)}) copy-start(f32[640]{0:T(1024)} %param.21) | copy-start | bytes 7684
  8.3 16.0 %copy-start.14 = (f32[640]{0:T(1024)S(1)}, f32[640]{0:T(1024)}, u32[]{:S(2)}) copy-start(f32[640]{0:T(1024)} %param.18) | copy-start | bytes 7684
  8.3 16.0 %copy-start.15 = (f32[640]{0:T(1024)S(1)}, f32[640]{0:T(1024)}, u32[]{:S(2)}) copy-start(f32[640]{0:T(1024)} %param.19) | copy-start | bytes 7684
  8.3 16.0 %copy-start.16 = (f32[640]{0:T(1024)S(1)}, f32[640]{0:T(1024)}, u32[]{:S(2)}) copy-start(f32[640]{0:T(1024)} %param.23) | copy-start | bytes 7684
  8.3 16.1 %copy-start.17 = (f32[640]{0:T(1024)S(1)}, f32[640]{0:T(1024)}, u32[]{:S(2)}) copy-start(f32[640]{0:T(1024)} %param.24) | copy-start | bytes 7684
  12.4 25.1 %all-to-all-start = ((bf16[4,128,640]{2,1,0:T(8,128)(2,1)}), bf16[4,128,640]{2,1,0:T(8,128)(2,1)S(1)}, u32[]{:S(2)}, u32[]{:S(2)}) async-start(bf16[4,128,640]{2,1,0:T(8,128)(2,1)} %pack.1), calls=%async_computation | async-start | bytes 1310720 | tf_op jit(solution)/shard_map/all_to_all | solution.py:400
  24.2 13.4 %copy-start.2 = (f32[2,16,640]{2,1,0:T(8,128)S(1)}, f32[2,16,640]{2,1,0:T(8,128)}, u32[]{:S(2)}) copy-start(f32[2,16,640]{2,1,0:T(8,128)} %param.14) | copy-start | bytes 245764
  24.2 73.2 %all-gather.6.cloned.1.call-start = ((), (), s32[]{:S(2)}) async-start(), calls=%async_computation.8 | async-start | bytes 1474560 | tf_op jit(solution)/shard_map/all_gather | solution.py:460
  39.0 15.1 %all-to-all-start.1 = ((f32[8,4,128]{2,1,0:T(4,128)}), f32[8,4,128]{2,1,0:T(4,128)S(1)}, u32[]{:S(2)}, u32[]{:S(2)}) async-start(f32[8,4,128]{2,1,0:T(4,128)} %get-tuple-element.36), calls=%async_computation.1 | async-start | bytes 32768 | tf_op jit(solution)/shard_map/all_to_all | solution.py:400
  45.8 4.7 %collective-permute-start = (bf16[16,640]{1,0:T(8,128)(2,1)S(1)}, bf16[16,640]{1,0:T(8,128)(2,1)S(1)}, u32[]{:S(2)}, u32[]{:S(2)}) collective-permute-start(bf16[16,640]{1,0:T(8,128)(2,1)S(1)} %get-tuple-element.37), channel_id=1, source_target_pairs={{0,4},{4,8},{8,12},{12,16},{16,20},{20,24},{24,28},{1,5},{5,9},{9,... | collective-permute-start | bytes 61448 | tf_op jit(solution)/shard_map/ppermute | solution.py:463
  49.2 4.9 %collective-permute-start.1 = (bf16[16,640]{1,0:T(8,128)(2,1)S(1)}, bf16[16,640]{1,0:T(8,128)(2,1)S(1)}, u32[]{:S(2)}, u32[]{:S(2)}) collective-permute-start(bf16[16,640]{1,0:T(8,128)(2,1)S(1)} %get-tuple-element.38), channel_id=1, source_target_pairs={{4,0},{8,4},{12,8},{16,12},{20,16},{24,20},{28,24},{5,1},{9,5},{13... | collective-permute-start | bytes 61448 | tf_op jit(solution)/shard_map/ppermute | solution.py:464
  54.1 1.5 copy-start.6
  57.3 38.8 %copy-start = (bf16[640,640]{1,0:T(8,128)(2,1)S(1)}, bf16[640,640]{1,0:T(8,128)(2,1)}, u32[]{:S(2)}) copy-start(bf16[640,640]{1,0:T(8,128)(2,1)} %keyvalue_ref.3) | copy-start | bytes 2457604
  79.6 17.8 %copy-start.10 = (bf16[320,640]{1,0:T(8,128)(2,1)S(1)}, bf16[320,640]{1,0:T(8,128)(2,1)}, u32[]{:S(2)}) copy-start(bf16[320,640]{1,0:T(8,128)(2,1)} %out_ref.3) | copy-start | bytes 1228804
  81.0 15.1 %all-to-all-start.3 = ((f32[8,4,128]{2,1,0:T(4,128)}), f32[8,4,128]{2,1,0:T(4,128)S(1)}, u32[]{:S(2)}, u32[]{:S(2)}) async-start(f32[8,4,128]{2,1,0:T(4,128)} %get-tuple-element.47), calls=%async_computation.3 | async-start | bytes 32768 | tf_op jit(solution)/shard_map/all_to_all | solution.py:400
  87.7 57.8 %all-gather.8.cloned.1.call-start = ((), (), s32[]{:S(2)}) async-start(), calls=%async_computation.9 | async-start | bytes 1474560 | tf_op jit(solution)/shard_map/all_gather | solution.py:493
  87.7 4.6 %collective-permute-start.2 = (bf16[16,640]{1,0:T(8,128)(2,1)S(1)}, bf16[16,640]{1,0:T(8,128)(2,1)S(1)}, u32[]{:S(2)}, u32[]{:S(2)}) collective-permute-start(bf16[16,640]{1,0:T(8,128)(2,1)S(1)} %get-tuple-element.48), channel_id=1, source_target_pairs={{0,4},{4,8},{8,12},{12,16},{16,20},{20,24},{24,28},{1,5},{5,9},{9,... | collective-permute-start | bytes 61448 | tf_op jit(solution)/shard_map/ppermute | solution.py:484
  91.0 5.0 %collective-permute-start.3 = (bf16[16,640]{1,0:T(8,128)(2,1)S(1)}, bf16[16,640]{1,0:T(8,128)(2,1)S(1)}, u32[]{:S(2)}, u32[]{:S(2)}) collective-permute-start(bf16[16,640]{1,0:T(8,128)(2,1)S(1)} %get-tuple-element.49), channel_id=1, source_target_pairs={{4,0},{8,4},{12,8},{16,12},{20,16},{24,20},{28,24},{5,1},{9,5},{13... | collective-permute-start | bytes 61448 | tf_op jit(solution)/shard_map/ppermute | solution.py:484
  97.4 1.3 copy-start.8
  98.7 16.3 %copy-start.7 = (bf16[8,180,640]{2,1,0:T(8,128)(2,1)S(1)}, bf16[8,180,640]{2,1,0:T(8,128)(2,1)}, u32[]{:S(2)}) copy-start(bf16[8,180,640]{2,1,0:T(8,128)(2,1)} %all-gather.4.cloned.1.call-done.weight_ref) | copy-start | bytes 5529604
  145.5 1.3 copy-start.9
  (4 other events, 3.2 us)
Sparse Core Ops, SparseCore 0:
  9.4 44.3 all-gather.3
  55.9 40.4 all-gather.5
  98.5 39.4 all-gather.7

commit v10 on v9

--- a/solution.py
+++ b/solution.py
@@ -355,28 +355,35 @@
     tell_sums(result, group_matrix(), told_ref)
 
 
-def attend_own_kernel(
+def project_own_kernel(
     place_ref,
     conv_ref,
     state_ref,
     vectors_ref,
     query_ref,
     keyvalue_ref,
-    out_ref,
-    kv_ref,
-    result_ref,
-):
-    a = place_ref[1]
-    earlier = state_ref[a]
-    hidden = earlier + (assembled(conv_ref, ROWS) + vectors_ref[5:6])
+    hidden_ref,
+    asked_ref,
+    fresh_ref,
+):
+    hidden = state_ref[place_ref[1]] + (assembled(conv_ref, ROWS) + vectors_ref[5:6])
     sums = jnp.zeros((8, LANES), F32)
     for t in range(4):
         sums += conv_ref[t, 48:56]
     mean, scale = spread_sums(sums, group_matrix())
-    query, fresh = project(hidden, mean, scale, vectors_ref, query_ref, keyvalue_ref)
-    attended = attend(query, fresh, a, place_ref[0], kv_ref)
-    result_ref[0] = earlier
-    result_ref[1] = hidden + dot(attended, out_ref[...])
+    asked, fresh = project(hidden, mean, scale, vectors_ref, query_ref, keyvalue_ref)
+    hidden_ref[...] = hidden
+    asked_ref[...] = asked
+    fresh_ref[...] = fresh
+
+
+def attend_own_kernel(
+    place_ref, asked_ref, fresh_ref, hidden_ref, state_ref, out_ref, kv_ref, result_ref
+):
+    a = place_ref[1]
+    attended = attend(asked_ref[...], fresh_ref[...], a, place_ref[0], kv_ref)
+    result_ref[0] = state_ref[a]
+    result_ref[1] = hidden_ref[...] + dot(attended, out_ref[...])
 
 
 VMEM = pl.BlockSpec(memory_space=pltpu.VMEM)
@@ -515,11 +522,20 @@
         (conv, to_all(stats, Y)),
         flops=1 << 24,
     )
+    conv, kv = lax.optimization_barrier((to_all(conv, QUAD), kv))
+    hidden, asked, fresh = call(
+        project_own_kernel,
+        "project1",
+        [((ROWS, CHANNELS), F32), ((ROWS, 3 * LANES), BF16), ((ROWS, CHANNELS), BF16)],
+        (place, conv, state, vectors, w_query, w_keyvalue),
+        scalars=1,
+        flops=1 << 30,
+    )
     (out,) = call(
         attend_own_kernel,
         "attend1",
         [((2, ROWS, CHANNELS), F32)],
-        (place, to_all(conv, QUAD), state, vectors, w_query, w_keyvalue, w_out, kv),
+        (place, asked, fresh, hidden, state, w_out, kv),
         scalars=1,
         flops=1 << 30,
     )

time: 158 us -> 158 us (level)
    pallas_call x9 -> x10, Pallas kernels: 16.1 us -> 16.8 us  [call(): pl.pallas_call(kernel, name=name, out_shape=[jax.ShapeDtypeStruct(s, t) f...]
where the time goes in v10:
time: 158 us; the launch traced here: 157 us
  blocking collectives  63.1 us (40%)
  starting transfers between devices  34.6 us (22%)
  waiting for transfers between devices  20.1 us (13%)
  Pallas kernels  16.8 us (11%)
  between operations  13.4 us (8%)
  local copies, waits for them, and re-layouts  8.51 us (5%)
    all_to_all x4, blocking collectives, to_all(): return lax.all_to_all(value, axes, 0, 0, tiled=True)  63.1 us
    all_to_all x3, starting transfers between devices, to_all(): return lax.all_to_all(value, axes, 0, 0, tiled=True)  25.3 us
    pallas_call x10, Pallas kernels, call(): pl.pallas_call(kernel, name=name, out_shape=[jax.ShapeDtypeStruct(s, t) f...  16.8 us
    all_to_all x3, waiting for transfers between devices, to_all(): return lax.all_to_all(value, axes, 0, 0, tiled=True)  12.7 us
    unnamed x37, local copies, waits for them, and re-layouts  6.6 us
    ppermute x1, waiting for transfers between devices, per_device(): lax.ppermute(first, Y, down)  3.71 us
    ppermute x1, waiting for transfers between devices, per_device(): below = lax.ppermute(first, Y, down)  3.63 us
    ppermute x1, starting transfers between devices, per_device(): above = lax.ppermute(last, Y, up)  3.35 us
  transfers between devices with their start and end apart: 10, of which 3 were waited for; matrix products, arithmetic and copies ran while one was open for 0% of the time, Pallas kernels for 8%

profile of v10, /device:TPU:1, one launch (start us, length us, event | category | flops | bytes accessed | tf_op | source)
XLA Modules:
  0.0 156.5 jit_solution(14592813933437521187)
XLA Ops:
  6.5 1.8 %all_gather_reshape.3 = bf16[1,180,640]{2,1,0:T(8,128)(2,1)} reshape(bf16[3,3,20,640]{3,2,1,0:T(8,128)(2,1)} %bitcast.10) | data formatting | bytes 460800 | tf_op jit(solution)/shard_map/all_gather;reshape | solution.py:434
  12.5 11.8 %all-to-all-start = ((bf16[4,128,640]{2,1,0:T(8,128)(2,1)}), bf16[4,128,640]{2,1,0:T(8,128)(2,1)S(1)}, u32[]{:S(2)}, u32[]{:S(2)}) async-start(bf16[4,128,640]{2,1,0:T(8,128)(2,1)} %pack.1), calls=%async_computation | async-start | bytes 1310720 | tf_op jit(solution)/shard_map/all_to_all | solution.py:407
  24.9 12.7 %all-to-all-done.packed_ref = bf16[4,128,640]{2,1,0:T(8,128)(2,1)S(1)} async-done(((bf16[4,128,640]{2,1,0:T(8,128)(2,1)}), bf16[4,128,640]{2,1,0:T(8,128)(2,1)S(1)}, u32[]{:S(2)}, u32[]{:S(2)}) %all-to-all-start) | async-done | bytes 655392 | tf_op jit(solution)/shard_map/all_to_all | solution.py:407
  37.6 1.4 unpack.1
  39.0 6.8 %all-to-all-start.1 = ((f32[8,4,128]{2,1,0:T(4,128)}), f32[8,4,128]{2,1,0:T(4,128)S(1)}, u32[]{:S(2)}, u32[]{:S(2)}) async-start(f32[8,4,128]{2,1,0:T(4,128)} %get-tuple-element.41), calls=%async_computation.1 | async-start | bytes 32768 | tf_op jit(solution)/shard_map/all_to_all | solution.py:407
  45.9 3.4 %collective-permute-start = (bf16[16,640]{1,0:T(8,128)(2,1)S(1)}, bf16[16,640]{1,0:T(8,128)(2,1)S(1)}, u32[]{:S(2)}, u32[]{:S(2)}) collective-permute-start(bf16[16,640]{1,0:T(8,128)(2,1)S(1)} %get-tuple-element.42), channel_id=1, source_target_pairs={{0,4},{4,8},{8,12},{12,16},{16,20},{20,24},{24,28},{1,5},{5,9},{9,... | collective-permute-start | bytes 61448 | tf_op jit(solution)/shard_map/ppermute | solution.py:470
  49.2 1.3 collective-permute-start.1
  50.5 3.6 %collective-permute-done.1.below_ref = bf16[16,640]{1,0:T(8,128)(2,1)S(1)} collective-permute-done((bf16[16,640]{1,0:T(8,128)(2,1)S(1)}, bf16[16,640]{1,0:T(8,128)(2,1)S(1)}, u32[]{:S(2)}, u32[]{:S(2)}) %collective-permute-start.1) | collective-permute-done | bytes 20512 | tf_op jit(solution)/shard_map/ppermute | solution.py:471
  54.2 1.5 copy-done.6
  55.7 1.7 %conv0.1 = (f32[4,192,128]{2,1,0:T(8,128)S(1)}, bf16[4,32,640]{2,1,0:T(8,128)(2,1)S(1)}, bf16[16,640]{1,0:T(8,128)(2,1)S(1)}, bf16[16,640]{1,0:T(8,128)(2,1)S(1)}) custom-call(f32[8,4,128]{2,1,0:T(4,128)S(1)} %all-to-all-done.1.stats_ref, bf16[16,640]{1,0:T(8,128)(2,1)S(1)} %collective-permute-done.above_ref, ...), custom_call_target="tpu_custom_call" | custom-call | flops 1073741824 | bytes 1048576 | tf_op jit(solution)/shard_map/conv0/pallas_call | solution.py:394
  57.4 22.3 %all_to_all.35.conv_ref = f32[4,192,128]{2,1,0:T(8,128)S(1)} all-to-all(f32[4,192,128]{2,1,0:T(8,128)S(1)} %get-tuple-element.49), channel_id=1, replica_groups=mesh['req'=16,'yh'=4,'yl'=2,'zh'=2,'core'=2] {'zh','core'}, dimensions={0} | all-to-all | bytes 786432 | tf_op jit(solution)/shard_map/all_to_all | solution.py:407
  79.6 1.4 hidden0.1
  81.0 6.7 %all-to-all-start.3 = ((f32[8,4,128]{2,1,0:T(4,128)}), f32[8,4,128]{2,1,0:T(4,128)S(1)}, u32[]{:S(2)}, u32[]{:S(2)}) async-start(f32[8,4,128]{2,1,0:T(4,128)} %get-tuple-element.52), calls=%async_computation.3 | async-start | bytes 32768 | tf_op jit(solution)/shard_map/all_to_all | solution.py:407
  87.7 3.3 %collective-permute-start.2 = (bf16[16,640]{1,0:T(8,128)(2,1)S(1)}, bf16[16,640]{1,0:T(8,128)(2,1)S(1)}, u32[]{:S(2)}, u32[]{:S(2)}) collective-permute-start(bf16[16,640]{1,0:T(8,128)(2,1)S(1)} %get-tuple-element.53), channel_id=1, source_target_pairs={{0,4},{4,8},{8,12},{12,16},{16,20},{20,24},{24,28},{1,5},{5,9},{9,... | collective-permute-start | bytes 61448 | tf_op jit(solution)/shard_map/ppermute | solution.py:491
  91.1 1.3 collective-permute-start.3
  92.4 3.7 %collective-permute-done.3.below_ref = bf16[16,640]{1,0:T(8,128)(2,1)S(1)} collective-permute-done((bf16[16,640]{1,0:T(8,128)(2,1)S(1)}, bf16[16,640]{1,0:T(8,128)(2,1)S(1)}, u32[]{:S(2)}, u32[]{:S(2)}) %collective-permute-start.3) | collective-permute-done | bytes 20512 | tf_op jit(solution)/shard_map/ppermute | solution.py:491
  96.1 1.3 project0.1
  97.4 1.3 copy-done.8
  98.7 3.7 %attend0.1 = (f32[4,32,640]{2,1,0:T(8,128)S(1)}, f32[8,4,128]{2,1,0:T(4,128)S(1)}) custom-call(s32[2]{0:T(128)S(1)} %pad_add_fusion.place_ref, bf16[128,384]{1,0:T(8,128)(2,1)S(1)} %get-tuple-element.58.asked_ref, bf16[128,640]{1,0:T(8,128)(2,1)} %get-tuple-element.59.fresh_ref, f32[4,32,640]{2,1,0:T(8,128)S(1)} %get-tuple-element.56.hidden_ref, ...), custom_call_target="tpu_custom_call" | custom-call | flops 1073741824 | bytes 1048576 | tf_op jit(solution)/shard_map/attend0/pallas_call | solution.py:394
  102.4 12.6 %all_to_all.36.stats_ref = f32[8,4,128]{2,1,0:T(4,128)S(1)} all-to-all(f32[8,4,128]{2,1,0:T(4,128)S(1)} %get-tuple-element.61), channel_id=1, replica_groups=mesh['req'=16,'yh'=4,'yl'=2,'zh'=2,'core'=2] {'yh','yl'}, dimensions={0} | all-to-all | bytes 32768 | tf_op jit(solution)/shard_map/all_to_all | solution.py:407
  115.1 2.3 %conv1.1 = (f32[4,48,128]{2,1,0:T(8,128)S(1)}, f32[8,4,128]{2,1,0:T(4,128)S(1)}) custom-call(s32[2]{0:T(128)S(1)} %pad_add_fusion.place_ref, f32[8,4,128]{2,1,0:T(4,128)S(1)} %all_to_all.36.stats_ref, bf16[16,640]{1,0:T(8,128)(2,1)S(1)} %collective-permute-done.2.above_ref, bf16[16,640]{1,0:T(8,128)(2,1)S(1)} %collective-permute-done.3.below_ref, ...), custom_call_target="tpu_custom_call" | custom-call | flops 1073741824 | bytes 1048576 | tf_op jit(solution)/shard_map/conv1/pallas_call | solution.py:394
  117.4 9.1 %all_to_all.37.stats_ref = f32[8,4,128]{2,1,0:T(4,128)S(1)} all-to-all(f32[8,4,128]{2,1,0:T(4,128)S(1)} %get-tuple-element.67), channel_id=1, replica_groups=mesh['req'=16,'yh'=4,'yl'=2,'zh'=2,'core'=2] {'yh','yl'}, dimensions={0} | all-to-all | bytes 32768 | tf_op jit(solution)/shard_map/all_to_all | solution.py:407
  126.4 19.1 %all_to_all.38.conv_ref = f32[4,56,128]{2,1,0:T(8,128)S(1)} all-to-all(f32[4,56,128]{2,1,0:T(8,128)S(1)} %insert1.1), channel_id=1, replica_groups=mesh['req'=16,'yh'=4,'yl'=2,'zh'=2,'core'=2] {'zh','core'}, dimensions={0} | all-to-all | bytes 229376 | tf_op jit(solution)/shard_map/all_to_all | solution.py:407
  146.9 3.1 %attend1.1 = f32[2,32,640]{2,1,0:T(8,128)} custom-call(s32[2]{0:T(128)S(1)} %pad_add_fusion.place_ref, bf16[32,384]{1,0:T(8,128)(2,1)S(1)} %get-tuple-element.69.asked_ref, bf16[32,640]{1,0:T(8,128)(2,1)S(1)} %get-tuple-element.70.fresh_ref, f32[32,640]{1,0:T(8,128)S(1)} %get-tuple-element.71.hidden_ref, f32[4,32,640]{2,1,0:T(8,128)S(1)} %get-tuple-element.64.state_ref, ...), custom_call_target="tpu_custom_call" | custom-call | flops 1073741824 | bytes 1048576 | tf_op jit(solution)/shard_map/attend1/pallas_call | solution.py:394
  (63 shorter events, 6.1 us)
Async XLA Ops:
  6.5 47.7 %all-gather.4.cloned.1.call-start = ((), (), s32[]{:S(2)}) async-start(), calls=%async_computation.7 | async-start | bytes 2119680 | tf_op jit(solution)/shard_map/all_gather | solution.py:434
  6.5 17.9 %copy-start.11 = (bf16[640,320]{0,1:T(8,128)(2,1)S(1)}, bf16[640,320]{0,1:T(8,128)(2,1)}, u32[]{:S(2)}) copy-start(bf16[640,320]{0,1:T(8,128)(2,1)} %param.25) | copy-start | bytes 1228804
  8.3 15.9 %copy-start.12 = (f32[2,640]{1,0:T(2,128)S(1)}, f32[2,640]{1,0:T(2,128)}, u32[]{:S(2)}) copy-start(f32[2,640]{1,0:T(2,128)} %param.22) | copy-start | bytes 15364
  8.3 16.0 %copy-start.13 = (f32[640]{0:T(1024)S(1)}, f32[640]{0:T(1024)}, u32[]{:S(2)}) copy-start(f32[640]{0:T(1024)} %param.21) | copy-start | bytes 7684
  8.3 16.0 %copy-start.14 = (f32[640]{0:T(1024)S(1)}, f32[640]{0:T(1024)}, u32[]{:S(2)}) copy-start(f32[640]{0:T(1024)} %param.18) | copy-start | bytes 7684
  8.3 16.0 %copy-start.15 = (f32[640]{0:T(1024)S(1)}, f32[640]{0:T(1024)}, u32[]{:S(2)}) copy-start(f32[640]{0:T(1024)} %param.19) | copy-start | bytes 7684
  8.3 16.1 %copy-start.16 = (f32[640]{0:T(1024)S(1)}, f32[640]{0:T(1024)}, u32[]{:S(2)}) copy-start(f32[640]{0:T(1024)} %param.23) | copy-start | bytes 7684
  8.3 16.1 %copy-start.17 = (f32[640]{0:T(1024)S(1)}, f32[640]{0:T(1024)}, u32[]{:S(2)}) copy-start(f32[640]{0:T(1024)} %param.24) | copy-start | bytes 7684
  12.5 25.1 %all-to-all-start = ((bf16[4,128,640]{2,1,0:T(8,128)(2,1)}), bf16[4,128,640]{2,1,0:T(8,128)(2,1)S(1)}, u32[]{:S(2)}, u32[]{:S(2)}) async-start(bf16[4,128,640]{2,1,0:T(8,128)(2,1)} %pack.1), calls=%async_computation | async-start | bytes 1310720 | tf_op jit(solution)/shard_map/all_to_all | solution.py:407
  24.2 13.4 %copy-start.2 = (f32[2,16,640]{2,1,0:T(8,128)S(1)}, f32[2,16,640]{2,1,0:T(8,128)}, u32[]{:S(2)}) copy-start(f32[2,16,640]{2,1,0:T(8,128)} %param.14) | copy-start | bytes 245764
  24.2 73.2 %all-gather.6.cloned.1.call-start = ((), (), s32[]{:S(2)}) async-start(), calls=%async_computation.8 | async-start | bytes 1474560 | tf_op jit(solution)/shard_map/all_gather | solution.py:467
  39.0 15.1 %all-to-all-start.1 = ((f32[8,4,128]{2,1,0:T(4,128)}), f32[8,4,128]{2,1,0:T(4,128)S(1)}, u32[]{:S(2)}, u32[]{:S(2)}) async-start(f32[8,4,128]{2,1,0:T(4,128)} %get-tuple-element.41), calls=%async_computation.1 | async-start | bytes 32768 | tf_op jit(solution)/shard_map/all_to_all | solution.py:407
  45.9 4.7 %collective-permute-start = (bf16[16,640]{1,0:T(8,128)(2,1)S(1)}, bf16[16,640]{1,0:T(8,128)(2,1)S(1)}, u32[]{:S(2)}, u32[]{:S(2)}) collective-permute-start(bf16[16,640]{1,0:T(8,128)(2,1)S(1)} %get-tuple-element.42), channel_id=1, source_target_pairs={{0,4},{4,8},{8,12},{12,16},{16,20},{20,24},{24,28},{1,5},{5,9},{9,... | collective-permute-start | bytes 61448 | tf_op jit(solution)/shard_map/ppermute | solution.py:470
  49.2 4.9 %collective-permute-start.1 = (bf16[16,640]{1,0:T(8,128)(2,1)S(1)}, bf16[16,640]{1,0:T(8,128)(2,1)S(1)}, u32[]{:S(2)}, u32[]{:S(2)}) collective-permute-start(bf16[16,640]{1,0:T(8,128)(2,1)S(1)} %get-tuple-element.43), channel_id=1, source_target_pairs={{4,0},{8,4},{12,8},{16,12},{20,16},{24,20},{28,24},{5,1},{9,5},{13... | collective-permute-start | bytes 61448 | tf_op jit(solution)/shard_map/ppermute | solution.py:471
  54.2 1.5 copy-start.6
  57.4 38.7 %copy-start = (bf16[640,640]{1,0:T(8,128)(2,1)S(1)}, bf16[640,640]{1,0:T(8,128)(2,1)}, u32[]{:S(2)}) copy-start(bf16[640,640]{1,0:T(8,128)(2,1)} %keyvalue_ref.3) | copy-start | bytes 2457604
  79.6 17.8 %copy-start.10 = (bf16[320,640]{1,0:T(8,128)(2,1)S(1)}, bf16[320,640]{1,0:T(8,128)(2,1)}, u32[]{:S(2)}) copy-start(bf16[320,640]{1,0:T(8,128)(2,1)} %out_ref.3) | copy-start | bytes 1228804
  81.0 15.1 %all-to-all-start.3 = ((f32[8,4,128]{2,1,0:T(4,128)}), f32[8,4,128]{2,1,0:T(4,128)S(1)}, u32[]{:S(2)}, u32[]{:S(2)}) async-start(f32[8,4,128]{2,1,0:T(4,128)} %get-tuple-element.52), calls=%async_computation.3 | async-start | bytes 32768 | tf_op jit(solution)/shard_map/all_to_all | solution.py:407
  87.7 57.9 %all-gather.8.cloned.1.call-start = ((), (), s32[]{:S(2)}) async-start(), calls=%async_computation.9 | async-start | bytes 1474560 | tf_op jit(solution)/shard_map/all_gather | solution.py:500
  87.7 4.6 %collective-permute-start.2 = (bf16[16,640]{1,0:T(8,128)(2,1)S(1)}, bf16[16,640]{1,0:T(8,128)(2,1)S(1)}, u32[]{:S(2)}, u32[]{:S(2)}) collective-permute-start(bf16[16,640]{1,0:T(8,128)(2,1)S(1)} %get-tuple-element.53), channel_id=1, source_target_pairs={{0,4},{4,8},{8,12},{12,16},{16,20},{20,24},{24,28},{1,5},{5,9},{9,... | collective-permute-start | bytes 61448 | tf_op jit(solution)/shard_map/ppermute | solution.py:491
  91.1 5.0 %collective-permute-start.3 = (bf16[16,640]{1,0:T(8,128)(2,1)S(1)}, bf16[16,640]{1,0:T(8,128)(2,1)S(1)}, u32[]{:S(2)}, u32[]{:S(2)}) collective-permute-start(bf16[16,640]{1,0:T(8,128)(2,1)S(1)} %get-tuple-element.54), channel_id=1, source_target_pairs={{4,0},{8,4},{12,8},{16,12},{20,16},{24,20},{28,24},{5,1},{9,5},{13... | collective-permute-start | bytes 61448 | tf_op jit(solution)/shard_map/ppermute | solution.py:491
  97.4 1.3 copy-start.8
  98.7 16.3 %copy-start.7 = (bf16[8,180,640]{2,1,0:T(8,128)(2,1)S(1)}, bf16[8,180,640]{2,1,0:T(8,128)(2,1)}, u32[]{:S(2)}) copy-start(bf16[8,180,640]{2,1,0:T(8,128)(2,1)} %all-gather.4.cloned.1.call-done.weight_ref) | copy-start | bytes 5529604
  145.6 1.3 copy-start.9
  (4 other events, 3.2 us)
Sparse Core Ops, SparseCore 0:
  9.4 44.3 all-gather.3
  55.9 40.4 all-gather.5
  98.5 39.4 all-gather.7

commit v11 on v10

--- a/solution.py
+++ b/solution.py
@@ -381,7 +381,27 @@
     place_ref, asked_ref, fresh_ref, hidden_ref, state_ref, out_ref, kv_ref, result_ref
 ):
     a = place_ref[1]
-    attended = attend(asked_ref[...], fresh_ref[...], a, place_ref[0], kv_ref)
+    lane = lax.broadcasted_iota(jnp.int32, (ROWS, 3 * LANES), 1)
+    query = asked_ref[...].astype(F32)
+    heads = jnp.concatenate(
+        [jnp.where(lane >> 6 == h, query, 0.0) for h in range(HEADS)], axis=0
+    ).astype(BF16)
+    low, high = slice(0, 3 * LANES), slice(2 * LANES, 5 * LANES)
+    old = dot(heads, kv_ref[:, low], NT) * HEAD_DIM ** (-0.5)
+    block = lax.broadcasted_iota(jnp.int32, old.shape, 1) >> 5
+    old = jnp.where(block == 4 * place_ref[0] + a, -jnp.inf, old)
+    new = dot(heads, fresh_ref[:, low], NT) * HEAD_DIM ** (-0.5)
+    peak = jnp.maximum(jnp.max(old, axis=1, keepdims=True), jnp.max(new, axis=1, keepdims=True))
+    old = jnp.exp(old - peak)
+    new = jnp.exp(new - peak)
+    total = jnp.sum(old, axis=1, keepdims=True) + jnp.sum(new, axis=1, keepdims=True)
+    summed = dot(old.astype(BF16), kv_ref[:, high]) + dot(new.astype(BF16), fresh_ref[:, high])
+    summed = summed / total
+    attended = jnp.zeros((ROWS, 3 * LANES), F32)
+    for h in range(HEADS):
+        mine = summed[h * ROWS : (h + 1) * ROWS]
+        attended = jnp.where(lane >> 6 == h + 1, mine, attended)
+    attended = pltpu.roll(attended, 3 * LANES - HEAD_DIM, 1)[:, :WIDTH].astype(BF16)
     result_ref[0] = state_ref[a]
     result_ref[1] = hidden_ref[...] + dot(attended, out_ref[...])
 

time: 158 us -> 157 us (level)
  no operation moved by 1% of the time
where the time goes in v11:
time: 157 us; the launch traced here: 156 us
  blocking collectives  63.1 us (40%)
  starting transfers between devices  34.6 us (22%)
  waiting for transfers between devices  20.1 us (13%)
  Pallas kernels  16 us (10%)
  between operations  13.4 us (9%)
  local copies, waits for them, and re-layouts  8.51 us (5%)
    all_to_all x4, blocking collectives, to_all(): return lax.all_to_all(value, axes, 0, 0, tiled=True)  63.1 us
    all_to_all x3, starting transfers between devices, to_all(): return lax.all_to_all(value, axes, 0, 0, tiled=True)  25.3 us
    pallas_call x10, Pallas kernels, call(): pl.pallas_call(kernel, name=name, out_shape=[jax.ShapeDtypeStruct(s, t) f...  16 us
    all_to_all x3, waiting for transfers between devices, to_all(): return lax.all_to_all(value, axes, 0, 0, tiled=True)  12.7 us
    unnamed x37, local copies, waits for them, and re-layouts  6.6 us
    ppermute x1, waiting for transfers between devices, per_device(): lax.ppermute(first, Y, down)  3.71 us
    ppermute x1, waiting for transfers between devices, per_device(): below = lax.ppermute(first, Y, down)  3.63 us
    ppermute x1, starting transfers between devices, per_device(): above = lax.ppermute(last, Y, up)  3.35 us
  transfers between devices with their start and end apart: 10, of which 3 were waited for; matrix products, arithmetic and copies ran while one was open for 0% of the time, Pallas kernels for 8%

profile of v11, /device:TPU:1, one launch (start us, length us, event | category | flops | bytes accessed | tf_op | source)
XLA Modules:
  0.0 155.7 jit_solution(16753001685181336408)
XLA Ops:
  6.5 1.8 %all_gather_reshape.3 = bf16[1,180,640]{2,1,0:T(8,128)(2,1)} reshape(bf16[3,3,20,640]{3,2,1,0:T(8,128)(2,1)} %bitcast.10) | data formatting | bytes 460800 | tf_op jit(solution)/shard_map/all_gather;reshape | solution.py:454
  12.5 11.8 %all-to-all-start = ((bf16[4,128,640]{2,1,0:T(8,128)(2,1)}), bf16[4,128,640]{2,1,0:T(8,128)(2,1)S(1)}, u32[]{:S(2)}, u32[]{:S(2)}) async-start(bf16[4,128,640]{2,1,0:T(8,128)(2,1)} %pack.1), calls=%async_computation | async-start | bytes 1310720 | tf_op jit(solution)/shard_map/all_to_all | solution.py:427
  24.9 12.7 %all-to-all-done.packed_ref = bf16[4,128,640]{2,1,0:T(8,128)(2,1)S(1)} async-done(((bf16[4,128,640]{2,1,0:T(8,128)(2,1)}), bf16[4,128,640]{2,1,0:T(8,128)(2,1)S(1)}, u32[]{:S(2)}, u32[]{:S(2)}) %all-to-all-start) | async-done | bytes 655392 | tf_op jit(solution)/shard_map/all_to_all | solution.py:427
  37.6 1.4 unpack.1
  39.0 6.8 %all-to-all-start.1 = ((f32[8,4,128]{2,1,0:T(4,128)}), f32[8,4,128]{2,1,0:T(4,128)S(1)}, u32[]{:S(2)}, u32[]{:S(2)}) async-start(f32[8,4,128]{2,1,0:T(4,128)} %get-tuple-element.41), calls=%async_computation.1 | async-start | bytes 32768 | tf_op jit(solution)/shard_map/all_to_all | solution.py:427
  45.9 3.4 %collective-permute-start = (bf16[16,640]{1,0:T(8,128)(2,1)S(1)}, bf16[16,640]{1,0:T(8,128)(2,1)S(1)}, u32[]{:S(2)}, u32[]{:S(2)}) collective-permute-start(bf16[16,640]{1,0:T(8,128)(2,1)S(1)} %get-tuple-element.42), channel_id=1, source_target_pairs={{0,4},{4,8},{8,12},{12,16},{16,20},{20,24},{24,28},{1,5},{5,9},{9,... | collective-permute-start | bytes 61448 | tf_op jit(solution)/shard_map/ppermute | solution.py:490
  49.2 1.3 collective-permute-start.1
  50.5 3.6 %collective-permute-done.1.below_ref = bf16[16,640]{1,0:T(8,128)(2,1)S(1)} collective-permute-done((bf16[16,640]{1,0:T(8,128)(2,1)S(1)}, bf16[16,640]{1,0:T(8,128)(2,1)S(1)}, u32[]{:S(2)}, u32[]{:S(2)}) %collective-permute-start.1) | collective-permute-done | bytes 20512 | tf_op jit(solution)/shard_map/ppermute | solution.py:491
  54.2 1.5 copy-done.6
  55.7 1.7 %conv0.1 = (f32[4,192,128]{2,1,0:T(8,128)S(1)}, bf16[4,32,640]{2,1,0:T(8,128)(2,1)S(1)}, bf16[16,640]{1,0:T(8,128)(2,1)S(1)}, bf16[16,640]{1,0:T(8,128)(2,1)S(1)}) custom-call(f32[8,4,128]{2,1,0:T(4,128)S(1)} %all-to-all-done.1.stats_ref, bf16[16,640]{1,0:T(8,128)(2,1)S(1)} %collective-permute-done.above_ref, ...), custom_call_target="tpu_custom_call" | custom-call | flops 1073741824 | bytes 1048576 | tf_op jit(solution)/shard_map/conv0/pallas_call | solution.py:414
  57.4 22.3 %all_to_all.35.conv_ref = f32[4,192,128]{2,1,0:T(8,128)S(1)} all-to-all(f32[4,192,128]{2,1,0:T(8,128)S(1)} %get-tuple-element.49), channel_id=1, replica_groups=mesh['req'=16,'yh'=4,'yl'=2,'zh'=2,'core'=2] {'zh','core'}, dimensions={0} | all-to-all | bytes 786432 | tf_op jit(solution)/shard_map/all_to_all | solution.py:427
  79.6 1.4 hidden0.1
  81.0 6.7 %all-to-all-start.3 = ((f32[8,4,128]{2,1,0:T(4,128)}), f32[8,4,128]{2,1,0:T(4,128)S(1)}, u32[]{:S(2)}, u32[]{:S(2)}) async-start(f32[8,4,128]{2,1,0:T(4,128)} %get-tuple-element.52), calls=%async_computation.3 | async-start | bytes 32768 | tf_op jit(solution)/shard_map/all_to_all | solution.py:427
  87.7 3.3 %collective-permute-start.2 = (bf16[16,640]{1,0:T(8,128)(2,1)S(1)}, bf16[16,640]{1,0:T(8,128)(2,1)S(1)}, u32[]{:S(2)}, u32[]{:S(2)}) collective-permute-start(bf16[16,640]{1,0:T(8,128)(2,1)S(1)} %get-tuple-element.53), channel_id=1, source_target_pairs={{0,4},{4,8},{8,12},{12,16},{16,20},{20,24},{24,28},{1,5},{5,9},{9,... | collective-permute-start | bytes 61448 | tf_op jit(solution)/shard_map/ppermute | solution.py:511
  91.1 1.3 collective-permute-start.3
  92.4 3.7 %collective-permute-done.3.below_ref = bf16[16,640]{1,0:T(8,128)(2,1)S(1)} collective-permute-done((bf16[16,640]{1,0:T(8,128)(2,1)S(1)}, bf16[16,640]{1,0:T(8,128)(2,1)S(1)}, u32[]{:S(2)}, u32[]{:S(2)}) %collective-permute-start.3) | collective-permute-done | bytes 20512 | tf_op jit(solution)/shard_map/ppermute | solution.py:511
  96.1 1.3 project0.1
  97.4 1.3 copy-done.8
  98.7 3.7 %attend0.1 = (f32[4,32,640]{2,1,0:T(8,128)S(1)}, f32[8,4,128]{2,1,0:T(4,128)S(1)}) custom-call(s32[2]{0:T(128)S(1)} %pad_add_fusion.place_ref, bf16[128,384]{1,0:T(8,128)(2,1)S(1)} %get-tuple-element.58.asked_ref, bf16[128,640]{1,0:T(8,128)(2,1)} %get-tuple-element.59.fresh_ref, f32[4,32,640]{2,1,0:T(8,128)S(1)} %get-tuple-element.56.hidden_ref, ...), custom_call_target="tpu_custom_call" | custom-call | flops 1073741824 | bytes 1048576 | tf_op jit(solution)/shard_map/attend0/pallas_call | solution.py:414
  102.4 12.6 %all_to_all.36.stats_ref = f32[8,4,128]{2,1,0:T(4,128)S(1)} all-to-all(f32[8,4,128]{2,1,0:T(4,128)S(1)} %get-tuple-element.61), channel_id=1, replica_groups=mesh['req'=16,'yh'=4,'yl'=2,'zh'=2,'core'=2] {'yh','yl'}, dimensions={0} | all-to-all | bytes 32768 | tf_op jit(solution)/shard_map/all_to_all | solution.py:427
  115.1 2.3 %conv1.1 = (f32[4,48,128]{2,1,0:T(8,128)S(1)}, f32[8,4,128]{2,1,0:T(4,128)S(1)}) custom-call(s32[2]{0:T(128)S(1)} %pad_add_fusion.place_ref, f32[8,4,128]{2,1,0:T(4,128)S(1)} %all_to_all.36.stats_ref, bf16[16,640]{1,0:T(8,128)(2,1)S(1)} %collective-permute-done.2.above_ref, bf16[16,640]{1,0:T(8,128)(2,1)S(1)} %collective-permute-done.3.below_ref, ...), custom_call_target="tpu_custom_call" | custom-call | flops 1073741824 | bytes 1048576 | tf_op jit(solution)/shard_map/conv1/pallas_call | solution.py:414
  117.4 9.1 %all_to_all.37.stats_ref = f32[8,4,128]{2,1,0:T(4,128)S(1)} all-to-all(f32[8,4,128]{2,1,0:T(4,128)S(1)} %get-tuple-element.67), channel_id=1, replica_groups=mesh['req'=16,'yh'=4,'yl'=2,'zh'=2,'core'=2] {'yh','yl'}, dimensions={0} | all-to-all | bytes 32768 | tf_op jit(solution)/shard_map/all_to_all | solution.py:427
  126.4 19.1 %all_to_all.38.conv_ref = f32[4,56,128]{2,1,0:T(8,128)S(1)} all-to-all(f32[4,56,128]{2,1,0:T(8,128)S(1)} %insert1.1), channel_id=1, replica_groups=mesh['req'=16,'yh'=4,'yl'=2,'zh'=2,'core'=2] {'zh','core'}, dimensions={0} | all-to-all | bytes 229376 | tf_op jit(solution)/shard_map/all_to_all | solution.py:427
  146.9 2.3 %attend1.1 = f32[2,32,640]{2,1,0:T(8,128)} custom-call(s32[2]{0:T(128)S(1)} %pad_add_fusion.place_ref, bf16[32,384]{1,0:T(8,128)(2,1)S(1)} %get-tuple-element.69.asked_ref, bf16[32,640]{1,0:T(8,128)(2,1)S(1)} %get-tuple-element.70.fresh_ref, f32[32,640]{1,0:T(8,128)S(1)} %get-tuple-element.71.hidden_ref, f32[4,32,640]{2,1,0:T(8,128)S(1)} %get-tuple-element.64.state_ref, ...), custom_call_target="tpu_custom_call" | custom-call | flops 1073741824 | bytes 1048576 | tf_op jit(solution)/shard_map/attend1/pallas_call | solution.py:414
  (63 shorter events, 6.1 us)
Async XLA Ops:
  6.5 47.7 %all-gather.4.cloned.1.call-start = ((), (), s32[]{:S(2)}) async-start(), calls=%async_computation.7 | async-start | bytes 2119680 | tf_op jit(solution)/shard_map/all_gather | solution.py:454
  6.5 17.9 %copy-start.11 = (bf16[640,320]{0,1:T(8,128)(2,1)S(1)}, bf16[640,320]{0,1:T(8,128)(2,1)}, u32[]{:S(2)}) copy-start(bf16[640,320]{0,1:T(8,128)(2,1)} %param.25) | copy-start | bytes 1228804
  8.3 15.9 %copy-start.12 = (f32[2,640]{1,0:T(2,128)S(1)}, f32[2,640]{1,0:T(2,128)}, u32[]{:S(2)}) copy-start(f32[2,640]{1,0:T(2,128)} %param.22) | copy-start | bytes 15364
  8.3 16.0 %copy-start.13 = (f32[640]{0:T(1024)S(1)}, f32[640]{0:T(1024)}, u32[]{:S(2)}) copy-start(f32[640]{0:T(1024)} %param.21) | copy-start | bytes 7684
  8.3 16.0 %copy-start.14 = (f32[640]{0:T(1024)S(1)}, f32[640]{0:T(1024)}, u32[]{:S(2)}) copy-start(f32[640]{0:T(1024)} %param.18) | copy-start | bytes 7684
  8.3 16.0 %copy-start.15 = (f32[640]{0:T(1024)S(1)}, f32[640]{0:T(1024)}, u32[]{:S(2)}) copy-start(f32[640]{0:T(1024)} %param.19) | copy-start | bytes 7684
  8.3 16.1 %copy-start.16 = (f32[640]{0:T(1024)S(1)}, f32[640]{0:T(1024)}, u32[]{:S(2)}) copy-start(f32[640]{0:T(1024)} %param.23) | copy-start | bytes 7684
  8.3 16.1 %copy-start.17 = (f32[640]{0:T(1024)S(1)}, f32[640]{0:T(1024)}, u32[]{:S(2)}) copy-start(f32[640]{0:T(1024)} %param.24) | copy-start | bytes 7684
  12.5 25.1 %all-to-all-start = ((bf16[4,128,640]{2,1,0:T(8,128)(2,1)}), bf16[4,128,640]{2,1,0:T(8,128)(2,1)S(1)}, u32[]{:S(2)}, u32[]{:S(2)}) async-start(bf16[4,128,640]{2,1,0:T(8,128)(2,1)} %pack.1), calls=%async_computation | async-start | bytes 1310720 | tf_op jit(solution)/shard_map/all_to_all | solution.py:427
  24.2 13.4 %copy-start.2 = (f32[2,16,640]{2,1,0:T(8,128)S(1)}, f32[2,16,640]{2,1,0:T(8,128)}, u32[]{:S(2)}) copy-start(f32[2,16,640]{2,1,0:T(8,128)} %param.14) | copy-start | bytes 245764
  24.2 73.2 %all-gather.6.cloned.1.call-start = ((), (), s32[]{:S(2)}) async-start(), calls=%async_computation.8 | async-start | bytes 1474560 | tf_op jit(solution)/shard_map/all_gather | solution.py:487
  39.0 15.1 %all-to-all-start.1 = ((f32[8,4,128]{2,1,0:T(4,128)}), f32[8,4,128]{2,1,0:T(4,128)S(1)}, u32[]{:S(2)}, u32[]{:S(2)}) async-start(f32[8,4,128]{2,1,0:T(4,128)} %get-tuple-element.41), calls=%async_computation.1 | async-start | bytes 32768 | tf_op jit(solution)/shard_map/all_to_all | solution.py:427
  45.9 4.7 %collective-permute-start = (bf16[16,640]{1,0:T(8,128)(2,1)S(1)}, bf16[16,640]{1,0:T(8,128)(2,1)S(1)}, u32[]{:S(2)}, u32[]{:S(2)}) collective-permute-start(bf16[16,640]{1,0:T(8,128)(2,1)S(1)} %get-tuple-element.42), channel_id=1, source_target_pairs={{0,4},{4,8},{8,12},{12,16},{16,20},{20,24},{24,28},{1,5},{5,9},{9,... | collective-permute-start | bytes 61448 | tf_op jit(solution)/shard_map/ppermute | solution.py:490
  49.2 4.9 %collective-permute-start.1 = (bf16[16,640]{1,0:T(8,128)(2,1)S(1)}, bf16[16,640]{1,0:T(8,128)(2,1)S(1)}, u32[]{:S(2)}, u32[]{:S(2)}) collective-permute-start(bf16[16,640]{1,0:T(8,128)(2,1)S(1)} %get-tuple-element.43), channel_id=1, source_target_pairs={{4,0},{8,4},{12,8},{16,12},{20,16},{24,20},{28,24},{5,1},{9,5},{13... | collective-permute-start | bytes 61448 | tf_op jit(solution)/shard_map/ppermute | solution.py:491
  54.2 1.5 copy-start.6
  57.4 38.7 %copy-start = (bf16[640,640]{1,0:T(8,128)(2,1)S(1)}, bf16[640,640]{1,0:T(8,128)(2,1)}, u32[]{:S(2)}) copy-start(bf16[640,640]{1,0:T(8,128)(2,1)} %keyvalue_ref.3) | copy-start | bytes 2457604
  79.6 17.8 %copy-start.10 = (bf16[320,640]{1,0:T(8,128)(2,1)S(1)}, bf16[320,640]{1,0:T(8,128)(2,1)}, u32[]{:S(2)}) copy-start(bf16[320,640]{1,0:T(8,128)(2,1)} %out_ref.3) | copy-start | bytes 1228804
  81.0 15.1 %all-to-all-start.3 = ((f32[8,4,128]{2,1,0:T(4,128)}), f32[8,4,128]{2,1,0:T(4,128)S(1)}, u32[]{:S(2)}, u32[]{:S(2)}) async-start(f32[8,4,128]{2,1,0:T(4,128)} %get-tuple-element.52), calls=%async_computation.3 | async-start | bytes 32768 | tf_op jit(solution)/shard_map/all_to_all | solution.py:427
  87.7 57.9 %all-gather.8.cloned.1.call-start = ((), (), s32[]{:S(2)}) async-start(), calls=%async_computation.9 | async-start | bytes 1474560 | tf_op jit(solution)/shard_map/all_gather | solution.py:520
  87.7 4.6 %collective-permute-start.2 = (bf16[16,640]{1,0:T(8,128)(2,1)S(1)}, bf16[16,640]{1,0:T(8,128)(2,1)S(1)}, u32[]{:S(2)}, u32[]{:S(2)}) collective-permute-start(bf16[16,640]{1,0:T(8,128)(2,1)S(1)} %get-tuple-element.53), channel_id=1, source_target_pairs={{0,4},{4,8},{8,12},{12,16},{16,20},{20,24},{24,28},{1,5},{5,9},{9,... | collective-permute-start | bytes 61448 | tf_op jit(solution)/shard_map/ppermute | solution.py:511
  91.1 5.0 %collective-permute-start.3 = (bf16[16,640]{1,0:T(8,128)(2,1)S(1)}, bf16[16,640]{1,0:T(8,128)(2,1)S(1)}, u32[]{:S(2)}, u32[]{:S(2)}) collective-permute-start(bf16[16,640]{1,0:T(8,128)(2,1)S(1)} %get-tuple-element.54), channel_id=1, source_target_pairs={{4,0},{8,4},{12,8},{16,12},{20,16},{24,20},{28,24},{5,1},{9,5},{13... | collective-permute-start | bytes 61448 | tf_op jit(solution)/shard_map/ppermute | solution.py:511
  97.4 1.3 copy-start.8
  98.7 16.3 %copy-start.7 = (bf16[8,180,640]{2,1,0:T(8,128)(2,1)S(1)}, bf16[8,180,640]{2,1,0:T(8,128)(2,1)}, u32[]{:S(2)}) copy-start(bf16[8,180,640]{2,1,0:T(8,128)(2,1)} %all-gather.4.cloned.1.call-done.weight_ref) | copy-start | bytes 5529604
  145.6 1.3 copy-start.9
  (4 other events, 3.2 us)
Sparse Core Ops, SparseCore 0:
  9.4 44.3 all-gather.3
  55.9 40.4 all-gather.5
  98.5 39.4 all-gather.7
